TPU v7x, 8 devices: a whole 2x2x1 slice. The times are simulated.
8 devices in a mesh: dp: 2 (over z, y), tp: 4 (over x, core).
Axes of the slice: x: 2, y: 2, z: 1, core: 2. Of those that a mesh axis runs over, the one named last changes fastest.
Arguments:
- token_ids: int32 [512], P('dp'), parts along dimension 0
- emb_table: bfloat16 [50304, 1024], P('tp')
- norm_gain: bfloat16 [1024], replicated
- w_in: bfloat16 [1024, 4096], P(None, 'tp')
- w_out: bfloat16 [4096, 1024], P('tp')
- d_out: bfloat16 [512, 1024], P(('dp', 'tp')), parts along dimension 0
Outputs:
- output 1: bfloat16 [512, 1024], P(('dp', 'tp')), parts along dimension 0
- output 2: float32 [100608, 1024], P(('dp', 'tp')), parts along dimension 0
- output 3: float32 [2048, 4096], P('dp', 'tp'), parts along dimension 0
- output 4: float32 [8192, 1024], P(('dp', 'tp')), parts along dimension 0
There are 2 independent parts. A program takes and returns all parts, laid end to end along the dimension named above; an argument that names none is the same for every part.
All inputs are finite; a program needn't handle non-finite values.
Results may differ from a plain program's by a relative error of at most 0.00879555.
Values are sent between devices in bfloat16 or wider.
A program may use at most 1 GiB of HBM per device.

v0:
```python
import jax
import jax.numpy as jnp
from jax import lax
from jax.sharding import PartitionSpec as P

EPS = 1e-6


def solution(mesh):
    def shard_step(token_ids, emb_table, norm_gain, w_in, w_out, d_out):
        shard_rank = lax.axis_index("tp")
        vocab_local = emb_table.shape[0]
        local_ids = token_ids - shard_rank * vocab_local
        is_owned = (local_ids >= 0) & (local_ids < vocab_local)
        table_rows = jnp.take(emb_table, jnp.where(is_owned, local_ids, 0), axis=0)
        lookup_part = jnp.where(is_owned[:, None], table_rows, jnp.zeros((), table_rows.dtype))
        embedded = lax.psum_scatter(lookup_part, "tp", scatter_dimension=0, tiled=True)
        embedded_f32 = embedded.astype(jnp.float32)
        inv_rms = lax.rsqrt(jnp.mean(embedded_f32 * embedded_f32, axis=-1, keepdims=True) + EPS)
        gain_f32 = norm_gain.astype(jnp.float32)
        normed_local = (embedded_f32 * inv_rms * gain_f32).astype(jnp.bfloat16)
        normed = lax.all_gather(normed_local, "tp", axis=0, tiled=True)
        pre_act = jnp.dot(normed, w_in, preferred_element_type=jnp.float32).astype(jnp.bfloat16)
        act_f32, gelu_vjp = jax.vjp(jax.nn.gelu, pre_act.astype(jnp.float32))
        hidden = act_f32.astype(jnp.bfloat16)
        mlp_part = jnp.dot(hidden, w_out, preferred_element_type=jnp.float32)
        mlp_out = lax.psum_scatter(mlp_part, "tp", scatter_dimension=0, tiled=True)
        block_out = (embedded_f32 + mlp_out).astype(jnp.bfloat16)

        d_out_full = lax.all_gather(d_out, "tp", axis=0, tiled=True)
        d_hidden = lax.dot_general(d_out_full, w_out, (((1,), (1,)), ((), ())), preferred_element_type=jnp.float32).astype(jnp.bfloat16)
        d_w_out = lax.dot_general(hidden, d_out_full, (((0,), (0,)), ((), ())), preferred_element_type=jnp.float32)
        (d_pre_f32,) = gelu_vjp(d_hidden.astype(jnp.float32))
        d_pre = d_pre_f32.astype(jnp.bfloat16)
        d_w_in = lax.dot_general(normed, d_pre, (((0,), (0,)), ((), ())), preferred_element_type=jnp.float32)
        d_norm_part = lax.dot_general(d_pre, w_in, (((1,), (1,)), ((), ())), preferred_element_type=jnp.float32)
        d_normed = lax.psum_scatter(d_norm_part, "tp", scatter_dimension=0, tiled=True)
        d_scaled = d_normed * gain_f32
        row_proj = jnp.mean(d_scaled * embedded_f32, axis=-1, keepdims=True)
        d_emb = (d_out.astype(jnp.float32) + inv_rms * (d_scaled - embedded_f32 * inv_rms * inv_rms * row_proj)).astype(jnp.bfloat16)
        d_emb_full = lax.all_gather(d_emb, "tp", axis=0, tiled=True)
        target_rows = jnp.where(is_owned, local_ids, vocab_local)
        d_table = jax.ops.segment_sum(d_emb_full.astype(jnp.float32), target_rows, num_segments=vocab_local)
        return block_out, d_table, d_w_in, d_w_out

    return jax.shard_map(
        shard_step,
        mesh=mesh,
        in_specs=(P("dp"), P("tp", None), P(None), P(None, "tp"), P("tp", None), P(("dp", "tp"), None)),
        out_specs=(P(("dp", "tp"), None), P(("dp", "tp"), None), P("dp", "tp"), P(("dp", "tp"), None)),
        check_vma=False,
    )
```

profile of v0, /device:TPU:0, one launch (start us, length us, event | category | flops | bytes accessed | tf_op | source)
XLA Modules:
  0.0 140.3 jit_solution(4536552907930655449)
XLA Ops:
  7.2 0.0 copy-start
  7.2 0.0 reduce-scatter.4.cloned.1.call-start
  7.2 0.8 compare_and_fusion
  8.1 0.0 copy-start.9
  8.1 0.0 copy-start.7
  8.1 13.2 %gather_fusion = bf16[256,1024]{1,0:T(8,128)(2,1)S(1)} fusion(bf16[12576,1024]{1,0:T(8,128)(2,1)} %param.7, s32[1024]{0:T(1024)S(1)} %pad_clamp_fusion), kind=kCustom, calls=%fused_computation | custom fusion | bytes 1049600 | tf_op jit(solution)/shard_map/jit(_take)/gather | solution.py:15
  21.3 0.9 select_select_fusion
  22.3 0.0 reduce-scatter.4.cloned.1.call-update
  22.3 0.0 reduce-scatter.8.cloned.1.call-start
  22.3 0.0 copy-done.9
  22.4 0.0 copy-done.7
  22.4 11.9 %all_gather.10 = bf16[256,1024]{1,0:T(8,128)(2,1)S(1)} all-gather(bf16[64,1024]{1,0:T(8,128)(2,1)S(1)} %copy-done.7), channel_id=1, replica_groups=mesh['dp'=2,'tp'=4] {'tp'}, dimensions={0}, use_global_device_ids=true | all-gather | bytes 655360 | tf_op jit(solution)/shard_map/all_gather | solution.py:30
  34.2 7.0 %reduce-scatter.4.cloned.1.call-done = bf16[64,1024]{1,0:T(8,128)(2,1)} async-done(((bf16[256,1024]{1,0:T(8,128)(2,1)}), bf16[64,1024]{1,0:T(8,128)(2,1)}) %reduce-scatter.4.cloned.1.call-update) | async-done | bytes 131088 | tf_op jit(solution)/shard_map/reduce_scatter | solution.py:17
  41.3 1.0 fusion.22
  42.3 1.0 fusion.16
  43.3 0.0 copy-start.10
  43.3 9.4 %all_gather.9 = bf16[256,1024]{1,0:T(8,128)(2,1)S(1)} all-gather(bf16[64,1024]{1,0:T(8,128)(2,1)S(1)} %fusion.16), channel_id=1, replica_groups=mesh['dp'=2,'tp'=4] {'tp'}, dimensions={0}, use_global_device_ids=true | all-gather | bytes 655360 | tf_op jit(solution)/shard_map/all_gather | solution.py:22
  52.8 0.0 copy-done
  52.8 0.7 convolution_convert_fusion.1
  53.5 0.0 copy-done.10
  53.5 0.0 copy-start.5
  53.5 1.3 fusion.5
  54.9 0.0 copy-done.5
  54.9 0.0 copy-start.2
  54.9 0.8 copy-done.2
  55.7 1.7 %fusion.29 = f32[256,1024]{1,0:T(8,128)} fusion(bf16[256,1024]{1,0:T(8,128)(2,1)S(1)} %fusion.5, bf16[1024,1024]{1,0:T(8,128)(2,1)S(1)} %copy-done), kind=kOutput, calls=%fused_computation.49 | convolution fusion | flops 536870912 | bytes 3670016 | tf_op jit(solution)/shard_map/dot_general | solution.py:36
  57.4 0.0 reduce-scatter.8.cloned.1.call-update
  57.4 0.0 copy-start.8
  57.4 0.0 copy-start.6
  57.4 0.0 reduce-scatter.6.cloned.1.call-start
  57.5 3.6 %fusion.27 = f32[256,1024]{1,0:T(8,128)} fusion(bf16[1024,1024]{1,0:T(8,128)(2,1)} %param.10, bf16[256,1024]{1,0:T(8,128)(2,1)} %copy-done.5), kind=kOutput, calls=%fused_computation.48 | convolution fusion | flops 539492352 | bytes 3670016 | tf_op jit(solution)/shard_map/dot_general | solution.py:26
  61.1 0.0 reduce-scatter.6.cloned.1.call-update
  61.1 0.0 copy-done.8
  61.2 0.0 copy-done.6
  61.2 0.0 copy-start.3
  61.2 3.0 %fusion.25 = f32[1024,1024]{1,0:T(8,128)} fusion(bf16[256,1024]{1,0:T(8,128)(2,1)S(1)} %all_gather.10, bf16[256,1024]{1,0:T(8,128)(2,1)S(1)} %copy-done.6), kind=kOutput, calls=%fused_computation.47 | convolution fusion | flops 539492352 | bytes 5242880 | tf_op jit(solution)/shard_map/dot_general | solution.py:32
  64.2 0.0 copy-done.3
  64.2 0.0 copy-start.4
  64.2 2.8 %fusion.30 = f32[1024,1024]{1,0:T(8,128)} fusion(bf16[256,1024]{1,0:T(8,128)(2,1)S(1)} %all_gather.9, bf16[256,1024]{1,0:T(8,128)(2,1)S(1)} %copy-done.3), kind=kOutput, calls=%fused_computation.50 | convolution fusion | flops 536870912 | bytes 5242880 | tf_op jit(solution)/shard_map/dot_general | solution.py:35
  66.9 10.4 %reduce-scatter.8.cloned.1.call-done = f32[64,1024]{1,0:T(8,128)} async-done(((f32[256,1024]{1,0:T(8,128)}), f32[64,1024]{1,0:T(8,128)}) %reduce-scatter.8.cloned.1.call-update) | async-done | bytes 262160 | tf_op jit(solution)/shard_map/reduce_scatter | solution.py:37
  77.4 0.0 copy-done.4
  77.4 1.1 fusion.24
  78.5 20.6 %reduce-scatter.6.cloned.1.call-done = f32[64,1024]{1,0:T(8,128)} async-done(((f32[256,1024]{1,0:T(8,128)}), f32[64,1024]{1,0:T(8,128)}) %reduce-scatter.6.cloned.1.call-update) | async-done | bytes 262160 | tf_op jit(solution)/shard_map/reduce_scatter | solution.py:27
  99.0 1.7 %fusion.21 = (bf16[64,1024]{1,0:T(8,128)(2,1)S(1)}, bf16[64,1024]{1,0:T(8,128)(2,1)}) fusion(bf16[64,1024]{1,0:T(8,128)(2,1)S(1)} %copy-done.4, bf16[64,1024]{1,0:T(8,128)(2,1)S(1)} %copy-done.7, f32[64,1024]{1,0:T(8,128)} %reduce-scatter.8.cloned.1.call-done, f32[64]{0:T(128)S(1)} %broadcast_multiply_fusion, f32[1024]{0:T(1024)S(1)} %convert_element_type.40, ...), kind=kLoop, calls=%fused_computation.36 | loop fusion | flops 786432 | bytes 1053184 | tf_op jit(solution)/shard_map/convert_element_type | solution.py:40
  100.8 9.5 %all_gather.11 = bf16[256,1024]{1,0:T(8,128)(2,1)S(1)} all-gather(bf16[64,1024]{1,0:T(8,128)(2,1)S(1)} %get-tuple-element.6), channel_id=1, replica_groups=mesh['dp'=2,'tp'=4] {'tp'}, dimensions={0}, use_global_device_ids=true | all-gather | bytes 655360 | tf_op jit(solution)/shard_map/all_gather | solution.py:41
  110.2 0.0 copy-start.1
  110.2 23.5 %scatter_custom_fusion = f32[12576,1024]{1,0:T(8,128)} fusion(s32[256]{0:T(256)S(1)} %subtract_select_fusion, f32[]{:T(128)} %constant.21.clone.1, bf16[256,1024]{1,0:T(8,128)(2,1)S(1)} %all_gather.11), kind=kCustom, calls=%fused_computation.2 | custom fusion | flops 524288 | bytes 52035588 | tf_op jit(solution)/shard_map/scatter-add | solution.py:43
  133.8 0.0 copy-done.1
  (5 shorter events, 0.0 us)
Async XLA Ops:
  7.2 45.6 %copy-start = (bf16[1024,1024]{1,0:T(8,128)(2,1)S(1)}, bf16[1024,1024]{1,0:T(8,128)(2,1)}, u32[]{:S(2)}) copy-start(bf16[1024,1024]{1,0:T(8,128)(2,1)} %param.9) | copy-start | bytes 6291460
  7.2 34.1 %reduce-scatter.4.cloned.1.call-start = ((), (), s32[]{:S(2)}) async-start(), calls=%async_computation.3 | async-start | bytes 655360 | tf_op jit(solution)/shard_map/reduce_scatter | solution.py:17
  8.1 14.3 %copy-start.9 = (bf16[1024]{0:T(1024)(128)(2,1)S(1)}, bf16[1024]{0:T(1024)(128)(2,1)}, u32[]{:S(2)}) copy-start(bf16[1024]{0:T(1024)(128)(2,1)} %param.8) | copy-start | bytes 6148
  8.1 14.3 %copy-start.7 = (bf16[64,1024]{1,0:T(8,128)(2,1)S(1)}, bf16[64,1024]{1,0:T(8,128)(2,1)}, u32[]{:S(2)}) copy-start(bf16[64,1024]{1,0:T(8,128)(2,1)} %param.11) | copy-start | bytes 393220
  22.3 55.1 %reduce-scatter.8.cloned.1.call-start = ((), (), s32[]{:S(2)}) async-start(), calls=%async_computation.5 | async-start | bytes 1310720 | tf_op jit(solution)/shard_map/reduce_scatter | solution.py:37
  43.3 10.2 %copy-start.10 = (bf16[1024,1024]{1,0:T(8,128)(2,1)S(1)}, bf16[1024,1024]{1,0:T(8,128)(2,1)}, u32[]{:S(2)}) copy-start(bf16[1024,1024]{1,0:T(8,128)(2,1)} %param.10) | copy-start | bytes 6291460
  53.5 1.3 copy-start.5
  54.9 0.8 copy-start.2
  57.4 3.7 %copy-start.8 = (s32[256]{0:T(256)S(1)}, s32[256]{0:T(256)}, u32[]{:S(2)}) copy-start(s32[256]{0:T(256)} %param.6) | copy-start | bytes 3076
  57.4 3.7 %copy-start.6 = (bf16[256,1024]{1,0:T(8,128)(2,1)S(1)}, bf16[256,1024]{1,0:T(8,128)(2,1)}, u32[]{:S(2)}) copy-start(bf16[256,1024]{1,0:T(8,128)(2,1)} %copy-done.5) | copy-start | bytes 1572868
  57.4 41.6 %reduce-scatter.6.cloned.1.call-start = ((), (), s32[]{:S(2)}) async-start(), calls=%async_computation.4 | async-start | bytes 1310720 | tf_op jit(solution)/shard_map/reduce_scatter | solution.py:27
  61.2 3.0 %copy-start.3 = (bf16[256,1024]{1,0:T(8,128)(2,1)S(1)}, bf16[256,1024]{1,0:T(8,128)(2,1)}, u32[]{:S(2)}) copy-start(bf16[256,1024]{1,0:T(8,128)(2,1)} %copy-done.2) | copy-start | bytes 1572868
  64.2 13.2 %copy-start.4 = (bf16[64,1024]{1,0:T(8,128)(2,1)S(1)}, bf16[64,1024]{1,0:T(8,128)(2,1)}, u32[]{:S(2)}) copy-start(bf16[64,1024]{1,0:T(8,128)(2,1)} %reduce-scatter.4.cloned.1.call-done) | copy-start | bytes 393220
  110.2 23.5 %copy-start.1 = (bf16[1024,1024]{1,0:T(8,128)(2,1)S(1)}, bf16[1024,1024]{1,0:T(8,128)(2,1)}, u32[]{:S(2)}) copy-start(bf16[1024,1024]{1,0:T(8,128)(2,1)} %param.9) | copy-start | bytes 6291460
Sparse Core Ops, SparseCore 0:
  22.4 18.8 reduce-scatter.3
  57.5 19.7 reduce-scatter.7
  79.9 19.1 reduce-scatter.5
where the time goes:
time: 141 us; the launch traced here: 140 us
  waiting for transfers between devices  38.1 us (27%)
  blocking collectives  30.8 us (22%)
  other arithmetic  30.2 us (21%)
  local copies, waits for them, and re-layouts  14.1 us (10%)
  between operations  13.9 us (10%)
  matrix products  13.1 us (9%)
    scatter-add x1, other arithmetic, shard_step(): jax.ops.segment_sum(d_emb_full.astype(jnp.float32), target_rows, num_segm...  23.5 us
    reduce_scatter x1, waiting for transfers between devices, shard_step(): mlp_out = lax.psum_scatter(mlp_part, 'tp', scatter_dimension=0, tiled=True)  20.6 us
    gather x1, local copies, waits for them, and re-layouts, shard_step(): table_rows = jnp.take(emb_table, jnp.where(is_owned, local_ids, 0), axis=0)  13.2 us
    all_gather x1, blocking collectives, shard_step(): d_out_full = lax.all_gather(d_out, 'tp', axis=0, tiled=True)  11.9 us
    reduce_scatter x1, waiting for transfers between devices, shard_step(): lax.psum_scatter(d_norm_part, 'tp', scatter_dimension=0, tiled=True)  10.4 us
    all_gather x1, blocking collectives, shard_step(): d_emb_full = lax.all_gather(d_emb, 'tp', axis=0, tiled=True)  9.47 us
    all_gather x1, blocking collectives, shard_step(): normed = lax.all_gather(normed_local, 'tp', axis=0, tiled=True)  9.45 us
    reduce_scatter x1, waiting for transfers between devices, shard_step(): lax.psum_scatter(lookup_part, 'tp', scatter_dimension=0, tiled=True)  7.03 us
  transfers between devices with their start and end apart: 3, of which 3 were waited for; matrix products, arithmetic and copies ran while one was open for 7% of the time, Pallas kernels for 0%

commit v1 on v0

v1 whole, which is shorter than its diff:
```python
import jax
import jax.numpy as jnp
from jax import lax
from jax.experimental import pallas as pl
from jax.experimental.pallas import tpu as pltpu
from jax.sharding import PartitionSpec as P

EPS = 1e-6
BF = jnp.bfloat16
F32 = jnp.float32
I32 = jnp.int32
GELU_C = 0.7978845608028654
GELU_A = 0.044715
VMEM = pltpu.VMEM
SMEM_SPEC = pl.BlockSpec(memory_space=pltpu.SMEM)
ANY_SPEC = pl.BlockSpec(memory_space=pl.ANY)
HBM_SPEC = pl.BlockSpec(memory_space=pltpu.HBM)
VMEM_SPEC = pl.BlockSpec(memory_space=VMEM)
DMA = pltpu.SemaphoreType.DMA
TILE = 256
ZERO_ROWS = 96
FILL_0, FILL_1, FILL_2 = 20, 52, 41
MIB = 1 << 20


def mm(a, b, ca, cb):
    return lax.dot_general(a, b, (((ca,), (cb,)), ((), ())), preferred_element_type=F32)


def sh(shape, dtype):
    return jax.ShapeDtypeStruct(shape, dtype)


def fill_copy(zero, table_g, sem, i):
    return pltpu.make_async_copy(zero, table_g.at[pl.ds(pl.multiple_of(i * ZERO_ROWS, ZERO_ROWS), ZERO_ROWS)], sem)


def fill_start(zero, table_g, sem, lo, hi):
    zero[...] = jnp.zeros_like(zero)

    def body(i, carry):
        fill_copy(zero, table_g, sem, i).start()
        return carry

    lax.fori_loop(lo, hi, body, 0)


def fill_wait(zero, table_g, sem, lo, hi):
    def body(i, carry):
        fill_copy(zero, table_g, sem, i).wait()
        return carry

    lax.fori_loop(lo, hi, body, 0)


def swap_with_sibling():
    sib = lax.axis_index("tp") ^ 1
    barrier = pltpu.get_barrier_semaphore()
    pl.semaphore_signal(barrier, inc=1, device_id={"tp": sib}, device_id_type=pl.DeviceIdType.MESH)
    pl.semaphore_wait(barrier, 1)

    def remote(src, dst, sems, i):
        return pltpu.make_async_remote_copy(
            src_ref=src, dst_ref=dst, send_sem=sems.at[0, i], recv_sem=sems.at[1, i],
            device_id={"tp": sib}, device_id_type=pl.DeviceIdType.MESH)

    return remote


def lookup_kernel(ids_s, ids_v, table, d_out, part, flags, same, d_own, table_g, slabs, zero, sems, s_zero, s_d):
    tokens, vocab = part.shape[0], table.shape[0]
    base = lax.axis_index("tp") * vocab
    group = 32
    groups = tokens // group

    def fetch(i, carry):
        lid = ids_s[i] - base
        owned = (lid >= 0) & (lid < vocab)
        slab = jnp.where(owned, lid >> 3, i)
        pltpu.make_async_copy(
            table.at[pl.ds(pl.multiple_of(slab << 3, 8), 8)],
            slabs.at[pl.ds(pl.multiple_of(i * 8, 8), 8)],
            sems.at[i // group],
        ).start()
        return carry

    lax.fori_loop(0, tokens, fetch, 0, unroll=8)
    load = pltpu.make_async_copy(d_out, d_own, s_d)
    load.start()
    fill_start(zero, table_g, s_zero, 0, FILL_0)
    row = jnp.broadcast_to(ids_v[...].astype(F32), (tokens, tokens))
    col = row.T
    equal = row == col
    same[...] = jnp.where(equal, 1.0, 0.0).astype(BF)
    earlier = lax.broadcasted_iota(I32, (tokens, tokens), 0) < lax.broadcasted_iota(I32, (tokens, tokens), 1)
    flags[...] = jnp.max(jnp.where(equal & earlier, 1, 0), axis=0, keepdims=True)
    ids_col = col.astype(I32) - base
    lane = lax.broadcasted_iota(I32, (group, group * 8), 1)
    first = lax.broadcasted_iota(I32, (group, group * 8), 0) * 8
    for k in range(groups):
        lid = ids_col[k * group:(k + 1) * group, :]
        owned = (lid >= 0) & (lid < vocab)
        pick = jnp.where(owned & (lane == first + (lid & 7)), 1.0, 0.0).astype(BF)
        rows = pl.ds(k * group * 8, group * 8)
        pltpu.make_async_copy(table.at[pl.ds(0, group * 8)], slabs.at[rows], sems.at[k]).wait()
        part[pl.ds(k * group, group), :] = mm(pick, slabs[rows, :], 1, 0).astype(BF)
    load.wait()
    fill_wait(zero, table_g, s_zero, 0, FILL_0)


def lookup(ids, table, d_out):
    tokens, (vocab, width) = ids.shape[0], table.shape
    return pl.pallas_call(
        lookup_kernel,
        name="lookup",
        out_shape=[sh((tokens, width), BF), sh((1, tokens), I32), sh((tokens, tokens), BF), sh(d_out.shape, BF), sh((vocab, width), F32)],
        in_specs=[SMEM_SPEC, VMEM_SPEC, HBM_SPEC, HBM_SPEC],
        out_specs=[VMEM_SPEC, VMEM_SPEC, VMEM_SPEC, VMEM_SPEC, HBM_SPEC],
        scratch_shapes=[VMEM((tokens * 8, width), BF), VMEM((ZERO_ROWS, width), F32), DMA((tokens // 32,)), DMA(()), DMA(())],
        compiler_params=pltpu.CompilerParams(vmem_limit_bytes=44 * MIB),
        cost_estimate=pl.CostEstimate(flops=5_000_000_000, bytes_accessed=10 * MIB, transcendentals=0),
    )(ids, ids.reshape(1, tokens), table, d_out)


def pair_kernel(part, d_own, d_far, comb, d_full, part_r, d_r, sems):
    me = lax.axis_index("tp")
    rows = d_own.shape[0]
    half = 2 * rows
    blocks = (me, me ^ 2, me ^ 1, me ^ 3)
    remote = swap_with_sibling()
    block = lambda k: pl.ds(pl.multiple_of(blocks[k] * rows, rows), rows)
    copies = [remote(part.at[block(2)], part_r.at[pl.ds(0, rows)], sems, 0),
              remote(part.at[block(3)], part_r.at[pl.ds(rows, rows)], sems, 1),
              remote(d_own, d_r.at[pl.ds(0, rows)], sems, 2),
              remote(d_far, d_r.at[pl.ds(rows, rows)], sems, 3)]
    for c in copies:
        c.start()
    d_full[pl.ds(0, rows), :] = d_own[...]
    d_full[pl.ds(rows, rows), :] = d_far[...]
    for k in range(2):
        copies[k].wait()
        at = pl.ds(k * rows, rows)
        comb[at, :] = part[block(k), :] + part_r[at, :]
    copies[2].wait()
    copies[3].wait()
    d_full[pl.ds(half, half), :] = d_r[...]


def pair(part, d_own, d_far):
    tokens, width = part.shape
    half = tokens // 2
    return pl.pallas_call(
        pair_kernel,
        name="pair",
        out_shape=[sh((half, width), BF), sh((tokens, width), BF)],
        in_specs=[VMEM_SPEC] * 3,
        out_specs=[VMEM_SPEC] * 2,
        scratch_shapes=[VMEM((half, width), BF), VMEM((half, width), BF), DMA((2, 4))],
        compiler_params=pltpu.CompilerParams(collective_id=0, has_side_effects=True, vmem_limit_bytes=8 * MIB),
        cost_estimate=pl.CostEstimate(flops=3_000_000_000, bytes_accessed=MIB, transcendentals=0),
    )(part, d_own, d_far)


def fill1_kernel(d_full, w2, table_in, dh, table_g, zero, s_zero):
    fill_start(zero, table_g, s_zero, FILL_0, FILL_0 + FILL_1)
    for j in range(dh.shape[1] // TILE):
        at = pl.ds(j * TILE, TILE)
        dh[:, at] = mm(d_full[...], w2[at, :], 1, 1).astype(BF)
    fill_wait(zero, table_g, s_zero, FILL_0, FILL_0 + FILL_1)


def fill1(d_full, w2, table_g):
    tokens, width = d_full.shape
    hid = w2.shape[0]
    return pl.pallas_call(
        fill1_kernel,
        name="fill1",
        out_shape=[sh((tokens, hid), BF), sh(table_g.shape, F32)],
        in_specs=[VMEM_SPEC, VMEM_SPEC, HBM_SPEC],
        out_specs=[VMEM_SPEC, HBM_SPEC],
        input_output_aliases={2: 1},
        scratch_shapes=[VMEM((ZERO_ROWS, width), F32), DMA(())],
        compiler_params=pltpu.CompilerParams(vmem_limit_bytes=12 * MIB),
        cost_estimate=pl.CostEstimate(flops=8_000_000_000, bytes_accessed=20 * MIB, transcendentals=0),
    )(d_full, w2, table_g)


def mlp_kernel(comb, e2, dh, w1, gain, n, h, du, x_own, dn_own, dn_far, x_f, dn_p, g1_r, sems):
    tokens, width = n.shape
    hid = h.shape[1]
    rows = x_own.shape[0]
    half = 2 * rows
    remote = swap_with_sibling()
    e3 = []
    for k in range(2):
        at, other = pl.ds(k * rows, rows), pl.ds((1 - k) * rows, rows)
        x_f[at, :] = comb[at, :] + e2[other, :]
        c = remote(x_f.at[at], x_f.at[pl.ds(half + k * rows, rows)], sems, k)
        c.start()
        e3.append(c)
    gain_f = gain[...].astype(F32).reshape(1, width)

    def norm_half(k):
        for j in range(4):
            at = pl.ds(k * half + j * 32, 32)
            x = x_f[at, :].astype(F32)
            r = lax.rsqrt(jnp.mean(x * x, axis=-1, keepdims=True) + EPS)
            n[at, :] = (x * r * gain_f).astype(BF)

    def fwd_half(k):
        at = pl.ds(k * half, half)
        for j in range(hid // TILE):
            cols = pl.ds(j * TILE, TILE)
            u = mm(n[at, :], w1[:, cols], 1, 0).astype(BF).astype(F32)
            t = jnp.tanh(GELU_C * (u + GELU_A * (u * u * u)))
            cdf = 0.5 * (1.0 + t)
            h[at, cols] = (u * cdf).astype(BF)
            g = dh[at, cols].astype(F32)
            du[at, cols] = (g * (cdf + u * (0.5 * (1.0 - t * t)) * (GELU_C * (1.0 + 3.0 * GELU_A * (u * u))))).astype(BF)

    def dn_half(k):
        at = pl.ds(k * half, half)
        for j in range(width // TILE):
            cols = pl.ds(j * TILE, TILE)
            dn_p[at, cols] = mm(du[at, :], w1[cols, :], 1, 1)

    norm_half(0)
    fwd_half(0)
    for c in e3:
        c.wait()
    norm_half(1)
    fwd_half(1)
    dn_half(1)
    g1 = [remote(dn_p.at[pl.ds(half + k * rows, rows)], g1_r.at[pl.ds(k * rows, rows)], sems, 2 + k) for k in range(2)]
    g1[1].start()
    g1[0].start()
    dn_half(0)
    x_own[...] = x_f[pl.ds(0, rows), :]
    g1[1].wait()
    dn_far[...] = dn_p[pl.ds(rows, rows), :] + g1_r[pl.ds(rows, rows), :]
    g1[0].wait()
    dn_own[...] = dn_p[pl.ds(0, rows), :] + g1_r[pl.ds(0, rows), :]


def mlp(comb, e2, dh, w1, gain):
    half, width = comb.shape
    tokens, rows = 2 * half, half // 2
    hid = w1.shape[1]
    return pl.pallas_call(
        mlp_kernel,
        name="mlp",
        out_shape=[sh((tokens, width), BF), sh((tokens, hid), BF), sh((tokens, hid), BF), sh((rows, width), BF),
                   sh((rows, width), F32), sh((rows, width), F32)],
        in_specs=[VMEM_SPEC] * 5,
        out_specs=[VMEM_SPEC] * 6,
        scratch_shapes=[VMEM((tokens, width), BF), VMEM((tokens, width), F32), VMEM((half, width), F32), DMA((2, 4))],
        compiler_params=pltpu.CompilerParams(collective_id=1, has_side_effects=True, vmem_limit_bytes=16 * MIB),
        cost_estimate=pl.CostEstimate(flops=6_000_000_000, bytes_accessed=4 * MIB, transcendentals=0),
    )(comb, e2, dh, w1, gain)


def grads_kernel(n, h, du, d_full, w2, table_in, y, dw1, dw2, table_g, zero, dw1_v, dw2_v, s_zero, s_w):
    lo, hi = FILL_0 + FILL_1, FILL_0 + FILL_1 + FILL_2
    fill_start(zero, table_g, s_zero, lo, hi)
    width, hid = dw1.shape
    for j in range(width // TILE):
        cols = pl.ds(j * TILE, TILE)
        y[:, cols] = mm(h[...], w2[:, cols], 1, 0)
    n_t = n[...].T
    for j in range(width // TILE):
        at = slice(j * TILE, (j + 1) * TILE)
        dw1_v[at, :] = mm(n_t[at, :], du[...], 1, 0)
        pltpu.make_async_copy(dw1_v.at[pl.ds(j * TILE, TILE)], dw1.at[pl.ds(j * TILE, TILE)], s_w).start()
    h_t = h[...].T
    for j in range(hid // TILE):
        at = slice(j * TILE, (j + 1) * TILE)
        dw2_v[at, :] = mm(h_t[at, :], d_full[...], 1, 0)
        pltpu.make_async_copy(dw2_v.at[pl.ds(j * TILE, TILE)], dw2.at[pl.ds(j * TILE, TILE)], s_w).start()
    pltpu.make_async_copy(dw1_v, dw1, s_w).wait()
    pltpu.make_async_copy(dw2_v, dw2, s_w).wait()
    fill_wait(zero, table_g, s_zero, lo, hi)


def grads(n, h, du, d_full, w2, table_g):
    tokens, width = n.shape
    hid = h.shape[1]
    return pl.pallas_call(
        grads_kernel,
        name="grads",
        out_shape=[sh((tokens, width), F32), sh((width, hid), F32), sh((hid, width), F32), sh(table_g.shape, F32)],
        in_specs=[VMEM_SPEC] * 5 + [HBM_SPEC],
        out_specs=[VMEM_SPEC, HBM_SPEC, HBM_SPEC, HBM_SPEC],
        input_output_aliases={5: 3},
        scratch_shapes=[VMEM((ZERO_ROWS, width), F32), VMEM((width, hid), F32), VMEM((hid, width), F32), DMA(()), DMA(())],
        compiler_params=pltpu.CompilerParams(vmem_limit_bytes=24 * MIB),
        cost_estimate=pl.CostEstimate(flops=8_000_000_000, bytes_accessed=20 * MIB, transcendentals=0),
    )(n, h, du, d_full, w2, table_g)


def ysum_kernel(y, order, y_own, y_far, y_r, sems):
    rows = y_own.shape[0]
    half = 2 * rows
    remote = swap_with_sibling()
    copies = [remote(y.at[pl.ds(half + k * rows, rows)], y_r.at[pl.ds(k * rows, rows)], sems, k) for k in range(2)]
    for c in copies:
        c.start()
    for k, out in enumerate((y_own, y_far)):
        copies[k].wait()
        at = pl.ds(k * rows, rows)
        out[...] = y[at, :] + y_r[at, :]


def ysum(y, order):
    tokens, width = y.shape
    rows = tokens // 4
    return pl.pallas_call(
        ysum_kernel,
        name="ysum",
        out_shape=[sh((rows, width), F32), sh((rows, width), F32)],
        in_specs=[VMEM_SPEC, ANY_SPEC],
        out_specs=[VMEM_SPEC] * 2,
        scratch_shapes=[VMEM((2 * rows, width), F32), DMA((2, 2))],
        compiler_params=pltpu.CompilerParams(collective_id=2, has_side_effects=True, vmem_limit_bytes=8 * MIB),
        cost_estimate=pl.CostEstimate(flops=3_000_000_000, bytes_accessed=4 * MIB, transcendentals=0),
    )(y, order)


def dx_kernel(dn_own, g2, x_own, d_own, gain, order, dx):
    gain_f = gain[...].astype(F32).reshape(1, dx.shape[1])
    for j in range(dx.shape[0] // 16):
        at = pl.ds(j * 16, 16)
        a = (dn_own[at, :] + g2[at, :]) * gain_f
        x = x_own[at, :].astype(F32)
        r = lax.rsqrt(jnp.mean(x * x, axis=-1, keepdims=True) + EPS)
        proj = jnp.mean(a * x, axis=-1, keepdims=True)
        dx[at, :] = (d_own[at, :].astype(F32) + r * (a - x * r * r * proj)).astype(BF)


def dx_rows(dn_own, g2, x_own, d_own, gain, order):
    return pl.pallas_call(
        dx_kernel,
        name="dx_rows",
        out_shape=sh(x_own.shape, BF),
        in_specs=[VMEM_SPEC] * 5 + [ANY_SPEC],
        out_specs=VMEM_SPEC,
        compiler_params=pltpu.CompilerParams(vmem_limit_bytes=4 * MIB),
        cost_estimate=pl.CostEstimate(flops=1_000_000_000, bytes_accessed=MIB, transcendentals=0),
    )(dn_own, g2, x_own, d_own, gain, order)


def fill3_kernel(order, table_in, token, table_g, zero, s_zero):
    lo, hi = FILL_0 + FILL_1 + FILL_2, table_g.shape[0] // ZERO_ROWS
    fill_start(zero, table_g, s_zero, lo, hi)
    token[...] = jnp.zeros_like(token)
    fill_wait(zero, table_g, s_zero, lo, hi)


def fill3(order, table_g):
    return pl.pallas_call(
        fill3_kernel,
        name="fill3",
        out_shape=[sh((8, 128), F32), sh(table_g.shape, F32)],
        in_specs=[ANY_SPEC, HBM_SPEC],
        out_specs=[VMEM_SPEC, HBM_SPEC],
        input_output_aliases={1: 1},
        scratch_shapes=[VMEM((ZERO_ROWS, table_g.shape[1]), F32), DMA(())],
        compiler_params=pltpu.CompilerParams(vmem_limit_bytes=4 * MIB),
        cost_estimate=pl.CostEstimate(flops=5_000_000_000, bytes_accessed=16 * MIB, transcendentals=0),
    )(order, table_g)


def dx_all_kernel(dx, dx_far, order, dx_out, dx_r, sems):
    me = lax.axis_index("tp")
    rows = dx.shape[0]
    remote = swap_with_sibling()
    block = lambda m: pl.ds(pl.multiple_of((me ^ m) * rows, rows), rows)
    copies = [remote(dx, dx_r.at[pl.ds(0, rows)], sems, 0), remote(dx_far, dx_r.at[pl.ds(rows, rows)], sems, 1)]
    for c in copies:
        c.start()
    dx_out[block(0), :] = dx[...]
    dx_out[block(2), :] = dx_far[...]
    copies[0].wait()
    dx_out[block(1), :] = dx_r[pl.ds(0, rows), :]
    copies[1].wait()
    dx_out[block(3), :] = dx_r[pl.ds(rows, rows), :]


def dx_all(dx, dx_far, order):
    rows, width = dx.shape
    return pl.pallas_call(
        dx_all_kernel,
        name="dx_all",
        out_shape=sh((4 * rows, width), BF),
        in_specs=[VMEM_SPEC, VMEM_SPEC, ANY_SPEC],
        out_specs=VMEM_SPEC,
        scratch_shapes=[VMEM((2 * rows, width), BF), DMA((2, 2))],
        compiler_params=pltpu.CompilerParams(collective_id=3, has_side_effects=True, vmem_limit_bytes=4 * MIB),
        cost_estimate=pl.CostEstimate(flops=2_000_000_000, bytes_accessed=MIB, transcendentals=0),
    )(dx, dx_far, order)


def put_kernel(ids_s, repeat_s, same, dx, table_in, table_g, token, total, s_row):
    tokens, vocab = dx.shape[0], table_g.shape[0]
    base = lax.axis_index("tp") * vocab
    total[...] = mm(same[...], dx[...], 1, 0)
    token[...] = jnp.zeros_like(token)

    def put(i, count):
        lid = ids_s[i] - base
        mine = (lid >= 0) & (lid < vocab) & (repeat_s[0, i] == 0)

        @pl.when(mine)
        def _():
            pltpu.make_async_copy(total.at[pl.ds(i, 1)], table_g.at[pl.ds(lid, 1)], s_row).start()

        return count + mine.astype(I32)

    count = lax.fori_loop(0, tokens, put, 0)

    def put_wait(i, carry):
        pltpu.make_async_copy(total.at[pl.ds(0, 1)], table_g.at[pl.ds(0, 1)], s_row).wait()
        return carry

    lax.fori_loop(0, count, put_wait, 0)


def put_rows(ids, repeat, same, dx, table_g):
    return pl.pallas_call(
        put_kernel,
        name="put_rows",
        out_shape=[sh(table_g.shape, F32), sh((8, 128), F32)],
        in_specs=[SMEM_SPEC, SMEM_SPEC, VMEM_SPEC, VMEM_SPEC, HBM_SPEC],
        out_specs=[HBM_SPEC, VMEM_SPEC],
        input_output_aliases={4: 0},
        scratch_shapes=[VMEM(dx.shape, F32), DMA(())],
        compiler_params=pltpu.CompilerParams(vmem_limit_bytes=4 * MIB),
        cost_estimate=pl.CostEstimate(flops=3_000_000_000, bytes_accessed=2 * MIB, transcendentals=0),
    )(ids, repeat, same, dx, table_g)


def finish_kernel(x, y, y_in, order, out):
    out[...] = (x[...].astype(F32) + (y[...] + y_in[...])).astype(BF)


def finish(x, y, y_in, order):
    return pl.pallas_call(
        finish_kernel,
        name="finish",
        out_shape=sh(x.shape, BF),
        in_specs=[VMEM_SPEC] * 3 + [ANY_SPEC],
        out_specs=VMEM_SPEC,
        compiler_params=pltpu.CompilerParams(vmem_limit_bytes=4 * MIB),
        cost_estimate=pl.CostEstimate(flops=1_000_000_000, bytes_accessed=MIB, transcendentals=0),
    )(x, y, y_in, order)


def solution(mesh):
    tp = mesh.shape["tp"]
    far_pairs = [(i, i ^ 2) for i in range(tp)]

    def shard_step(ids, table, gain, w1, w2, d_out):
        d_far = lax.ppermute(d_out, "tp", far_pairs)
        part, repeat, same, d_own, d_table = lookup(ids, table, d_out)
        comb, d_full = pair(part, d_own, d_far)
        e2 = lax.ppermute(comb, "tp", far_pairs)
        dh, d_table = fill1(d_full, w2, d_table)
        n, h, du, x_own, dn_own, dn_far = mlp(comb, e2, dh, w1, gain)
        g2 = lax.ppermute(dn_far, "tp", far_pairs)
        y, d_w1, d_w2, d_table = grads(n, h, du, d_full, w2, d_table)
        dx = dx_rows(dn_own, g2, x_own, d_own, gain, y)
        dx_far = lax.ppermute(dx, "tp", far_pairs)
        y_own, y_far = ysum(y, dx)
        token, d_table = fill3(y_own, d_table)
        y_in = lax.ppermute(y_far, "tp", far_pairs)
        dx_full = dx_all(dx, dx_far, token)
        d_table, done = put_rows(ids, repeat, same, dx_full, d_table)
        out = finish(x_own, y_own, y_in, done)
        return out, d_table, d_w1, d_w2

    return jax.shard_map(
        shard_step,
        mesh=mesh,
        in_specs=(P("dp"), P("tp", None), P(None), P(None, "tp"), P("tp", None), P(("dp", "tp"), None)),
        out_specs=(P(("dp", "tp"), None), P(("dp", "tp"), None), P("dp", "tp"), P(("dp", "tp"), None)),
        check_vma=False,
    )
```

time: 141 us -> 52.4 us (0.37)
  Pallas kernels: 0 us -> 40.8 us
  waiting for transfers between devices: 38.1 us -> 0.01 us
  blocking collectives: 30.8 us -> 0 us
  other arithmetic: 30.2 us -> 0 us
  between operations: 13.9 us -> 0.79 us
  matrix products: 13.1 us -> 0 us
  local copies, waits for them, and re-layouts: 14.1 us -> 3.18 us
  starting transfers between devices: 0.12 us -> 7.49 us
    pallas_call x0 -> x11, Pallas kernels: none -> 40.8 us  [the longest x1 8.37 us: grads(): pl.pallas_call(grads_kernel, name='grads', out_shape=[sh((tokens, width),...]
    reduce_scatter x3 -> x0, waiting for transfers between devices: 38 us -> none  [the longest x1 20.6 us: shard_step(): mlp_out = lax.psum_scatter(mlp_part, 'tp', scatter_dimension=0, tiled=True)]
    all_gather x3 -> x0, blocking collectives: 30.8 us -> none  [the longest x1 11.9 us: shard_step(): d_out_full = lax.all_gather(d_out, 'tp', axis=0, tiled=True)]
    scatter-add x1 -> x0, other arithmetic: 23.5 us -> none  [shard_step(): jax.ops.segment_sum(d_emb_full.astype(jnp.float32), target_rows, num_segm...]
    gather x1 -> x0, local copies, waits for them, and re-layouts: 13.2 us -> none  [shard_step(): table_rows = jnp.take(emb_table, jnp.where(is_owned, local_ids, 0), axis=0)]
    dot_general x6 -> x0, matrix products: 13.1 us -> none  [the longest x1 3.62 us: shard_step(): mlp_part = jnp.dot(hidden, w_out, preferred_element_type=jnp.float32)]
    ppermute x0 -> x5, starting transfers between devices: none -> 7.49 us  [the longest x1 3.36 us: shard_step(): d_far = lax.ppermute(d_out, 'tp', far_pairs)]
    convert_element_type x3 -> x0, other arithmetic: 2.74 us -> none  [the longest x1 1.73 us: shard_step(): (d_out.astype(jnp.float32) + inv_rms * (d_scaled - embedded_f32 * inv_rms...]
  transfers between devices with their start and end apart: 3 -> 5, of which waited for: 3 -> 0; matrix products, arithmetic and copies ran while one was open for 7% -> 0% of each run, Pallas kernels for 0% -> 63%
where the time goes in v1:
time: 52.4 us; the launch traced here: 52.3 us
  Pallas kernels  40.8 us (78%)
  starting transfers between devices  7.49 us (14%)
  local copies, waits for them, and re-layouts  3.18 us (6%)
  between operations  0.79 us (2%)
    pallas_call x1, Pallas kernels, grads(): pl.pallas_call(grads_kernel, name='grads', out_shape=[sh((tokens, width),...  8.37 us
    pallas_call x1, Pallas kernels, lookup(): pl.pallas_call(lookup_kernel, name='lookup', out_shape=[sh((tokens, width...  7.01 us
    pallas_call x1, Pallas kernels, fill1(): pl.pallas_call(fill1_kernel, name='fill1', out_shape=[sh((tokens, hid), B...  6.91 us
    pallas_call x1, Pallas kernels, mlp(): pl.pallas_call(mlp_kernel, name='mlp', out_shape=[sh((tokens, width), BF)...  4.71 us
    pallas_call x1, Pallas kernels, put_rows(): pl.pallas_call(put_kernel, name='put_rows', out_shape=[sh(table_g.shape,...  4.43 us
    ppermute x1, starting transfers between devices, shard_step(): d_far = lax.ppermute(d_out, 'tp', far_pairs)  3.36 us
    unnamed x12, local copies, waits for them, and re-layouts  3.18 us
    pallas_call x1, Pallas kernels, fill3(): pl.pallas_call(fill3_kernel, name='fill3', out_shape=[sh((8, 128), F32),...  2.9 us
  transfers between devices with their start and end apart: 5, of which 0 were waited for; matrix products, arithmetic and copies ran while one was open for 0% of the time, Pallas kernels for 63%

profile of v1, /device:TPU:0, one launch (start us, length us, event | category | flops | bytes accessed | tf_op | source)
XLA Modules:
  0.0 52.3 jit_solution(9648832138250672865)
XLA Ops:
  0.6 3.4 %collective-permute-start = (bf16[64,1024]{1,0:T(8,128)(2,1)}, bf16[64,1024]{1,0:T(8,128)(2,1)S(1)}, u32[]{:S(2)}, u32[]{:S(2)}) collective-permute-start(bf16[64,1024]{1,0:T(8,128)(2,1)} %d_out.1), channel_id=1, source_target_pairs={{0,2},{1,3},{2,0},{3,1},{4,6},{5,7},{6,4},{7,5}} | collective-permute-start | bytes 393224 | tf_op jit(solution)/shard_map/ppermute | solution.py:462
  4.0 0.0 copy-start.2
  4.0 0.9 %copy-done.2 = bf16[64,1024]{1,0:T(8,128)(2,1)S(1)} copy-done((bf16[64,1024]{1,0:T(8,128)(2,1)S(1)}, bf16[64,1024]{1,0:T(8,128)(2,1)}, u32[]{:S(2)}) %copy-start.2) | copy-done | bytes 131096
  4.9 0.0 copy-start.3
  4.9 0.7 %copy-done.3 = s32[256]{0:T(256)S(1)} copy-done((s32[256]{0:T(256)S(1)}, s32[256]{0:T(256)}, u32[]{:S(2)}) %copy-start.3) | copy-done | bytes 1048
  5.6 0.0 copy-start.4
  5.6 0.0 copy-start.5
  5.6 0.0 copy-start.1
  5.6 7.0 %lookup.1 = (bf16[256,1024]{1,0:T(8,128)(2,1)S(1)}, s32[1,256]{1,0:T(1,128)S(1)}, bf16[256,256]{1,0:T(8,128)(2,1)S(1)}, bf16[64,1024]{1,0:T(8,128)(2,1)S(1)}, f32[12576,1024]{1,0:T(8,128)}) custom-call(s32[256]{0:T(256)S(1)} %copy-done.3, s32[1,256]{1,0:T(1,128)S(1)} %bitcast.1, bf16[12576,1024]{1,0:T(8,128)(2,1)} %table.1, bf16[64,1024]{1,0:T(8,128)(2,1)S(1)} %copy-done.2), custom_call_target="tpu_custom_call" | custom-call | flops 5000000000 | bytes 10485760 | tf_op jit(solution)/shard_map/lookup/pallas_call | solution.py:113
  12.6 0.0 collective-permute-done.d_far
  12.6 2.0 %pair.1 = (bf16[128,1024]{1,0:T(8,128)(2,1)S(1)}, bf16[256,1024]{1,0:T(8,128)(2,1)S(1)}) custom-call(bf16[256,1024]{1,0:T(8,128)(2,1)S(1)} %get-tuple-element.29.part, bf16[64,1024]{1,0:T(8,128)(2,1)S(1)} %get-tuple-element.30.d_own, bf16[64,1024]{1,0:T(8,128)(2,1)S(1)} %collective-permute-done.d_far), custom_call_target="tpu_custom_call" | custom-call | flops 3000000000 | bytes 1048576 | tf_op jit(solution)/shard_map/pair/pallas_call | solution.py:152
  14.6 0.0 collective-permute-start.1
  14.7 0.0 copy-start
  14.7 1.6 %copy-done = bf16[1024,1024]{1,0:T(8,128)(2,1)S(1)} copy-done((bf16[1024,1024]{1,0:T(8,128)(2,1)S(1)}, bf16[1024,1024]{1,0:T(8,128)(2,1)}, u32[]{:S(2)}) %copy-start) | copy-done | bytes 2097176
  16.3 6.9 %fill1.1 = (bf16[256,1024]{1,0:T(8,128)(2,1)S(1)}, f32[12576,1024]{1,0:T(8,128)}) custom-call(bf16[256,1024]{1,0:T(8,128)(2,1)S(1)} %get-tuple-element.32.d_full, bf16[1024,1024]{1,0:T(8,128)(2,1)S(1)} %copy-done, f32[12576,1024]{1,0:T(8,128)} %get-tuple-element.33.table_in), custom_call_target="tpu_custom_call", output_to_operand_aliasing={{1}: (2, {})} | custom-call | flops 8000000000 | bytes 20971520 | tf_op jit(solution)/shard_map/fill1/pallas_call | solution.py:175
  23.2 0.0 collective-permute-done.1.e2
  23.2 0.0 copy-done.4
  23.2 0.0 copy-done.5
  23.2 4.7 %mlp.1 = (bf16[256,1024]{1,0:T(8,128)(2,1)S(1)}, bf16[256,1024]{1,0:T(8,128)(2,1)S(1)}, bf16[256,1024]{1,0:T(8,128)(2,1)S(1)}, bf16[64,1024]{1,0:T(8,128)(2,1)S(...) custom-call(bf16[128,1024]{1,0:T(8,128)(2,1)S(1)} %get-tuple-element.31.comb, ...), custom_call_target="tpu_custom_call" | custom-call | flops 6000000000 | bytes 4194304 | tf_op jit(solution)/shard_map/mlp/pallas_call | solution.py:249
  27.9 2.0 %collective-permute-start.2 = (f32[64,1024]{1,0:T(8,128)S(1)}, f32[64,1024]{1,0:T(8,128)S(1)}, u32[]{:S(2)}, u32[]{:S(2)}) collective-permute-start(f32[64,1024]{1,0:T(8,128)S(1)} %get-tuple-element.42), channel_id=1, source_target_pairs={{0,2},{1,3},{2,0},{3,1},{4,6},{5,7},{6,4},{7,5}} | collective-permute-start | bytes 786440 | tf_op jit(solution)/shard_map/ppermute | solution.py:468
  30.0 0.0 copy-done.1
  30.0 8.4 %grads.1 = (f32[256,1024]{1,0:T(8,128)S(1)}, f32[1024,1024]{1,0:T(8,128)}, f32[1024,1024]{1,0:T(8,128)}, f32[12576,1024]{1,0:T(8,128)}) custom-call(bf16[256,1024]{1,0:T(8,128)(2,1)S(1)} %get-tuple-element.36.n, bf16[256,1024]{1,0:T(8,128)(2,1)S(1)} %get-tuple-element.37.h, ...), custom_call_target="tpu_custom_call", output_to_operand_aliasing={{3}: (5, {})} | custom-call | flops 8000000000 | bytes 20971520 | tf_op jit(solution)/shard_map/grads/pallas_call | solution.py:287
  38.3 0.0 collective-permute-done.2.g2
  38.3 0.2 dx_rows.1.order.dx
  38.5 0.2 collective-permute-start.4
  38.7 2.0 %ysum.1 = (f32[64,1024]{1,0:T(8,128)S(1)}, f32[64,1024]{1,0:T(8,128)S(1)}) custom-call(f32[256,1024]{1,0:T(8,128)S(1)} %get-tuple-element.40.order.y, bf16[64,1024]{1,0:T(8,128)(2,1)S(1)} %dx_rows.1.order.dx), custom_call_target="tpu_custom_call" | custom-call | flops 3000000000 | bytes 4194304 | tf_op jit(solution)/shard_map/ysum/pallas_call | solution.py:316
  40.7 1.9 %collective-permute-start.3 = (f32[64,1024]{1,0:T(8,128)S(1)}, f32[64,1024]{1,0:T(8,128)S(1)}, u32[]{:S(2)}, u32[]{:S(2)}) collective-permute-start(f32[64,1024]{1,0:T(8,128)S(1)} %get-tuple-element.44), channel_id=1, source_target_pairs={{0,2},{1,3},{2,0},{3,1},{4,6},{5,7},{6,4},{7,5}} | collective-permute-start | bytes 786440 | tf_op jit(solution)/shard_map/ppermute | solution.py:474
  42.6 2.9 %fill3.1 = (f32[8,128]{1,0:T(8,128)S(1)}, f32[12576,1024]{1,0:T(8,128)}) custom-call(f32[64,1024]{1,0:T(8,128)S(1)} %get-tuple-element.43.order.y, f32[12576,1024]{1,0:T(8,128)} %get-tuple-element.47.table_in), custom_call_target="tpu_custom_call", output_to_operand_aliasing={{1}: (1, {})} | custom-call | flops 5000000000 | bytes 16777216 | tf_op jit(solution)/shard_map/fill3/pallas_call | solution.py:359
  45.5 0.0 collective-permute-done.4.dx_far
  45.5 1.6 %dx_all.1.dx = bf16[256,1024]{1,0:T(8,128)(2,1)S(1)} custom-call(bf16[64,1024]{1,0:T(8,128)(2,1)S(1)} %dx_rows.1.order.dx, bf16[64,1024]{1,0:T(8,128)(2,1)S(1)} %collective-permute-done.4.dx_far, f32[8,128]{1,0:T(8,128)S(1)} %get-tuple-element.48.order), custom_call_target="tpu_custom_call" | custom-call | flops 2000000000 | bytes 1048576 | tf_op jit(solution)/shard_map/dx_all/pallas_call | solution.py:390
  47.1 4.4 %put_rows.1 = (f32[12576,1024]{1,0:T(8,128)}, f32[8,128]{1,0:T(8,128)S(1)}) custom-call(s32[256]{0:T(256)S(1)} %copy-done.3, s32[1,256]{1,0:T(1,128)S(1)} %get-tuple-element.45.repeat_s, bf16[256,256]{1,0:T(8,128)(2,1)S(1)} %get-tuple-element.46.same, bf16[256,1024]{1,0:T(8,128)(2,1)S(1)} %dx_all.1.dx, ...), custom_call_target="tpu_custom_call", output_to_operand_aliasing={{0}: (4, {})} | custom-call | flops 3000000000 | bytes 2097152 | tf_op jit(solution)/shard_map/put_rows/pallas_call | solution.py:428
  51.5 0.0 collective-permute-done.3.y_in
  51.6 0.7 %finish.1 = bf16[64,1024]{1,0:T(8,128)(2,1)} custom-call(bf16[64,1024]{1,0:T(8,128)(2,1)S(1)} %get-tuple-element.35.x_own.x, f32[64,1024]{1,0:T(8,128)S(1)} %get-tuple-element.43.order.y, f32[64,1024]{1,0:T(8,128)S(1)} %collective-permute-done.3.y_in, f32[8,128]{1,0:T(8,128)S(1)} %get-tuple-element.50.order), custom_call_target="tpu_custom_call" | custom-call | flops 1000000000 | bytes 1048576 | tf_op jit(solution)/shard_map/finish/pallas_call | solution.py:446
Async XLA Ops:
  0.6 12.0 %collective-permute-start = (bf16[64,1024]{1,0:T(8,128)(2,1)}, bf16[64,1024]{1,0:T(8,128)(2,1)S(1)}, u32[]{:S(2)}, u32[]{:S(2)}) collective-permute-start(bf16[64,1024]{1,0:T(8,128)(2,1)} %d_out.1), channel_id=1, source_target_pairs={{0,2},{1,3},{2,0},{3,1},{4,6},{5,7},{6,4},{7,5}} | collective-permute-start | bytes 393224 | tf_op jit(solution)/shard_map/ppermute | solution.py:462
  4.0 0.9 %copy-start.2 = (bf16[64,1024]{1,0:T(8,128)(2,1)S(1)}, bf16[64,1024]{1,0:T(8,128)(2,1)}, u32[]{:S(2)}) copy-start(bf16[64,1024]{1,0:T(8,128)(2,1)} %d_out.1) | copy-start | bytes 393220
  4.9 0.7 %copy-start.3 = (s32[256]{0:T(256)S(1)}, s32[256]{0:T(256)}, u32[]{:S(2)}) copy-start(s32[256]{0:T(256)} %ids_s.3) | copy-start | bytes 3076
  5.6 17.6 %copy-start.4 = (bf16[1024,1024]{1,0:T(8,128)(2,1)S(1)}, bf16[1024,1024]{1,0:T(8,128)(2,1)}, u32[]{:S(2)}) copy-start(bf16[1024,1024]{1,0:T(8,128)(2,1)} %w1.1) | copy-start | bytes 6291460
  5.6 17.6 %copy-start.5 = (bf16[1024]{0:T(1024)(128)(2,1)S(1)}, bf16[1024]{0:T(1024)(128)(2,1)}, u32[]{:S(2)}) copy-start(bf16[1024]{0:T(1024)(128)(2,1)} %gain.3) | copy-start | bytes 6148
  5.6 24.4 %copy-start.1 = (bf16[1024,1024]{1,0:T(8,128)(2,1)S(1)}, bf16[1024,1024]{1,0:T(8,128)(2,1)}, u32[]{:S(2)}) copy-start(bf16[1024,1024]{1,0:T(8,128)(2,1)} %w2.3) | copy-start | bytes 6291460
  14.6 8.6 %collective-permute-start.1 = (bf16[128,1024]{1,0:T(8,128)(2,1)S(1)}, bf16[128,1024]{1,0:T(8,128)(2,1)S(1)}, u32[]{:S(2)}, u32[]{:S(2)}) collective-permute-start(bf16[128,1024]{1,0:T(8,128)(2,1)S(1)} %get-tuple-element.31.comb), channel_id=1, source_target_pairs={{0,2},{1,3},{2,0},{3,1},{4,6},{5,7},{6,4},{7,5}} | collective-permute-start | bytes 786440 | tf_op jit(solution)/shard_map/ppermute | solution.py:465
  14.7 1.6 %copy-start = (bf16[1024,1024]{1,0:T(8,128)(2,1)S(1)}, bf16[1024,1024]{1,0:T(8,128)(2,1)}, u32[]{:S(2)}) copy-start(bf16[1024,1024]{1,0:T(8,128)(2,1)} %w2.3) | copy-start | bytes 6291460
  27.9 10.4 %collective-permute-start.2 = (f32[64,1024]{1,0:T(8,128)S(1)}, f32[64,1024]{1,0:T(8,128)S(1)}, u32[]{:S(2)}, u32[]{:S(2)}) collective-permute-start(f32[64,1024]{1,0:T(8,128)S(1)} %get-tuple-element.42), channel_id=1, source_target_pairs={{0,2},{1,3},{2,0},{3,1},{4,6},{5,7},{6,4},{7,5}} | collective-permute-start | bytes 786440 | tf_op jit(solution)/shard_map/ppermute | solution.py:468
  38.5 7.0 %collective-permute-start.4 = (bf16[64,1024]{1,0:T(8,128)(2,1)S(1)}, bf16[64,1024]{1,0:T(8,128)(2,1)S(1)}, u32[]{:S(2)}, u32[]{:S(2)}) collective-permute-start(bf16[64,1024]{1,0:T(8,128)(2,1)S(1)} %dx_rows.1.order.dx), channel_id=1, source_target_pairs={{0,2},{1,3},{2,0},{3,1},{4,6},{5,7},{6,4},{7,5}} | collective-permute-start | bytes 393224 | tf_op jit(solution)/shard_map/ppermute | solution.py:471
  40.7 10.8 %collective-permute-start.3 = (f32[64,1024]{1,0:T(8,128)S(1)}, f32[64,1024]{1,0:T(8,128)S(1)}, u32[]{:S(2)}, u32[]{:S(2)}) collective-permute-start(f32[64,1024]{1,0:T(8,128)S(1)} %get-tuple-element.44), channel_id=1, source_target_pairs={{0,2},{1,3},{2,0},{3,1},{4,6},{5,7},{6,4},{7,5}} | collective-permute-start | bytes 786440 | tf_op jit(solution)/shard_map/ppermute | solution.py:474

commit v2 on v1

--- a/solution.py
+++ b/solution.py
@@ -19,8 +19,9 @@
 DMA = pltpu.SemaphoreType.DMA
 TILE = 256
 ZERO_ROWS = 96
-FILL_0, FILL_1, FILL_2 = 20, 52, 41
+FILL_0, FILL_1, FILL_2 = 25, 60, 36
 MIB = 1 << 20
+LOOKUP_VMEM = 48 * MIB
 
 
 def mm(a, b, ca, cb):
@@ -67,7 +68,7 @@
     return remote
 
 
-def lookup_kernel(ids_s, ids_v, table, d_out, part, flags, same, d_own, table_g, slabs, zero, sems, s_zero, s_d):
+def lookup_kernel(ids_s, ids_v, table, w1, w2, part, flags, same, w1_v, w2_v, table_g, slabs, zero, sems, s_zero, s_in):
     tokens, vocab = part.shape[0], table.shape[0]
     base = lax.axis_index("tp") * vocab
     group = 32
@@ -84,10 +85,11 @@
         ).start()
         return carry
 
+    fill_start(zero, table_g, s_zero, 0, FILL_0)
     lax.fori_loop(0, tokens, fetch, 0, unroll=8)
-    load = pltpu.make_async_copy(d_out, d_own, s_d)
-    load.start()
-    fill_start(zero, table_g, s_zero, 0, FILL_0)
+    loads = [pltpu.make_async_copy(a, b, s_in.at[k]) for k, (a, b) in enumerate(((w2, w2_v), (w1, w1_v)))]
+    for c in loads:
+        c.start()
     row = jnp.broadcast_to(ids_v[...].astype(F32), (tokens, tokens))
     col = row.T
     equal = row == col
@@ -104,88 +106,89 @@
         rows = pl.ds(k * group * 8, group * 8)
         pltpu.make_async_copy(table.at[pl.ds(0, group * 8)], slabs.at[rows], sems.at[k]).wait()
         part[pl.ds(k * group, group), :] = mm(pick, slabs[rows, :], 1, 0).astype(BF)
-    load.wait()
+    for c in loads:
+        c.wait()
     fill_wait(zero, table_g, s_zero, 0, FILL_0)
 
 
-def lookup(ids, table, d_out):
+def lookup(ids, table, w1, w2):
     tokens, (vocab, width) = ids.shape[0], table.shape
     return pl.pallas_call(
         lookup_kernel,
         name="lookup",
-        out_shape=[sh((tokens, width), BF), sh((1, tokens), I32), sh((tokens, tokens), BF), sh(d_out.shape, BF), sh((vocab, width), F32)],
-        in_specs=[SMEM_SPEC, VMEM_SPEC, HBM_SPEC, HBM_SPEC],
-        out_specs=[VMEM_SPEC, VMEM_SPEC, VMEM_SPEC, VMEM_SPEC, HBM_SPEC],
-        scratch_shapes=[VMEM((tokens * 8, width), BF), VMEM((ZERO_ROWS, width), F32), DMA((tokens // 32,)), DMA(()), DMA(())],
-        compiler_params=pltpu.CompilerParams(vmem_limit_bytes=44 * MIB),
+        out_shape=[sh((tokens, width), BF), sh((1, tokens), I32), sh((tokens, tokens), BF),
+                   sh(w1.shape, BF), sh(w2.shape, BF), sh((vocab, width), F32)],
+        in_specs=[SMEM_SPEC, VMEM_SPEC] + [HBM_SPEC] * 3,
+        out_specs=[VMEM_SPEC] * 5 + [HBM_SPEC],
+        scratch_shapes=[VMEM((tokens * 8, width), BF), VMEM((ZERO_ROWS, width), F32), DMA((tokens // 32,)), DMA(()), DMA((2,))],
+        compiler_params=pltpu.CompilerParams(vmem_limit_bytes=LOOKUP_VMEM),
         cost_estimate=pl.CostEstimate(flops=5_000_000_000, bytes_accessed=10 * MIB, transcendentals=0),
-    )(ids, ids.reshape(1, tokens), table, d_out)
-
-
-def pair_kernel(part, d_own, d_far, comb, d_full, part_r, d_r, sems):
+    )(ids, ids.reshape(1, tokens), table, w1, w2)
+
+
+def pair_kernel(part, comb, part_r, sems):
     me = lax.axis_index("tp")
-    rows = d_own.shape[0]
-    half = 2 * rows
+    rows = part.shape[0] // 4
     blocks = (me, me ^ 2, me ^ 1, me ^ 3)
     remote = swap_with_sibling()
     block = lambda k: pl.ds(pl.multiple_of(blocks[k] * rows, rows), rows)
-    copies = [remote(part.at[block(2)], part_r.at[pl.ds(0, rows)], sems, 0),
-              remote(part.at[block(3)], part_r.at[pl.ds(rows, rows)], sems, 1),
-              remote(d_own, d_r.at[pl.ds(0, rows)], sems, 2),
-              remote(d_far, d_r.at[pl.ds(rows, rows)], sems, 3)]
+    copies = [remote(part.at[block(2 + k)], part_r.at[pl.ds(k * rows, rows)], sems, k) for k in range(2)]
     for c in copies:
         c.start()
-    d_full[pl.ds(0, rows), :] = d_own[...]
-    d_full[pl.ds(rows, rows), :] = d_far[...]
     for k in range(2):
         copies[k].wait()
         at = pl.ds(k * rows, rows)
         comb[at, :] = part[block(k), :] + part_r[at, :]
-    copies[2].wait()
-    copies[3].wait()
-    d_full[pl.ds(half, half), :] = d_r[...]
-
-
-def pair(part, d_own, d_far):
+
+
+def pair(part):
     tokens, width = part.shape
     half = tokens // 2
     return pl.pallas_call(
         pair_kernel,
         name="pair",
-        out_shape=[sh((half, width), BF), sh((tokens, width), BF)],
-        in_specs=[VMEM_SPEC] * 3,
-        out_specs=[VMEM_SPEC] * 2,
-        scratch_shapes=[VMEM((half, width), BF), VMEM((half, width), BF), DMA((2, 4))],
+        out_shape=sh((half, width), BF),
+        in_specs=[VMEM_SPEC],
+        out_specs=VMEM_SPEC,
+        scratch_shapes=[VMEM((half, width), BF), DMA((2, 2))],
         compiler_params=pltpu.CompilerParams(collective_id=0, has_side_effects=True, vmem_limit_bytes=8 * MIB),
         cost_estimate=pl.CostEstimate(flops=3_000_000_000, bytes_accessed=MIB, transcendentals=0),
-    )(part, d_own, d_far)
-
-
-def fill1_kernel(d_full, w2, table_in, dh, table_g, zero, s_zero):
+    )(part)
+
+
+def fill1_kernel(ids_s, repeat_s, order, table_in, puts, token, table_g, zero, s_zero):
     fill_start(zero, table_g, s_zero, FILL_0, FILL_0 + FILL_1)
-    for j in range(dh.shape[1] // TILE):
-        at = pl.ds(j * TILE, TILE)
-        dh[:, at] = mm(d_full[...], w2[at, :], 1, 1).astype(BF)
+    tokens, vocab = puts.shape[0] // 2, table_g.shape[0]
+    base = lax.axis_index("tp") * vocab
+
+    def body(i, count):
+        lid = ids_s[i] - base
+        mine = (lid >= 0) & (lid < vocab) & (repeat_s[0, i] == 0)
+        slot = jnp.where(mine, count, tokens - 1 - (i - count))
+        puts[slot] = i
+        puts[tokens + slot] = jnp.where(mine, lid, -1)
+        return count + mine.astype(I32)
+
+    lax.fori_loop(0, tokens, body, 0, unroll=4)
+    token[...] = jnp.zeros_like(token)
     fill_wait(zero, table_g, s_zero, FILL_0, FILL_0 + FILL_1)
 
 
-def fill1(d_full, w2, table_g):
-    tokens, width = d_full.shape
-    hid = w2.shape[0]
+def fill1(ids, repeat, order, table_g):
     return pl.pallas_call(
         fill1_kernel,
         name="fill1",
-        out_shape=[sh((tokens, hid), BF), sh(table_g.shape, F32)],
-        in_specs=[VMEM_SPEC, VMEM_SPEC, HBM_SPEC],
-        out_specs=[VMEM_SPEC, HBM_SPEC],
-        input_output_aliases={2: 1},
-        scratch_shapes=[VMEM((ZERO_ROWS, width), F32), DMA(())],
+        out_shape=[sh((2 * ids.shape[0],), I32), sh((8, 128), F32), sh(table_g.shape, F32)],
+        in_specs=[SMEM_SPEC, SMEM_SPEC, ANY_SPEC, HBM_SPEC],
+        out_specs=[SMEM_SPEC, VMEM_SPEC, HBM_SPEC],
+        input_output_aliases={3: 2},
+        scratch_shapes=[VMEM((ZERO_ROWS, table_g.shape[1]), F32), DMA(())],
         compiler_params=pltpu.CompilerParams(vmem_limit_bytes=12 * MIB),
         cost_estimate=pl.CostEstimate(flops=8_000_000_000, bytes_accessed=20 * MIB, transcendentals=0),
-    )(d_full, w2, table_g)
-
-
-def mlp_kernel(comb, e2, dh, w1, gain, n, h, du, x_own, dn_own, dn_far, x_f, dn_p, g1_r, sems):
+    )(ids, repeat, order, table_g)
+
+
+def mlp_kernel(comb, e2, d_own, d_far, w1, w2, gain, order, n, h, du, d_full, x_own, dn_own, dn_far, x_f, d_r, dn_p, g1_r, sems):
     tokens, width = n.shape
     hid = h.shape[1]
     rows = x_own.shape[0]
@@ -198,6 +201,11 @@
         c = remote(x_f.at[at], x_f.at[pl.ds(half + k * rows, rows)], sems, k)
         c.start()
         e3.append(c)
+    ds = [remote(src, d_r.at[pl.ds(k * rows, rows)], sems, 4 + k) for k, src in enumerate((d_own, d_far))]
+    for c in ds:
+        c.start()
+    d_full[pl.ds(0, rows), :] = d_own[...]
+    d_full[pl.ds(rows, rows), :] = d_far[...]
     gain_f = gain[...].astype(F32).reshape(1, width)
 
     def norm_half(k):
@@ -211,11 +219,11 @@
         at = pl.ds(k * half, half)
         for j in range(hid // TILE):
             cols = pl.ds(j * TILE, TILE)
+            g = mm(d_full[at, :], w2[cols, :], 1, 1).astype(BF).astype(F32)
             u = mm(n[at, :], w1[:, cols], 1, 0).astype(BF).astype(F32)
             t = jnp.tanh(GELU_C * (u + GELU_A * (u * u * u)))
             cdf = 0.5 * (1.0 + t)
             h[at, cols] = (u * cdf).astype(BF)
-            g = dh[at, cols].astype(F32)
             du[at, cols] = (g * (cdf + u * (0.5 * (1.0 - t * t)) * (GELU_C * (1.0 + 3.0 * GELU_A * (u * u))))).astype(BF)
 
     def dn_half(k):
@@ -226,8 +234,9 @@
 
     norm_half(0)
     fwd_half(0)
-    for c in e3:
+    for c in e3 + ds:
         c.wait()
+    d_full[pl.ds(half, half), :] = d_r[...]
     norm_half(1)
     fwd_half(1)
     dn_half(1)
@@ -242,21 +251,21 @@
     dn_own[...] = dn_p[pl.ds(0, rows), :] + g1_r[pl.ds(0, rows), :]
 
 
-def mlp(comb, e2, dh, w1, gain):
+def mlp(comb, e2, d_own, d_far, w1, w2, gain, order):
     half, width = comb.shape
     tokens, rows = 2 * half, half // 2
     hid = w1.shape[1]
     return pl.pallas_call(
         mlp_kernel,
         name="mlp",
-        out_shape=[sh((tokens, width), BF), sh((tokens, hid), BF), sh((tokens, hid), BF), sh((rows, width), BF),
+        out_shape=[sh((tokens, width), BF), sh((tokens, hid), BF), sh((tokens, hid), BF), sh((tokens, width), BF), sh((rows, width), BF),
                    sh((rows, width), F32), sh((rows, width), F32)],
-        in_specs=[VMEM_SPEC] * 5,
-        out_specs=[VMEM_SPEC] * 6,
-        scratch_shapes=[VMEM((tokens, width), BF), VMEM((tokens, width), F32), VMEM((half, width), F32), DMA((2, 4))],
+        in_specs=[VMEM_SPEC] * 7 + [ANY_SPEC],
+        out_specs=[VMEM_SPEC] * 7,
+        scratch_shapes=[VMEM((tokens, width), BF), VMEM((half, width), BF), VMEM((tokens, width), F32), VMEM((half, width), F32), DMA((2, 6))],
         compiler_params=pltpu.CompilerParams(collective_id=1, has_side_effects=True, vmem_limit_bytes=16 * MIB),
         cost_estimate=pl.CostEstimate(flops=6_000_000_000, bytes_accessed=4 * MIB, transcendentals=0),
-    )(comb, e2, dh, w1, gain)
+    )(comb, e2, d_own, d_far, w1, w2, gain, order)
 
 
 def grads_kernel(n, h, du, d_full, w2, table_in, y, dw1, dw2, table_g, zero, dw1_v, dw2_v, s_zero, s_w):
@@ -297,32 +306,35 @@
     )(n, h, du, d_full, w2, table_g)
 
 
-def ysum_kernel(y, order, y_own, y_far, y_r, sems):
+def ysum_kernel(y, dx, y_own, y_far, dx_sib, y_r, dx_r, sems):
     rows = y_own.shape[0]
     half = 2 * rows
     remote = swap_with_sibling()
-    copies = [remote(y.at[pl.ds(half + k * rows, rows)], y_r.at[pl.ds(k * rows, rows)], sems, k) for k in range(2)]
+    copies = [remote(y.at[pl.ds(half + k * rows, rows)], y_r.at[pl.ds(k * rows, rows)], sems, k) for k in (1, 0)]
+    copies.append(remote(dx, dx_r, sems, 2))
     for c in copies:
         c.start()
-    for k, out in enumerate((y_own, y_far)):
-        copies[k].wait()
+    for c, k, out in zip(copies, (1, 0), (y_far, y_own)):
+        c.wait()
         at = pl.ds(k * rows, rows)
         out[...] = y[at, :] + y_r[at, :]
-
-
-def ysum(y, order):
+    copies[2].wait()
+    dx_sib[...] = dx_r[...]
+
+
+def ysum(y, dx):
     tokens, width = y.shape
     rows = tokens // 4
     return pl.pallas_call(
         ysum_kernel,
         name="ysum",
-        out_shape=[sh((rows, width), F32), sh((rows, width), F32)],
-        in_specs=[VMEM_SPEC, ANY_SPEC],
-        out_specs=[VMEM_SPEC] * 2,
-        scratch_shapes=[VMEM((2 * rows, width), F32), DMA((2, 2))],
+        out_shape=[sh((rows, width), F32), sh((rows, width), F32), sh((rows, width), BF)],
+        in_specs=[VMEM_SPEC, VMEM_SPEC],
+        out_specs=[VMEM_SPEC] * 3,
+        scratch_shapes=[VMEM((2 * rows, width), F32), VMEM((rows, width), BF), DMA((2, 3))],
         compiler_params=pltpu.CompilerParams(collective_id=2, has_side_effects=True, vmem_limit_bytes=8 * MIB),
         cost_estimate=pl.CostEstimate(flops=3_000_000_000, bytes_accessed=4 * MIB, transcendentals=0),
-    )(y, order)
+    )(y, dx)
 
 
 def dx_kernel(dn_own, g2, x_own, d_own, gain, order, dx):
@@ -369,53 +381,47 @@
     )(order, table_g)
 
 
-def dx_all_kernel(dx, dx_far, order, dx_out, dx_r, sems):
+def dx_all_kernel(dx, dx_sib, dx_far, order, dx_out, dx_r, sems):
     me = lax.axis_index("tp")
     rows = dx.shape[0]
     remote = swap_with_sibling()
     block = lambda m: pl.ds(pl.multiple_of((me ^ m) * rows, rows), rows)
-    copies = [remote(dx, dx_r.at[pl.ds(0, rows)], sems, 0), remote(dx_far, dx_r.at[pl.ds(rows, rows)], sems, 1)]
-    for c in copies:
-        c.start()
+    copy = remote(dx_far, dx_r, sems, 0)
+    copy.start()
     dx_out[block(0), :] = dx[...]
+    dx_out[block(1), :] = dx_sib[...]
     dx_out[block(2), :] = dx_far[...]
-    copies[0].wait()
-    dx_out[block(1), :] = dx_r[pl.ds(0, rows), :]
-    copies[1].wait()
-    dx_out[block(3), :] = dx_r[pl.ds(rows, rows), :]
-
-
-def dx_all(dx, dx_far, order):
+    copy.wait()
+    dx_out[block(3), :] = dx_r[...]
+
+
+def dx_all(dx, dx_sib, dx_far, order):
     rows, width = dx.shape
     return pl.pallas_call(
         dx_all_kernel,
         name="dx_all",
         out_shape=sh((4 * rows, width), BF),
-        in_specs=[VMEM_SPEC, VMEM_SPEC, ANY_SPEC],
+        in_specs=[VMEM_SPEC] * 3 + [ANY_SPEC],
         out_specs=VMEM_SPEC,
-        scratch_shapes=[VMEM((2 * rows, width), BF), DMA((2, 2))],
+        scratch_shapes=[VMEM((rows, width), BF), DMA((2, 1))],
         compiler_params=pltpu.CompilerParams(collective_id=3, has_side_effects=True, vmem_limit_bytes=4 * MIB),
         cost_estimate=pl.CostEstimate(flops=2_000_000_000, bytes_accessed=MIB, transcendentals=0),
-    )(dx, dx_far, order)
-
-
-def put_kernel(ids_s, repeat_s, same, dx, table_in, table_g, token, total, s_row):
-    tokens, vocab = dx.shape[0], table_g.shape[0]
-    base = lax.axis_index("tp") * vocab
+    )(dx, dx_sib, dx_far, order)
+
+
+def put_kernel(puts, same, dx, table_in, table_g, token, puts_s, total, s_in, s_row):
+    tokens = dx.shape[0]
+    load = pltpu.make_async_copy(puts, puts_s, s_in)
+    load.start()
     total[...] = mm(same[...], dx[...], 1, 0)
     token[...] = jnp.zeros_like(token)
-
-    def put(i, count):
-        lid = ids_s[i] - base
-        mine = (lid >= 0) & (lid < vocab) & (repeat_s[0, i] == 0)
-
-        @pl.when(mine)
-        def _():
-            pltpu.make_async_copy(total.at[pl.ds(i, 1)], table_g.at[pl.ds(lid, 1)], s_row).start()
-
-        return count + mine.astype(I32)
-
-    count = lax.fori_loop(0, tokens, put, 0)
+    load.wait()
+
+    def put(i):
+        pltpu.make_async_copy(total.at[pl.ds(puts_s[i], 1)], table_g.at[pl.ds(puts_s[tokens + i], 1)], s_row).start()
+        return i + 1
+
+    count = lax.while_loop(lambda i: (i < tokens) & (puts_s[tokens + jnp.minimum(i, tokens - 1)] >= 0), put, 0)
 
     def put_wait(i, carry):
         pltpu.make_async_copy(total.at[pl.ds(0, 1)], table_g.at[pl.ds(0, 1)], s_row).wait()
@@ -424,18 +430,18 @@
     lax.fori_loop(0, count, put_wait, 0)
 
 
-def put_rows(ids, repeat, same, dx, table_g):
+def put_rows(puts, same, dx, table_g):
     return pl.pallas_call(
         put_kernel,
         name="put_rows",
         out_shape=[sh(table_g.shape, F32), sh((8, 128), F32)],
-        in_specs=[SMEM_SPEC, SMEM_SPEC, VMEM_SPEC, VMEM_SPEC, HBM_SPEC],
+        in_specs=[ANY_SPEC, VMEM_SPEC, VMEM_SPEC, HBM_SPEC],
         out_specs=[HBM_SPEC, VMEM_SPEC],
-        input_output_aliases={4: 0},
-        scratch_shapes=[VMEM(dx.shape, F32), DMA(())],
+        input_output_aliases={3: 0},
+        scratch_shapes=[pltpu.SMEM(puts.shape, I32), VMEM(dx.shape, F32), DMA(()), DMA(())],
         compiler_params=pltpu.CompilerParams(vmem_limit_bytes=4 * MIB),
         cost_estimate=pl.CostEstimate(flops=3_000_000_000, bytes_accessed=2 * MIB, transcendentals=0),
-    )(ids, repeat, same, dx, table_g)
+    )(puts, same, dx, table_g)
 
 
 def finish_kernel(x, y, y_in, order, out):
@@ -459,21 +465,22 @@
     far_pairs = [(i, i ^ 2) for i in range(tp)]
 
     def shard_step(ids, table, gain, w1, w2, d_out):
-        d_far = lax.ppermute(d_out, "tp", far_pairs)
-        part, repeat, same, d_own, d_table = lookup(ids, table, d_out)
-        comb, d_full = pair(part, d_own, d_far)
+        part, repeat, same, w1_v, w2_v, d_table = lookup(ids, table, w1, w2)
+        part, d_send = lax.optimization_barrier((part, d_out))
+        d_far = lax.ppermute(d_send, "tp", far_pairs)
+        comb = pair(part)
         e2 = lax.ppermute(comb, "tp", far_pairs)
-        dh, d_table = fill1(d_full, w2, d_table)
-        n, h, du, x_own, dn_own, dn_far = mlp(comb, e2, dh, w1, gain)
+        puts, token, d_table = fill1(ids, repeat, comb, d_table)
+        n, h, du, d_full, x_own, dn_own, dn_far = mlp(comb, e2, d_out, d_far, w1_v, w2_v, gain, token)
         g2 = lax.ppermute(dn_far, "tp", far_pairs)
-        y, d_w1, d_w2, d_table = grads(n, h, du, d_full, w2, d_table)
-        dx = dx_rows(dn_own, g2, x_own, d_own, gain, y)
+        y, d_w1, d_w2, d_table = grads(n, h, du, d_full, w2_v, d_table)
+        dx = dx_rows(dn_own, g2, x_own, d_out, gain, y)
         dx_far = lax.ppermute(dx, "tp", far_pairs)
-        y_own, y_far = ysum(y, dx)
+        y_own, y_far, dx_sib = ysum(y, dx)
         token, d_table = fill3(y_own, d_table)
         y_in = lax.ppermute(y_far, "tp", far_pairs)
-        dx_full = dx_all(dx, dx_far, token)
-        d_table, done = put_rows(ids, repeat, same, dx_full, d_table)
+        dx_full = dx_all(dx, dx_sib, dx_far, token)
+        d_table, done = put_rows(puts, same, dx_full, d_table)
         out = finish(x_own, y_own, y_in, done)
         return out, d_table, d_w1, d_w2
 

time: 52.4 us -> 51 us (0.973)
  local copies, waits for them, and re-layouts: 3.18 us -> 0.68 us
  Pallas kernels: 40.8 us -> 41.5 us
    unnamed x12 -> x6, local copies, waits for them, and re-layouts: 3.18 us -> 0.68 us
    pallas_call x2, Pallas kernels: 8.93 us -> 10.6 us  [the longest x1 9.04 us: fill1(): pl.pallas_call(fill1_kernel, name='fill1', out_shape=[sh((2 * ids.shape[0...]
    pallas_call x1, Pallas kernels: 4.43 us -> 3.35 us  [put_rows(): pl.pallas_call(put_kernel, name='put_rows', out_shape=[sh(table_g.shape,...]
    pallas_call x1, Pallas kernels: 2.9 us -> 1.94 us  [fill3(): pl.pallas_call(fill3_kernel, name='fill3', out_shape=[sh((8, 128), F32),...]
    pallas_call x1, Pallas kernels: 4.71 us -> 5.6 us  [mlp(): pl.pallas_call(mlp_kernel, name='mlp', out_shape=[sh((tokens, width), BF)...]
    pallas_call x1, Pallas kernels: 7.01 us -> 7.77 us  [lookup(): pl.pallas_call(lookup_kernel, name='lookup', out_shape=[sh((tokens, width...]
    ppermute x1, starting transfers between devices: 1.86 us -> 1.23 us  [shard_step(): y_in = lax.ppermute(y_far, 'tp', far_pairs)]
    ppermute x1, starting transfers between devices: 0.21 us -> 0.83 us  [shard_step(): dx_far = lax.ppermute(dx, 'tp', far_pairs)]
  transfers between devices with their start and end apart: 5 -> 5, of which waited for: 0 -> 1; matrix products, arithmetic and copies ran while one was open for 0% -> 0% of each run, Pallas kernels for 63% -> 54%
where the time goes in v2:
time: 51 us; the launch traced here: 50.8 us
  Pallas kernels  41.5 us (81%)
  starting transfers between devices  7.5 us (15%)
  between operations  0.77 us (2%)
  local copies, waits for them, and re-layouts  0.68 us (1%)
    pallas_call x1, Pallas kernels, fill1(): pl.pallas_call(fill1_kernel, name='fill1', out_shape=[sh((2 * ids.shape[0...  9.04 us
    pallas_call x1, Pallas kernels, lookup(): pl.pallas_call(lookup_kernel, name='lookup', out_shape=[sh((tokens, width...  7.77 us
    pallas_call x1, Pallas kernels, grads(): pl.pallas_call(grads_kernel, name='grads', out_shape=[sh((tokens, width),...  7.75 us
    pallas_call x1, Pallas kernels, mlp(): pl.pallas_call(mlp_kernel, name='mlp', out_shape=[sh((tokens, width), BF)...  5.6 us
    ppermute x1, starting transfers between devices, shard_step(): d_far = lax.ppermute(d_send, 'tp', far_pairs)  3.36 us
    pallas_call x1, Pallas kernels, put_rows(): pl.pallas_call(put_kernel, name='put_rows', out_shape=[sh(table_g.shape,...  3.35 us
    pallas_call x1, Pallas kernels, ysum(): pl.pallas_call(ysum_kernel, name='ysum', out_shape=[sh((rows, width), F32...  2.16 us
    ppermute x1, starting transfers between devices, shard_step(): g2 = lax.ppermute(dn_far, 'tp', far_pairs)  2.02 us
  transfers between devices with their start and end apart: 5, of which 1 were waited for; matrix products, arithmetic and copies ran while one was open for 0% of the time, Pallas kernels for 54%

profile of v2, /device:TPU:0, one launch (start us, length us, event | category | flops | bytes accessed | tf_op | source)
XLA Modules:
  0.0 50.8 jit_solution(8251048384515988833)
XLA Ops:
  0.6 0.0 copy-start
  0.6 0.7 %copy-done = s32[256]{0:T(256)S(1)} copy-done((s32[256]{0:T(256)S(1)}, s32[256]{0:T(256)}, u32[]{:S(2)}) %copy-start) | copy-done | bytes 1048
  1.3 0.0 copy-start.1
  1.3 7.8 %lookup.1 = (bf16[256,1024]{1,0:T(8,128)(2,1)S(1)}, s32[1,256]{1,0:T(1,128)S(1)}, bf16[256,256]{1,0:T(8,128)(2,1)S(1)}, bf16[1024,1024]{1,0:T(8,128)(2,1)S(1)}, ...) custom-call(s32[256]{0:T(256)S(1)} %copy-done, s32[1,256]{1,0:T(1,128)S(1)} %bitcast.1, bf16[12576,1024]{1,0:T(8,128)(2,1)} %table.1, ...), custom_call_target="tpu_custom_call" | custom-call | flops 5000000000 | bytes 10485760 | tf_op jit(solution)/shard_map/lookup/pallas_call | solution.py:116
  9.1 0.0 copy-done.1
  9.1 3.4 %collective-permute-start.1 = (bf16[64,1024]{1,0:T(8,128)(2,1)S(1)}, bf16[64,1024]{1,0:T(8,128)(2,1)S(1)}, u32[]{:S(2)}, u32[]{:S(2)}) collective-permute-start(bf16[64,1024]{1,0:T(8,128)(2,1)S(1)} %copy-done.1), channel_id=1, source_target_pairs={{0,2},{1,3},{2,0},{3,1},{4,6},{5,7},{6,4},{7,5}} | collective-permute-start | bytes 393224 | tf_op jit(solution)/shard_map/ppermute | solution.py:470
  12.5 1.6 %pair.1.order.comb = bf16[128,1024]{1,0:T(8,128)(2,1)S(1)} custom-call(bf16[256,1024]{1,0:T(8,128)(2,1)S(1)} %get-tuple-element.34.part), custom_call_target="tpu_custom_call" | custom-call | flops 3000000000 | bytes 1048576 | tf_op jit(solution)/shard_map/pair/pallas_call | solution.py:147
  14.1 0.0 collective-permute-start
  14.1 0.0 copy-start.2
  14.1 9.0 %fill1.1 = (s32[512]{0:T(512)S(1)}, f32[8,128]{1,0:T(8,128)S(1)}, f32[12576,1024]{1,0:T(8,128)}) custom-call(s32[256]{0:T(256)S(1)} %copy-done, s32[1,256]{1,0:T(1,128)S(1)} %get-tuple-element.38.repeat_s, bf16[128,1024]{1,0:T(8,128)(2,1)S(1)} %pair.1.order.comb, f32[12576,1024]{1,0:T(8,128)} %get-tuple-element.39.table_in), custom_call_target="tpu_custom_call", output_to_operand_aliasing={{2}: (3, {})} | custom-call | flops 8000000000 | bytes 20971520 | tf_op jit(solution)/shard_map/fill1/pallas_call | solution.py:178
  23.2 0.0 collective-permute-done.1.d_far
  23.2 0.0 collective-permute-done.e2
  23.2 0.0 copy-done.2
  23.2 5.6 %mlp.1 = (bf16[256,1024]{1,0:T(8,128)(2,1)S(1)}, bf16[256,1024]{1,0:T(8,128)(2,1)S(1)}, bf16[256,1024]{1,0:T(8,128)(2,1)S(1)}, bf16[256,1024]{1,0:T(8,128)(2,1)S...) custom-call(bf16[128,1024]{1,0:T(8,128)(2,1)S(1)} %pair.1.order.comb, ...), custom_call_target="tpu_custom_call" | custom-call | flops 6000000000 | bytes 4194304 | tf_op jit(solution)/shard_map/mlp/pallas_call | solution.py:258
  28.8 2.0 %collective-permute-start.2 = (f32[64,1024]{1,0:T(8,128)S(1)}, f32[64,1024]{1,0:T(8,128)S(1)}, u32[]{:S(2)}, u32[]{:S(2)}) collective-permute-start(f32[64,1024]{1,0:T(8,128)S(1)} %get-tuple-element.49), channel_id=1, source_target_pairs={{0,2},{1,3},{2,0},{3,1},{4,6},{5,7},{6,4},{7,5}} | collective-permute-start | bytes 786440 | tf_op jit(solution)/shard_map/ppermute | solution.py:475
  30.8 7.7 %grads.1 = (f32[256,1024]{1,0:T(8,128)S(1)}, f32[1024,1024]{1,0:T(8,128)}, f32[1024,1024]{1,0:T(8,128)}, f32[12576,1024]{1,0:T(8,128)}) custom-call(bf16[256,1024]{1,0:T(8,128)(2,1)S(1)} %get-tuple-element.42.n, bf16[256,1024]{1,0:T(8,128)(2,1)S(1)} %get-tuple-element.43.h, ...), custom_call_target="tpu_custom_call", output_to_operand_aliasing={{3}: (5, {})} | custom-call | flops 8000000000 | bytes 20971520 | tf_op jit(solution)/shard_map/grads/pallas_call | solution.py:296
  38.6 0.0 collective-permute-done.2.g2
  38.6 0.2 dx_rows.1.dx
  38.8 0.8 %collective-permute-start.4 = (bf16[64,1024]{1,0:T(8,128)(2,1)S(1)}, bf16[64,1024]{1,0:T(8,128)(2,1)S(1)}, u32[]{:S(2)}, u32[]{:S(2)}) collective-permute-start(bf16[64,1024]{1,0:T(8,128)(2,1)S(1)} %dx_rows.1.dx), channel_id=1, source_target_pairs={{0,2},{1,3},{2,0},{3,1},{4,6},{5,7},{6,4},{7,5}} | collective-permute-start | bytes 393224 | tf_op jit(solution)/shard_map/ppermute | solution.py:478
  39.6 2.2 %ysum.1 = (f32[64,1024]{1,0:T(8,128)S(1)}, f32[64,1024]{1,0:T(8,128)S(1)}, bf16[64,1024]{1,0:T(8,128)(2,1)S(1)}) custom-call(f32[256,1024]{1,0:T(8,128)S(1)} %get-tuple-element.47.order.y, bf16[64,1024]{1,0:T(8,128)(2,1)S(1)} %dx_rows.1.dx), custom_call_target="tpu_custom_call" | custom-call | flops 3000000000 | bytes 4194304 | tf_op jit(solution)/shard_map/ysum/pallas_call | solution.py:328
  41.8 1.2 %collective-permute-start.3 = (f32[64,1024]{1,0:T(8,128)S(1)}, f32[64,1024]{1,0:T(8,128)S(1)}, u32[]{:S(2)}, u32[]{:S(2)}) collective-permute-start(f32[64,1024]{1,0:T(8,128)S(1)} %get-tuple-element.51), channel_id=1, source_target_pairs={{0,2},{1,3},{2,0},{3,1},{4,6},{5,7},{6,4},{7,5}} | collective-permute-start | bytes 786440 | tf_op jit(solution)/shard_map/ppermute | solution.py:481
  43.0 1.9 %fill3.1 = (f32[8,128]{1,0:T(8,128)S(1)}, f32[12576,1024]{1,0:T(8,128)}) custom-call(f32[64,1024]{1,0:T(8,128)S(1)} %get-tuple-element.50.order.y, f32[12576,1024]{1,0:T(8,128)} %get-tuple-element.55.table_in), custom_call_target="tpu_custom_call", output_to_operand_aliasing={{1}: (1, {})} | custom-call | flops 5000000000 | bytes 16777216 | tf_op jit(solution)/shard_map/fill3/pallas_call | solution.py:371
  44.9 0.0 collective-permute-done.4.dx_far
  45.0 1.4 %dx_all.1.dx = bf16[256,1024]{1,0:T(8,128)(2,1)S(1)} custom-call(bf16[64,1024]{1,0:T(8,128)(2,1)S(1)} %dx_rows.1.dx, bf16[64,1024]{1,0:T(8,128)(2,1)S(1)} %get-tuple-element.54.dx_sib, bf16[64,1024]{1,0:T(8,128)(2,1)S(1)} %collective-permute-done.4.dx_far, f32[8,128]{1,0:T(8,128)S(1)} %get-tuple-element.56.order), custom_call_target="tpu_custom_call" | custom-call | flops 2000000000 | bytes 1048576 | tf_op jit(solution)/shard_map/dx_all/pallas_call | solution.py:400
  46.4 3.4 %put_rows.1 = (f32[12576,1024]{1,0:T(8,128)}, f32[8,128]{1,0:T(8,128)S(1)}) custom-call(s32[512]{0:T(512)S(1)} %get-tuple-element.52.puts, bf16[256,256]{1,0:T(8,128)(2,1)S(1)} %get-tuple-element.53.same, bf16[256,1024]{1,0:T(8,128)(2,1)S(1)} %dx_all.1.dx, f32[12576,1024]{1,0:T(8,128)} %get-tuple-element.57.table_in), custom_call_target="tpu_custom_call", output_to_operand_aliasing={{0}: (3, {})} | custom-call | flops 3000000000 | bytes 2097152 | tf_op jit(solution)/shard_map/put_rows/pallas_call | solution.py:434
  49.7 0.4 collective-permute-done.3.y_in
  50.1 0.7 %finish.1 = bf16[64,1024]{1,0:T(8,128)(2,1)} custom-call(bf16[64,1024]{1,0:T(8,128)(2,1)S(1)} %get-tuple-element.41.x_own.x, f32[64,1024]{1,0:T(8,128)S(1)} %get-tuple-element.50.order.y, f32[64,1024]{1,0:T(8,128)S(1)} %collective-permute-done.3.y_in, f32[8,128]{1,0:T(8,128)S(1)} %get-tuple-element.58.order), custom_call_target="tpu_custom_call" | custom-call | flops 1000000000 | bytes 1048576 | tf_op jit(solution)/shard_map/finish/pallas_call | solution.py:452
Async XLA Ops:
  0.6 0.7 %copy-start = (s32[256]{0:T(256)S(1)}, s32[256]{0:T(256)}, u32[]{:S(2)}) copy-start(s32[256]{0:T(256)} %ids_s.3) | copy-start | bytes 3076
  1.3 7.8 %copy-start.1 = (bf16[64,1024]{1,0:T(8,128)(2,1)S(1)}, bf16[64,1024]{1,0:T(8,128)(2,1)}, u32[]{:S(2)}) copy-start(bf16[64,1024]{1,0:T(8,128)(2,1)} %d_own.3) | copy-start | bytes 393220
  9.1 14.1 %collective-permute-start.1 = (bf16[64,1024]{1,0:T(8,128)(2,1)S(1)}, bf16[64,1024]{1,0:T(8,128)(2,1)S(1)}, u32[]{:S(2)}, u32[]{:S(2)}) collective-permute-start(bf16[64,1024]{1,0:T(8,128)(2,1)S(1)} %copy-done.1), channel_id=1, source_target_pairs={{0,2},{1,3},{2,0},{3,1},{4,6},{5,7},{6,4},{7,5}} | collective-permute-start | bytes 393224 | tf_op jit(solution)/shard_map/ppermute | solution.py:470
  14.1 9.1 %collective-permute-start = (bf16[128,1024]{1,0:T(8,128)(2,1)S(1)}, bf16[128,1024]{1,0:T(8,128)(2,1)S(1)}, u32[]{:S(2)}, u32[]{:S(2)}) collective-permute-start(bf16[128,1024]{1,0:T(8,128)(2,1)S(1)} %pair.1.order.comb), channel_id=1, source_target_pairs={{0,2},{1,3},{2,0},{3,1},{4,6},{5,7},{6,4},{7,5}} | collective-permute-start | bytes 786440 | tf_op jit(solution)/shard_map/ppermute | solution.py:472
  14.1 9.1 %copy-start.2 = (bf16[1024]{0:T(1024)(128)(2,1)S(1)}, bf16[1024]{0:T(1024)(128)(2,1)}, u32[]{:S(2)}) copy-start(bf16[1024]{0:T(1024)(128)(2,1)} %gain.3) | copy-start | bytes 6148
  28.8 9.8 %collective-permute-start.2 = (f32[64,1024]{1,0:T(8,128)S(1)}, f32[64,1024]{1,0:T(8,128)S(1)}, u32[]{:S(2)}, u32[]{:S(2)}) collective-permute-start(f32[64,1024]{1,0:T(8,128)S(1)} %get-tuple-element.49), channel_id=1, source_target_pairs={{0,2},{1,3},{2,0},{3,1},{4,6},{5,7},{6,4},{7,5}} | collective-permute-start | bytes 786440 | tf_op jit(solution)/shard_map/ppermute | solution.py:475
  38.8 6.2 %collective-permute-start.4 = (bf16[64,1024]{1,0:T(8,128)(2,1)S(1)}, bf16[64,1024]{1,0:T(8,128)(2,1)S(1)}, u32[]{:S(2)}, u32[]{:S(2)}) collective-permute-start(bf16[64,1024]{1,0:T(8,128)(2,1)S(1)} %dx_rows.1.dx), channel_id=1, source_target_pairs={{0,2},{1,3},{2,0},{3,1},{4,6},{5,7},{6,4},{7,5}} | collective-permute-start | bytes 393224 | tf_op jit(solution)/shard_map/ppermute | solution.py:478
  41.8 8.4 %collective-permute-start.3 = (f32[64,1024]{1,0:T(8,128)S(1)}, f32[64,1024]{1,0:T(8,128)S(1)}, u32[]{:S(2)}, u32[]{:S(2)}) collective-permute-start(f32[64,1024]{1,0:T(8,128)S(1)} %get-tuple-element.51), channel_id=1, source_target_pairs={{0,2},{1,3},{2,0},{3,1},{4,6},{5,7},{6,4},{7,5}} | collective-permute-start | bytes 786440 | tf_op jit(solution)/shard_map/ppermute | solution.py:481

commit v3 on v2

v3 whole, which is shorter than its diff:
```python
import jax
import jax.numpy as jnp
from jax import lax
from jax.experimental import pallas as pl
from jax.experimental.pallas import tpu as pltpu
from jax.sharding import PartitionSpec as P

EPS = 1e-6
BF = jnp.bfloat16
F32 = jnp.float32
I32 = jnp.int32
GELU_C = 0.7978845608028654
GELU_A = 0.044715
VMEM = pltpu.VMEM
SMEM_SPEC = pl.BlockSpec(memory_space=pltpu.SMEM)
ANY_SPEC = pl.BlockSpec(memory_space=pl.ANY)
HBM_SPEC = pl.BlockSpec(memory_space=pltpu.HBM)
VMEM_SPEC = pl.BlockSpec(memory_space=VMEM)
DMA = pltpu.SemaphoreType.DMA
TILE = 256
ZERO_ROWS = 96
FILL_0, FILL_1, FILL_2 = 15, 62, 20
MIB = 1 << 20
LOOKUP_VMEM = 48 * MIB


def mm(a, b, ca, cb):
    return lax.dot_general(a, b, (((ca,), (cb,)), ((), ())), preferred_element_type=F32)


def sh(shape, dtype):
    return jax.ShapeDtypeStruct(shape, dtype)


def fill_copy(zero, table_g, sem, i):
    return pltpu.make_async_copy(zero, table_g.at[pl.ds(pl.multiple_of(i * ZERO_ROWS, ZERO_ROWS), ZERO_ROWS)], sem)


def fill_start(zero, table_g, sem, lo, hi):
    zero[...] = jnp.zeros_like(zero)

    def body(i, carry):
        fill_copy(zero, table_g, sem, i).start()
        return carry

    lax.fori_loop(lo, hi, body, 0)


def fill_wait(zero, table_g, sem, lo, hi):
    def body(i, carry):
        fill_copy(zero, table_g, sem, i).wait()
        return carry

    lax.fori_loop(lo, hi, body, 0)


def swap_with_sibling():
    sib = lax.axis_index("tp") ^ 1
    barrier = pltpu.get_barrier_semaphore()
    pl.semaphore_signal(barrier, inc=1, device_id={"tp": sib}, device_id_type=pl.DeviceIdType.MESH)
    pl.semaphore_wait(barrier, 1)

    def remote(src, dst, sems, i):
        return pltpu.make_async_remote_copy(
            src_ref=src, dst_ref=dst, send_sem=sems.at[0, i], recv_sem=sems.at[1, i],
            device_id={"tp": sib}, device_id_type=pl.DeviceIdType.MESH)

    return remote


def lookup_kernel(ids_s, ids_v, table, part, rows_mine, same, table_g, pairs, zero, sems, s_zero):
    tokens, vocab = part.shape[0], table.shape[0]
    base = lax.axis_index("tp") * vocab
    group = 64
    groups = tokens // group
    fill_start(zero, table_g, s_zero, 0, FILL_0)
    for k in range(groups):
        def fetch(i, carry):
            lid = ids_s[k * group + i] - base
            owned = (lid >= 0) & (lid < vocab)
            pair_id = jnp.where(owned, lid >> 1, i)
            pltpu.make_async_copy(
                table.at[pl.ds(pl.multiple_of(pair_id << 1, 2), 2)],
                pairs.at[pl.ds(pl.multiple_of(k * group * 2 + i * 2, 2), 2)],
                sems.at[k],
            ).start()
            return carry

        lax.fori_loop(0, group, fetch, 0, unroll=8)
    row = jnp.broadcast_to(ids_v[...].astype(F32), (tokens, tokens))
    col = row.T
    equal = row == col
    same[...] = jnp.where(equal, 1.0, 0.0).astype(BF)
    earlier = lax.broadcasted_iota(I32, (tokens, tokens), 0) < lax.broadcasted_iota(I32, (tokens, tokens), 1)
    repeat = jnp.max(jnp.where(equal & earlier, 1, 0), axis=0, keepdims=True)
    mine = ids_v[...] - base
    rows_mine[...] = jnp.where((mine >= 0) & (mine < vocab) & (repeat == 0), mine, -1)
    lid = col.astype(I32) - base
    lane = lax.broadcasted_iota(I32, (group, 2 * group), 1)
    first = lax.broadcasted_iota(I32, (group, 2 * group), 0) * 2
    for k in range(groups):
        at = lid[k * group:(k + 1) * group, :2 * group]
        owned = (at >= 0) & (at < vocab)
        pick = jnp.where(owned & (lane == first + (at & 1)), 1.0, 0.0).astype(BF)
        rows = pl.ds(k * group * 2, group * 2)
        pltpu.make_async_copy(table.at[pl.ds(0, group * 2)], pairs.at[rows], sems.at[k]).wait()
        part[pl.ds(k * group, group), :] = mm(pick, pairs[rows, :], 1, 0).astype(BF)
    fill_wait(zero, table_g, s_zero, 0, FILL_0)


def lookup(ids, table):
    tokens, (vocab, width) = ids.shape[0], table.shape
    return pl.pallas_call(
        lookup_kernel,
        name="lookup",
        out_shape=[sh((tokens, width), BF), sh((1, tokens), I32), sh((tokens, tokens), BF), sh((vocab, width), F32)],
        in_specs=[SMEM_SPEC, VMEM_SPEC, HBM_SPEC],
        out_specs=[VMEM_SPEC] * 3 + [HBM_SPEC],
        scratch_shapes=[VMEM((tokens * 2, width), BF), VMEM((ZERO_ROWS, width), F32), DMA((4,)), DMA(())],
        compiler_params=pltpu.CompilerParams(vmem_limit_bytes=LOOKUP_VMEM),
        cost_estimate=pl.CostEstimate(flops=5_000_000_000, bytes_accessed=10 * MIB, transcendentals=0),
    )(ids, ids.reshape(1, tokens), table)


def pair_kernel(part, comb, part_r, sems):
    me = lax.axis_index("tp")
    rows = part.shape[0] // 4
    blocks = (me, me ^ 2, me ^ 1, me ^ 3)
    remote = swap_with_sibling()
    block = lambda k: pl.ds(pl.multiple_of(blocks[k] * rows, rows), rows)
    copies = [remote(part.at[block(2 + k)], part_r.at[pl.ds(k * rows, rows)], sems, k) for k in range(2)]
    for c in copies:
        c.start()
    for k in range(2):
        copies[k].wait()
        at = pl.ds(k * rows, rows)
        comb[at, :] = part[block(k), :] + part_r[at, :]


def pair(part):
    tokens, width = part.shape
    half = tokens // 2
    return pl.pallas_call(
        pair_kernel,
        name="pair",
        out_shape=sh((half, width), BF),
        in_specs=[VMEM_SPEC],
        out_specs=VMEM_SPEC,
        scratch_shapes=[VMEM((half, width), BF), DMA((2, 2))],
        compiler_params=pltpu.CompilerParams(collective_id=0, has_side_effects=True, vmem_limit_bytes=8 * MIB),
        cost_estimate=pl.CostEstimate(flops=3_000_000_000, bytes_accessed=MIB, transcendentals=0),
    )(part)


def fill1_kernel(rows_mine, order, table_in, puts, token, table_g, zero, s_zero):
    fill_start(zero, table_g, s_zero, FILL_0, FILL_0 + FILL_1)
    tokens = rows_mine.shape[1]

    def body(i, count):
        lid = rows_mine[0, i]
        puts[count] = lid | (i << 16)
        return count + (lid >= 0).astype(I32)

    puts[tokens] = lax.fori_loop(0, tokens, body, 0, unroll=8)
    token[...] = jnp.zeros_like(token)
    fill_wait(zero, table_g, s_zero, FILL_0, FILL_0 + FILL_1)


def fill1(rows_mine, order, table_g):
    return pl.pallas_call(
        fill1_kernel,
        name="fill1",
        out_shape=[sh((2 * rows_mine.shape[1],), I32), sh((8, 128), F32), sh(table_g.shape, F32)],
        in_specs=[SMEM_SPEC, ANY_SPEC, HBM_SPEC],
        out_specs=[SMEM_SPEC, VMEM_SPEC, HBM_SPEC],
        input_output_aliases={2: 2},
        scratch_shapes=[VMEM((ZERO_ROWS, table_g.shape[1]), F32), DMA(())],
        compiler_params=pltpu.CompilerParams(vmem_limit_bytes=12 * MIB),
        cost_estimate=pl.CostEstimate(flops=8_000_000_000, bytes_accessed=20 * MIB, transcendentals=0),
    )(rows_mine, order, table_g)


def mlp_kernel(comb, e2, d_own, d_far, w1, w2, gain, order, n, h, du, d_full, x_own, dn_own, dn_far, x_f, d_r, dn_p, g1_r, sems):
    tokens, width = n.shape
    hid = h.shape[1]
    rows = x_own.shape[0]
    half = 2 * rows
    remote = swap_with_sibling()
    e3 = []
    for k in range(2):
        at, other = pl.ds(k * rows, rows), pl.ds((1 - k) * rows, rows)
        x_f[at, :] = comb[at, :] + e2[other, :]
        c = remote(x_f.at[at], x_f.at[pl.ds(half + k * rows, rows)], sems, k)
        c.start()
        e3.append(c)
    ds = [remote(src, d_r.at[pl.ds(k * rows, rows)], sems, 2 + k) for k, src in enumerate((d_own, d_far))]
    for c in ds:
        c.start()
    d_full[pl.ds(0, rows), :] = d_own[...]
    d_full[pl.ds(rows, rows), :] = d_far[...]
    gain_f = gain[...].astype(F32).reshape(1, width)

    def norm_half(k):
        for j in range(4):
            at = pl.ds(k * half + j * 32, 32)
            x = x_f[at, :].astype(F32)
            r = lax.rsqrt(jnp.mean(x * x, axis=-1, keepdims=True) + EPS)
            n[at, :] = (x * r * gain_f).astype(BF)

    def fwd_half(k):
        at = pl.ds(k * half, half)
        for j in range(hid // TILE):
            cols = pl.ds(j * TILE, TILE)
            g = mm(d_full[at, :], w2[cols, :], 1, 1).astype(BF).astype(F32)
            u = mm(n[at, :], w1[:, cols], 1, 0).astype(BF).astype(F32)
            t = jnp.tanh(GELU_C * (u + GELU_A * (u * u * u)))
            cdf = 0.5 * (1.0 + t)
            h[at, cols] = (u * cdf).astype(BF)
            du[at, cols] = (g * (cdf + u * (0.5 * (1.0 - t * t)) * (GELU_C * (1.0 + 3.0 * GELU_A * (u * u))))).astype(BF)

    def dn_half(k, sent):
        at = pl.ds(k * half, half)
        for j in range(width // TILE):
            cols = pl.ds(j * TILE, TILE)
            dn_p[at, cols] = mm(du[at, :], w1[cols, :], 1, 1)
            if sent is not None:
                sent.append(remote(dn_p.at[at, cols], g1_r.at[:, cols], sems, 4 + j))
                sent[-1].start()

    norm_half(0)
    fwd_half(0)
    for c in e3 + ds:
        c.wait()
    d_full[pl.ds(half, half), :] = d_r[...]
    norm_half(1)
    fwd_half(1)
    g1 = []
    dn_half(1, g1)
    dn_half(0, None)
    x_own[...] = x_f[pl.ds(0, rows), :]
    for j, c in enumerate(g1):
        c.wait()
        cols = pl.ds(j * TILE, TILE)
        dn_far[:, cols] = dn_p[pl.ds(rows, rows), cols] + g1_r[pl.ds(rows, rows), cols]
        dn_own[:, cols] = dn_p[pl.ds(0, rows), cols] + g1_r[pl.ds(0, rows), cols]


def mlp(comb, e2, d_own, d_far, w1, w2, gain, order):
    half, width = comb.shape
    tokens, rows = 2 * half, half // 2
    hid = w1.shape[1]
    return pl.pallas_call(
        mlp_kernel,
        name="mlp",
        out_shape=[sh((tokens, width), BF), sh((tokens, hid), BF), sh((tokens, hid), BF), sh((tokens, width), BF), sh((rows, width), BF),
                   sh((rows, width), F32), sh((rows, width), F32)],
        in_specs=[VMEM_SPEC] * 7 + [ANY_SPEC],
        out_specs=[VMEM_SPEC] * 7,
        scratch_shapes=[VMEM((tokens, width), BF), VMEM((half, width), BF), VMEM((tokens, width), F32), VMEM((half, width), F32), DMA((2, 8))],
        compiler_params=pltpu.CompilerParams(collective_id=1, has_side_effects=True, vmem_limit_bytes=16 * MIB),
        cost_estimate=pl.CostEstimate(flops=6_000_000_000, bytes_accessed=4 * MIB, transcendentals=0),
    )(comb, e2, d_own, d_far, w1, w2, gain, order)


def ysum_kernel(h, w2, y_own, y_far0, y_far1, y_p, y_r, sems):
    rows, width = y_own.shape
    half = 2 * rows
    remote = swap_with_sibling()
    copies = []
    for k in (1, 0):
        at = pl.ds(k * half, half)
        for j in range(width // TILE):
            cols = pl.ds(j * TILE, TILE)
            y_p[at, cols] = mm(h[at, :], w2[:, cols], 1, 0)
            if k == 1:
                copies.append(remote(y_p.at[at, cols], y_r.at[:, cols], sems, j))
                copies[-1].start()
    for j, c in enumerate(copies):
        c.wait()
        cols = pl.ds(j * TILE, TILE)
        y_own[:, cols] = y_p[pl.ds(0, rows), cols] + y_r[pl.ds(0, rows), cols]
        for k, out in enumerate((y_far0, y_far1)):
            at = pl.ds(rows + k * (rows // 2), rows // 2)
            out[:, cols] = y_p[at, cols] + y_r[at, cols]


def ysum(h, w2):
    tokens, width = h.shape[0], w2.shape[1]
    rows = tokens // 4
    return pl.pallas_call(
        ysum_kernel,
        name="ysum",
        out_shape=[sh((rows, width), F32), sh((rows // 2, width), F32), sh((rows // 2, width), F32)],
        in_specs=[VMEM_SPEC, VMEM_SPEC],
        out_specs=[VMEM_SPEC] * 3,
        scratch_shapes=[VMEM((tokens, width), F32), VMEM((2 * rows, width), F32), DMA((2, 4))],
        compiler_params=pltpu.CompilerParams(collective_id=2, has_side_effects=True, vmem_limit_bytes=12 * MIB),
        cost_estimate=pl.CostEstimate(flops=3_000_000_000, bytes_accessed=4 * MIB, transcendentals=0),
    )(h, w2)


def grads_kernel(n, h, du, d_full, order, table_in, token, dw1, dw2, table_g, zero, dw1_v, dw2_v, s_zero, s_w):
    lo, hi = FILL_0 + FILL_1, FILL_0 + FILL_1 + FILL_2
    fill_start(zero, table_g, s_zero, lo, hi)
    token[...] = jnp.zeros_like(token)
    width, hid = dw1.shape
    n_t = n[...].T
    for j in range(width // TILE):
        at = slice(j * TILE, (j + 1) * TILE)
        dw1_v[at, :] = mm(n_t[at, :], du[...], 1, 0)
        pltpu.make_async_copy(dw1_v.at[pl.ds(j * TILE, TILE)], dw1.at[pl.ds(j * TILE, TILE)], s_w).start()
    h_t = h[...].T
    for j in range(hid // TILE):
        at = slice(j * TILE, (j + 1) * TILE)
        dw2_v[at, :] = mm(h_t[at, :], d_full[...], 1, 0)
        pltpu.make_async_copy(dw2_v.at[pl.ds(j * TILE, TILE)], dw2.at[pl.ds(j * TILE, TILE)], s_w).start()
    pltpu.make_async_copy(dw1_v, dw1, s_w).wait()
    pltpu.make_async_copy(dw2_v, dw2, s_w).wait()
    fill_wait(zero, table_g, s_zero, lo, hi)


def grads(n, h, du, d_full, order, table_g):
    tokens, width = n.shape
    hid = h.shape[1]
    return pl.pallas_call(
        grads_kernel,
        name="grads",
        out_shape=[sh((8, 128), F32), sh((width, hid), F32), sh((hid, width), F32), sh(table_g.shape, F32)],
        in_specs=[VMEM_SPEC] * 4 + [ANY_SPEC, HBM_SPEC],
        out_specs=[VMEM_SPEC, HBM_SPEC, HBM_SPEC, HBM_SPEC],
        input_output_aliases={5: 3},
        scratch_shapes=[VMEM((ZERO_ROWS, width), F32), VMEM((width, hid), F32), VMEM((hid, width), F32), DMA(()), DMA(())],
        compiler_params=pltpu.CompilerParams(vmem_limit_bytes=24 * MIB),
        cost_estimate=pl.CostEstimate(flops=8_000_000_000, bytes_accessed=20 * MIB, transcendentals=0),
    )(n, h, du, d_full, order, table_g)


def dx_kernel(dn_own, g2, x_own, d_own, gain, order, dx):
    gain_f = gain[...].astype(F32).reshape(1, dx.shape[1])
    for j in range(dx.shape[0] // 16):
        at = pl.ds(j * 16, 16)
        a = (dn_own[at, :] + g2[at, :]) * gain_f
        x = x_own[at, :].astype(F32)
        r = lax.rsqrt(jnp.mean(x * x, axis=-1, keepdims=True) + EPS)
        proj = jnp.mean(a * x, axis=-1, keepdims=True)
        dx[at, :] = (d_own[at, :].astype(F32) + r * (a - x * r * r * proj)).astype(BF)


def dx_rows(dn_own, g2, x_own, d_own, gain, order):
    return pl.pallas_call(
        dx_kernel,
        name="dx_rows",
        out_shape=sh(x_own.shape, BF),
        in_specs=[VMEM_SPEC] * 5 + [ANY_SPEC],
        out_specs=VMEM_SPEC,
        compiler_params=pltpu.CompilerParams(vmem_limit_bytes=4 * MIB),
        cost_estimate=pl.CostEstimate(flops=1_000_000_000, bytes_accessed=MIB, transcendentals=0),
    )(dn_own, g2, x_own, d_own, gain, order)


def fill3_kernel(order, table_in, token, table_g, zero, s_zero):
    lo, hi = FILL_0 + FILL_1 + FILL_2, table_g.shape[0] // ZERO_ROWS
    fill_start(zero, table_g, s_zero, lo, hi)
    token[...] = jnp.zeros_like(token)
    fill_wait(zero, table_g, s_zero, lo, hi)


def fill3(order, table_g):
    return pl.pallas_call(
        fill3_kernel,
        name="fill3",
        out_shape=[sh((8, 128), F32), sh(table_g.shape, F32)],
        in_specs=[ANY_SPEC, HBM_SPEC],
        out_specs=[VMEM_SPEC, HBM_SPEC],
        input_output_aliases={1: 1},
        scratch_shapes=[VMEM((ZERO_ROWS, table_g.shape[1]), F32), DMA(())],
        compiler_params=pltpu.CompilerParams(vmem_limit_bytes=4 * MIB),
        cost_estimate=pl.CostEstimate(flops=5_000_000_000, bytes_accessed=16 * MIB, transcendentals=0),
    )(order, table_g)


def dx_all_kernel(dx, dx_far, order, dx_out, dx_r, sems):
    me = lax.axis_index("tp")
    rows = dx.shape[0]
    remote = swap_with_sibling()
    block = lambda m: pl.ds(pl.multiple_of((me ^ m) * rows, rows), rows)
    copies = [remote(src, dx_r.at[pl.ds(k * rows, rows)], sems, k) for k, src in enumerate((dx, dx_far))]
    for c in copies:
        c.start()
    dx_out[block(0), :] = dx[...]
    dx_out[block(2), :] = dx_far[...]
    for k, c in enumerate(copies):
        c.wait()
        dx_out[block(1 + 2 * k), :] = dx_r[pl.ds(k * rows, rows), :]


def dx_all(dx, dx_far, order):
    rows, width = dx.shape
    return pl.pallas_call(
        dx_all_kernel,
        name="dx_all",
        out_shape=sh((4 * rows, width), BF),
        in_specs=[VMEM_SPEC] * 2 + [ANY_SPEC],
        out_specs=VMEM_SPEC,
        scratch_shapes=[VMEM((2 * rows, width), BF), DMA((2, 2))],
        compiler_params=pltpu.CompilerParams(collective_id=3, has_side_effects=True, vmem_limit_bytes=4 * MIB),
        cost_estimate=pl.CostEstimate(flops=2_000_000_000, bytes_accessed=MIB, transcendentals=0),
    )(dx, dx_far, order)


def put_kernel(puts, same, dx, table_in, table_g, token, puts_s, total, s_in, s_row):
    tokens = dx.shape[0]
    load = pltpu.make_async_copy(puts, puts_s, s_in)
    load.start()
    total[...] = mm(same[...], dx[...], 1, 0)
    token[...] = jnp.zeros_like(token)
    load.wait()
    count = puts_s[tokens]

    def put(i, carry):
        word = puts_s[i]
        pltpu.make_async_copy(total.at[pl.ds(word >> 16, 1)], table_g.at[pl.ds(word & 0xFFFF, 1)], s_row).start()
        return carry

    lax.fori_loop(0, count, put, 0)

    def put_wait(size):
        def body(i, carry):
            pltpu.make_async_copy(total.at[pl.ds(0, size)], table_g.at[pl.ds(0, size)], s_row).wait()
            return carry

        return body

    lax.fori_loop(0, count >> 3, put_wait(8), 0)
    lax.fori_loop(0, count & 7, put_wait(1), 0)


def put_rows(puts, same, dx, table_g):
    return pl.pallas_call(
        put_kernel,
        name="put_rows",
        out_shape=[sh(table_g.shape, F32), sh((8, 128), F32)],
        in_specs=[ANY_SPEC, VMEM_SPEC, VMEM_SPEC, HBM_SPEC],
        out_specs=[HBM_SPEC, VMEM_SPEC],
        input_output_aliases={3: 0},
        scratch_shapes=[pltpu.SMEM(puts.shape, I32), VMEM(dx.shape, F32), DMA(()), DMA(())],
        compiler_params=pltpu.CompilerParams(vmem_limit_bytes=4 * MIB),
        cost_estimate=pl.CostEstimate(flops=3_000_000_000, bytes_accessed=2 * MIB, transcendentals=0),
    )(puts, same, dx, table_g)


def finish_kernel(x, y, y_in0, y_in1, order, out):
    part = y_in0.shape[0]
    for k, y_in in enumerate((y_in0, y_in1)):
        at = pl.ds(k * part, part)
        out[at, :] = (x[at, :].astype(F32) + (y[at, :] + y_in[...])).astype(BF)


def finish(x, y, y_in0, y_in1, order):
    return pl.pallas_call(
        finish_kernel,
        name="finish",
        out_shape=sh(x.shape, BF),
        in_specs=[VMEM_SPEC] * 4 + [ANY_SPEC],
        out_specs=VMEM_SPEC,
        compiler_params=pltpu.CompilerParams(vmem_limit_bytes=4 * MIB),
        cost_estimate=pl.CostEstimate(flops=1_000_000_000, bytes_accessed=MIB, transcendentals=0),
    )(x, y, y_in0, y_in1, order)


def solution(mesh):
    tp = mesh.shape["tp"]
    far_pairs = [(i, i ^ 2) for i in range(tp)]

    def shard_step(ids, table, gain, w1, w2, d_out):
        part, rows_mine, same, d_table = lookup(ids, table)
        part, d_send = lax.optimization_barrier((part, d_out))
        d_far = lax.ppermute(d_send, "tp", far_pairs)
        comb = pair(part)
        e2 = lax.ppermute(comb, "tp", far_pairs)
        puts, token, d_table = fill1(rows_mine, comb, d_table)
        n, h, du, d_full, x_own, dn_own, dn_far = mlp(comb, e2, d_out, d_far, w1, w2, gain, token)
        g2 = lax.ppermute(dn_far, "tp", far_pairs)
        y_own, y_far0, y_far1 = ysum(h, w2)
        y_in0 = lax.ppermute(y_far0, "tp", far_pairs)
        token, d_w1, d_w2, d_table = grads(n, h, du, d_full, y_own, d_table)
        dx = dx_rows(dn_own, g2, x_own, d_out, gain, token)
        dx_far = lax.ppermute(dx, "tp", far_pairs)
        dx, y_far1 = lax.optimization_barrier((dx, y_far1))
        y_in1 = lax.ppermute(y_far1, "tp", far_pairs)
        token, d_table = fill3(dx, d_table)
        dx_full = dx_all(dx, dx_far, token)
        d_table, done = put_rows(puts, same, dx_full, d_table)
        out = finish(x_own, y_own, y_in0, y_in1, done)
        return out, d_table, d_w1, d_w2

    return jax.shard_map(
        shard_step,
        mesh=mesh,
        in_specs=(P("dp"), P("tp", None), P(None), P(None, "tp"), P("tp", None), P(("dp", "tp"), None)),
        out_specs=(P(("dp", "tp"), None), P(("dp", "tp"), None), P("dp", "tp"), P(("dp", "tp"), None)),
        check_vma=False,
    )
```

time: 51 us -> 49.6 us (0.973)
  Pallas kernels: 41.5 us -> 40.2 us
    pallas_call x1, Pallas kernels: 1.94 us -> 4.79 us  [fill3(): pl.pallas_call(fill3_kernel, name='fill3', out_shape=[sh((8, 128), F32),...]
    pallas_call x1, Pallas kernels: 7.77 us -> 5.47 us  [lookup(): pl.pallas_call(lookup_kernel, name='lookup', out_shape=[sh((tokens, width...]
    pallas_call x2, Pallas kernels: 16.8 us -> 15 us  [the longest x1 9.26 us: fill1(): pl.pallas_call(fill1_kernel, name='fill1', out_shape=[sh((2 * rows_mine.s...]
    ppermute x1, starting transfers between devices: 0.83 us -> 2.02 us  [shard_step(): dx_far = lax.ppermute(dx, 'tp', far_pairs)]
    ppermute x1 -> x2, starting transfers between devices: 1.23 us -> 0.09 us  [the longest x1 0.05 us: shard_step(): y_in0 = lax.ppermute(y_far0, 'tp', far_pairs)]
    pallas_call x1, Pallas kernels: 3.35 us -> 2.41 us  [put_rows(): pl.pallas_call(put_kernel, name='put_rows', out_shape=[sh(table_g.shape,...]
  transfers between devices with their start and end apart: 5 -> 6, of which waited for: 1 -> 0; matrix products, arithmetic and copies ran while one was open for 0% -> 0% of each run, Pallas kernels for 54% -> 57%
where the time goes in v3:
time: 49.6 us; the launch traced here: 49.3 us
  Pallas kernels  40.2 us (81%)
  starting transfers between devices  7.53 us (15%)
  between operations  0.81 us (2%)
  local copies, waits for them, and re-layouts  0.69 us (1%)
    pallas_call x1, Pallas kernels, fill1(): pl.pallas_call(fill1_kernel, name='fill1', out_shape=[sh((2 * rows_mine.s...  9.26 us
    pallas_call x1, Pallas kernels, mlp(): pl.pallas_call(mlp_kernel, name='mlp', out_shape=[sh((tokens, width), BF)...  5.89 us
    pallas_call x1, Pallas kernels, grads(): pl.pallas_call(grads_kernel, name='grads', out_shape=[sh((8, 128), F32),...  5.77 us
    pallas_call x1, Pallas kernels, lookup(): pl.pallas_call(lookup_kernel, name='lookup', out_shape=[sh((tokens, width...  5.47 us
    pallas_call x1, Pallas kernels, fill3(): pl.pallas_call(fill3_kernel, name='fill3', out_shape=[sh((8, 128), F32),...  4.79 us
    ppermute x1, starting transfers between devices, shard_step(): d_far = lax.ppermute(d_send, 'tp', far_pairs)  3.36 us
    pallas_call x1, Pallas kernels, ysum(): pl.pallas_call(ysum_kernel, name='ysum', out_shape=[sh((rows, width), F32...  2.59 us
    pallas_call x1, Pallas kernels, put_rows(): pl.pallas_call(put_kernel, name='put_rows', out_shape=[sh(table_g.shape,...  2.41 us
  transfers between devices with their start and end apart: 6, of which 0 were waited for; matrix products, arithmetic and copies ran while one was open for 0% of the time, Pallas kernels for 57%

profile of v3, /device:TPU:0, one launch (start us, length us, event | category | flops | bytes accessed | tf_op | source)
XLA Modules:
  0.0 49.3 jit_solution(14735812043448986018)
XLA Ops:
  0.6 0.0 copy-start
  0.6 0.7 %copy-done = s32[256]{0:T(256)S(1)} copy-done((s32[256]{0:T(256)S(1)}, s32[256]{0:T(256)}, u32[]{:S(2)}) %copy-start) | copy-done | bytes 1048
  1.3 0.0 copy-start.1
  1.3 0.0 copy-start.2
  1.3 0.0 copy-start.3
  1.3 0.0 copy-start.4
  1.3 5.5 %lookup.1 = (bf16[256,1024]{1,0:T(8,128)(2,1)S(1)}, s32[1,256]{1,0:T(1,128)S(1)}, bf16[256,256]{1,0:T(8,128)(2,1)S(1)}, f32[12576,1024]{1,0:T(8,128)}) custom-call(s32[256]{0:T(256)S(1)} %copy-done, s32[1,256]{1,0:T(1,128)S(1)} %bitcast.1, bf16[12576,1024]{1,0:T(8,128)(2,1)} %table.1), custom_call_target="tpu_custom_call" | custom-call | flops 5000000000 | bytes 10485760 | tf_op jit(solution)/shard_map/lookup/pallas_call | solution.py:113
  6.8 3.4 %collective-permute-start.1 = (bf16[64,1024]{1,0:T(8,128)(2,1)}, bf16[64,1024]{1,0:T(8,128)(2,1)S(1)}, u32[]{:S(2)}, u32[]{:S(2)}) collective-permute-start(bf16[64,1024]{1,0:T(8,128)(2,1)} %d_own.3), channel_id=1, source_target_pairs={{0,2},{1,3},{2,0},{3,1},{4,6},{5,7},{6,4},{7,5}} | collective-permute-start | bytes 393224 | tf_op jit(solution)/shard_map/ppermute | solution.py:478
  10.2 1.6 %pair.1.order.comb = bf16[128,1024]{1,0:T(8,128)(2,1)S(1)} custom-call(bf16[256,1024]{1,0:T(8,128)(2,1)S(1)} %get-tuple-element.34.part), custom_call_target="tpu_custom_call" | custom-call | flops 3000000000 | bytes 1048576 | tf_op jit(solution)/shard_map/pair/pallas_call | solution.py:143
  11.8 0.1 collective-permute-start
  11.8 9.3 %fill1.1 = (s32[512]{0:T(512)S(1)}, f32[8,128]{1,0:T(8,128)S(1)}, f32[12576,1024]{1,0:T(8,128)}) custom-call(s32[1,256]{1,0:T(1,128)S(1)} %get-tuple-element.36.rows_mine, bf16[128,1024]{1,0:T(8,128)(2,1)S(1)} %pair.1.order.comb, f32[12576,1024]{1,0:T(8,128)} %get-tuple-element.37.table_in), custom_call_target="tpu_custom_call", output_to_operand_aliasing={{2}: (2, {})} | custom-call | flops 8000000000 | bytes 20971520 | tf_op jit(solution)/shard_map/fill1/pallas_call | solution.py:170
  21.1 0.0 collective-permute-done.1.d_far
  21.1 0.0 collective-permute-done.e2
  21.1 0.0 copy-done.1
  21.1 0.0 copy-done.2
  21.1 0.0 copy-done.3
  21.1 0.0 copy-done.4
  21.1 5.9 %mlp.1 = (bf16[256,1024]{1,0:T(8,128)(2,1)S(1)}, bf16[256,1024]{1,0:T(8,128)(2,1)S(1)}, bf16[256,1024]{1,0:T(8,128)(2,1)S(1)}, bf16[256,1024]{1,0:T(8,128)(2,1)S...) custom-call(bf16[128,1024]{1,0:T(8,128)(2,1)S(1)} %pair.1.order.comb, ...), custom_call_target="tpu_custom_call" | custom-call | flops 6000000000 | bytes 4194304 | tf_op jit(solution)/shard_map/mlp/pallas_call | solution.py:252
  27.0 2.0 %collective-permute-start.3 = (f32[64,1024]{1,0:T(8,128)S(1)}, f32[64,1024]{1,0:T(8,128)S(1)}, u32[]{:S(2)}, u32[]{:S(2)}) collective-permute-start(f32[64,1024]{1,0:T(8,128)S(1)} %get-tuple-element.44), channel_id=1, source_target_pairs={{0,2},{1,3},{2,0},{3,1},{4,6},{5,7},{6,4},{7,5}} | collective-permute-start | bytes 786440 | tf_op jit(solution)/shard_map/ppermute | solution.py:483
  29.1 2.6 %ysum.1 = (f32[64,1024]{1,0:T(8,128)S(1)}, f32[32,1024]{1,0:T(8,128)S(1)}, f32[32,1024]{1,0:T(8,128)S(1)}) custom-call(bf16[256,1024]{1,0:T(8,128)(2,1)S(1)} %get-tuple-element.40.h, bf16[1024,1024]{1,0:T(8,128)(2,1)S(1)} %copy-done.2), custom_call_target="tpu_custom_call" | custom-call | flops 3000000000 | bytes 4194304 | tf_op jit(solution)/shard_map/ysum/pallas_call | solution.py:290
  31.6 0.1 collective-permute-start.2
  31.7 5.8 %grads.1 = (f32[8,128]{1,0:T(8,128)S(1)}, f32[1024,1024]{1,0:T(8,128)}, f32[1024,1024]{1,0:T(8,128)}, f32[12576,1024]{1,0:T(8,128)}) custom-call(bf16[256,1024]{1,0:T(8,128)(2,1)S(1)} %get-tuple-element.45.n, bf16[256,1024]{1,0:T(8,128)(2,1)S(1)} %get-tuple-element.40.h, ...), custom_call_target="tpu_custom_call", output_to_operand_aliasing={{3}: (5, {})} | custom-call | flops 8000000000 | bytes 20971520 | tf_op jit(solution)/shard_map/grads/pallas_call | solution.py:325
  37.5 0.0 collective-permute-done.3.g2
  37.5 0.2 dx_rows.1.order.dx
  37.7 2.0 %collective-permute-start.5 = (bf16[64,1024]{1,0:T(8,128)(2,1)S(1)}, bf16[64,1024]{1,0:T(8,128)(2,1)S(1)}, u32[]{:S(2)}, u32[]{:S(2)}) collective-permute-start(bf16[64,1024]{1,0:T(8,128)(2,1)S(1)} %dx_rows.1.order.dx), channel_id=1, source_target_pairs={{0,2},{1,3},{2,0},{3,1},{4,6},{5,7},{6,4},{7,5}} | collective-permute-start | bytes 393224 | tf_op jit(solution)/shard_map/ppermute | solution.py:488
  39.7 0.0 collective-permute-start.4
  39.7 4.8 %fill3.1 = (f32[8,128]{1,0:T(8,128)S(1)}, f32[12576,1024]{1,0:T(8,128)}) custom-call(bf16[64,1024]{1,0:T(8,128)(2,1)S(1)} %dx_rows.1.order.dx, f32[12576,1024]{1,0:T(8,128)} %get-tuple-element.55.table_in), custom_call_target="tpu_custom_call", output_to_operand_aliasing={{1}: (1, {})} | custom-call | flops 5000000000 | bytes 16777216 | tf_op jit(solution)/shard_map/fill3/pallas_call | solution.py:369
  44.5 0.0 collective-permute-done.5.dx_far
  44.5 1.6 %dx_all.1.dx = bf16[256,1024]{1,0:T(8,128)(2,1)S(1)} custom-call(bf16[64,1024]{1,0:T(8,128)(2,1)S(1)} %dx_rows.1.order.dx, bf16[64,1024]{1,0:T(8,128)(2,1)S(1)} %collective-permute-done.5.dx_far, f32[8,128]{1,0:T(8,128)S(1)} %get-tuple-element.56.order), custom_call_target="tpu_custom_call" | custom-call | flops 2000000000 | bytes 1048576 | tf_op jit(solution)/shard_map/dx_all/pallas_call | solution.py:399
  46.1 2.4 %put_rows.1 = (f32[12576,1024]{1,0:T(8,128)}, f32[8,128]{1,0:T(8,128)S(1)}) custom-call(s32[512]{0:T(512)S(1)} %get-tuple-element.52.puts, bf16[256,256]{1,0:T(8,128)(2,1)S(1)} %get-tuple-element.53.same, bf16[256,1024]{1,0:T(8,128)(2,1)S(1)} %dx_all.1.dx, f32[12576,1024]{1,0:T(8,128)} %get-tuple-element.57.table_in), custom_call_target="tpu_custom_call", output_to_operand_aliasing={{0}: (3, {})} | custom-call | flops 3000000000 | bytes 2097152 | tf_op jit(solution)/shard_map/put_rows/pallas_call | solution.py:439
  48.6 0.0 collective-permute-done.2.y_in0
  48.6 0.0 collective-permute-done.4.y_in1
  48.6 0.7 %finish.1 = bf16[64,1024]{1,0:T(8,128)(2,1)} custom-call(bf16[64,1024]{1,0:T(8,128)(2,1)S(1)} %get-tuple-element.39.x_own.x, f32[64,1024]{1,0:T(8,128)S(1)} %get-tuple-element.41.order.y, f32[32,1024]{1,0:T(8,128)S(1)} %collective-permute-done.2.y_in0, f32[32,1024]{1,0:T(8,128)S(1)} %collective-permute-done.4.y_in1, f32[8,128]{1,0:T(8,128)S(1)} %get-tuple-element.58.order), custom_call_target="tpu_custom_call" | custom-call | flops 1000000000 | bytes 1048576 | tf_op jit(solution)/shard_map/finish/pallas_call | solution.py:460
Async XLA Ops:
  0.6 0.7 %copy-start = (s32[256]{0:T(256)S(1)}, s32[256]{0:T(256)}, u32[]{:S(2)}) copy-start(s32[256]{0:T(256)} %ids_s.1) | copy-start | bytes 3076
  1.3 19.8 %copy-start.1 = (bf16[1024,1024]{1,0:T(8,128)(2,1)S(1)}, bf16[1024,1024]{1,0:T(8,128)(2,1)}, u32[]{:S(2)}) copy-start(bf16[1024,1024]{1,0:T(8,128)(2,1)} %w1.1) | copy-start | bytes 6291460
  1.3 19.8 %copy-start.2 = (bf16[1024,1024]{1,0:T(8,128)(2,1)S(1)}, bf16[1024,1024]{1,0:T(8,128)(2,1)}, u32[]{:S(2)}) copy-start(bf16[1024,1024]{1,0:T(8,128)(2,1)} %w2.3) | copy-start | bytes 6291460
  1.3 19.8 %copy-start.3 = (bf16[64,1024]{1,0:T(8,128)(2,1)S(1)}, bf16[64,1024]{1,0:T(8,128)(2,1)}, u32[]{:S(2)}) copy-start(bf16[64,1024]{1,0:T(8,128)(2,1)} %d_own.3) | copy-start | bytes 393220
  1.3 19.8 %copy-start.4 = (bf16[1024]{0:T(1024)(128)(2,1)S(1)}, bf16[1024]{0:T(1024)(128)(2,1)}, u32[]{:S(2)}) copy-start(bf16[1024]{0:T(1024)(128)(2,1)} %gain.3) | copy-start | bytes 6148
  6.8 14.3 %collective-permute-start.1 = (bf16[64,1024]{1,0:T(8,128)(2,1)}, bf16[64,1024]{1,0:T(8,128)(2,1)S(1)}, u32[]{:S(2)}, u32[]{:S(2)}) collective-permute-start(bf16[64,1024]{1,0:T(8,128)(2,1)} %d_own.3), channel_id=1, source_target_pairs={{0,2},{1,3},{2,0},{3,1},{4,6},{5,7},{6,4},{7,5}} | collective-permute-start | bytes 393224 | tf_op jit(solution)/shard_map/ppermute | solution.py:478
  11.8 9.3 %collective-permute-start = (bf16[128,1024]{1,0:T(8,128)(2,1)S(1)}, bf16[128,1024]{1,0:T(8,128)(2,1)S(1)}, u32[]{:S(2)}, u32[]{:S(2)}) collective-permute-start(bf16[128,1024]{1,0:T(8,128)(2,1)S(1)} %pair.1.order.comb), channel_id=1, source_target_pairs={{0,2},{1,3},{2,0},{3,1},{4,6},{5,7},{6,4},{7,5}} | collective-permute-start | bytes 786440 | tf_op jit(solution)/shard_map/ppermute | solution.py:480
  27.0 10.4 %collective-permute-start.3 = (f32[64,1024]{1,0:T(8,128)S(1)}, f32[64,1024]{1,0:T(8,128)S(1)}, u32[]{:S(2)}, u32[]{:S(2)}) collective-permute-start(f32[64,1024]{1,0:T(8,128)S(1)} %get-tuple-element.44), channel_id=1, source_target_pairs={{0,2},{1,3},{2,0},{3,1},{4,6},{5,7},{6,4},{7,5}} | collective-permute-start | bytes 786440 | tf_op jit(solution)/shard_map/ppermute | solution.py:483
  31.6 16.9 %collective-permute-start.2 = (f32[32,1024]{1,0:T(8,128)S(1)}, f32[32,1024]{1,0:T(8,128)S(1)}, u32[]{:S(2)}, u32[]{:S(2)}) collective-permute-start(f32[32,1024]{1,0:T(8,128)S(1)} %get-tuple-element.42), channel_id=1, source_target_pairs={{0,2},{1,3},{2,0},{3,1},{4,6},{5,7},{6,4},{7,5}} | collective-permute-start | bytes 393224 | tf_op jit(solution)/shard_map/ppermute | solution.py:485
  37.7 6.9 %collective-permute-start.5 = (bf16[64,1024]{1,0:T(8,128)(2,1)S(1)}, bf16[64,1024]{1,0:T(8,128)(2,1)S(1)}, u32[]{:S(2)}, u32[]{:S(2)}) collective-permute-start(bf16[64,1024]{1,0:T(8,128)(2,1)S(1)} %dx_rows.1.order.dx), channel_id=1, source_target_pairs={{0,2},{1,3},{2,0},{3,1},{4,6},{5,7},{6,4},{7,5}} | collective-permute-start | bytes 393224 | tf_op jit(solution)/shard_map/ppermute | solution.py:488
  39.7 8.9 %collective-permute-start.4 = (f32[32,1024]{1,0:T(8,128)S(1)}, f32[32,1024]{1,0:T(8,128)S(1)}, u32[]{:S(2)}, u32[]{:S(2)}) collective-permute-start(f32[32,1024]{1,0:T(8,128)S(1)} %get-tuple-element.51), channel_id=1, source_target_pairs={{0,2},{1,3},{2,0},{3,1},{4,6},{5,7},{6,4},{7,5}} | collective-permute-start | bytes 393224 | tf_op jit(solution)/shard_map/ppermute | solution.py:490

commit v4 on v3

v4 whole, which is shorter than its diff:
```python
import jax
import jax.numpy as jnp
from jax import lax
from jax.experimental import pallas as pl
from jax.experimental.pallas import tpu as pltpu
from jax.sharding import PartitionSpec as P

EPS = 1e-6
BF = jnp.bfloat16
F32 = jnp.float32
I32 = jnp.int32
GELU_C = 0.7978845608028654
GELU_A = 0.044715
VMEM = pltpu.VMEM
SMEM_SPEC = pl.BlockSpec(memory_space=pltpu.SMEM)
ANY_SPEC = pl.BlockSpec(memory_space=pl.ANY)
HBM_SPEC = pl.BlockSpec(memory_space=pltpu.HBM)
VMEM_SPEC = pl.BlockSpec(memory_space=VMEM)
DMA = pltpu.SemaphoreType.DMA
TILE = 256
ZERO_ROWS = 96
FILL_AT = (0, 15, 83, 102, 124, 131)
MIB = 1 << 20
LOOKUP_VMEM = 48 * MIB
PAIR_VMEM = 8 * MIB


def mm(a, b, ca, cb):
    return lax.dot_general(a, b, (((ca,), (cb,)), ((), ())), preferred_element_type=F32)


def in_hbm(x):
    return pltpu.with_memory_space_constraint(x, pltpu.HBM)


def sh(shape, dtype):
    return jax.ShapeDtypeStruct(shape, dtype)


def fill_copy(zero, table_g, sem, i):
    return pltpu.make_async_copy(zero, table_g.at[pl.ds(pl.multiple_of(i * ZERO_ROWS, ZERO_ROWS), ZERO_ROWS)], sem)


def fill_start(zero, table_g, sem, part):
    def body(i, carry):
        fill_copy(zero, table_g, sem, i).start()
        return carry

    lax.fori_loop(FILL_AT[part], FILL_AT[part + 1], body, 0)


def fill_wait(zero, table_g, sem, part):
    def body(i, carry):
        fill_copy(zero, table_g, sem, i).wait()
        return carry

    lax.fori_loop(FILL_AT[part], FILL_AT[part + 1], body, 0)


def swap_with_sibling():
    sib = lax.axis_index("tp") ^ 1
    barrier = pltpu.get_barrier_semaphore()
    pl.semaphore_signal(barrier, inc=1, device_id={"tp": sib}, device_id_type=pl.DeviceIdType.MESH)
    pl.semaphore_wait(barrier, 1)

    def remote(src, dst, sems, i):
        return pltpu.make_async_remote_copy(
            src_ref=src, dst_ref=dst, send_sem=sems.at[0, i], recv_sem=sems.at[1, i],
            device_id={"tp": sib}, device_id_type=pl.DeviceIdType.MESH)

    return remote


def lookup_kernel(ids, ids_row, table, part, rows_mine, same, zero, table_g, ids_s, ids_v, pairs, sems, s_zero, s_ids):
    tokens, vocab = part.shape[0], table.shape[0]
    base = lax.axis_index("tp") * vocab
    group = 64
    groups = tokens // group
    loads = [pltpu.make_async_copy(ids, ids_s, s_ids.at[0]), pltpu.make_async_copy(ids_row, ids_v, s_ids.at[1])]
    for c in loads:
        c.start()
    zero[...] = jnp.zeros_like(zero)
    fill_start(zero, table_g, s_zero, 0)
    loads[0].wait()
    for k in range(groups):
        def fetch(i, carry):
            lid = ids_s[k * group + i] - base
            owned = (lid >= 0) & (lid < vocab)
            pair_id = jnp.where(owned, lid >> 1, i)
            pltpu.make_async_copy(
                table.at[pl.ds(pl.multiple_of(pair_id << 1, 2), 2)],
                pairs.at[pl.ds(pl.multiple_of(k * group * 2 + i * 2, 2), 2)],
                sems.at[k],
            ).start()
            return carry

        lax.fori_loop(0, group, fetch, 0, unroll=8)
    loads[1].wait()
    row = jnp.broadcast_to(ids_v[...].astype(F32), (tokens, tokens))
    col = row.T
    equal = row == col
    same[...] = jnp.where(equal, 1.0, 0.0).astype(BF)
    earlier = lax.broadcasted_iota(I32, (tokens, tokens), 0) < lax.broadcasted_iota(I32, (tokens, tokens), 1)
    repeat = jnp.max(jnp.where(equal & earlier, 1, 0), axis=0, keepdims=True)
    mine = ids_v[...] - base
    rows_mine[...] = jnp.where((mine >= 0) & (mine < vocab) & (repeat == 0), mine, -1)
    lid = col.astype(I32) - base
    lane = lax.broadcasted_iota(I32, (group, 2 * group), 1)
    first = lax.broadcasted_iota(I32, (group, 2 * group), 0) * 2
    for k in range(groups):
        at = lid[k * group:(k + 1) * group, :2 * group]
        owned = (at >= 0) & (at < vocab)
        pick = jnp.where(owned & (lane == first + (at & 1)), 1.0, 0.0).astype(BF)
        rows = pl.ds(k * group * 2, group * 2)
        pltpu.make_async_copy(table.at[pl.ds(0, group * 2)], pairs.at[rows], sems.at[k]).wait()
        part[pl.ds(k * group, group), :] = mm(pick, pairs[rows, :], 1, 0).astype(BF)
    fill_wait(zero, table_g, s_zero, 0)


def lookup(ids, table):
    tokens, (vocab, width) = ids.shape[0], table.shape
    return pl.pallas_call(
        lookup_kernel,
        name="lookup",
        out_shape=[sh((tokens, width), BF), sh((1, tokens), I32), sh((tokens, tokens), BF), sh((ZERO_ROWS, width), F32), sh((vocab, width), F32)],
        in_specs=[HBM_SPEC] * 3,
        out_specs=[VMEM_SPEC] * 4 + [HBM_SPEC],
        scratch_shapes=[pltpu.SMEM((tokens,), I32), VMEM((1, tokens), I32), VMEM((tokens * 2, width), BF), DMA((4,)), DMA(()), DMA((2,))],
        compiler_params=pltpu.CompilerParams(vmem_limit_bytes=LOOKUP_VMEM),
        cost_estimate=pl.CostEstimate(flops=5_000_000_000, bytes_accessed=10 * MIB, transcendentals=0),
    )(in_hbm(ids), in_hbm(ids.reshape(1, tokens)), in_hbm(table))


def pair_kernel(part, d_out, send, part_r, sems, s_in):
    me = lax.axis_index("tp")
    rows = d_out.shape[0]
    blocks = (me, me ^ 2, me ^ 1, me ^ 3)
    load = pltpu.make_async_copy(d_out, send.at[pl.ds(2 * rows, rows)], s_in)
    load.start()
    remote = swap_with_sibling()
    block = lambda k: pl.ds(pl.multiple_of(blocks[k] * rows, rows), rows)
    copies = [remote(part.at[block(2 + k)], part_r.at[pl.ds(k * rows, rows)], sems, k) for k in range(2)]
    for c in copies:
        c.start()
    for k in range(2):
        copies[k].wait()
        at = pl.ds(k * rows, rows)
        send[at, :] = part[block(k), :] + part_r[at, :]
    load.wait()


def pair(part, d_out):
    rows, width = d_out.shape
    return pl.pallas_call(
        pair_kernel,
        name="pair",
        out_shape=sh((3 * rows, width), BF),
        in_specs=[VMEM_SPEC, HBM_SPEC],
        out_specs=VMEM_SPEC,
        scratch_shapes=[VMEM((2 * rows, width), BF), DMA((2, 2)), DMA(())],
        compiler_params=pltpu.CompilerParams(collective_id=0, has_side_effects=True, vmem_limit_bytes=PAIR_VMEM),
        cost_estimate=pl.CostEstimate(flops=3_000_000_000, bytes_accessed=MIB, transcendentals=0),
    )(part, d_out)


def fill1_kernel(rows_mine, zero, order, table_in, puts, token, table_g, mine_s, puts_s, s_zero, s_list):
    load = pltpu.make_async_copy(rows_mine, mine_s, s_list)
    load.start()
    fill_start(zero, table_g, s_zero, 1)
    tokens = rows_mine.shape[1]
    token[...] = jnp.zeros_like(token)
    load.wait()

    def body(i, count):
        lid = mine_s[0, i]
        puts_s[count] = lid | (i << 16)
        return count + (lid >= 0).astype(I32)

    puts_s[tokens] = lax.fori_loop(0, tokens, body, 0, unroll=8)
    store = pltpu.make_async_copy(puts_s, puts, s_list)
    store.start()
    store.wait()
    fill_wait(zero, table_g, s_zero, 1)


def fill1(rows_mine, zero, order, table_g):
    tokens = rows_mine.shape[1]
    return pl.pallas_call(
        fill1_kernel,
        name="fill1",
        out_shape=[sh((2 * tokens,), I32), sh((8, 128), F32), sh(table_g.shape, F32)],
        in_specs=[ANY_SPEC, VMEM_SPEC, ANY_SPEC, HBM_SPEC],
        out_specs=[ANY_SPEC, VMEM_SPEC, HBM_SPEC],
        input_output_aliases={3: 2},
        scratch_shapes=[pltpu.SMEM((1, tokens), I32), pltpu.SMEM((2 * tokens,), I32), DMA(()), DMA(())],
        compiler_params=pltpu.CompilerParams(vmem_limit_bytes=8 * MIB),
        cost_estimate=pl.CostEstimate(flops=9_000_000_000, bytes_accessed=20 * MIB, transcendentals=0),
    )(rows_mine, zero, order, table_g)


def share_kernel(send, got, order, x_f, d_full, x_r, d_r, sems):
    rows = send.shape[0] // 3
    half = 2 * rows
    remote = swap_with_sibling()
    copies = []
    for k in range(2):
        at, other = pl.ds(k * rows, rows), pl.ds((1 - k) * rows, rows)
        x_f[at, :] = send[at, :] + got[other, :]
        copies.append(remote(x_f.at[at], x_r.at[at], sems, k))
        copies[-1].start()
    for k, src in enumerate((send, got)):
        copies.append(remote(src.at[pl.ds(half, rows)], d_r.at[pl.ds(k * rows, rows)], sems, 2 + k))
        copies[-1].start()
        d_full[pl.ds(k * rows, rows), :] = src[pl.ds(half, rows), :]
    for k in range(2):
        copies[k].wait()
        x_f[pl.ds(half + k * rows, rows), :] = x_r[pl.ds(k * rows, rows), :]
    for k in range(2):
        copies[2 + k].wait()
        d_full[pl.ds(half + k * rows, rows), :] = d_r[pl.ds(k * rows, rows), :]


def share(send, got, order):
    rows, width = send.shape[0] // 3, send.shape[1]
    return pl.pallas_call(
        share_kernel,
        name="share",
        out_shape=[sh((4 * rows, width), BF)] * 2,
        in_specs=[VMEM_SPEC] * 2 + [ANY_SPEC],
        out_specs=[VMEM_SPEC] * 2,
        scratch_shapes=[VMEM((2 * rows, width), BF), VMEM((2 * rows, width), BF), DMA((2, 4))],
        compiler_params=pltpu.CompilerParams(collective_id=1, has_side_effects=True, vmem_limit_bytes=8 * MIB),
        cost_estimate=pl.CostEstimate(flops=3_000_000_000, bytes_accessed=MIB, transcendentals=0),
    )(send, got, order)


def mlp_kernel(x_f, d_full, w1, w2, gain, zero, table_in, n, h, du, dn_p, y_p, table_g, s_zero):
    fill_start(zero, table_g, s_zero, 2)
    tokens, width = n.shape
    hid = h.shape[1]
    gain_f = gain[...].astype(F32).reshape(1, width)
    for j in range(tokens // 32):
        at = pl.ds(j * 32, 32)
        x = x_f[at, :].astype(F32)
        r = lax.rsqrt(jnp.mean(x * x, axis=-1, keepdims=True) + EPS)
        n[at, :] = (x * r * gain_f).astype(BF)
    for j in range(hid // TILE):
        cols = pl.ds(j * TILE, TILE)
        g = mm(d_full[...], w2[cols, :], 1, 1).astype(BF).astype(F32)
        u = mm(n[...], w1[:, cols], 1, 0).astype(BF).astype(F32)
        t = jnp.tanh(GELU_C * (u + GELU_A * (u * u * u)))
        cdf = 0.5 * (1.0 + t)
        h[:, cols] = (u * cdf).astype(BF)
        du[:, cols] = (g * (cdf + u * (0.5 * (1.0 - t * t)) * (GELU_C * (1.0 + 3.0 * GELU_A * (u * u))))).astype(BF)
    for j in range(width // TILE):
        cols = pl.ds(j * TILE, TILE)
        dn_p[:, cols] = mm(du[...], w1[cols, :], 1, 1)
        y_p[:, cols] = mm(h[...], w2[:, cols], 1, 0)
    fill_wait(zero, table_g, s_zero, 2)


def mlp(x_f, d_full, w1, w2, gain, zero, table_g):
    tokens, width = x_f.shape
    hid = w1.shape[1]
    return pl.pallas_call(
        mlp_kernel,
        name="mlp",
        out_shape=[sh((tokens, width), BF), sh((tokens, hid), BF), sh((tokens, hid), BF), sh((tokens, width), F32),
                   sh((tokens, width), F32), sh(table_g.shape, F32)],
        in_specs=[VMEM_SPEC] * 6 + [HBM_SPEC],
        out_specs=[VMEM_SPEC] * 5 + [HBM_SPEC],
        input_output_aliases={6: 5},
        scratch_shapes=[DMA(())],
        compiler_params=pltpu.CompilerParams(vmem_limit_bytes=16 * MIB),
        cost_estimate=pl.CostEstimate(flops=6_000_000_000, bytes_accessed=4 * MIB, transcendentals=0),
    )(x_f, d_full, w1, w2, gain, zero, table_g)


def sums_kernel(dn_p, y_p, dn_own, dn_far, y_own, y_far, dn_r, y_r, sems):
    rows = dn_own.shape[0]
    half = 2 * rows
    remote = swap_with_sibling()
    copies = []
    for i, (src, dst) in enumerate(((dn_p, dn_r), (y_p, y_r))):
        for k in (1, 0):
            copies.append(remote(src.at[pl.ds(half + k * rows, rows)], dst.at[pl.ds(k * rows, rows)], sems, 2 * i + k))
            copies[-1].start()
    for c, out, src, dst, k in zip(copies, (dn_far, dn_own, y_far, y_own), (dn_p, dn_p, y_p, y_p), (dn_r, dn_r, y_r, y_r), (1, 0, 1, 0)):
        c.wait()
        at = pl.ds(k * rows, rows)
        out[...] = src[at, :] + dst[at, :]


def sums(dn_p, y_p):
    tokens, width = dn_p.shape
    rows = tokens // 4
    return pl.pallas_call(
        sums_kernel,
        name="sums",
        out_shape=[sh((rows, width), F32)] * 4,
        in_specs=[VMEM_SPEC] * 2,
        out_specs=[VMEM_SPEC] * 4,
        scratch_shapes=[VMEM((2 * rows, width), F32), VMEM((2 * rows, width), F32), DMA((2, 4))],
        compiler_params=pltpu.CompilerParams(collective_id=2, has_side_effects=True, vmem_limit_bytes=8 * MIB),
        cost_estimate=pl.CostEstimate(flops=4_000_000_000, bytes_accessed=4 * MIB, transcendentals=0),
    )(dn_p, y_p)


def grads_kernel(n, h, du, d_full, zero, order, table_in, token, dw1, dw2, table_g, dw1_v, dw2_v, s_zero, s_w):
    fill_start(zero, table_g, s_zero, 3)
    token[...] = jnp.zeros_like(token)
    width, hid = dw1.shape
    n_t = n[...].T
    for j in range(width // TILE):
        at = slice(j * TILE, (j + 1) * TILE)
        dw1_v[at, :] = mm(n_t[at, :], du[...], 1, 0)
        pltpu.make_async_copy(dw1_v.at[pl.ds(j * TILE, TILE)], dw1.at[pl.ds(j * TILE, TILE)], s_w).start()
    h_t = h[...].T
    for j in range(hid // TILE):
        at = slice(j * TILE, (j + 1) * TILE)
        dw2_v[at, :] = mm(h_t[at, :], d_full[...], 1, 0)
        pltpu.make_async_copy(dw2_v.at[pl.ds(j * TILE, TILE)], dw2.at[pl.ds(j * TILE, TILE)], s_w).start()
    pltpu.make_async_copy(dw1_v, dw1, s_w).wait()
    pltpu.make_async_copy(dw2_v, dw2, s_w).wait()
    fill_wait(zero, table_g, s_zero, 3)


def grads(n, h, du, d_full, zero, order, table_g):
    tokens, width = n.shape
    hid = h.shape[1]
    return pl.pallas_call(
        grads_kernel,
        name="grads",
        out_shape=[sh((8, 128), F32), sh((width, hid), F32), sh((hid, width), F32), sh(table_g.shape, F32)],
        in_specs=[VMEM_SPEC] * 5 + [ANY_SPEC, HBM_SPEC],
        out_specs=[VMEM_SPEC, HBM_SPEC, HBM_SPEC, HBM_SPEC],
        input_output_aliases={6: 3},
        scratch_shapes=[VMEM((width, hid), F32), VMEM((hid, width), F32), DMA(()), DMA(())],
        compiler_params=pltpu.CompilerParams(vmem_limit_bytes=24 * MIB),
        cost_estimate=pl.CostEstimate(flops=8_000_000_000, bytes_accessed=20 * MIB, transcendentals=0),
    )(n, h, du, d_full, zero, order, table_g)


def dx_kernel(dn_own, g2, x_own, d_own, gain, order, dx):
    gain_f = gain[...].astype(F32).reshape(1, dx.shape[1])
    for j in range(dx.shape[0] // 16):
        at = pl.ds(j * 16, 16)
        a = (dn_own[at, :] + g2[at, :]) * gain_f
        x = x_own[at, :].astype(F32)
        r = lax.rsqrt(jnp.mean(x * x, axis=-1, keepdims=True) + EPS)
        proj = jnp.mean(a * x, axis=-1, keepdims=True)
        dx[at, :] = (d_own[at, :].astype(F32) + r * (a - x * r * r * proj)).astype(BF)


def dx_rows(dn_own, g2, x_own, d_own, gain, order):
    return pl.pallas_call(
        dx_kernel,
        name="dx_rows",
        out_shape=sh(d_own.shape, BF),
        in_specs=[VMEM_SPEC] * 5 + [ANY_SPEC],
        out_specs=VMEM_SPEC,
        compiler_params=pltpu.CompilerParams(vmem_limit_bytes=4 * MIB),
        cost_estimate=pl.CostEstimate(flops=1_000_000_000, bytes_accessed=MIB, transcendentals=0),
    )(dn_own, g2, x_own, d_own, gain, order)


def fill3_kernel(zero, order, table_in, token, table_g, s_zero):
    fill_start(zero, table_g, s_zero, 4)
    token[...] = jnp.zeros_like(token)
    fill_wait(zero, table_g, s_zero, 4)


def fill3(zero, order, table_g):
    return pl.pallas_call(
        fill3_kernel,
        name="fill3",
        out_shape=[sh((8, 128), F32), sh(table_g.shape, F32)],
        in_specs=[VMEM_SPEC, ANY_SPEC, HBM_SPEC],
        out_specs=[VMEM_SPEC, HBM_SPEC],
        input_output_aliases={2: 1},
        scratch_shapes=[DMA(())],
        compiler_params=pltpu.CompilerParams(vmem_limit_bytes=4 * MIB),
        cost_estimate=pl.CostEstimate(flops=4_000_000_000, bytes_accessed=16 * MIB, transcendentals=0),
    )(zero, order, table_g)


def dx_all_kernel(dx, dx_far, order, dx_out, dx_r, sems):
    me = lax.axis_index("tp")
    rows = dx.shape[0]
    remote = swap_with_sibling()
    block = lambda m: pl.ds(pl.multiple_of((me ^ m) * rows, rows), rows)
    copies = [remote(src, dx_r.at[pl.ds(k * rows, rows)], sems, k) for k, src in enumerate((dx, dx_far))]
    for c in copies:
        c.start()
    dx_out[block(0), :] = dx[...]
    dx_out[block(2), :] = dx_far[...]
    for k, c in enumerate(copies):
        c.wait()
        dx_out[block(1 + 2 * k), :] = dx_r[pl.ds(k * rows, rows), :]


def dx_all(dx, dx_far, order):
    rows, width = dx.shape
    return pl.pallas_call(
        dx_all_kernel,
        name="dx_all",
        out_shape=sh((4 * rows, width), BF),
        in_specs=[VMEM_SPEC] * 2 + [ANY_SPEC],
        out_specs=VMEM_SPEC,
        scratch_shapes=[VMEM((2 * rows, width), BF), DMA((2, 2))],
        compiler_params=pltpu.CompilerParams(collective_id=3, has_side_effects=True, vmem_limit_bytes=4 * MIB),
        cost_estimate=pl.CostEstimate(flops=2_000_000_000, bytes_accessed=MIB, transcendentals=0),
    )(dx, dx_far, order)


def put_kernel(puts, same, dx, table_in, table_g, token, puts_s, total, s_in, s_row):
    tokens = dx.shape[0]
    load = pltpu.make_async_copy(puts, puts_s, s_in)
    load.start()
    total[...] = mm(same[...], dx[...], 1, 0)
    token[...] = jnp.zeros_like(token)
    load.wait()
    count = puts_s[tokens]

    def put(i, carry):
        word = puts_s[i]
        pltpu.make_async_copy(total.at[pl.ds(word >> 16, 1)], table_g.at[pl.ds(word & 0xFFFF, 1)], s_row).start()
        return carry

    lax.fori_loop(0, count, put, 0)

    def put_wait(size):
        def body(i, carry):
            pltpu.make_async_copy(total.at[pl.ds(0, size)], table_g.at[pl.ds(0, size)], s_row).wait()
            return carry

        return body

    lax.fori_loop(0, count >> 3, put_wait(8), 0)
    lax.fori_loop(0, count & 7, put_wait(1), 0)


def put_rows(puts, same, dx, table_g):
    return pl.pallas_call(
        put_kernel,
        name="put_rows",
        out_shape=[sh(table_g.shape, F32), sh((8, 128), F32)],
        in_specs=[ANY_SPEC, VMEM_SPEC, VMEM_SPEC, HBM_SPEC],
        out_specs=[HBM_SPEC, VMEM_SPEC],
        input_output_aliases={3: 0},
        scratch_shapes=[pltpu.SMEM(puts.shape, I32), VMEM(dx.shape, F32), DMA(()), DMA(())],
        compiler_params=pltpu.CompilerParams(vmem_limit_bytes=4 * MIB),
        cost_estimate=pl.CostEstimate(flops=3_000_000_000, bytes_accessed=2 * MIB, transcendentals=0),
    )(puts, same, dx, table_g)


def finish_kernel(x, y, y_in, order, out):
    out[...] = (x[pl.ds(0, out.shape[0]), :].astype(F32) + (y[...] + y_in[...])).astype(BF)


def finish(x, y, y_in, order):
    return pl.pallas_call(
        finish_kernel,
        name="finish",
        out_shape=sh(y.shape, BF),
        in_specs=[VMEM_SPEC] * 3 + [ANY_SPEC],
        out_specs=VMEM_SPEC,
        compiler_params=pltpu.CompilerParams(vmem_limit_bytes=4 * MIB),
        cost_estimate=pl.CostEstimate(flops=1_000_000_000, bytes_accessed=MIB, transcendentals=0),
    )(x, y, y_in, order)


def solution(mesh):
    tp = mesh.shape["tp"]
    far_pairs = [(i, i ^ 2) for i in range(tp)]

    def shard_step(ids, table, gain, w1, w2, d_out):
        part, rows_mine, same, zero, d_table = lookup(ids, table)
        send = pair(part, in_hbm(d_out))
        got = lax.ppermute(send, "tp", far_pairs)
        puts, token, d_table = fill1(rows_mine, zero, send, d_table)
        x_f, d_full = share(send, got, token)
        n, h, du, dn_p, y_p, d_table = mlp(x_f, d_full, w1, w2, gain, zero, d_table)
        dn_own, dn_far, y_own, y_far = sums(dn_p, y_p)
        g2 = lax.ppermute(dn_far, "tp", far_pairs)
        token, d_w1, d_w2, d_table = grads(n, h, du, d_full, zero, dn_own, d_table)
        dx = dx_rows(dn_own, g2, x_f, d_out, gain, token)
        dx_far = lax.ppermute(dx, "tp", far_pairs)
        dx, y_far = lax.optimization_barrier((dx, y_far))
        y_in = lax.ppermute(y_far, "tp", far_pairs)
        token, d_table = fill3(zero, dx, d_table)
        dx_full = dx_all(dx, dx_far, token)
        d_table, done = put_rows(puts, same, dx_full, d_table)
        out = finish(x_f, y_own, y_in, done)
        return out, d_table, d_w1, d_w2

    return jax.shard_map(
        shard_step,
        mesh=mesh,
        in_specs=(P("dp"), P("tp", None), P(None), P(None, "tp"), P("tp", None), P(("dp", "tp"), None)),
        out_specs=(P(("dp", "tp"), None), P(("dp", "tp"), None), P("dp", "tp"), P(("dp", "tp"), None)),
        check_vma=False,
    )
```

time: 49.6 us -> 48.6 us (0.980)
  waiting for transfers between devices: 0.02 us -> 4.07 us
  Pallas kernels: 40.2 us -> 36.9 us
  starting transfers between devices: 7.53 us -> 6.68 us
  local copies, waits for them, and re-layouts: 0.69 us -> 0.02 us
    pallas_call x1, Pallas kernels: 4.79 us -> 1.53 us  [fill3(): pl.pallas_call(fill3_kernel, name='fill3', out_shape=[sh((8, 128), F32),...]
    ppermute x1, waiting for transfers between devices: 0.01 us -> 2.81 us  [shard_step(): dx_far = lax.ppermute(dx, 'tp', far_pairs)]
    pallas_call x1, Pallas kernels: 5.89 us -> 3.27 us  [mlp(): pl.pallas_call(mlp_kernel, name='mlp', out_shape=[sh((tokens, width), BF)...]
    pallas_call x5 -> x6, Pallas kernels: 14.3 us -> 16.5 us  [the longest x1 8.78 us: fill1(): pl.pallas_call(fill1_kernel, name='fill1', out_shape=[sh((2 * tokens,), I...]
    unnamed x10 -> x8, local copies, waits for them, and re-layouts: 0.69 us -> 0.02 us
    ppermute x1, waiting for transfers between devices: 0.01 us -> 0.63 us  [shard_step(): g2 = lax.ppermute(dn_far, 'tp', far_pairs)]
    ppermute x4 -> x2, waiting for transfers between devices: 0.01 us -> 0.63 us  [the longest x1 0.63 us: shard_step(): got = lax.ppermute(send, 'tp', far_pairs)]
    ppermute x4 -> x2, starting transfers between devices: 3.5 us -> 3.16 us  [the longest x1 2.87 us: shard_step(): got = lax.ppermute(send, 'tp', far_pairs)]
  transfers between devices with their start and end apart: 6 -> 4, of which waited for: 0 -> 3; matrix products, arithmetic and copies ran while one was open for 0% -> 0% of each run, Pallas kernels for 57% -> 42%
where the time goes in v4:
time: 48.6 us; the launch traced here: 48.4 us
  Pallas kernels  36.9 us (76%)
  starting transfers between devices  6.68 us (14%)
  waiting for transfers between devices  4.07 us (8%)
  between operations  0.78 us (2%)
    pallas_call x1, Pallas kernels, fill1(): pl.pallas_call(fill1_kernel, name='fill1', out_shape=[sh((2 * tokens,), I...  8.78 us
    pallas_call x1, Pallas kernels, grads(): pl.pallas_call(grads_kernel, name='grads', out_shape=[sh((8, 128), F32),...  5.99 us
    pallas_call x1, Pallas kernels, lookup(): pl.pallas_call(lookup_kernel, name='lookup', out_shape=[sh((tokens, width...  5.46 us
    pallas_call x1, Pallas kernels, mlp(): pl.pallas_call(mlp_kernel, name='mlp', out_shape=[sh((tokens, width), BF)...  3.27 us
    ppermute x1, starting transfers between devices, shard_step(): got = lax.ppermute(send, 'tp', far_pairs)  2.87 us
    ppermute x1, waiting for transfers between devices, shard_step(): dx_far = lax.ppermute(dx, 'tp', far_pairs)  2.81 us
    pallas_call x1, Pallas kernels, sums(): pl.pallas_call(sums_kernel, name='sums', out_shape=[sh((rows, width), F32...  2.77 us
    pallas_call x1, Pallas kernels, put_rows(): pl.pallas_call(put_kernel, name='put_rows', out_shape=[sh(table_g.shape,...  2.5 us
  transfers between devices with their start and end apart: 4, of which 3 were waited for; matrix products, arithmetic and copies ran while one was open for 0% of the time, Pallas kernels for 42%

profile of v4, /device:TPU:0, one launch (start us, length us, event | category | flops | bytes accessed | tf_op | source)
XLA Modules:
  0.0 48.4 jit_solution(14071775090000826073)
XLA Ops:
  0.6 0.0 copy-start.2
  0.6 0.0 copy-start.1
  0.7 0.0 copy-start
  0.7 5.5 %lookup.1 = (bf16[256,1024]{1,0:T(8,128)(2,1)S(1)}, s32[1,256]{1,0:T(1,128)S(1)}, bf16[256,256]{1,0:T(8,128)(2,1)S(1)}, f32[96,1024]{1,0:T(8,128)S(1)}, f32[12576,1024]{1,0:T(8,128)}) custom-call(s32[256]{0:T(256)} %ids.1, s32[1,256]{1,0:T(1,128)} %bitcast.1, bf16[12576,1024]{1,0:T(8,128)(2,1)} %table.1), custom_call_target="tpu_custom_call" | custom-call | flops 5000000000 | bytes 10485760 | tf_op jit(solution)/shard_map/lookup/pallas_call | solution.py:122
  6.1 2.1 %pair.1.order.send = bf16[192,1024]{1,0:T(8,128)(2,1)S(1)} custom-call(bf16[256,1024]{1,0:T(8,128)(2,1)S(1)} %get-tuple-element.34.part, bf16[64,1024]{1,0:T(8,128)(2,1)} %d_own.1), custom_call_target="tpu_custom_call" | custom-call | flops 3000000000 | bytes 1048576 | tf_op jit(solution)/shard_map/pair/pallas_call | solution.py:154
  8.2 2.9 %collective-permute-start = (bf16[192,1024]{1,0:T(8,128)(2,1)S(1)}, bf16[192,1024]{1,0:T(8,128)(2,1)S(1)}, u32[]{:S(2)}, u32[]{:S(2)}) collective-permute-start(bf16[192,1024]{1,0:T(8,128)(2,1)S(1)} %pair.1.order.send), channel_id=1, source_target_pairs={{0,2},{1,3},{2,0},{3,1},{4,6},{5,7},{6,4},{7,5}} | collective-permute-start | bytes 1179656 | tf_op jit(solution)/shard_map/ppermute | solution.py:480
  11.1 8.8 %fill1.1 = (s32[512]{0:T(512)S(1)}, f32[8,128]{1,0:T(8,128)S(1)}, f32[12576,1024]{1,0:T(8,128)}) custom-call(s32[1,256]{1,0:T(1,128)S(1)} %get-tuple-element.35.rows_mine, f32[96,1024]{1,0:T(8,128)S(1)} %get-tuple-element.36.zero, bf16[192,1024]{1,0:T(8,128)(2,1)S(1)} %pair.1.order.send, ...), custom_call_target="tpu_custom_call", output_to_operand_aliasing={{2}: (3, {})} | custom-call | flops 8999999488 | bytes 20971520 | tf_op jit(solution)/shard_map/fill1/pallas_call | solution.py:188
  19.9 0.6 %collective-permute-done.got = bf16[192,1024]{1,0:T(8,128)(2,1)S(1)} collective-permute-done((bf16[192,1024]{1,0:T(8,128)(2,1)S(1)}, bf16[192,1024]{1,0:T(8,128)(2,1)S(1)}, u32[]{:S(2)}, u32[]{:S(2)}) %collective-permute-start) | collective-permute-done | bytes 393248 | tf_op jit(solution)/shard_map/ppermute | solution.py:480
  20.5 2.0 %share.1 = (bf16[256,1024]{1,0:T(8,128)(2,1)S(1)}, bf16[256,1024]{1,0:T(8,128)(2,1)S(1)}) custom-call(bf16[192,1024]{1,0:T(8,128)(2,1)S(1)} %pair.1.order.send, bf16[192,1024]{1,0:T(8,128)(2,1)S(1)} %collective-permute-done.got, f32[8,128]{1,0:T(8,128)S(1)} %get-tuple-element.38.order), custom_call_target="tpu_custom_call" | custom-call | flops 3000000000 | bytes 1048576 | tf_op jit(solution)/shard_map/share/pallas_call | solution.py:225
  22.6 0.0 copy-done.2
  22.6 0.0 copy-done.1
  22.6 0.0 copy-done
  22.6 0.0 copy-start.3
  22.6 3.3 %mlp.1 = (bf16[256,1024]{1,0:T(8,128)(2,1)S(1)}, bf16[256,1024]{1,0:T(8,128)(2,1)S(1)}, bf16[256,1024]{1,0:T(8,128)(2,1)S(1)}, f32[256,1024]{1,0:T(8,128)S(1)}, ...) custom-call(bf16[256,1024]{1,0:T(8,128)(2,1)S(1)} %get-tuple-element.39.x_f.x_own.x, ...), custom_call_target="tpu_custom_call", output_to_operand_aliasing={{5}: (6, {})} | custom-call | flops 6000000000 | bytes 4194304 | tf_op jit(solution)/shard_map/mlp/pallas_call | solution.py:265
  25.9 2.8 %sums.1 = (f32[64,1024]{1,0:T(8,128)S(1)}, f32[64,1024]{1,0:T(8,128)S(1)}, f32[64,1024]{1,0:T(8,128)S(1)}, f32[64,1024]{1,0:T(8,128)S(1)}) custom-call(f32[256,1024]{1,0:T(8,128)S(1)} %get-tuple-element.42.dn_p, f32[256,1024]{1,0:T(8,128)S(1)} %get-tuple-element.43.y_p), custom_call_target="tpu_custom_call" | custom-call | flops 4000000000 | bytes 4194304 | tf_op jit(solution)/shard_map/sums/pallas_call | solution.py:297
  28.7 1.8 %collective-permute-start.1 = (f32[64,1024]{1,0:T(8,128)S(1)}, f32[64,1024]{1,0:T(8,128)S(1)}, u32[]{:S(2)}, u32[]{:S(2)}) collective-permute-start(f32[64,1024]{1,0:T(8,128)S(1)} %get-tuple-element.46), channel_id=1, source_target_pairs={{0,2},{1,3},{2,0},{3,1},{4,6},{5,7},{6,4},{7,5}} | collective-permute-start | bytes 786440 | tf_op jit(solution)/shard_map/ppermute | solution.py:485
  30.4 6.0 %grads.1 = (f32[8,128]{1,0:T(8,128)S(1)}, f32[1024,1024]{1,0:T(8,128)}, f32[1024,1024]{1,0:T(8,128)}, f32[12576,1024]{1,0:T(8,128)}) custom-call(bf16[256,1024]{1,0:T(8,128)(2,1)S(1)} %get-tuple-element.47.n, bf16[256,1024]{1,0:T(8,128)(2,1)S(1)} %get-tuple-element.48.h, ...), custom_call_target="tpu_custom_call", output_to_operand_aliasing={{3}: (6, {})} | custom-call | flops 8000000000 | bytes 20971520 | tf_op jit(solution)/shard_map/grads/pallas_call | solution.py:331
  36.4 0.6 %collective-permute-done.1.g2 = f32[64,1024]{1,0:T(8,128)S(1)} collective-permute-done((f32[64,1024]{1,0:T(8,128)S(1)}, f32[64,1024]{1,0:T(8,128)S(1)}, u32[]{:S(2)}, u32[]{:S(2)}) %collective-permute-start.1) | collective-permute-done | bytes 262176 | tf_op jit(solution)/shard_map/ppermute | solution.py:485
  37.0 0.0 copy-done.3
  37.0 0.2 dx_rows.1.order.dx
  37.2 1.8 %collective-permute-start.3 = (bf16[64,1024]{1,0:T(8,128)(2,1)S(1)}, bf16[64,1024]{1,0:T(8,128)(2,1)S(1)}, u32[]{:S(2)}, u32[]{:S(2)}) collective-permute-start(bf16[64,1024]{1,0:T(8,128)(2,1)S(1)} %dx_rows.1.order.dx), channel_id=1, source_target_pairs={{0,2},{1,3},{2,0},{3,1},{4,6},{5,7},{6,4},{7,5}} | collective-permute-start | bytes 393224 | tf_op jit(solution)/shard_map/ppermute | solution.py:488
  39.0 0.3 collective-permute-start.2
  39.3 1.5 %fill3.1 = (f32[8,128]{1,0:T(8,128)S(1)}, f32[12576,1024]{1,0:T(8,128)}) custom-call(f32[96,1024]{1,0:T(8,128)S(1)} %get-tuple-element.36.zero, bf16[64,1024]{1,0:T(8,128)(2,1)S(1)} %dx_rows.1.order.dx, f32[12576,1024]{1,0:T(8,128)} %get-tuple-element.57.table_in), custom_call_target="tpu_custom_call", output_to_operand_aliasing={{1}: (2, {})} | custom-call | flops 4000000000 | bytes 16777216 | tf_op jit(solution)/shard_map/fill3/pallas_call | solution.py:374
  40.8 2.8 %collective-permute-done.3.dx_far = bf16[64,1024]{1,0:T(8,128)(2,1)S(1)} collective-permute-done((bf16[64,1024]{1,0:T(8,128)(2,1)S(1)}, bf16[64,1024]{1,0:T(8,128)(2,1)S(1)}, u32[]{:S(2)}, u32[]{:S(2)}) %collective-permute-start.3) | collective-permute-done | bytes 131104 | tf_op jit(solution)/shard_map/ppermute | solution.py:488
  43.6 1.6 %dx_all.1.dx = bf16[256,1024]{1,0:T(8,128)(2,1)S(1)} custom-call(bf16[64,1024]{1,0:T(8,128)(2,1)S(1)} %dx_rows.1.order.dx, bf16[64,1024]{1,0:T(8,128)(2,1)S(1)} %collective-permute-done.3.dx_far, f32[8,128]{1,0:T(8,128)S(1)} %get-tuple-element.58.order), custom_call_target="tpu_custom_call" | custom-call | flops 2000000000 | bytes 1048576 | tf_op jit(solution)/shard_map/dx_all/pallas_call | solution.py:404
  45.2 2.5 %put_rows.1 = (f32[12576,1024]{1,0:T(8,128)}, f32[8,128]{1,0:T(8,128)S(1)}) custom-call(s32[512]{0:T(512)S(1)} %get-tuple-element.54.puts, bf16[256,256]{1,0:T(8,128)(2,1)S(1)} %get-tuple-element.55.same, bf16[256,1024]{1,0:T(8,128)(2,1)S(1)} %dx_all.1.dx, f32[12576,1024]{1,0:T(8,128)} %get-tuple-element.59.table_in), custom_call_target="tpu_custom_call", output_to_operand_aliasing={{0}: (3, {})} | custom-call | flops 3000000000 | bytes 2097152 | tf_op jit(solution)/shard_map/put_rows/pallas_call | solution.py:444
  47.7 0.0 collective-permute-done.2.y_in
  47.7 0.7 %finish.1 = bf16[64,1024]{1,0:T(8,128)(2,1)} custom-call(bf16[256,1024]{1,0:T(8,128)(2,1)S(1)} %get-tuple-element.39.x_f.x_own.x, f32[64,1024]{1,0:T(8,128)S(1)} %get-tuple-element.44.y, f32[64,1024]{1,0:T(8,128)S(1)} %collective-permute-done.2.y_in, f32[8,128]{1,0:T(8,128)S(1)} %get-tuple-element.60.order), custom_call_target="tpu_custom_call" | custom-call | flops 1000000000 | bytes 1048576 | tf_op jit(solution)/shard_map/finish/pallas_call | solution.py:462
Async XLA Ops:
  0.6 21.9 %copy-start.2 = (bf16[1024]{0:T(1024)(128)(2,1)S(1)}, bf16[1024]{0:T(1024)(128)(2,1)}, u32[]{:S(2)}) copy-start(bf16[1024]{0:T(1024)(128)(2,1)} %gain.3) | copy-start | bytes 6148
  0.6 21.9 %copy-start.1 = (bf16[1024,1024]{1,0:T(8,128)(2,1)S(1)}, bf16[1024,1024]{1,0:T(8,128)(2,1)}, u32[]{:S(2)}) copy-start(bf16[1024,1024]{1,0:T(8,128)(2,1)} %w2.1) | copy-start | bytes 6291460
  0.7 21.9 %copy-start = (bf16[1024,1024]{1,0:T(8,128)(2,1)S(1)}, bf16[1024,1024]{1,0:T(8,128)(2,1)}, u32[]{:S(2)}) copy-start(bf16[1024,1024]{1,0:T(8,128)(2,1)} %w1.1) | copy-start | bytes 6291460
  8.2 12.3 %collective-permute-start = (bf16[192,1024]{1,0:T(8,128)(2,1)S(1)}, bf16[192,1024]{1,0:T(8,128)(2,1)S(1)}, u32[]{:S(2)}, u32[]{:S(2)}) collective-permute-start(bf16[192,1024]{1,0:T(8,128)(2,1)S(1)} %pair.1.order.send), channel_id=1, source_target_pairs={{0,2},{1,3},{2,0},{3,1},{4,6},{5,7},{6,4},{7,5}} | collective-permute-start | bytes 1179656 | tf_op jit(solution)/shard_map/ppermute | solution.py:480
  22.6 14.5 %copy-start.3 = (bf16[64,1024]{1,0:T(8,128)(2,1)S(1)}, bf16[64,1024]{1,0:T(8,128)(2,1)}, u32[]{:S(2)}) copy-start(bf16[64,1024]{1,0:T(8,128)(2,1)} %d_own.1) | copy-start | bytes 393220
  28.7 8.4 %collective-permute-start.1 = (f32[64,1024]{1,0:T(8,128)S(1)}, f32[64,1024]{1,0:T(8,128)S(1)}, u32[]{:S(2)}, u32[]{:S(2)}) collective-permute-start(f32[64,1024]{1,0:T(8,128)S(1)} %get-tuple-element.46), channel_id=1, source_target_pairs={{0,2},{1,3},{2,0},{3,1},{4,6},{5,7},{6,4},{7,5}} | collective-permute-start | bytes 786440 | tf_op jit(solution)/shard_map/ppermute | solution.py:485
  37.2 6.4 %collective-permute-start.3 = (bf16[64,1024]{1,0:T(8,128)(2,1)S(1)}, bf16[64,1024]{1,0:T(8,128)(2,1)S(1)}, u32[]{:S(2)}, u32[]{:S(2)}) collective-permute-start(bf16[64,1024]{1,0:T(8,128)(2,1)S(1)} %dx_rows.1.order.dx), channel_id=1, source_target_pairs={{0,2},{1,3},{2,0},{3,1},{4,6},{5,7},{6,4},{7,5}} | collective-permute-start | bytes 393224 | tf_op jit(solution)/shard_map/ppermute | solution.py:488
  39.0 8.7 %collective-permute-start.2 = (f32[64,1024]{1,0:T(8,128)S(1)}, f32[64,1024]{1,0:T(8,128)S(1)}, u32[]{:S(2)}, u32[]{:S(2)}) collective-permute-start(f32[64,1024]{1,0:T(8,128)S(1)} %get-tuple-element.53), channel_id=1, source_target_pairs={{0,2},{1,3},{2,0},{3,1},{4,6},{5,7},{6,4},{7,5}} | collective-permute-start | bytes 786440 | tf_op jit(solution)/shard_map/ppermute | solution.py:490

commit v5 on v4

--- a/solution.py
+++ b/solution.py
@@ -19,7 +19,7 @@
 DMA = pltpu.SemaphoreType.DMA
 TILE = 256
 ZERO_ROWS = 96
-FILL_AT = (0, 15, 83, 102, 124, 131)
+FILL_AT = (0, 15, 95, 106, 108, 131)
 MIB = 1 << 20
 LOOKUP_VMEM = 48 * MIB
 PAIR_VMEM = 8 * MIB
@@ -82,19 +82,17 @@
     zero[...] = jnp.zeros_like(zero)
     fill_start(zero, table_g, s_zero, 0)
     loads[0].wait()
-    for k in range(groups):
-        def fetch(i, carry):
-            lid = ids_s[k * group + i] - base
+
+    def fetch(k, carry):
+        for i in range(group):
+            token = k * group + i
+            lid = ids_s[token] - base
             owned = (lid >= 0) & (lid < vocab)
-            pair_id = jnp.where(owned, lid >> 1, i)
-            pltpu.make_async_copy(
-                table.at[pl.ds(pl.multiple_of(pair_id << 1, 2), 2)],
-                pairs.at[pl.ds(pl.multiple_of(k * group * 2 + i * 2, 2), 2)],
-                sems.at[k],
-            ).start()
-            return carry
-
-        lax.fori_loop(0, group, fetch, 0, unroll=8)
+            row = jnp.where(owned, lid & -2, 2 * token)
+            pltpu.make_async_copy(table.at[pl.ds(pl.multiple_of(row, 2), 2)], pairs.at[k, pl.ds(2 * i, 2)], sems.at[k]).start()
+        return carry
+
+    lax.fori_loop(0, groups, fetch, 0)
     loads[1].wait()
     row = jnp.broadcast_to(ids_v[...].astype(F32), (tokens, tokens))
     col = row.T
@@ -111,9 +109,8 @@
         at = lid[k * group:(k + 1) * group, :2 * group]
         owned = (at >= 0) & (at < vocab)
         pick = jnp.where(owned & (lane == first + (at & 1)), 1.0, 0.0).astype(BF)
-        rows = pl.ds(k * group * 2, group * 2)
-        pltpu.make_async_copy(table.at[pl.ds(0, group * 2)], pairs.at[rows], sems.at[k]).wait()
-        part[pl.ds(k * group, group), :] = mm(pick, pairs[rows, :], 1, 0).astype(BF)
+        pltpu.make_async_copy(table.at[pl.ds(0, group * 2)], pairs.at[k], sems.at[k]).wait()
+        part[pl.ds(k * group, group), :] = mm(pick, pairs[k], 1, 0).astype(BF)
     fill_wait(zero, table_g, s_zero, 0)
 
 
@@ -125,7 +122,7 @@
         out_shape=[sh((tokens, width), BF), sh((1, tokens), I32), sh((tokens, tokens), BF), sh((ZERO_ROWS, width), F32), sh((vocab, width), F32)],
         in_specs=[HBM_SPEC] * 3,
         out_specs=[VMEM_SPEC] * 4 + [HBM_SPEC],
-        scratch_shapes=[pltpu.SMEM((tokens,), I32), VMEM((1, tokens), I32), VMEM((tokens * 2, width), BF), DMA((4,)), DMA(()), DMA((2,))],
+        scratch_shapes=[pltpu.SMEM((tokens,), I32), VMEM((1, tokens), I32), VMEM((4, tokens // 2, width), BF), DMA((4,)), DMA(()), DMA((2,))],
         compiler_params=pltpu.CompilerParams(vmem_limit_bytes=LOOKUP_VMEM),
         cost_estimate=pl.CostEstimate(flops=5_000_000_000, bytes_accessed=10 * MIB, transcendentals=0),
     )(in_hbm(ids), in_hbm(ids.reshape(1, tokens)), in_hbm(table))
@@ -234,7 +231,7 @@
     )(send, got, order)
 
 
-def mlp_kernel(x_f, d_full, w1, w2, gain, zero, table_in, n, h, du, dn_p, y_p, table_g, s_zero):
+def mlp_kernel(x_f, d_full, w1, w2, gain, zero, table_in, n, h, du, dn_p, table_g, s_zero):
     fill_start(zero, table_g, s_zero, 2)
     tokens, width = n.shape
     hid = h.shape[1]
@@ -252,10 +249,10 @@
         cdf = 0.5 * (1.0 + t)
         h[:, cols] = (u * cdf).astype(BF)
         du[:, cols] = (g * (cdf + u * (0.5 * (1.0 - t * t)) * (GELU_C * (1.0 + 3.0 * GELU_A * (u * u))))).astype(BF)
+    half = tokens // 2
     for j in range(width // TILE):
         cols = pl.ds(j * TILE, TILE)
-        dn_p[:, cols] = mm(du[...], w1[cols, :], 1, 1)
-        y_p[:, cols] = mm(h[...], w2[:, cols], 1, 0)
+        dn_p[:, cols] = mm(du[pl.ds(half, half), :], w1[cols, :], 1, 1)
     fill_wait(zero, table_g, s_zero, 2)
 
 
@@ -265,45 +262,78 @@
     return pl.pallas_call(
         mlp_kernel,
         name="mlp",
-        out_shape=[sh((tokens, width), BF), sh((tokens, hid), BF), sh((tokens, hid), BF), sh((tokens, width), F32),
-                   sh((tokens, width), F32), sh(table_g.shape, F32)],
+        out_shape=[sh((tokens, width), BF), sh((tokens, hid), BF), sh((tokens, hid), BF), sh((tokens // 2, width), F32),
+                   sh(table_g.shape, F32)],
         in_specs=[VMEM_SPEC] * 6 + [HBM_SPEC],
-        out_specs=[VMEM_SPEC] * 5 + [HBM_SPEC],
-        input_output_aliases={6: 5},
+        out_specs=[VMEM_SPEC] * 4 + [HBM_SPEC],
+        input_output_aliases={6: 4},
         scratch_shapes=[DMA(())],
         compiler_params=pltpu.CompilerParams(vmem_limit_bytes=16 * MIB),
         cost_estimate=pl.CostEstimate(flops=6_000_000_000, bytes_accessed=4 * MIB, transcendentals=0),
     )(x_f, d_full, w1, w2, gain, zero, table_g)
 
 
-def sums_kernel(dn_p, y_p, dn_own, dn_far, y_own, y_far, dn_r, y_r, sems):
-    rows = dn_own.shape[0]
+def sums_kernel(dn_p, du, h, w1, w2, dn_own, dn_far, y_p, dn_r, dn_m, sems):
+    rows, width = dn_own.shape
     half = 2 * rows
     remote = swap_with_sibling()
-    copies = []
-    for i, (src, dst) in enumerate(((dn_p, dn_r), (y_p, y_r))):
-        for k in (1, 0):
-            copies.append(remote(src.at[pl.ds(half + k * rows, rows)], dst.at[pl.ds(k * rows, rows)], sems, 2 * i + k))
-            copies[-1].start()
-    for c, out, src, dst, k in zip(copies, (dn_far, dn_own, y_far, y_own), (dn_p, dn_p, y_p, y_p), (dn_r, dn_r, y_r, y_r), (1, 0, 1, 0)):
+    copies = [remote(dn_p.at[pl.ds(k * rows, rows)], dn_r.at[pl.ds(k * rows, rows)], sems, k) for k in (1, 0)]
+    for c in copies:
+        c.start()
+    for j in range(width // TILE):
+        cols = pl.ds(j * TILE, TILE)
+        dn_m[:, cols] = mm(du[pl.ds(0, half), :], w1[cols, :], 1, 1)
+    for j in range(width // TILE):
+        cols = pl.ds(j * TILE, TILE)
+        y_p[:, cols] = mm(h[...], w2[:, cols], 1, 0)
+    for c, out, k in zip(copies, (dn_far, dn_own), (1, 0)):
         c.wait()
         at = pl.ds(k * rows, rows)
-        out[...] = src[at, :] + dst[at, :]
-
-
-def sums(dn_p, y_p):
-    tokens, width = dn_p.shape
-    rows = tokens // 4
+        out[...] = dn_m[at, :] + dn_r[at, :]
+
+
+def sums(dn_p, du, h, w1, w2):
+    half, width = dn_p.shape
+    rows = half // 2
     return pl.pallas_call(
         sums_kernel,
         name="sums",
-        out_shape=[sh((rows, width), F32)] * 4,
-        in_specs=[VMEM_SPEC] * 2,
-        out_specs=[VMEM_SPEC] * 4,
-        scratch_shapes=[VMEM((2 * rows, width), F32), VMEM((2 * rows, width), F32), DMA((2, 4))],
-        compiler_params=pltpu.CompilerParams(collective_id=2, has_side_effects=True, vmem_limit_bytes=8 * MIB),
+        out_shape=[sh((rows, width), F32), sh((rows, width), F32), sh((2 * half, width), F32)],
+        in_specs=[VMEM_SPEC] * 5,
+        out_specs=[VMEM_SPEC] * 3,
+        scratch_shapes=[VMEM((half, width), F32), VMEM((half, width), F32), DMA((2, 2))],
+        compiler_params=pltpu.CompilerParams(collective_id=2, has_side_effects=True, vmem_limit_bytes=16 * MIB),
         cost_estimate=pl.CostEstimate(flops=4_000_000_000, bytes_accessed=4 * MIB, transcendentals=0),
-    )(dn_p, y_p)
+    )(dn_p, du, h, w1, w2)
+
+
+def ysum_kernel(y_p, order, y_own, y_far0, y_far1, y_r, sems):
+    rows, _ = y_own.shape
+    half, part = 2 * rows, rows // 2
+    remote = swap_with_sibling()
+    places = ((rows, y_far0), (rows + part, y_far1), (0, y_own))
+    copies = [remote(y_p.at[pl.ds(half + at, out.shape[0])], y_r.at[pl.ds(at, out.shape[0])], sems, k) for k, (at, out) in enumerate(places)]
+    for c in copies:
+        c.start()
+    for c, (at, out) in zip(copies, places):
+        c.wait()
+        rows_at = pl.ds(at, out.shape[0])
+        out[...] = y_p[rows_at, :] + y_r[rows_at, :]
+
+
+def ysum(y_p, order):
+    tokens, width = y_p.shape
+    rows = tokens // 4
+    return pl.pallas_call(
+        ysum_kernel,
+        name="ysum",
+        out_shape=[sh((rows, width), F32), sh((rows // 2, width), F32), sh((rows // 2, width), F32)],
+        in_specs=[VMEM_SPEC, ANY_SPEC],
+        out_specs=[VMEM_SPEC] * 3,
+        scratch_shapes=[VMEM((2 * rows, width), F32), DMA((2, 3))],
+        compiler_params=pltpu.CompilerParams(collective_id=4, has_side_effects=True, vmem_limit_bytes=8 * MIB),
+        cost_estimate=pl.CostEstimate(flops=3_000_000_000, bytes_accessed=4 * MIB, transcendentals=0),
+    )(y_p, order)
 
 
 def grads_kernel(n, h, du, d_full, zero, order, table_in, token, dw1, dw2, table_g, dw1_v, dw2_v, s_zero, s_w):
@@ -326,7 +356,7 @@
 
 
 def grads(n, h, du, d_full, zero, order, table_g):
-    tokens, width = n.shape
+    _, width = n.shape
     hid = h.shape[1]
     return pl.pallas_call(
         grads_kernel,
@@ -422,12 +452,21 @@
     load.wait()
     count = puts_s[tokens]
 
-    def put(i, carry):
+    def put(i):
         word = puts_s[i]
         pltpu.make_async_copy(total.at[pl.ds(word >> 16, 1)], table_g.at[pl.ds(word & 0xFFFF, 1)], s_row).start()
+
+    def put_four(i, carry):
+        for k in range(4):
+            put(i * 4 + k)
         return carry
 
-    lax.fori_loop(0, count, put, 0)
+    def put_one(i, carry):
+        put(i)
+        return carry
+
+    lax.fori_loop(0, count >> 2, put_four, 0)
+    lax.fori_loop((count >> 2) * 4, count, put_one, 0)
 
     def put_wait(size):
         def body(i, carry):
@@ -454,25 +493,31 @@
     )(puts, same, dx, table_g)
 
 
-def finish_kernel(x, y, y_in, order, out):
-    out[...] = (x[pl.ds(0, out.shape[0]), :].astype(F32) + (y[...] + y_in[...])).astype(BF)
-
-
-def finish(x, y, y_in, order):
+def finish_kernel(x, y, y_in0, y_in1, order, out):
+    part = y_in0.shape[0]
+    for k, y_in in enumerate((y_in0, y_in1)):
+        at = pl.ds(k * part, part)
+        out[at, :] = (x[at, :].astype(F32) + (y[at, :] + y_in[...])).astype(BF)
+
+
+def finish(x, y, y_in0, y_in1, order):
     return pl.pallas_call(
         finish_kernel,
         name="finish",
         out_shape=sh(y.shape, BF),
-        in_specs=[VMEM_SPEC] * 3 + [ANY_SPEC],
+        in_specs=[VMEM_SPEC] * 4 + [ANY_SPEC],
         out_specs=VMEM_SPEC,
         compiler_params=pltpu.CompilerParams(vmem_limit_bytes=4 * MIB),
         cost_estimate=pl.CostEstimate(flops=1_000_000_000, bytes_accessed=MIB, transcendentals=0),
-    )(x, y, y_in, order)
+    )(x, y, y_in0, y_in1, order)
 
 
 def solution(mesh):
     tp = mesh.shape["tp"]
     far_pairs = [(i, i ^ 2) for i in range(tp)]
+
+    def far_permute(x):
+        return lax.ppermute(x, "tp", far_pairs)
 
     def shard_step(ids, table, gain, w1, w2, d_out):
         part, rows_mine, same, zero, d_table = lookup(ids, table)
@@ -480,18 +525,20 @@
         got = lax.ppermute(send, "tp", far_pairs)
         puts, token, d_table = fill1(rows_mine, zero, send, d_table)
         x_f, d_full = share(send, got, token)
-        n, h, du, dn_p, y_p, d_table = mlp(x_f, d_full, w1, w2, gain, zero, d_table)
-        dn_own, dn_far, y_own, y_far = sums(dn_p, y_p)
-        g2 = lax.ppermute(dn_far, "tp", far_pairs)
-        token, d_w1, d_w2, d_table = grads(n, h, du, d_full, zero, dn_own, d_table)
+        n, h, du, dn_p, d_table = mlp(x_f, d_full, w1, w2, gain, zero, d_table)
+        dn_own, dn_far, y_p = sums(dn_p, du, h, w1, w2)
+        g2 = far_permute(dn_far)
+        y_own, y_far0, y_far1 = ysum(y_p, dn_own)
+        y_in0 = lax.ppermute(y_far0, "tp", far_pairs)
+        token, d_w1, d_w2, d_table = grads(n, h, du, d_full, zero, y_own, d_table)
         dx = dx_rows(dn_own, g2, x_f, d_out, gain, token)
-        dx_far = lax.ppermute(dx, "tp", far_pairs)
-        dx, y_far = lax.optimization_barrier((dx, y_far))
-        y_in = lax.ppermute(y_far, "tp", far_pairs)
+        dx_far = far_permute(dx)
+        dx, y_far1 = lax.optimization_barrier((dx, y_far1))
+        y_in1 = far_permute(y_far1)
         token, d_table = fill3(zero, dx, d_table)
         dx_full = dx_all(dx, dx_far, token)
         d_table, done = put_rows(puts, same, dx_full, d_table)
-        out = finish(x_f, y_own, y_in, done)
+        out = finish(x_f, y_own, y_in0, y_in1, done)
         return out, d_table, d_w1, d_w2
 
     return jax.shard_map(

time: 48.6 us -> 51.6 us (1.062)
  waiting for transfers between devices: 4.07 us -> 6.07 us
  Pallas kernels: 36.9 us -> 37.7 us
    ppermute x3 -> x4, waiting for transfers between devices: 3.44 us -> 6.07 us  [the longest x3 6.07 us: far_permute(): return lax.ppermute(x, 'tp', far_pairs)]
    pallas_call x1, Pallas kernels: 5.99 us -> 3.64 us  [grads(): pl.pallas_call(grads_kernel, name='grads', out_shape=[sh((8, 128), F32),...]
    pallas_call x0 -> x1, Pallas kernels: none -> 2.01 us  [ysum(): pl.pallas_call(ysum_kernel, name='ysum', out_shape=[sh((rows, width), F32...]
    pallas_call x1, Pallas kernels: 1.53 us -> 3.47 us  [fill3(): pl.pallas_call(fill3_kernel, name='fill3', out_shape=[sh((8, 128), F32),...]
    pallas_call x1, Pallas kernels: 8.78 us -> 10.2 us  [fill1(): pl.pallas_call(fill1_kernel, name='fill1', out_shape=[sh((2 * tokens,), I...]
    pallas_call x1, Pallas kernels: 2.77 us -> 1.99 us  [sums(): pl.pallas_call(sums_kernel, name='sums', out_shape=[sh((rows, width), F32...]
    pallas_call x1, Pallas kernels: 3.27 us -> 2.52 us  [mlp(): pl.pallas_call(mlp_kernel, name='mlp', out_shape=[sh((tokens, width), BF)...]
    ppermute x1, waiting for transfers between devices: 0.63 us -> 0.01 us  [shard_step(): got = lax.ppermute(send, 'tp', far_pairs)]
  transfers between devices with their start and end apart: 4 -> 5, of which waited for: 3 -> 2; matrix products, arithmetic and copies ran while one was open for 0% -> 0% of each run, Pallas kernels for 42% -> 41%
where the time goes in v5:
time: 51.6 us; the launch traced here: 51.5 us
  Pallas kernels  37.7 us (73%)
  starting transfers between devices  6.96 us (13%)
  waiting for transfers between devices  6.07 us (12%)
  between operations  0.81 us (2%)
    pallas_call x1, Pallas kernels, fill1(): pl.pallas_call(fill1_kernel, name='fill1', out_shape=[sh((2 * tokens,), I...  10.2 us
    ppermute x3, waiting for transfers between devices, far_permute(): return lax.ppermute(x, 'tp', far_pairs)  6.07 us
    pallas_call x1, Pallas kernels, lookup(): pl.pallas_call(lookup_kernel, name='lookup', out_shape=[sh((tokens, width...  5.22 us
    pallas_call x1, Pallas kernels, grads(): pl.pallas_call(grads_kernel, name='grads', out_shape=[sh((8, 128), F32),...  3.64 us
    pallas_call x1, Pallas kernels, fill3(): pl.pallas_call(fill3_kernel, name='fill3', out_shape=[sh((8, 128), F32),...  3.47 us
    ppermute x3, starting transfers between devices, far_permute(): return lax.ppermute(x, 'tp', far_pairs)  3.15 us
    ppermute x1, starting transfers between devices, shard_step(): got = lax.ppermute(send, 'tp', far_pairs)  2.87 us
    pallas_call x1, Pallas kernels, mlp(): pl.pallas_call(mlp_kernel, name='mlp', out_shape=[sh((tokens, width), BF)...  2.52 us
  transfers between devices with their start and end apart: 5, of which 2 were waited for; matrix products, arithmetic and copies ran while one was open for 0% of the time, Pallas kernels for 41%

profile of v5, /device:TPU:0, one launch (start us, length us, event | category | flops | bytes accessed | tf_op | source)
XLA Modules:
  0.0 51.5 jit_solution(14374845421107390903)
XLA Ops:
  0.6 0.0 copy-start.1
  0.6 0.0 copy-start
  0.7 0.0 copy-start.2
  0.7 5.2 %lookup.1 = (bf16[256,1024]{1,0:T(8,128)(2,1)S(1)}, s32[1,256]{1,0:T(1,128)S(1)}, bf16[256,256]{1,0:T(8,128)(2,1)S(1)}, f32[96,1024]{1,0:T(8,128)S(1)}, f32[12576,1024]{1,0:T(8,128)}) custom-call(s32[256]{0:T(256)} %ids.1, s32[1,256]{1,0:T(1,128)} %bitcast.1, bf16[12576,1024]{1,0:T(8,128)(2,1)} %table.1), custom_call_target="tpu_custom_call" | custom-call | flops 5000000000 | bytes 10485760 | tf_op jit(solution)/shard_map/lookup/pallas_call | solution.py:119
  5.9 2.1 %pair.1.order.send = bf16[192,1024]{1,0:T(8,128)(2,1)S(1)} custom-call(bf16[256,1024]{1,0:T(8,128)(2,1)S(1)} %get-tuple-element.35.part, bf16[64,1024]{1,0:T(8,128)(2,1)} %d_own.1), custom_call_target="tpu_custom_call" | custom-call | flops 3000000000 | bytes 1048576 | tf_op jit(solution)/shard_map/pair/pallas_call | solution.py:151
  8.0 2.9 %collective-permute-start = (bf16[192,1024]{1,0:T(8,128)(2,1)S(1)}, bf16[192,1024]{1,0:T(8,128)(2,1)S(1)}, u32[]{:S(2)}, u32[]{:S(2)}) collective-permute-start(bf16[192,1024]{1,0:T(8,128)(2,1)S(1)} %pair.1.order.send), channel_id=1, source_target_pairs={{0,2},{1,3},{2,0},{3,1},{4,6},{5,7},{6,4},{7,5}} | collective-permute-start | bytes 1179656 | tf_op jit(solution)/shard_map/ppermute | solution.py:525
  10.8 10.2 %fill1.1 = (s32[512]{0:T(512)S(1)}, f32[8,128]{1,0:T(8,128)S(1)}, f32[12576,1024]{1,0:T(8,128)}) custom-call(s32[1,256]{1,0:T(1,128)S(1)} %get-tuple-element.36.rows_mine, f32[96,1024]{1,0:T(8,128)S(1)} %get-tuple-element.37.zero, bf16[192,1024]{1,0:T(8,128)(2,1)S(1)} %pair.1.order.send, ...), custom_call_target="tpu_custom_call", output_to_operand_aliasing={{2}: (3, {})} | custom-call | flops 8999999488 | bytes 20971520 | tf_op jit(solution)/shard_map/fill1/pallas_call | solution.py:185
  21.0 0.0 collective-permute-done.got
  21.1 2.0 %share.1 = (bf16[256,1024]{1,0:T(8,128)(2,1)S(1)}, bf16[256,1024]{1,0:T(8,128)(2,1)S(1)}) custom-call(bf16[192,1024]{1,0:T(8,128)(2,1)S(1)} %pair.1.order.send, bf16[192,1024]{1,0:T(8,128)(2,1)S(1)} %collective-permute-done.got, f32[8,128]{1,0:T(8,128)S(1)} %get-tuple-element.39.order), custom_call_target="tpu_custom_call" | custom-call | flops 3000000000 | bytes 1048576 | tf_op jit(solution)/shard_map/share/pallas_call | solution.py:222
  23.1 0.0 copy-done.1
  23.1 0.0 copy-done
  23.1 0.0 copy-done.2
  23.1 2.5 %mlp.1 = (bf16[256,1024]{1,0:T(8,128)(2,1)S(1)}, bf16[256,1024]{1,0:T(8,128)(2,1)S(1)}, bf16[256,1024]{1,0:T(8,128)(2,1)S(1)}, f32[128,1024]{1,0:T(8,128)S(1)}, f32[12576,1024]{1,0:T(8,128)}) custom-call(bf16[256,1024]{1,0:T(8,128)(2,1)S(1)} %get-tuple-element.40.x_f.x_own.x, ...), custom_call_target="tpu_custom_call", output_to_operand_aliasing={{4}: (6, {})} | custom-call | flops 6000000000 | bytes 4194304 | tf_op jit(solution)/shard_map/mlp/pallas_call | solution.py:262
  25.6 0.0 copy-start.3
  25.7 2.0 %sums.1 = (f32[64,1024]{1,0:T(8,128)S(1)}, f32[64,1024]{1,0:T(8,128)S(1)}, f32[256,1024]{1,0:T(8,128)S(1)}) custom-call(f32[128,1024]{1,0:T(8,128)S(1)} %get-tuple-element.43.dn_p, bf16[256,1024]{1,0:T(8,128)(2,1)S(1)} %get-tuple-element.44.du, bf16[256,1024]{1,0:T(8,128)(2,1)S(1)} %get-tuple-element.45.h, bf16[1024,1024]{1,0:T(8,128)(2,1)S(1)} %copy-done, ...), custom_call_target="tpu_custom_call" | custom-call | flops 4000000000 | bytes 4194304 | tf_op jit(solution)/shard_map/sums/pallas_call | solution.py:298
  27.7 2.0 %ysum.1 = (f32[64,1024]{1,0:T(8,128)S(1)}, f32[32,1024]{1,0:T(8,128)S(1)}, f32[32,1024]{1,0:T(8,128)S(1)}) custom-call(f32[256,1024]{1,0:T(8,128)S(1)} %get-tuple-element.46.y_p, f32[64,1024]{1,0:T(8,128)S(1)} %get-tuple-element.47.order.dn_own), custom_call_target="tpu_custom_call" | custom-call | flops 3000000000 | bytes 4194304 | tf_op jit(solution)/shard_map/ysum/pallas_call | solution.py:327
  29.7 0.9 %collective-permute-start.1 = (f32[32,1024]{1,0:T(8,128)S(1)}, f32[32,1024]{1,0:T(8,128)S(1)}, u32[]{:S(2)}, u32[]{:S(2)}) collective-permute-start(f32[32,1024]{1,0:T(8,128)S(1)} %get-tuple-element.49), channel_id=1, source_target_pairs={{0,2},{1,3},{2,0},{3,1},{4,6},{5,7},{6,4},{7,5}} | collective-permute-start | bytes 393224 | tf_op jit(solution)/shard_map/ppermute | solution.py:532
  30.6 1.1 %collective-permute-start.2 = (f32[64,1024]{1,0:T(8,128)S(1)}, f32[64,1024]{1,0:T(8,128)S(1)}, u32[]{:S(2)}, u32[]{:S(2)}) collective-permute-start(f32[64,1024]{1,0:T(8,128)S(1)} %get-tuple-element.50), channel_id=1, source_target_pairs={{0,2},{1,3},{2,0},{3,1},{4,6},{5,7},{6,4},{7,5}} | collective-permute-start | bytes 786440 | tf_op jit(solution)/shard_map/ppermute | solution.py:520
  31.7 3.6 %grads.1 = (f32[8,128]{1,0:T(8,128)S(1)}, f32[1024,1024]{1,0:T(8,128)}, f32[1024,1024]{1,0:T(8,128)}, f32[12576,1024]{1,0:T(8,128)}) custom-call(bf16[256,1024]{1,0:T(8,128)(2,1)S(1)} %get-tuple-element.51.n, bf16[256,1024]{1,0:T(8,128)(2,1)S(1)} %get-tuple-element.45.h, ...), custom_call_target="tpu_custom_call", output_to_operand_aliasing={{3}: (6, {})} | custom-call | flops 8000000000 | bytes 20971520 | tf_op jit(solution)/shard_map/grads/pallas_call | solution.py:361
  35.4 5.5 %collective-permute-done.2.g2 = f32[64,1024]{1,0:T(8,128)S(1)} collective-permute-done((f32[64,1024]{1,0:T(8,128)S(1)}, f32[64,1024]{1,0:T(8,128)S(1)}, u32[]{:S(2)}, u32[]{:S(2)}) %collective-permute-start.2) | collective-permute-done | bytes 262176 | tf_op jit(solution)/shard_map/ppermute | solution.py:520
  40.8 0.0 copy-done.3
  40.8 0.2 dx_rows.1.order.dx
  41.0 0.9 %collective-permute-start.4 = (bf16[64,1024]{1,0:T(8,128)(2,1)S(1)}, bf16[64,1024]{1,0:T(8,128)(2,1)S(1)}, u32[]{:S(2)}, u32[]{:S(2)}) collective-permute-start(bf16[64,1024]{1,0:T(8,128)(2,1)S(1)} %dx_rows.1.order.dx), channel_id=1, source_target_pairs={{0,2},{1,3},{2,0},{3,1},{4,6},{5,7},{6,4},{7,5}} | collective-permute-start | bytes 393224 | tf_op jit(solution)/shard_map/ppermute | solution.py:520
  42.0 1.1 %collective-permute-start.3 = (f32[32,1024]{1,0:T(8,128)S(1)}, f32[32,1024]{1,0:T(8,128)S(1)}, u32[]{:S(2)}, u32[]{:S(2)}) collective-permute-start(f32[32,1024]{1,0:T(8,128)S(1)} %get-tuple-element.55), channel_id=1, source_target_pairs={{0,2},{1,3},{2,0},{3,1},{4,6},{5,7},{6,4},{7,5}} | collective-permute-start | bytes 393224 | tf_op jit(solution)/shard_map/ppermute | solution.py:520
  43.1 3.5 %fill3.1 = (f32[8,128]{1,0:T(8,128)S(1)}, f32[12576,1024]{1,0:T(8,128)}) custom-call(f32[96,1024]{1,0:T(8,128)S(1)} %get-tuple-element.37.zero, bf16[64,1024]{1,0:T(8,128)(2,1)S(1)} %dx_rows.1.order.dx, f32[12576,1024]{1,0:T(8,128)} %get-tuple-element.59.table_in), custom_call_target="tpu_custom_call", output_to_operand_aliasing={{1}: (2, {})} | custom-call | flops 4000000000 | bytes 16777216 | tf_op jit(solution)/shard_map/fill3/pallas_call | solution.py:404
  46.6 0.6 %collective-permute-done.4.dx_far = bf16[64,1024]{1,0:T(8,128)(2,1)S(1)} collective-permute-done((bf16[64,1024]{1,0:T(8,128)(2,1)S(1)}, bf16[64,1024]{1,0:T(8,128)(2,1)S(1)}, u32[]{:S(2)}, u32[]{:S(2)}) %collective-permute-start.4) | collective-permute-done | bytes 131104 | tf_op jit(solution)/shard_map/ppermute | solution.py:520
  47.1 1.6 %dx_all.1.dx = bf16[256,1024]{1,0:T(8,128)(2,1)S(1)} custom-call(bf16[64,1024]{1,0:T(8,128)(2,1)S(1)} %dx_rows.1.order.dx, bf16[64,1024]{1,0:T(8,128)(2,1)S(1)} %collective-permute-done.4.dx_far, f32[8,128]{1,0:T(8,128)S(1)} %get-tuple-element.60.order), custom_call_target="tpu_custom_call" | custom-call | flops 2000000000 | bytes 1048576 | tf_op jit(solution)/shard_map/dx_all/pallas_call | solution.py:434
  48.7 2.1 %put_rows.1 = (f32[12576,1024]{1,0:T(8,128)}, f32[8,128]{1,0:T(8,128)S(1)}) custom-call(s32[512]{0:T(512)S(1)} %get-tuple-element.56.puts, bf16[256,256]{1,0:T(8,128)(2,1)S(1)} %get-tuple-element.57.same, bf16[256,1024]{1,0:T(8,128)(2,1)S(1)} %dx_all.1.dx, f32[12576,1024]{1,0:T(8,128)} %get-tuple-element.61.table_in), custom_call_target="tpu_custom_call", output_to_operand_aliasing={{0}: (3, {})} | custom-call | flops 3000000000 | bytes 2097152 | tf_op jit(solution)/shard_map/put_rows/pallas_call | solution.py:483
  50.8 0.0 collective-permute-done.1.y_in0
  50.8 0.0 collective-permute-done.3.y_in1
  50.8 0.7 %finish.1 = bf16[64,1024]{1,0:T(8,128)(2,1)} custom-call(bf16[256,1024]{1,0:T(8,128)(2,1)S(1)} %get-tuple-element.40.x_f.x_own.x, f32[64,1024]{1,0:T(8,128)S(1)} %get-tuple-element.48.order.y, f32[32,1024]{1,0:T(8,128)S(1)} %collective-permute-done.1.y_in0, f32[32,1024]{1,0:T(8,128)S(1)} %collective-permute-done.3.y_in1, f32[8,128]{1,0:T(8,128)S(1)} %get-tuple-element.62.order), custom_call_target="tpu_custom_call" | custom-call | flops 1000000000 | bytes 1048576 | tf_op jit(solution)/shard_map/finish/pallas_call | solution.py:504
Async XLA Ops:
  0.6 22.5 %copy-start.1 = (bf16[1024,1024]{1,0:T(8,128)(2,1)S(1)}, bf16[1024,1024]{1,0:T(8,128)(2,1)}, u32[]{:S(2)}) copy-start(bf16[1024,1024]{1,0:T(8,128)(2,1)} %w2.3) | copy-start | bytes 6291460
  0.6 22.5 %copy-start = (bf16[1024,1024]{1,0:T(8,128)(2,1)S(1)}, bf16[1024,1024]{1,0:T(8,128)(2,1)}, u32[]{:S(2)}) copy-start(bf16[1024,1024]{1,0:T(8,128)(2,1)} %w1.3) | copy-start | bytes 6291460
  0.7 22.5 %copy-start.2 = (bf16[1024]{0:T(1024)(128)(2,1)S(1)}, bf16[1024]{0:T(1024)(128)(2,1)}, u32[]{:S(2)}) copy-start(bf16[1024]{0:T(1024)(128)(2,1)} %gain.3) | copy-start | bytes 6148
  8.0 13.1 %collective-permute-start = (bf16[192,1024]{1,0:T(8,128)(2,1)S(1)}, bf16[192,1024]{1,0:T(8,128)(2,1)S(1)}, u32[]{:S(2)}, u32[]{:S(2)}) collective-permute-start(bf16[192,1024]{1,0:T(8,128)(2,1)S(1)} %pair.1.order.send), channel_id=1, source_target_pairs={{0,2},{1,3},{2,0},{3,1},{4,6},{5,7},{6,4},{7,5}} | collective-permute-start | bytes 1179656 | tf_op jit(solution)/shard_map/ppermute | solution.py:525
  25.6 15.2 %copy-start.3 = (bf16[64,1024]{1,0:T(8,128)(2,1)S(1)}, bf16[64,1024]{1,0:T(8,128)(2,1)}, u32[]{:S(2)}) copy-start(bf16[64,1024]{1,0:T(8,128)(2,1)} %d_own.1) | copy-start | bytes 393220
  29.7 21.1 %collective-permute-start.1 = (f32[32,1024]{1,0:T(8,128)S(1)}, f32[32,1024]{1,0:T(8,128)S(1)}, u32[]{:S(2)}, u32[]{:S(2)}) collective-permute-start(f32[32,1024]{1,0:T(8,128)S(1)} %get-tuple-element.49), channel_id=1, source_target_pairs={{0,2},{1,3},{2,0},{3,1},{4,6},{5,7},{6,4},{7,5}} | collective-permute-start | bytes 393224 | tf_op jit(solution)/shard_map/ppermute | solution.py:532
  30.6 10.2 %collective-permute-start.2 = (f32[64,1024]{1,0:T(8,128)S(1)}, f32[64,1024]{1,0:T(8,128)S(1)}, u32[]{:S(2)}, u32[]{:S(2)}) collective-permute-start(f32[64,1024]{1,0:T(8,128)S(1)} %get-tuple-element.50), channel_id=1, source_target_pairs={{0,2},{1,3},{2,0},{3,1},{4,6},{5,7},{6,4},{7,5}} | collective-permute-start | bytes 786440 | tf_op jit(solution)/shard_map/ppermute | solution.py:520
  41.0 6.1 %collective-permute-start.4 = (bf16[64,1024]{1,0:T(8,128)(2,1)S(1)}, bf16[64,1024]{1,0:T(8,128)(2,1)S(1)}, u32[]{:S(2)}, u32[]{:S(2)}) collective-permute-start(bf16[64,1024]{1,0:T(8,128)(2,1)S(1)} %dx_rows.1.order.dx), channel_id=1, source_target_pairs={{0,2},{1,3},{2,0},{3,1},{4,6},{5,7},{6,4},{7,5}} | collective-permute-start | bytes 393224 | tf_op jit(solution)/shard_map/ppermute | solution.py:520
  42.0 8.8 %collective-permute-start.3 = (f32[32,1024]{1,0:T(8,128)S(1)}, f32[32,1024]{1,0:T(8,128)S(1)}, u32[]{:S(2)}, u32[]{:S(2)}) collective-permute-start(f32[32,1024]{1,0:T(8,128)S(1)} %get-tuple-element.55), channel_id=1, source_target_pairs={{0,2},{1,3},{2,0},{3,1},{4,6},{5,7},{6,4},{7,5}} | collective-permute-start | bytes 393224 | tf_op jit(solution)/shard_map/ppermute | solution.py:520

commit v6 on v5

--- a/solution.py
+++ b/solution.py
@@ -19,7 +19,7 @@
 DMA = pltpu.SemaphoreType.DMA
 TILE = 256
 ZERO_ROWS = 96
-FILL_AT = (0, 15, 95, 106, 108, 131)
+FILL_AT = (0, 12, 92, 103, 117, 131)
 MIB = 1 << 20
 LOOKUP_VMEM = 48 * MIB
 PAIR_VMEM = 8 * MIB
@@ -128,12 +128,13 @@
     )(in_hbm(ids), in_hbm(ids.reshape(1, tokens)), in_hbm(table))
 
 
-def pair_kernel(part, d_out, send, part_r, sems, s_in):
+def pair_kernel(part, d_out, w1, send, w1_v, part_r, sems, s_in):
     me = lax.axis_index("tp")
     rows = d_out.shape[0]
     blocks = (me, me ^ 2, me ^ 1, me ^ 3)
-    load = pltpu.make_async_copy(d_out, send.at[pl.ds(2 * rows, rows)], s_in)
-    load.start()
+    loads = [pltpu.make_async_copy(d_out, send.at[pl.ds(2 * rows, rows)], s_in.at[0]), pltpu.make_async_copy(w1, w1_v, s_in.at[1])]
+    for c in loads:
+        c.start()
     remote = swap_with_sibling()
     block = lambda k: pl.ds(pl.multiple_of(blocks[k] * rows, rows), rows)
     copies = [remote(part.at[block(2 + k)], part_r.at[pl.ds(k * rows, rows)], sems, k) for k in range(2)]
@@ -143,21 +144,22 @@
         copies[k].wait()
         at = pl.ds(k * rows, rows)
         send[at, :] = part[block(k), :] + part_r[at, :]
-    load.wait()
-
-
-def pair(part, d_out):
+    for c in loads:
+        c.wait()
+
+
+def pair(part, d_out, w1):
     rows, width = d_out.shape
     return pl.pallas_call(
         pair_kernel,
         name="pair",
-        out_shape=sh((3 * rows, width), BF),
-        in_specs=[VMEM_SPEC, HBM_SPEC],
-        out_specs=VMEM_SPEC,
-        scratch_shapes=[VMEM((2 * rows, width), BF), DMA((2, 2)), DMA(())],
+        out_shape=[sh((3 * rows, width), BF), sh(w1.shape, BF)],
+        in_specs=[VMEM_SPEC, HBM_SPEC, HBM_SPEC],
+        out_specs=[VMEM_SPEC] * 2,
+        scratch_shapes=[VMEM((2 * rows, width), BF), DMA((2, 2)), DMA((2,))],
         compiler_params=pltpu.CompilerParams(collective_id=0, has_side_effects=True, vmem_limit_bytes=PAIR_VMEM),
         cost_estimate=pl.CostEstimate(flops=3_000_000_000, bytes_accessed=MIB, transcendentals=0),
-    )(part, d_out)
+    )(part, in_hbm(d_out), in_hbm(w1))
 
 
 def fill1_kernel(rows_mine, zero, order, table_in, puts, token, table_g, mine_s, puts_s, s_zero, s_list):
@@ -195,9 +197,11 @@
     )(rows_mine, zero, order, table_g)
 
 
-def share_kernel(send, got, order, x_f, d_full, x_r, d_r, sems):
+def share_kernel(send, got, w2, order, x_f, d_full, w2_v, x_r, d_r, sems, s_in):
     rows = send.shape[0] // 3
     half = 2 * rows
+    load = pltpu.make_async_copy(w2, w2_v, s_in)
+    load.start()
     remote = swap_with_sibling()
     copies = []
     for k in range(2):
@@ -215,20 +219,21 @@
     for k in range(2):
         copies[2 + k].wait()
         d_full[pl.ds(half + k * rows, rows), :] = d_r[pl.ds(k * rows, rows), :]
-
-
-def share(send, got, order):
+    load.wait()
+
+
+def share(send, got, w2, order):
     rows, width = send.shape[0] // 3, send.shape[1]
     return pl.pallas_call(
         share_kernel,
         name="share",
-        out_shape=[sh((4 * rows, width), BF)] * 2,
-        in_specs=[VMEM_SPEC] * 2 + [ANY_SPEC],
-        out_specs=[VMEM_SPEC] * 2,
-        scratch_shapes=[VMEM((2 * rows, width), BF), VMEM((2 * rows, width), BF), DMA((2, 4))],
+        out_shape=[sh((4 * rows, width), BF)] * 2 + [sh(w2.shape, BF)],
+        in_specs=[VMEM_SPEC] * 2 + [HBM_SPEC, ANY_SPEC],
+        out_specs=[VMEM_SPEC] * 3,
+        scratch_shapes=[VMEM((2 * rows, width), BF), VMEM((2 * rows, width), BF), DMA((2, 4)), DMA(())],
         compiler_params=pltpu.CompilerParams(collective_id=1, has_side_effects=True, vmem_limit_bytes=8 * MIB),
         cost_estimate=pl.CostEstimate(flops=3_000_000_000, bytes_accessed=MIB, transcendentals=0),
-    )(send, got, order)
+    )(send, got, in_hbm(w2), order)
 
 
 def mlp_kernel(x_f, d_full, w1, w2, gain, zero, table_in, n, h, du, dn_p, table_g, s_zero):
@@ -521,16 +526,17 @@
 
     def shard_step(ids, table, gain, w1, w2, d_out):
         part, rows_mine, same, zero, d_table = lookup(ids, table)
-        send = pair(part, in_hbm(d_out))
+        send, w1 = pair(part, d_out, w1)
         got = lax.ppermute(send, "tp", far_pairs)
         puts, token, d_table = fill1(rows_mine, zero, send, d_table)
-        x_f, d_full = share(send, got, token)
+        x_f, d_full, w2 = share(send, got, w2, token)
         n, h, du, dn_p, d_table = mlp(x_f, d_full, w1, w2, gain, zero, d_table)
         dn_own, dn_far, y_p = sums(dn_p, du, h, w1, w2)
         g2 = far_permute(dn_far)
         y_own, y_far0, y_far1 = ysum(y_p, dn_own)
+        token, d_w1, d_w2, d_table = grads(n, h, du, d_full, zero, y_own, d_table)
+        token, y_far0 = lax.optimization_barrier((token, y_far0))
         y_in0 = lax.ppermute(y_far0, "tp", far_pairs)
-        token, d_w1, d_w2, d_table = grads(n, h, du, d_full, zero, y_own, d_table)
         dx = dx_rows(dn_own, g2, x_f, d_out, gain, token)
         dx_far = far_permute(dx)
         dx, y_far1 = lax.optimization_barrier((dx, y_far1))

time: 51.6 us -> 48.1 us (0.932)
  waiting for transfers between devices: 6.07 us -> 3.34 us
  Pallas kernels: 37.7 us -> 36.6 us
    ppermute x3, waiting for transfers between devices: 6.07 us -> 3.33 us  [far_permute(): return lax.ppermute(x, 'tp', far_pairs)]
    pallas_call x1, Pallas kernels: 5.22 us -> 3.8 us  [lookup(): pl.pallas_call(lookup_kernel, name='lookup', out_shape=[sh((tokens, width...]
    pallas_call x1, Pallas kernels: 3.64 us -> 5.01 us  [grads(): pl.pallas_call(grads_kernel, name='grads', out_shape=[sh((8, 128), F32),...]
    pallas_call x1, Pallas kernels: 3.47 us -> 2.41 us  [fill3(): pl.pallas_call(fill3_kernel, name='fill3', out_shape=[sh((8, 128), F32),...]
  transfers between devices with their start and end apart: 5 -> 5, of which waited for: 2 -> 1; matrix products, arithmetic and copies ran while one was open for 0% -> 0% of each run, Pallas kernels for 41% -> 49%
where the time goes in v6:
time: 48.1 us; the launch traced here: 47.8 us
  Pallas kernels  36.6 us (76%)
  starting transfers between devices  7.08 us (15%)
  waiting for transfers between devices  3.34 us (7%)
  between operations  0.77 us (2%)
    pallas_call x1, Pallas kernels, fill1(): pl.pallas_call(fill1_kernel, name='fill1', out_shape=[sh((2 * tokens,), I...  10.2 us
    pallas_call x1, Pallas kernels, grads(): pl.pallas_call(grads_kernel, name='grads', out_shape=[sh((8, 128), F32),...  5.01 us
    pallas_call x1, Pallas kernels, lookup(): pl.pallas_call(lookup_kernel, name='lookup', out_shape=[sh((tokens, width...  3.8 us
    ppermute x3, waiting for transfers between devices, far_permute(): return lax.ppermute(x, 'tp', far_pairs)  3.33 us
    ppermute x1, starting transfers between devices, shard_step(): got = lax.ppermute(send, 'tp', far_pairs)  2.97 us
    ppermute x3, starting transfers between devices, far_permute(): return lax.ppermute(x, 'tp', far_pairs)  2.89 us
    pallas_call x1, Pallas kernels, mlp(): pl.pallas_call(mlp_kernel, name='mlp', out_shape=[sh((tokens, width), BF)...  2.57 us
    pallas_call x1, Pallas kernels, fill3(): pl.pallas_call(fill3_kernel, name='fill3', out_shape=[sh((8, 128), F32),...  2.41 us
  transfers between devices with their start and end apart: 5, of which 1 were waited for; matrix products, arithmetic and copies ran while one was open for 0% of the time, Pallas kernels for 49%

profile of v6, /device:TPU:0, one launch (start us, length us, event | category | flops | bytes accessed | tf_op | source)
XLA Modules:
  0.0 47.8 jit_solution(16692052058820714993)
XLA Ops:
  0.6 3.8 %lookup.1 = (bf16[256,1024]{1,0:T(8,128)(2,1)S(1)}, s32[1,256]{1,0:T(1,128)S(1)}, bf16[256,256]{1,0:T(8,128)(2,1)S(1)}, f32[96,1024]{1,0:T(8,128)S(1)}, f32[12576,1024]{1,0:T(8,128)}) custom-call(s32[256]{0:T(256)} %ids.1, s32[1,256]{1,0:T(1,128)} %bitcast.1, bf16[12576,1024]{1,0:T(8,128)(2,1)} %table.1), custom_call_target="tpu_custom_call" | custom-call | flops 5000000000 | bytes 10485760 | tf_op jit(solution)/shard_map/lookup/pallas_call | solution.py:119
  4.4 2.1 %pair.1 = (bf16[192,1024]{1,0:T(8,128)(2,1)S(1)}, bf16[1024,1024]{1,0:T(8,128)(2,1)S(1)}) custom-call(bf16[256,1024]{1,0:T(8,128)(2,1)S(1)} %get-tuple-element.40.part, bf16[64,1024]{1,0:T(8,128)(2,1)} %d_own.1, bf16[1024,1024]{1,0:T(8,128)(2,1)} %w1.1), custom_call_target="tpu_custom_call" | custom-call | flops 3000000000 | bytes 1048576 | tf_op jit(solution)/shard_map/pair/pallas_call | solution.py:153
  6.5 3.0 %collective-permute-start = (bf16[192,1024]{1,0:T(8,128)(2,1)S(1)}, bf16[192,1024]{1,0:T(8,128)(2,1)S(1)}, u32[]{:S(2)}, u32[]{:S(2)}) collective-permute-start(bf16[192,1024]{1,0:T(8,128)(2,1)S(1)} %get-tuple-element.41.order.send), channel_id=1, source_target_pairs={{0,2},{1,3},{2,0},{3,1},{4,6},{5,7},{6,4},{7,5}} | collective-permute-start | bytes 1179656 | tf_op jit(solution)/shard_map/ppermute | solution.py:530
  9.5 0.0 copy-start
  9.5 10.2 %fill1.1 = (s32[512]{0:T(512)S(1)}, f32[8,128]{1,0:T(8,128)S(1)}, f32[12576,1024]{1,0:T(8,128)}) custom-call(s32[1,256]{1,0:T(1,128)S(1)} %get-tuple-element.42.rows_mine, f32[96,1024]{1,0:T(8,128)S(1)} %get-tuple-element.43.zero, bf16[192,1024]{1,0:T(8,128)(2,1)S(1)} %get-tuple-element.41.order.send, ...), custom_call_target="tpu_custom_call", output_to_operand_aliasing={{2}: (3, {})} | custom-call | flops 8999999488 | bytes 20971520 | tf_op jit(solution)/shard_map/fill1/pallas_call | solution.py:187
  19.7 0.0 collective-permute-done.got
  19.7 2.0 %share.1 = (bf16[256,1024]{1,0:T(8,128)(2,1)S(1)}, bf16[256,1024]{1,0:T(8,128)(2,1)S(1)}, bf16[1024,1024]{1,0:T(8,128)(2,1)S(1)}) custom-call(bf16[192,1024]{1,0:T(8,128)(2,1)S(1)} %get-tuple-element.41.order.send, bf16[192,1024]{1,0:T(8,128)(2,1)S(1)} %collective-permute-done.got, bf16[1024,1024]{1,0:T(8,128)(2,1)} %w2.1, f32[8,128]{1,0:T(8,128)S(1)} %get-tuple-element.45.order), custom_call_target="tpu_custom_call" | custom-call | flops 3000000000 | bytes 1048576 | tf_op jit(solution)/shard_map/share/pallas_call | solution.py:227
  21.8 0.0 copy-done
  21.8 2.6 %mlp.1 = (bf16[256,1024]{1,0:T(8,128)(2,1)S(1)}, bf16[256,1024]{1,0:T(8,128)(2,1)S(1)}, bf16[256,1024]{1,0:T(8,128)(2,1)S(1)}, f32[128,1024]{1,0:T(8,128)S(1)}, f32[12576,1024]{1,0:T(8,128)}) custom-call(bf16[256,1024]{1,0:T(8,128)(2,1)S(1)} %get-tuple-element.46.x_f.x_own.x, ...), custom_call_target="tpu_custom_call", output_to_operand_aliasing={{4}: (6, {})} | custom-call | flops 6000000000 | bytes 4194304 | tf_op jit(solution)/shard_map/mlp/pallas_call | solution.py:267
  24.3 2.0 %sums.1 = (f32[64,1024]{1,0:T(8,128)S(1)}, f32[64,1024]{1,0:T(8,128)S(1)}, f32[256,1024]{1,0:T(8,128)S(1)}) custom-call(f32[128,1024]{1,0:T(8,128)S(1)} %get-tuple-element.51.dn_p, bf16[256,1024]{1,0:T(8,128)(2,1)S(1)} %get-tuple-element.52.du, bf16[256,1024]{1,0:T(8,128)(2,1)S(1)} %get-tuple-element.53.h, bf16[1024,1024]{1,0:T(8,128)(2,1)S(1)} %get-tuple-element.48.w1, ...), custom_call_target="tpu_custom_call" | custom-call | flops 4000000000 | bytes 4194304 | tf_op jit(solution)/shard_map/sums/pallas_call | solution.py:303
  26.3 0.8 %collective-permute-start.2 = (f32[64,1024]{1,0:T(8,128)S(1)}, f32[64,1024]{1,0:T(8,128)S(1)}, u32[]{:S(2)}, u32[]{:S(2)}) collective-permute-start(f32[64,1024]{1,0:T(8,128)S(1)} %get-tuple-element.62), channel_id=1, source_target_pairs={{0,2},{1,3},{2,0},{3,1},{4,6},{5,7},{6,4},{7,5}} | collective-permute-start | bytes 786440 | tf_op jit(solution)/shard_map/ppermute | solution.py:525
  27.2 2.0 %ysum.1 = (f32[64,1024]{1,0:T(8,128)S(1)}, f32[32,1024]{1,0:T(8,128)S(1)}, f32[32,1024]{1,0:T(8,128)S(1)}) custom-call(f32[256,1024]{1,0:T(8,128)S(1)} %get-tuple-element.54.y_p, f32[64,1024]{1,0:T(8,128)S(1)} %get-tuple-element.55.order.dn_own), custom_call_target="tpu_custom_call" | custom-call | flops 3000000000 | bytes 4194304 | tf_op jit(solution)/shard_map/ysum/pallas_call | solution.py:332
  29.2 0.0 copy-start.1
  29.2 5.0 %grads.1 = (f32[8,128]{1,0:T(8,128)S(1)}, f32[1024,1024]{1,0:T(8,128)}, f32[1024,1024]{1,0:T(8,128)}, f32[12576,1024]{1,0:T(8,128)}) custom-call(bf16[256,1024]{1,0:T(8,128)(2,1)S(1)} %get-tuple-element.57.n, bf16[256,1024]{1,0:T(8,128)(2,1)S(1)} %get-tuple-element.53.h, ...), custom_call_target="tpu_custom_call", output_to_operand_aliasing={{3}: (6, {})} | custom-call | flops 8000000000 | bytes 20971520 | tf_op jit(solution)/shard_map/grads/pallas_call | solution.py:366
  34.2 1.2 %collective-permute-start.1 = (f32[32,1024]{1,0:T(8,128)S(1)}, f32[32,1024]{1,0:T(8,128)S(1)}, u32[]{:S(2)}, u32[]{:S(2)}) collective-permute-start(f32[32,1024]{1,0:T(8,128)S(1)} %get-tuple-element.61), channel_id=1, source_target_pairs={{0,2},{1,3},{2,0},{3,1},{4,6},{5,7},{6,4},{7,5}} | collective-permute-start | bytes 393224 | tf_op jit(solution)/shard_map/ppermute | solution.py:539
  35.4 0.0 collective-permute-done.2.g2
  35.4 0.0 copy-done.1
  35.4 0.2 dx_rows.1.order.dx
  35.6 0.8 %collective-permute-start.4 = (bf16[64,1024]{1,0:T(8,128)(2,1)S(1)}, bf16[64,1024]{1,0:T(8,128)(2,1)S(1)}, u32[]{:S(2)}, u32[]{:S(2)}) collective-permute-start(bf16[64,1024]{1,0:T(8,128)(2,1)S(1)} %dx_rows.1.order.dx), channel_id=1, source_target_pairs={{0,2},{1,3},{2,0},{3,1},{4,6},{5,7},{6,4},{7,5}} | collective-permute-start | bytes 393224 | tf_op jit(solution)/shard_map/ppermute | solution.py:525
  36.5 1.2 %collective-permute-start.3 = (f32[32,1024]{1,0:T(8,128)S(1)}, f32[32,1024]{1,0:T(8,128)S(1)}, u32[]{:S(2)}, u32[]{:S(2)}) collective-permute-start(f32[32,1024]{1,0:T(8,128)S(1)} %get-tuple-element.65), channel_id=1, source_target_pairs={{0,2},{1,3},{2,0},{3,1},{4,6},{5,7},{6,4},{7,5}} | collective-permute-start | bytes 393224 | tf_op jit(solution)/shard_map/ppermute | solution.py:525
  37.7 2.4 %fill3.1 = (f32[8,128]{1,0:T(8,128)S(1)}, f32[12576,1024]{1,0:T(8,128)}) custom-call(f32[96,1024]{1,0:T(8,128)S(1)} %get-tuple-element.43.zero, bf16[64,1024]{1,0:T(8,128)(2,1)S(1)} %dx_rows.1.order.dx, f32[12576,1024]{1,0:T(8,128)} %get-tuple-element.69.table_in), custom_call_target="tpu_custom_call", output_to_operand_aliasing={{1}: (2, {})} | custom-call | flops 4000000000 | bytes 16777216 | tf_op jit(solution)/shard_map/fill3/pallas_call | solution.py:409
  40.1 3.3 %collective-permute-done.4.dx_far = bf16[64,1024]{1,0:T(8,128)(2,1)S(1)} collective-permute-done((bf16[64,1024]{1,0:T(8,128)(2,1)S(1)}, bf16[64,1024]{1,0:T(8,128)(2,1)S(1)}, u32[]{:S(2)}, u32[]{:S(2)}) %collective-permute-start.4) | collective-permute-done | bytes 131104 | tf_op jit(solution)/shard_map/ppermute | solution.py:525
  43.4 1.6 %dx_all.1.dx = bf16[256,1024]{1,0:T(8,128)(2,1)S(1)} custom-call(bf16[64,1024]{1,0:T(8,128)(2,1)S(1)} %dx_rows.1.order.dx, bf16[64,1024]{1,0:T(8,128)(2,1)S(1)} %collective-permute-done.4.dx_far, f32[8,128]{1,0:T(8,128)S(1)} %get-tuple-element.70.order), custom_call_target="tpu_custom_call" | custom-call | flops 2000000000 | bytes 1048576 | tf_op jit(solution)/shard_map/dx_all/pallas_call | solution.py:439
  45.0 2.1 %put_rows.1 = (f32[12576,1024]{1,0:T(8,128)}, f32[8,128]{1,0:T(8,128)S(1)}) custom-call(s32[512]{0:T(512)S(1)} %get-tuple-element.66.puts, bf16[256,256]{1,0:T(8,128)(2,1)S(1)} %get-tuple-element.67.same, bf16[256,1024]{1,0:T(8,128)(2,1)S(1)} %dx_all.1.dx, f32[12576,1024]{1,0:T(8,128)} %get-tuple-element.71.table_in), custom_call_target="tpu_custom_call", output_to_operand_aliasing={{0}: (3, {})} | custom-call | flops 3000000000 | bytes 2097152 | tf_op jit(solution)/shard_map/put_rows/pallas_call | solution.py:488
  47.1 0.0 collective-permute-done.1.y_in0
  47.1 0.0 collective-permute-done.3.y_in1
  47.1 0.7 %finish.1 = bf16[64,1024]{1,0:T(8,128)(2,1)} custom-call(bf16[256,1024]{1,0:T(8,128)(2,1)S(1)} %get-tuple-element.46.x_f.x_own.x, f32[64,1024]{1,0:T(8,128)S(1)} %get-tuple-element.56.order.y, f32[32,1024]{1,0:T(8,128)S(1)} %collective-permute-done.1.y_in0, f32[32,1024]{1,0:T(8,128)S(1)} %collective-permute-done.3.y_in1, f32[8,128]{1,0:T(8,128)S(1)} %get-tuple-element.72.order), custom_call_target="tpu_custom_call" | custom-call | flops 1000000000 | bytes 1048576 | tf_op jit(solution)/shard_map/finish/pallas_call | solution.py:509
Async XLA Ops:
  6.5 13.2 %collective-permute-start = (bf16[192,1024]{1,0:T(8,128)(2,1)S(1)}, bf16[192,1024]{1,0:T(8,128)(2,1)S(1)}, u32[]{:S(2)}, u32[]{:S(2)}) collective-permute-start(bf16[192,1024]{1,0:T(8,128)(2,1)S(1)} %get-tuple-element.41.order.send), channel_id=1, source_target_pairs={{0,2},{1,3},{2,0},{3,1},{4,6},{5,7},{6,4},{7,5}} | collective-permute-start | bytes 1179656 | tf_op jit(solution)/shard_map/ppermute | solution.py:530
  9.5 12.3 %copy-start = (bf16[1024]{0:T(1024)(128)(2,1)S(1)}, bf16[1024]{0:T(1024)(128)(2,1)}, u32[]{:S(2)}) copy-start(bf16[1024]{0:T(1024)(128)(2,1)} %gain.3) | copy-start | bytes 6148
  26.3 9.1 %collective-permute-start.2 = (f32[64,1024]{1,0:T(8,128)S(1)}, f32[64,1024]{1,0:T(8,128)S(1)}, u32[]{:S(2)}, u32[]{:S(2)}) collective-permute-start(f32[64,1024]{1,0:T(8,128)S(1)} %get-tuple-element.62), channel_id=1, source_target_pairs={{0,2},{1,3},{2,0},{3,1},{4,6},{5,7},{6,4},{7,5}} | collective-permute-start | bytes 786440 | tf_op jit(solution)/shard_map/ppermute | solution.py:525
  29.2 6.3 %copy-start.1 = (bf16[64,1024]{1,0:T(8,128)(2,1)S(1)}, bf16[64,1024]{1,0:T(8,128)(2,1)}, u32[]{:S(2)}) copy-start(bf16[64,1024]{1,0:T(8,128)(2,1)} %d_own.1) | copy-start | bytes 393220
  34.2 12.9 %collective-permute-start.1 = (f32[32,1024]{1,0:T(8,128)S(1)}, f32[32,1024]{1,0:T(8,128)S(1)}, u32[]{:S(2)}, u32[]{:S(2)}) collective-permute-start(f32[32,1024]{1,0:T(8,128)S(1)} %get-tuple-element.61), channel_id=1, source_target_pairs={{0,2},{1,3},{2,0},{3,1},{4,6},{5,7},{6,4},{7,5}} | collective-permute-start | bytes 393224 | tf_op jit(solution)/shard_map/ppermute | solution.py:539
  35.6 7.8 %collective-permute-start.4 = (bf16[64,1024]{1,0:T(8,128)(2,1)S(1)}, bf16[64,1024]{1,0:T(8,128)(2,1)S(1)}, u32[]{:S(2)}, u32[]{:S(2)}) collective-permute-start(bf16[64,1024]{1,0:T(8,128)(2,1)S(1)} %dx_rows.1.order.dx), channel_id=1, source_target_pairs={{0,2},{1,3},{2,0},{3,1},{4,6},{5,7},{6,4},{7,5}} | collective-permute-start | bytes 393224 | tf_op jit(solution)/shard_map/ppermute | solution.py:525
  36.5 10.6 %collective-permute-start.3 = (f32[32,1024]{1,0:T(8,128)S(1)}, f32[32,1024]{1,0:T(8,128)S(1)}, u32[]{:S(2)}, u32[]{:S(2)}) collective-permute-start(f32[32,1024]{1,0:T(8,128)S(1)} %get-tuple-element.65), channel_id=1, source_target_pairs={{0,2},{1,3},{2,0},{3,1},{4,6},{5,7},{6,4},{7,5}} | collective-permute-start | bytes 393224 | tf_op jit(solution)/shard_map/ppermute | solution.py:525

commit v7 on v6

--- a/solution.py
+++ b/solution.py
@@ -19,7 +19,8 @@
 DMA = pltpu.SemaphoreType.DMA
 TILE = 256
 ZERO_ROWS = 96
-FILL_AT = (0, 12, 92, 103, 117, 131)
+FILL_AT = (0, 14, 91, 96, 106, 131)
+Y_FIRST = 16
 MIB = 1 << 20
 LOOKUP_VMEM = 48 * MIB
 PAIR_VMEM = 8 * MIB
@@ -162,12 +163,13 @@
     )(part, in_hbm(d_out), in_hbm(w1))
 
 
-def fill1_kernel(rows_mine, zero, order, table_in, puts, token, table_g, mine_s, puts_s, s_zero, s_list):
+def fill1_kernel(rows_mine, zero, w2, order, table_in, puts, w2_v, table_g, mine_s, puts_s, s_zero, s_list, s_w):
     load = pltpu.make_async_copy(rows_mine, mine_s, s_list)
     load.start()
+    load_w = pltpu.make_async_copy(w2, w2_v, s_w)
+    load_w.start()
     fill_start(zero, table_g, s_zero, 1)
     tokens = rows_mine.shape[1]
-    token[...] = jnp.zeros_like(token)
     load.wait()
 
     def body(i, count):
@@ -179,29 +181,48 @@
     store = pltpu.make_async_copy(puts_s, puts, s_list)
     store.start()
     store.wait()
+    load_w.wait()
     fill_wait(zero, table_g, s_zero, 1)
 
 
-def fill1(rows_mine, zero, order, table_g):
+def fill1(rows_mine, zero, w2, order, table_g):
     tokens = rows_mine.shape[1]
     return pl.pallas_call(
         fill1_kernel,
         name="fill1",
-        out_shape=[sh((2 * tokens,), I32), sh((8, 128), F32), sh(table_g.shape, F32)],
-        in_specs=[ANY_SPEC, VMEM_SPEC, ANY_SPEC, HBM_SPEC],
+        out_shape=[sh((2 * tokens,), I32), sh(w2.shape, BF), sh(table_g.shape, F32)],
+        in_specs=[ANY_SPEC, VMEM_SPEC, HBM_SPEC, ANY_SPEC, HBM_SPEC],
         out_specs=[ANY_SPEC, VMEM_SPEC, HBM_SPEC],
-        input_output_aliases={3: 2},
-        scratch_shapes=[pltpu.SMEM((1, tokens), I32), pltpu.SMEM((2 * tokens,), I32), DMA(()), DMA(())],
+        input_output_aliases={4: 2},
+        scratch_shapes=[pltpu.SMEM((1, tokens), I32), pltpu.SMEM((2 * tokens,), I32), DMA(()), DMA(()), DMA(())],
         compiler_params=pltpu.CompilerParams(vmem_limit_bytes=8 * MIB),
         cost_estimate=pl.CostEstimate(flops=9_000_000_000, bytes_accessed=20 * MIB, transcendentals=0),
-    )(rows_mine, zero, order, table_g)
-
-
-def share_kernel(send, got, w2, order, x_f, d_full, w2_v, x_r, d_r, sems, s_in):
+    )(rows_mine, zero, in_hbm(w2), order, table_g)
+
+
+def mlp_half(x, d, n, h, du, at, w1, w2, gain):
+    first, count = at
+    width, hid = n.shape[1], h.shape[1]
+    gain_f = gain[...].astype(F32).reshape(1, width)
+    for j in range(count // 32):
+        rows = pl.ds(first + j * 32, 32)
+        x_f = x[rows, :].astype(F32)
+        r = lax.rsqrt(jnp.mean(x_f * x_f, axis=-1, keepdims=True) + EPS)
+        n[rows, :] = (x_f * r * gain_f).astype(BF)
+    rows = pl.ds(first, count)
+    for j in range(hid // TILE):
+        cols = pl.ds(j * TILE, TILE)
+        g = mm(d[rows, :], w2[cols, :], 1, 1).astype(BF).astype(F32)
+        u = mm(n[rows, :], w1[:, cols], 1, 0).astype(BF).astype(F32)
+        t = jnp.tanh(GELU_C * (u + GELU_A * (u * u * u)))
+        cdf = 0.5 * (1.0 + t)
+        h[rows, cols] = (u * cdf).astype(BF)
+        du[rows, cols] = (g * (cdf + u * (0.5 * (1.0 - t * t)) * (GELU_C * (1.0 + 3.0 * GELU_A * (u * u))))).astype(BF)
+
+
+def share_kernel(send, got, w1, w2, gain, x_f, d_full, n_a, h_a, du_a, x_r, d_r, sems):
     rows = send.shape[0] // 3
     half = 2 * rows
-    load = pltpu.make_async_copy(w2, w2_v, s_in)
-    load.start()
     remote = swap_with_sibling()
     copies = []
     for k in range(2):
@@ -213,55 +234,44 @@
         copies.append(remote(src.at[pl.ds(half, rows)], d_r.at[pl.ds(k * rows, rows)], sems, 2 + k))
         copies[-1].start()
         d_full[pl.ds(k * rows, rows), :] = src[pl.ds(half, rows), :]
+    mlp_half(x_f, d_full, n_a, h_a, du_a, (0, half), w1, w2, gain)
     for k in range(2):
         copies[k].wait()
         x_f[pl.ds(half + k * rows, rows), :] = x_r[pl.ds(k * rows, rows), :]
     for k in range(2):
         copies[2 + k].wait()
         d_full[pl.ds(half + k * rows, rows), :] = d_r[pl.ds(k * rows, rows), :]
-    load.wait()
-
-
-def share(send, got, w2, order):
+
+
+def share(send, got, w1, w2, gain):
     rows, width = send.shape[0] // 3, send.shape[1]
+    hid = w1.shape[1]
     return pl.pallas_call(
         share_kernel,
         name="share",
-        out_shape=[sh((4 * rows, width), BF)] * 2 + [sh(w2.shape, BF)],
-        in_specs=[VMEM_SPEC] * 2 + [HBM_SPEC, ANY_SPEC],
-        out_specs=[VMEM_SPEC] * 3,
-        scratch_shapes=[VMEM((2 * rows, width), BF), VMEM((2 * rows, width), BF), DMA((2, 4)), DMA(())],
-        compiler_params=pltpu.CompilerParams(collective_id=1, has_side_effects=True, vmem_limit_bytes=8 * MIB),
+        out_shape=[sh((4 * rows, width), BF)] * 2 + [sh((2 * rows, width), BF)] + [sh((2 * rows, hid), BF)] * 2,
+        in_specs=[VMEM_SPEC] * 5,
+        out_specs=[VMEM_SPEC] * 5,
+        scratch_shapes=[VMEM((2 * rows, width), BF), VMEM((2 * rows, width), BF), DMA((2, 4))],
+        compiler_params=pltpu.CompilerParams(collective_id=1, has_side_effects=True, vmem_limit_bytes=16 * MIB),
         cost_estimate=pl.CostEstimate(flops=3_000_000_000, bytes_accessed=MIB, transcendentals=0),
-    )(send, got, in_hbm(w2), order)
-
-
-def mlp_kernel(x_f, d_full, w1, w2, gain, zero, table_in, n, h, du, dn_p, table_g, s_zero):
+    )(send, got, w1, w2, gain)
+
+
+def mlp_kernel(x_f, d_full, n_a, h_a, du_a, w1, w2, gain, zero, table_in, n, h, du, dn_p, table_g, s_zero):
     fill_start(zero, table_g, s_zero, 2)
     tokens, width = n.shape
-    hid = h.shape[1]
-    gain_f = gain[...].astype(F32).reshape(1, width)
-    for j in range(tokens // 32):
-        at = pl.ds(j * 32, 32)
-        x = x_f[at, :].astype(F32)
-        r = lax.rsqrt(jnp.mean(x * x, axis=-1, keepdims=True) + EPS)
-        n[at, :] = (x * r * gain_f).astype(BF)
-    for j in range(hid // TILE):
-        cols = pl.ds(j * TILE, TILE)
-        g = mm(d_full[...], w2[cols, :], 1, 1).astype(BF).astype(F32)
-        u = mm(n[...], w1[:, cols], 1, 0).astype(BF).astype(F32)
-        t = jnp.tanh(GELU_C * (u + GELU_A * (u * u * u)))
-        cdf = 0.5 * (1.0 + t)
-        h[:, cols] = (u * cdf).astype(BF)
-        du[:, cols] = (g * (cdf + u * (0.5 * (1.0 - t * t)) * (GELU_C * (1.0 + 3.0 * GELU_A * (u * u))))).astype(BF)
     half = tokens // 2
+    for out, src in ((n, n_a), (h, h_a), (du, du_a)):
+        out[pl.ds(0, half), :] = src[...]
+    mlp_half(x_f, d_full, n, h, du, (half, half), w1, w2, gain)
     for j in range(width // TILE):
         cols = pl.ds(j * TILE, TILE)
         dn_p[:, cols] = mm(du[pl.ds(half, half), :], w1[cols, :], 1, 1)
     fill_wait(zero, table_g, s_zero, 2)
 
 
-def mlp(x_f, d_full, w1, w2, gain, zero, table_g):
+def mlp(x_f, d_full, n_a, h_a, du_a, w1, w2, gain, zero, table_g):
     tokens, width = x_f.shape
     hid = w1.shape[1]
     return pl.pallas_call(
@@ -269,13 +279,13 @@
         name="mlp",
         out_shape=[sh((tokens, width), BF), sh((tokens, hid), BF), sh((tokens, hid), BF), sh((tokens // 2, width), F32),
                    sh(table_g.shape, F32)],
-        in_specs=[VMEM_SPEC] * 6 + [HBM_SPEC],
+        in_specs=[VMEM_SPEC] * 9 + [HBM_SPEC],
         out_specs=[VMEM_SPEC] * 4 + [HBM_SPEC],
-        input_output_aliases={6: 4},
+        input_output_aliases={9: 4},
         scratch_shapes=[DMA(())],
         compiler_params=pltpu.CompilerParams(vmem_limit_bytes=16 * MIB),
         cost_estimate=pl.CostEstimate(flops=6_000_000_000, bytes_accessed=4 * MIB, transcendentals=0),
-    )(x_f, d_full, w1, w2, gain, zero, table_g)
+    )(x_f, d_full, n_a, h_a, du_a, w1, w2, gain, zero, table_g)
 
 
 def sums_kernel(dn_p, du, h, w1, w2, dn_own, dn_far, y_p, dn_r, dn_m, sems):
@@ -314,9 +324,9 @@
 
 def ysum_kernel(y_p, order, y_own, y_far0, y_far1, y_r, sems):
     rows, _ = y_own.shape
-    half, part = 2 * rows, rows // 2
+    half = 2 * rows
     remote = swap_with_sibling()
-    places = ((rows, y_far0), (rows + part, y_far1), (0, y_own))
+    places = ((rows, y_far0), (rows + Y_FIRST, y_far1), (0, y_own))
     copies = [remote(y_p.at[pl.ds(half + at, out.shape[0])], y_r.at[pl.ds(at, out.shape[0])], sems, k) for k, (at, out) in enumerate(places)]
     for c in copies:
         c.start()
@@ -332,7 +342,7 @@
     return pl.pallas_call(
         ysum_kernel,
         name="ysum",
-        out_shape=[sh((rows, width), F32), sh((rows // 2, width), F32), sh((rows // 2, width), F32)],
+        out_shape=[sh((rows, width), F32), sh((Y_FIRST, width), F32), sh((rows - Y_FIRST, width), F32)],
         in_specs=[VMEM_SPEC, ANY_SPEC],
         out_specs=[VMEM_SPEC] * 3,
         scratch_shapes=[VMEM((2 * rows, width), F32), DMA((2, 3))],
@@ -499,9 +509,8 @@
 
 
 def finish_kernel(x, y, y_in0, y_in1, order, out):
-    part = y_in0.shape[0]
-    for k, y_in in enumerate((y_in0, y_in1)):
-        at = pl.ds(k * part, part)
+    for first, y_in in ((0, y_in0), (Y_FIRST, y_in1)):
+        at = pl.ds(first, y_in.shape[0])
         out[at, :] = (x[at, :].astype(F32) + (y[at, :] + y_in[...])).astype(BF)
 
 
@@ -528,15 +537,14 @@
         part, rows_mine, same, zero, d_table = lookup(ids, table)
         send, w1 = pair(part, d_out, w1)
         got = lax.ppermute(send, "tp", far_pairs)
-        puts, token, d_table = fill1(rows_mine, zero, send, d_table)
-        x_f, d_full, w2 = share(send, got, w2, token)
-        n, h, du, dn_p, d_table = mlp(x_f, d_full, w1, w2, gain, zero, d_table)
+        puts, w2, d_table = fill1(rows_mine, zero, w2, send, d_table)
+        x_f, d_full, n_a, h_a, du_a = share(send, got, w1, w2, gain)
+        n, h, du, dn_p, d_table = mlp(x_f, d_full, n_a, h_a, du_a, w1, w2, gain, zero, d_table)
         dn_own, dn_far, y_p = sums(dn_p, du, h, w1, w2)
         g2 = far_permute(dn_far)
         y_own, y_far0, y_far1 = ysum(y_p, dn_own)
+        y_in0 = lax.ppermute(y_far0, "tp", far_pairs)
         token, d_w1, d_w2, d_table = grads(n, h, du, d_full, zero, y_own, d_table)
-        token, y_far0 = lax.optimization_barrier((token, y_far0))
-        y_in0 = lax.ppermute(y_far0, "tp", far_pairs)
         dx = dx_rows(dn_own, g2, x_f, d_out, gain, token)
         dx_far = far_permute(dx)
         dx, y_far1 = lax.optimization_barrier((dx, y_far1))

time: 48.1 us -> 49 us (1.019)
  waiting for transfers between devices: 3.34 us -> 3.84 us
    pallas_call x1, Pallas kernels: 2.41 us -> 3.7 us  [fill3(): pl.pallas_call(fill3_kernel, name='fill3', out_shape=[sh((8, 128), F32),...]
    ppermute x3, waiting for transfers between devices: 3.33 us -> 3.83 us  [far_permute(): return lax.ppermute(x, 'tp', far_pairs)]
    pallas_call x1, Pallas kernels: 2.57 us -> 2.06 us  [mlp(): pl.pallas_call(mlp_kernel, name='mlp', out_shape=[sh((tokens, width), BF)...]
  transfers between devices with their start and end apart: 5 -> 5, of which waited for: 1 -> 2; matrix products, arithmetic and copies ran while one was open for 0% -> 0% of each run, Pallas kernels for 49% -> 45%
where the time goes in v7:
time: 49 us; the launch traced here: 48.6 us
  Pallas kernels  37 us (76%)
  starting transfers between devices  7.06 us (14%)
  waiting for transfers between devices  3.84 us (8%)
  between operations  0.76 us (2%)
    pallas_call x1, Pallas kernels, fill1(): pl.pallas_call(fill1_kernel, name='fill1', out_shape=[sh((2 * tokens,), I...  10 us
    pallas_call x1, Pallas kernels, grads(): pl.pallas_call(grads_kernel, name='grads', out_shape=[sh((8, 128), F32),...  4.53 us
    pallas_call x1, Pallas kernels, lookup(): pl.pallas_call(lookup_kernel, name='lookup', out_shape=[sh((tokens, width...  4.07 us
    ppermute x3, waiting for transfers between devices, far_permute(): return lax.ppermute(x, 'tp', far_pairs)  3.83 us
    pallas_call x1, Pallas kernels, fill3(): pl.pallas_call(fill3_kernel, name='fill3', out_shape=[sh((8, 128), F32),...  3.7 us
    ppermute x3, starting transfers between devices, far_permute(): return lax.ppermute(x, 'tp', far_pairs)  3.08 us
    ppermute x1, starting transfers between devices, shard_step(): got = lax.ppermute(send, 'tp', far_pairs)  2.97 us
    pallas_call x1, Pallas kernels, pair(): pl.pallas_call(pair_kernel, name='pair', out_shape=[sh((3 * rows, width),...  2.08 us
  transfers between devices with their start and end apart: 5, of which 2 were waited for; matrix products, arithmetic and copies ran while one was open for 0% of the time, Pallas kernels for 45%

profile of v7, /device:TPU:0, one launch (start us, length us, event | category | flops | bytes accessed | tf_op | source)
XLA Modules:
  0.0 48.6 jit_solution(8099203909192147073)
XLA Ops:
  0.6 4.1 %lookup.1 = (bf16[256,1024]{1,0:T(8,128)(2,1)S(1)}, s32[1,256]{1,0:T(1,128)S(1)}, bf16[256,256]{1,0:T(8,128)(2,1)S(1)}, f32[96,1024]{1,0:T(8,128)S(1)}, f32[12576,1024]{1,0:T(8,128)}) custom-call(s32[256]{0:T(256)} %ids.1, s32[1,256]{1,0:T(1,128)} %bitcast.1, bf16[12576,1024]{1,0:T(8,128)(2,1)} %table.1), custom_call_target="tpu_custom_call" | custom-call | flops 5000000000 | bytes 10485760 | tf_op jit(solution)/shard_map/lookup/pallas_call | solution.py:120
  4.7 2.1 %pair.1 = (bf16[192,1024]{1,0:T(8,128)(2,1)S(1)}, bf16[1024,1024]{1,0:T(8,128)(2,1)S(1)}) custom-call(bf16[256,1024]{1,0:T(8,128)(2,1)S(1)} %get-tuple-element.40.part, bf16[64,1024]{1,0:T(8,128)(2,1)} %d_own.1, bf16[1024,1024]{1,0:T(8,128)(2,1)} %w1.1), custom_call_target="tpu_custom_call" | custom-call | flops 3000000000 | bytes 1048576 | tf_op jit(solution)/shard_map/pair/pallas_call | solution.py:154
  6.8 3.0 %collective-permute-start = (bf16[192,1024]{1,0:T(8,128)(2,1)S(1)}, bf16[192,1024]{1,0:T(8,128)(2,1)S(1)}, u32[]{:S(2)}, u32[]{:S(2)}) collective-permute-start(bf16[192,1024]{1,0:T(8,128)(2,1)S(1)} %get-tuple-element.41.order.send), channel_id=1, source_target_pairs={{0,2},{1,3},{2,0},{3,1},{4,6},{5,7},{6,4},{7,5}} | collective-permute-start | bytes 1179656 | tf_op jit(solution)/shard_map/ppermute | solution.py:539
  9.8 0.0 copy-start
  9.8 10.0 %fill1.1 = (s32[512]{0:T(512)S(1)}, bf16[1024,1024]{1,0:T(8,128)(2,1)S(1)}, f32[12576,1024]{1,0:T(8,128)}) custom-call(s32[1,256]{1,0:T(1,128)S(1)} %get-tuple-element.43.rows_mine, f32[96,1024]{1,0:T(8,128)S(1)} %get-tuple-element.44.zero, bf16[1024,1024]{1,0:T(8,128)(2,1)} %w2.1, ...), custom_call_target="tpu_custom_call", output_to_operand_aliasing={{2}: (4, {})} | custom-call | flops 8999999488 | bytes 20971520 | tf_op jit(solution)/shard_map/fill1/pallas_call | solution.py:190
  19.8 0.0 collective-permute-done.got
  19.8 0.0 copy-done
  19.8 2.0 %share.1 = (bf16[256,1024]{1,0:T(8,128)(2,1)S(1)}, bf16[256,1024]{1,0:T(8,128)(2,1)S(1)}, bf16[128,1024]{1,0:T(8,128)(2,1)S(1)}, bf16[128,1024]{1,0:T(8,128)(2,1)S(1)}, bf16[128,1024]{1,0:T(8,128)(2,1)S(1)}) custom-call(bf16[192,1024]{1,0:T(8,128)(2,1)S(1)} %get-tuple-element.41.order.send, bf16[192,1024]{1,0:T(8,128)(2,1)S(1)} %collective-permute-done.got, ...), custom_call_target="tpu_custom_call" | custom-call | flops 3000000000 | bytes 1048576 | tf_op jit(solution)/shard_map/share/pallas_call | solution.py:249
  21.8 2.1 %mlp.1 = (bf16[256,1024]{1,0:T(8,128)(2,1)S(1)}, bf16[256,1024]{1,0:T(8,128)(2,1)S(1)}, bf16[256,1024]{1,0:T(8,128)(2,1)S(1)}, f32[128,1024]{1,0:T(8,128)S(1)}, f32[12576,1024]{1,0:T(8,128)}) custom-call(bf16[256,1024]{1,0:T(8,128)(2,1)S(1)} %get-tuple-element.47.x_f.x_own.x, ...), custom_call_target="tpu_custom_call", output_to_operand_aliasing={{4}: (9, {})} | custom-call | flops 6000000000 | bytes 4194304 | tf_op jit(solution)/shard_map/mlp/pallas_call | solution.py:277
  23.9 2.0 %sums.1 = (f32[64,1024]{1,0:T(8,128)S(1)}, f32[64,1024]{1,0:T(8,128)S(1)}, f32[256,1024]{1,0:T(8,128)S(1)}) custom-call(f32[128,1024]{1,0:T(8,128)S(1)} %get-tuple-element.53.dn_p, bf16[256,1024]{1,0:T(8,128)(2,1)S(1)} %get-tuple-element.54.du, bf16[256,1024]{1,0:T(8,128)(2,1)S(1)} %get-tuple-element.55.h, bf16[1024,1024]{1,0:T(8,128)(2,1)S(1)} %get-tuple-element.42.w1, ...), custom_call_target="tpu_custom_call" | custom-call | flops 4000000000 | bytes 4194304 | tf_op jit(solution)/shard_map/sums/pallas_call | solution.py:313
  25.9 2.0 %ysum.1 = (f32[64,1024]{1,0:T(8,128)S(1)}, f32[16,1024]{1,0:T(8,128)S(1)}, f32[48,1024]{1,0:T(8,128)S(1)}) custom-call(f32[256,1024]{1,0:T(8,128)S(1)} %get-tuple-element.56.y_p, f32[64,1024]{1,0:T(8,128)S(1)} %get-tuple-element.57.order.dn_own), custom_call_target="tpu_custom_call" | custom-call | flops 3000000000 | bytes 4194304 | tf_op jit(solution)/shard_map/ysum/pallas_call | solution.py:342
  27.9 1.0 %collective-permute-start.1 = (f32[16,1024]{1,0:T(8,128)S(1)}, f32[16,1024]{1,0:T(8,128)S(1)}, u32[]{:S(2)}, u32[]{:S(2)}) collective-permute-start(f32[16,1024]{1,0:T(8,128)S(1)} %get-tuple-element.59), channel_id=1, source_target_pairs={{0,2},{1,3},{2,0},{3,1},{4,6},{5,7},{6,4},{7,5}} | collective-permute-start | bytes 196616 | tf_op jit(solution)/shard_map/ppermute | solution.py:546
  28.9 1.0 %collective-permute-start.2 = (f32[64,1024]{1,0:T(8,128)S(1)}, f32[64,1024]{1,0:T(8,128)S(1)}, u32[]{:S(2)}, u32[]{:S(2)}) collective-permute-start(f32[64,1024]{1,0:T(8,128)S(1)} %get-tuple-element.60), channel_id=1, source_target_pairs={{0,2},{1,3},{2,0},{3,1},{4,6},{5,7},{6,4},{7,5}} | collective-permute-start | bytes 786440 | tf_op jit(solution)/shard_map/ppermute | solution.py:534
  30.0 0.0 copy-start.1
  30.0 4.5 %grads.1 = (f32[8,128]{1,0:T(8,128)S(1)}, f32[1024,1024]{1,0:T(8,128)}, f32[1024,1024]{1,0:T(8,128)}, f32[12576,1024]{1,0:T(8,128)}) custom-call(bf16[256,1024]{1,0:T(8,128)(2,1)S(1)} %get-tuple-element.61.n, bf16[256,1024]{1,0:T(8,128)(2,1)S(1)} %get-tuple-element.55.h, ...), custom_call_target="tpu_custom_call", output_to_operand_aliasing={{3}: (6, {})} | custom-call | flops 8000000000 | bytes 20971520 | tf_op jit(solution)/shard_map/grads/pallas_call | solution.py:376
  34.5 3.2 %collective-permute-done.2.g2 = f32[64,1024]{1,0:T(8,128)S(1)} collective-permute-done((f32[64,1024]{1,0:T(8,128)S(1)}, f32[64,1024]{1,0:T(8,128)S(1)}, u32[]{:S(2)}, u32[]{:S(2)}) %collective-permute-start.2) | collective-permute-done | bytes 262176 | tf_op jit(solution)/shard_map/ppermute | solution.py:534
  37.7 0.0 copy-done.1
  37.7 0.2 dx_rows.1.order.dx
  37.9 1.1 %collective-permute-start.4 = (bf16[64,1024]{1,0:T(8,128)(2,1)S(1)}, bf16[64,1024]{1,0:T(8,128)(2,1)S(1)}, u32[]{:S(2)}, u32[]{:S(2)}) collective-permute-start(bf16[64,1024]{1,0:T(8,128)(2,1)S(1)} %dx_rows.1.order.dx), channel_id=1, source_target_pairs={{0,2},{1,3},{2,0},{3,1},{4,6},{5,7},{6,4},{7,5}} | collective-permute-start | bytes 393224 | tf_op jit(solution)/shard_map/ppermute | solution.py:534
  38.9 1.0 %collective-permute-start.3 = (f32[48,1024]{1,0:T(8,128)S(1)}, f32[48,1024]{1,0:T(8,128)S(1)}, u32[]{:S(2)}, u32[]{:S(2)}) collective-permute-start(f32[48,1024]{1,0:T(8,128)S(1)} %get-tuple-element.65), channel_id=1, source_target_pairs={{0,2},{1,3},{2,0},{3,1},{4,6},{5,7},{6,4},{7,5}} | collective-permute-start | bytes 589832 | tf_op jit(solution)/shard_map/ppermute | solution.py:534
  39.9 3.7 %fill3.1 = (f32[8,128]{1,0:T(8,128)S(1)}, f32[12576,1024]{1,0:T(8,128)}) custom-call(f32[96,1024]{1,0:T(8,128)S(1)} %get-tuple-element.44.zero, bf16[64,1024]{1,0:T(8,128)(2,1)S(1)} %dx_rows.1.order.dx, f32[12576,1024]{1,0:T(8,128)} %get-tuple-element.69.table_in), custom_call_target="tpu_custom_call", output_to_operand_aliasing={{1}: (2, {})} | custom-call | flops 4000000000 | bytes 16777216 | tf_op jit(solution)/shard_map/fill3/pallas_call | solution.py:419
  43.6 0.6 %collective-permute-done.4.dx_far = bf16[64,1024]{1,0:T(8,128)(2,1)S(1)} collective-permute-done((bf16[64,1024]{1,0:T(8,128)(2,1)S(1)}, bf16[64,1024]{1,0:T(8,128)(2,1)S(1)}, u32[]{:S(2)}, u32[]{:S(2)}) %collective-permute-start.4) | collective-permute-done | bytes 131104 | tf_op jit(solution)/shard_map/ppermute | solution.py:534
  44.3 1.6 %dx_all.1.dx = bf16[256,1024]{1,0:T(8,128)(2,1)S(1)} custom-call(bf16[64,1024]{1,0:T(8,128)(2,1)S(1)} %dx_rows.1.order.dx, bf16[64,1024]{1,0:T(8,128)(2,1)S(1)} %collective-permute-done.4.dx_far, f32[8,128]{1,0:T(8,128)S(1)} %get-tuple-element.70.order), custom_call_target="tpu_custom_call" | custom-call | flops 2000000000 | bytes 1048576 | tf_op jit(solution)/shard_map/dx_all/pallas_call | solution.py:449
  45.9 2.1 %put_rows.1 = (f32[12576,1024]{1,0:T(8,128)}, f32[8,128]{1,0:T(8,128)S(1)}) custom-call(s32[512]{0:T(512)S(1)} %get-tuple-element.66.puts, bf16[256,256]{1,0:T(8,128)(2,1)S(1)} %get-tuple-element.67.same, bf16[256,1024]{1,0:T(8,128)(2,1)S(1)} %dx_all.1.dx, f32[12576,1024]{1,0:T(8,128)} %get-tuple-element.71.table_in), custom_call_target="tpu_custom_call", output_to_operand_aliasing={{0}: (3, {})} | custom-call | flops 3000000000 | bytes 2097152 | tf_op jit(solution)/shard_map/put_rows/pallas_call | solution.py:498
  47.9 0.0 collective-permute-done.1.y_in0
  47.9 0.0 collective-permute-done.3.y_in1
  48.0 0.7 %finish.1 = bf16[64,1024]{1,0:T(8,128)(2,1)} custom-call(bf16[256,1024]{1,0:T(8,128)(2,1)S(1)} %get-tuple-element.47.x_f.x_own.x, f32[64,1024]{1,0:T(8,128)S(1)} %get-tuple-element.58.order.y, f32[16,1024]{1,0:T(8,128)S(1)} %collective-permute-done.1.y_in0, f32[48,1024]{1,0:T(8,128)S(1)} %collective-permute-done.3.y_in1, f32[8,128]{1,0:T(8,128)S(1)} %get-tuple-element.72.order), custom_call_target="tpu_custom_call" | custom-call | flops 1000000000 | bytes 1048576 | tf_op jit(solution)/shard_map/finish/pallas_call | solution.py:518
Async XLA Ops:
  6.8 13.0 %collective-permute-start = (bf16[192,1024]{1,0:T(8,128)(2,1)S(1)}, bf16[192,1024]{1,0:T(8,128)(2,1)S(1)}, u32[]{:S(2)}, u32[]{:S(2)}) collective-permute-start(bf16[192,1024]{1,0:T(8,128)(2,1)S(1)} %get-tuple-element.41.order.send), channel_id=1, source_target_pairs={{0,2},{1,3},{2,0},{3,1},{4,6},{5,7},{6,4},{7,5}} | collective-permute-start | bytes 1179656 | tf_op jit(solution)/shard_map/ppermute | solution.py:539
  9.8 10.0 %copy-start = (bf16[1024]{0:T(1024)(128)(2,1)S(1)}, bf16[1024]{0:T(1024)(128)(2,1)}, u32[]{:S(2)}) copy-start(bf16[1024]{0:T(1024)(128)(2,1)} %gain.5) | copy-start | bytes 6148
  27.9 20.0 %collective-permute-start.1 = (f32[16,1024]{1,0:T(8,128)S(1)}, f32[16,1024]{1,0:T(8,128)S(1)}, u32[]{:S(2)}, u32[]{:S(2)}) collective-permute-start(f32[16,1024]{1,0:T(8,128)S(1)} %get-tuple-element.59), channel_id=1, source_target_pairs={{0,2},{1,3},{2,0},{3,1},{4,6},{5,7},{6,4},{7,5}} | collective-permute-start | bytes 196616 | tf_op jit(solution)/shard_map/ppermute | solution.py:546
  28.9 8.8 %collective-permute-start.2 = (f32[64,1024]{1,0:T(8,128)S(1)}, f32[64,1024]{1,0:T(8,128)S(1)}, u32[]{:S(2)}, u32[]{:S(2)}) collective-permute-start(f32[64,1024]{1,0:T(8,128)S(1)} %get-tuple-element.60), channel_id=1, source_target_pairs={{0,2},{1,3},{2,0},{3,1},{4,6},{5,7},{6,4},{7,5}} | collective-permute-start | bytes 786440 | tf_op jit(solution)/shard_map/ppermute | solution.py:534
  30.0 7.7 %copy-start.1 = (bf16[64,1024]{1,0:T(8,128)(2,1)S(1)}, bf16[64,1024]{1,0:T(8,128)(2,1)}, u32[]{:S(2)}) copy-start(bf16[64,1024]{1,0:T(8,128)(2,1)} %d_own.1) | copy-start | bytes 393220
  37.9 6.4 %collective-permute-start.4 = (bf16[64,1024]{1,0:T(8,128)(2,1)S(1)}, bf16[64,1024]{1,0:T(8,128)(2,1)S(1)}, u32[]{:S(2)}, u32[]{:S(2)}) collective-permute-start(bf16[64,1024]{1,0:T(8,128)(2,1)S(1)} %dx_rows.1.order.dx), channel_id=1, source_target_pairs={{0,2},{1,3},{2,0},{3,1},{4,6},{5,7},{6,4},{7,5}} | collective-permute-start | bytes 393224 | tf_op jit(solution)/shard_map/ppermute | solution.py:534
  38.9 9.0 %collective-permute-start.3 = (f32[48,1024]{1,0:T(8,128)S(1)}, f32[48,1024]{1,0:T(8,128)S(1)}, u32[]{:S(2)}, u32[]{:S(2)}) collective-permute-start(f32[48,1024]{1,0:T(8,128)S(1)} %get-tuple-element.65), channel_id=1, source_target_pairs={{0,2},{1,3},{2,0},{3,1},{4,6},{5,7},{6,4},{7,5}} | collective-permute-start | bytes 589832 | tf_op jit(solution)/shard_map/ppermute | solution.py:534

commit v8 on v7

--- a/solution.py
+++ b/solution.py
@@ -19,8 +19,7 @@
 DMA = pltpu.SemaphoreType.DMA
 TILE = 256
 ZERO_ROWS = 96
-FILL_AT = (0, 14, 91, 96, 106, 131)
-Y_FIRST = 16
+FILL_AT = (0, 4, 81, 93, 103, 112, 131)
 MIB = 1 << 20
 LOOKUP_VMEM = 48 * MIB
 PAIR_VMEM = 8 * MIB
@@ -288,7 +287,7 @@
     )(x_f, d_full, n_a, h_a, du_a, w1, w2, gain, zero, table_g)
 
 
-def sums_kernel(dn_p, du, h, w1, w2, dn_own, dn_far, y_p, dn_r, dn_m, sems):
+def sums_kernel(dn_p, du, h, w1, w2, dn_own, dn_far, y_a, y_b, dn_r, dn_m, sems):
     rows, width = dn_own.shape
     half = 2 * rows
     remote = swap_with_sibling()
@@ -300,7 +299,9 @@
         dn_m[:, cols] = mm(du[pl.ds(0, half), :], w1[cols, :], 1, 1)
     for j in range(width // TILE):
         cols = pl.ds(j * TILE, TILE)
-        y_p[:, cols] = mm(h[...], w2[:, cols], 1, 0)
+        y = mm(h[...], w2[:, cols], 1, 0)
+        y_a[:, cols] = y[:half]
+        y_b[:, cols] = y[half:]
     for c, out, k in zip(copies, (dn_far, dn_own), (1, 0)):
         c.wait()
         at = pl.ds(k * rows, rows)
@@ -313,77 +314,73 @@
     return pl.pallas_call(
         sums_kernel,
         name="sums",
-        out_shape=[sh((rows, width), F32), sh((rows, width), F32), sh((2 * half, width), F32)],
+        out_shape=[sh((rows, width), F32)] * 2 + [sh((half, width), F32)] * 2,
         in_specs=[VMEM_SPEC] * 5,
-        out_specs=[VMEM_SPEC] * 3,
+        out_specs=[VMEM_SPEC] * 4,
         scratch_shapes=[VMEM((half, width), F32), VMEM((half, width), F32), DMA((2, 2))],
         compiler_params=pltpu.CompilerParams(collective_id=2, has_side_effects=True, vmem_limit_bytes=16 * MIB),
         cost_estimate=pl.CostEstimate(flops=4_000_000_000, bytes_accessed=4 * MIB, transcendentals=0),
     )(dn_p, du, h, w1, w2)
 
 
-def ysum_kernel(y_p, order, y_own, y_far0, y_far1, y_r, sems):
-    rows, _ = y_own.shape
-    half = 2 * rows
-    remote = swap_with_sibling()
-    places = ((rows, y_far0), (rows + Y_FIRST, y_far1), (0, y_own))
-    copies = [remote(y_p.at[pl.ds(half + at, out.shape[0])], y_r.at[pl.ds(at, out.shape[0])], sems, k) for k, (at, out) in enumerate(places)]
-    for c in copies:
-        c.start()
-    for c, (at, out) in zip(copies, places):
-        c.wait()
-        rows_at = pl.ds(at, out.shape[0])
-        out[...] = y_p[rows_at, :] + y_r[rows_at, :]
-
-
-def ysum(y_p, order):
-    tokens, width = y_p.shape
-    rows = tokens // 4
-    return pl.pallas_call(
-        ysum_kernel,
-        name="ysum",
-        out_shape=[sh((rows, width), F32), sh((Y_FIRST, width), F32), sh((rows - Y_FIRST, width), F32)],
-        in_specs=[VMEM_SPEC, ANY_SPEC],
-        out_specs=[VMEM_SPEC] * 3,
-        scratch_shapes=[VMEM((2 * rows, width), F32), DMA((2, 3))],
-        compiler_params=pltpu.CompilerParams(collective_id=4, has_side_effects=True, vmem_limit_bytes=8 * MIB),
-        cost_estimate=pl.CostEstimate(flops=3_000_000_000, bytes_accessed=4 * MIB, transcendentals=0),
-    )(y_p, order)
-
-
-def grads_kernel(n, h, du, d_full, zero, order, table_in, token, dw1, dw2, table_g, dw1_v, dw2_v, s_zero, s_w):
-    fill_start(zero, table_g, s_zero, 3)
-    token[...] = jnp.zeros_like(token)
-    width, hid = dw1.shape
+def grads1_kernel(n, du, zero, order, table_in, dw1, table_g, dw1_v, s_zero, s_w):
+    width = n.shape[1]
     n_t = n[...].T
     for j in range(width // TILE):
         at = slice(j * TILE, (j + 1) * TILE)
         dw1_v[at, :] = mm(n_t[at, :], du[...], 1, 0)
         pltpu.make_async_copy(dw1_v.at[pl.ds(j * TILE, TILE)], dw1.at[pl.ds(j * TILE, TILE)], s_w).start()
+        if j == 0:
+            fill_start(zero, table_g, s_zero, 3)
+    pltpu.make_async_copy(dw1_v, dw1, s_w).wait()
+    fill_wait(zero, table_g, s_zero, 3)
+
+
+def grads1(n, du, zero, order, table_g):
+    width, hid = n.shape[1], du.shape[1]
+    return pl.pallas_call(
+        grads1_kernel,
+        name="grads1",
+        out_shape=[sh((width, hid), F32), sh(table_g.shape, F32)],
+        in_specs=[VMEM_SPEC] * 3 + [ANY_SPEC, HBM_SPEC],
+        out_specs=[HBM_SPEC, HBM_SPEC],
+        input_output_aliases={4: 1},
+        scratch_shapes=[VMEM((width, hid), F32), DMA(()), DMA(())],
+        compiler_params=pltpu.CompilerParams(vmem_limit_bytes=16 * MIB),
+        cost_estimate=pl.CostEstimate(flops=4_000_000_000, bytes_accessed=8 * MIB, transcendentals=0),
+    )(n, du, zero, order, table_g)
+
+
+def grads2_kernel(h, d_full, y_a, y_sib, zero, table_in, dw2, y_own, y_far, table_g, dw2_v, s_zero, s_w):
+    rows = y_own.shape[0]
+    hid = h.shape[1]
+    fill_start(zero, table_g, s_zero, 4)
+    for k, out in enumerate((y_own, y_far)):
+        at = pl.ds(k * rows, rows)
+        out[...] = y_a[at, :] + y_sib[at, :]
     h_t = h[...].T
     for j in range(hid // TILE):
         at = slice(j * TILE, (j + 1) * TILE)
         dw2_v[at, :] = mm(h_t[at, :], d_full[...], 1, 0)
         pltpu.make_async_copy(dw2_v.at[pl.ds(j * TILE, TILE)], dw2.at[pl.ds(j * TILE, TILE)], s_w).start()
-    pltpu.make_async_copy(dw1_v, dw1, s_w).wait()
     pltpu.make_async_copy(dw2_v, dw2, s_w).wait()
-    fill_wait(zero, table_g, s_zero, 3)
-
-
-def grads(n, h, du, d_full, zero, order, table_g):
-    _, width = n.shape
-    hid = h.shape[1]
-    return pl.pallas_call(
-        grads_kernel,
-        name="grads",
-        out_shape=[sh((8, 128), F32), sh((width, hid), F32), sh((hid, width), F32), sh(table_g.shape, F32)],
-        in_specs=[VMEM_SPEC] * 5 + [ANY_SPEC, HBM_SPEC],
-        out_specs=[VMEM_SPEC, HBM_SPEC, HBM_SPEC, HBM_SPEC],
-        input_output_aliases={6: 3},
-        scratch_shapes=[VMEM((width, hid), F32), VMEM((hid, width), F32), DMA(()), DMA(())],
-        compiler_params=pltpu.CompilerParams(vmem_limit_bytes=24 * MIB),
-        cost_estimate=pl.CostEstimate(flops=8_000_000_000, bytes_accessed=20 * MIB, transcendentals=0),
-    )(n, h, du, d_full, zero, order, table_g)
+    fill_wait(zero, table_g, s_zero, 4)
+
+
+def grads2(h, d_full, y_a, y_sib, zero, table_g):
+    hid, width = h.shape[1], d_full.shape[1]
+    rows = y_a.shape[0] // 2
+    return pl.pallas_call(
+        grads2_kernel,
+        name="grads2",
+        out_shape=[sh((hid, width), F32)] + [sh((rows, width), F32)] * 2 + [sh(table_g.shape, F32)],
+        in_specs=[VMEM_SPEC] * 5 + [HBM_SPEC],
+        out_specs=[HBM_SPEC, VMEM_SPEC, VMEM_SPEC, HBM_SPEC],
+        input_output_aliases={5: 3},
+        scratch_shapes=[VMEM((hid, width), F32), DMA(()), DMA(())],
+        compiler_params=pltpu.CompilerParams(vmem_limit_bytes=16 * MIB),
+        cost_estimate=pl.CostEstimate(flops=4_000_000_000, bytes_accessed=8 * MIB, transcendentals=0),
+    )(h, d_full, y_a, y_sib, zero, table_g)
 
 
 def dx_kernel(dn_own, g2, x_own, d_own, gain, order, dx):
@@ -410,9 +407,9 @@
 
 
 def fill3_kernel(zero, order, table_in, token, table_g, s_zero):
-    fill_start(zero, table_g, s_zero, 4)
+    fill_start(zero, table_g, s_zero, 5)
     token[...] = jnp.zeros_like(token)
-    fill_wait(zero, table_g, s_zero, 4)
+    fill_wait(zero, table_g, s_zero, 5)
 
 
 def fill3(zero, order, table_g):
@@ -508,51 +505,48 @@
     )(puts, same, dx, table_g)
 
 
-def finish_kernel(x, y, y_in0, y_in1, order, out):
-    for first, y_in in ((0, y_in0), (Y_FIRST, y_in1)):
-        at = pl.ds(first, y_in.shape[0])
-        out[at, :] = (x[at, :].astype(F32) + (y[at, :] + y_in[...])).astype(BF)
-
-
-def finish(x, y, y_in0, y_in1, order):
+def finish_kernel(x, y, y_in, order, out):
+    out[...] = (x[pl.ds(0, out.shape[0]), :].astype(F32) + (y[...] + y_in[...])).astype(BF)
+
+
+def finish(x, y, y_in, order):
     return pl.pallas_call(
         finish_kernel,
         name="finish",
         out_shape=sh(y.shape, BF),
-        in_specs=[VMEM_SPEC] * 4 + [ANY_SPEC],
+        in_specs=[VMEM_SPEC] * 3 + [ANY_SPEC],
         out_specs=VMEM_SPEC,
         compiler_params=pltpu.CompilerParams(vmem_limit_bytes=4 * MIB),
         cost_estimate=pl.CostEstimate(flops=1_000_000_000, bytes_accessed=MIB, transcendentals=0),
-    )(x, y, y_in0, y_in1, order)
+    )(x, y, y_in, order)
 
 
 def solution(mesh):
     tp = mesh.shape["tp"]
-    far_pairs = [(i, i ^ 2) for i in range(tp)]
-
-    def far_permute(x):
-        return lax.ppermute(x, "tp", far_pairs)
+
+    def permute(x, hop):
+        return lax.ppermute(x, "tp", [(i, i ^ hop) for i in range(tp)])
 
     def shard_step(ids, table, gain, w1, w2, d_out):
         part, rows_mine, same, zero, d_table = lookup(ids, table)
         send, w1 = pair(part, d_out, w1)
-        got = lax.ppermute(send, "tp", far_pairs)
+        got = permute(send, 2)
         puts, w2, d_table = fill1(rows_mine, zero, w2, send, d_table)
         x_f, d_full, n_a, h_a, du_a = share(send, got, w1, w2, gain)
         n, h, du, dn_p, d_table = mlp(x_f, d_full, n_a, h_a, du_a, w1, w2, gain, zero, d_table)
-        dn_own, dn_far, y_p = sums(dn_p, du, h, w1, w2)
-        g2 = far_permute(dn_far)
-        y_own, y_far0, y_far1 = ysum(y_p, dn_own)
-        y_in0 = lax.ppermute(y_far0, "tp", far_pairs)
-        token, d_w1, d_w2, d_table = grads(n, h, du, d_full, zero, y_own, d_table)
-        dx = dx_rows(dn_own, g2, x_f, d_out, gain, token)
-        dx_far = far_permute(dx)
-        dx, y_far1 = lax.optimization_barrier((dx, y_far1))
-        y_in1 = far_permute(y_far1)
+        dn_own, dn_far, y_a, y_b = sums(dn_p, du, h, w1, w2)
+        g2 = permute(dn_far, 2)
+        y_sib = permute(y_b, 1)
+        d_w1, d_table = grads1(n, du, zero, dn_own, d_table)
+        d_w2, y_own, y_far, d_table = grads2(h, d_full, y_a, y_sib, zero, d_table)
+        dx = dx_rows(dn_own, g2, x_f, d_out, gain, y_own)
+        dx_far = permute(dx, 2)
+        dx, y_far = lax.optimization_barrier((dx, y_far))
+        y_in = permute(y_far, 2)
         token, d_table = fill3(zero, dx, d_table)
         dx_full = dx_all(dx, dx_far, token)
         d_table, done = put_rows(puts, same, dx_full, d_table)
-        out = finish(x_f, y_own, y_in0, y_in1, done)
+        out = finish(x_f, y_own, y_in, done)
         return out, d_table, d_w1, d_w2
 
     return jax.shard_map(

time: 49 us -> 45.8 us (0.935)
  waiting for transfers between devices: 3.84 us -> 2.66 us
  Pallas kernels: 37 us -> 36 us
  starting transfers between devices: 7.06 us -> 6.2 us
    ppermute x5, waiting for transfers between devices: 3.84 us -> 2.66 us  [permute(): return lax.ppermute(x, 'tp', [(i, i ^ hop) for i in range(tp)])]
    ppermute x5, starting transfers between devices: 7.06 us -> 6.2 us  [permute(): return lax.ppermute(x, 'tp', [(i, i ^ hop) for i in range(tp)])]
    pallas_call x1, Pallas kernels: 3.7 us -> 3 us  [fill3(): pl.pallas_call(fill3_kernel, name='fill3', out_shape=[sh((8, 128), F32),...]
    pallas_call x1, Pallas kernels: 4.07 us -> 3.53 us  [lookup(): pl.pallas_call(lookup_kernel, name='lookup', out_shape=[sh((tokens, width...]
  transfers between devices with their start and end apart: 5 -> 5, of which waited for: 2 -> 3; matrix products, arithmetic and copies ran while one was open for 0% -> 0% of each run, Pallas kernels for 45% -> 51%
where the time goes in v8:
time: 45.8 us; the launch traced here: 45.6 us
  Pallas kernels  36 us (79%)
  starting transfers between devices  6.2 us (14%)
  waiting for transfers between devices  2.66 us (6%)
  between operations  0.76 us (2%)
    pallas_call x1, Pallas kernels, fill1(): pl.pallas_call(fill1_kernel, name='fill1', out_shape=[sh((2 * tokens,), I...  10 us
    ppermute x5, starting transfers between devices, permute(): return lax.ppermute(x, 'tp', [(i, i ^ hop) for i in range(tp)])  6.2 us
    pallas_call x1, Pallas kernels, grads1(): pl.pallas_call(grads1_kernel, name='grads1', out_shape=[sh((width, hid),...  3.58 us
    pallas_call x1, Pallas kernels, lookup(): pl.pallas_call(lookup_kernel, name='lookup', out_shape=[sh((tokens, width...  3.53 us
    pallas_call x1, Pallas kernels, grads2(): pl.pallas_call(grads2_kernel, name='grads2', out_shape=[sh((hid, width),...  3.15 us
    pallas_call x1, Pallas kernels, fill3(): pl.pallas_call(fill3_kernel, name='fill3', out_shape=[sh((8, 128), F32),...  3 us
    ppermute x5, waiting for transfers between devices, permute(): return lax.ppermute(x, 'tp', [(i, i ^ hop) for i in range(tp)])  2.66 us
    pallas_call x1, Pallas kernels, mlp(): pl.pallas_call(mlp_kernel, name='mlp', out_shape=[sh((tokens, width), BF)...  2.18 us
  transfers between devices with their start and end apart: 5, of which 3 were waited for; matrix products, arithmetic and copies ran while one was open for 0% of the time, Pallas kernels for 51%

profile of v8, /device:TPU:0, one launch (start us, length us, event | category | flops | bytes accessed | tf_op | source)
XLA Modules:
  0.0 45.6 jit_solution(9916113942624398631)
XLA Ops:
  0.6 0.0 copy-start
  0.6 3.5 %lookup.1 = (bf16[256,1024]{1,0:T(8,128)(2,1)S(1)}, s32[1,256]{1,0:T(1,128)S(1)}, bf16[256,256]{1,0:T(8,128)(2,1)S(1)}, f32[96,1024]{1,0:T(8,128)S(1)}, f32[12576,1024]{1,0:T(8,128)}) custom-call(s32[256]{0:T(256)} %ids.1, s32[1,256]{1,0:T(1,128)} %bitcast.1, bf16[12576,1024]{1,0:T(8,128)(2,1)} %table.1), custom_call_target="tpu_custom_call" | custom-call | flops 5000000000 | bytes 10485760 | tf_op jit(solution)/shard_map/lookup/pallas_call | solution.py:119
  4.2 2.1 %pair.1 = (bf16[192,1024]{1,0:T(8,128)(2,1)S(1)}, bf16[1024,1024]{1,0:T(8,128)(2,1)S(1)}) custom-call(bf16[256,1024]{1,0:T(8,128)(2,1)S(1)} %get-tuple-element.40.part, bf16[64,1024]{1,0:T(8,128)(2,1)} %d_own.1, bf16[1024,1024]{1,0:T(8,128)(2,1)} %w1.1), custom_call_target="tpu_custom_call" | custom-call | flops 3000000000 | bytes 1048576 | tf_op jit(solution)/shard_map/pair/pallas_call | solution.py:153
  6.3 3.0 %collective-permute-start = (bf16[192,1024]{1,0:T(8,128)(2,1)S(1)}, bf16[192,1024]{1,0:T(8,128)(2,1)S(1)}, u32[]{:S(2)}, u32[]{:S(2)}) collective-permute-start(bf16[192,1024]{1,0:T(8,128)(2,1)S(1)} %get-tuple-element.41.order.send), channel_id=1, source_target_pairs={{0,2},{1,3},{2,0},{3,1},{4,6},{5,7},{6,4},{7,5}} | collective-permute-start | bytes 1179656 | tf_op jit(solution)/shard_map/ppermute | solution.py:528
  9.2 10.0 %fill1.1 = (s32[512]{0:T(512)S(1)}, bf16[1024,1024]{1,0:T(8,128)(2,1)S(1)}, f32[12576,1024]{1,0:T(8,128)}) custom-call(s32[1,256]{1,0:T(1,128)S(1)} %get-tuple-element.43.rows_mine, f32[96,1024]{1,0:T(8,128)S(1)} %get-tuple-element.44.zero, bf16[1024,1024]{1,0:T(8,128)(2,1)} %w2.1, ...), custom_call_target="tpu_custom_call", output_to_operand_aliasing={{2}: (4, {})} | custom-call | flops 8999999488 | bytes 20971520 | tf_op jit(solution)/shard_map/fill1/pallas_call | solution.py:189
  19.2 0.0 collective-permute-done.got
  19.2 0.0 copy-done
  19.3 2.0 %share.1 = (bf16[256,1024]{1,0:T(8,128)(2,1)S(1)}, bf16[256,1024]{1,0:T(8,128)(2,1)S(1)}, bf16[128,1024]{1,0:T(8,128)(2,1)S(1)}, bf16[128,1024]{1,0:T(8,128)(2,1)S(1)}, bf16[128,1024]{1,0:T(8,128)(2,1)S(1)}) custom-call(bf16[192,1024]{1,0:T(8,128)(2,1)S(1)} %get-tuple-element.41.order.send, bf16[192,1024]{1,0:T(8,128)(2,1)S(1)} %collective-permute-done.got, ...), custom_call_target="tpu_custom_call" | custom-call | flops 3000000000 | bytes 1048576 | tf_op jit(solution)/shard_map/share/pallas_call | solution.py:248
  21.3 2.2 %mlp.1 = (bf16[256,1024]{1,0:T(8,128)(2,1)S(1)}, bf16[256,1024]{1,0:T(8,128)(2,1)S(1)}, bf16[256,1024]{1,0:T(8,128)(2,1)S(1)}, f32[128,1024]{1,0:T(8,128)S(1)}, f32[12576,1024]{1,0:T(8,128)}) custom-call(bf16[256,1024]{1,0:T(8,128)(2,1)S(1)} %get-tuple-element.47.x_f.x_own.x, ...), custom_call_target="tpu_custom_call", output_to_operand_aliasing={{4}: (9, {})} | custom-call | flops 6000000000 | bytes 4194304 | tf_op jit(solution)/shard_map/mlp/pallas_call | solution.py:276
  23.5 2.0 %sums.1 = (f32[64,1024]{1,0:T(8,128)S(1)}, f32[64,1024]{1,0:T(8,128)S(1)}, f32[128,1024]{1,0:T(8,128)S(1)}, f32[128,1024]{1,0:T(8,128)S(1)}) custom-call(f32[128,1024]{1,0:T(8,128)S(1)} %get-tuple-element.54.dn_p, bf16[256,1024]{1,0:T(8,128)(2,1)S(1)} %get-tuple-element.55.du, bf16[256,1024]{1,0:T(8,128)(2,1)S(1)} %get-tuple-element.53.h, ...), custom_call_target="tpu_custom_call" | custom-call | flops 4000000000 | bytes 4194304 | tf_op jit(solution)/shard_map/sums/pallas_call | solution.py:314
  25.5 0.2 collective-permute-start.1
  25.6 1.0 %collective-permute-start.2 = (f32[64,1024]{1,0:T(8,128)S(1)}, f32[64,1024]{1,0:T(8,128)S(1)}, u32[]{:S(2)}, u32[]{:S(2)}) collective-permute-start(f32[64,1024]{1,0:T(8,128)S(1)} %get-tuple-element.63), channel_id=1, source_target_pairs={{0,2},{1,3},{2,0},{3,1},{4,6},{5,7},{6,4},{7,5}} | collective-permute-start | bytes 786440 | tf_op jit(solution)/shard_map/ppermute | solution.py:528
  26.6 0.0 copy-start.1
  26.6 3.6 %grads1.1 = (f32[1024,1024]{1,0:T(8,128)}, f32[12576,1024]{1,0:T(8,128)}) custom-call(bf16[256,1024]{1,0:T(8,128)(2,1)S(1)} %get-tuple-element.58.n, bf16[256,1024]{1,0:T(8,128)(2,1)S(1)} %get-tuple-element.55.du, f32[96,1024]{1,0:T(8,128)S(1)} %get-tuple-element.44.zero, ...), custom_call_target="tpu_custom_call", output_to_operand_aliasing={{1}: (4, {})} | custom-call | flops 4000000000 | bytes 8388608 | tf_op jit(solution)/shard_map/grads1/pallas_call | solution.py:341
  30.2 0.0 collective-permute-done.1.y_sib
  30.2 3.1 %grads2.1 = (f32[1024,1024]{1,0:T(8,128)}, f32[64,1024]{1,0:T(8,128)S(1)}, f32[64,1024]{1,0:T(8,128)S(1)}, f32[12576,1024]{1,0:T(8,128)}) custom-call(bf16[256,1024]{1,0:T(8,128)(2,1)S(1)} %get-tuple-element.53.h, bf16[256,1024]{1,0:T(8,128)(2,1)S(1)} %get-tuple-element.48.d_full, ...), custom_call_target="tpu_custom_call", output_to_operand_aliasing={{3}: (5, {})} | custom-call | flops 4000000000 | bytes 8388608 | tf_op jit(solution)/shard_map/grads2/pallas_call | solution.py:373
  33.4 0.8 %collective-permute-done.2.g2 = f32[64,1024]{1,0:T(8,128)S(1)} collective-permute-done((f32[64,1024]{1,0:T(8,128)S(1)}, f32[64,1024]{1,0:T(8,128)S(1)}, u32[]{:S(2)}, u32[]{:S(2)}) %collective-permute-start.2) | collective-permute-done | bytes 262176 | tf_op jit(solution)/shard_map/ppermute | solution.py:528
  34.2 0.0 copy-done.1
  34.2 0.2 dx_rows.1.order.dx
  34.4 1.0 %collective-permute-start.4 = (bf16[64,1024]{1,0:T(8,128)(2,1)S(1)}, bf16[64,1024]{1,0:T(8,128)(2,1)S(1)}, u32[]{:S(2)}, u32[]{:S(2)}) collective-permute-start(bf16[64,1024]{1,0:T(8,128)(2,1)S(1)} %dx_rows.1.order.dx), channel_id=1, source_target_pairs={{0,2},{1,3},{2,0},{3,1},{4,6},{5,7},{6,4},{7,5}} | collective-permute-start | bytes 393224 | tf_op jit(solution)/shard_map/ppermute | solution.py:528
  35.4 1.0 %collective-permute-start.3 = (f32[64,1024]{1,0:T(8,128)S(1)}, f32[64,1024]{1,0:T(8,128)S(1)}, u32[]{:S(2)}, u32[]{:S(2)}) collective-permute-start(f32[64,1024]{1,0:T(8,128)S(1)} %get-tuple-element.65), channel_id=1, source_target_pairs={{0,2},{1,3},{2,0},{3,1},{4,6},{5,7},{6,4},{7,5}} | collective-permute-start | bytes 786440 | tf_op jit(solution)/shard_map/ppermute | solution.py:528
  36.4 3.0 %fill3.1 = (f32[8,128]{1,0:T(8,128)S(1)}, f32[12576,1024]{1,0:T(8,128)}) custom-call(f32[96,1024]{1,0:T(8,128)S(1)} %get-tuple-element.44.zero, bf16[64,1024]{1,0:T(8,128)(2,1)S(1)} %dx_rows.1.order.dx, f32[12576,1024]{1,0:T(8,128)} %get-tuple-element.69.table_in), custom_call_target="tpu_custom_call", output_to_operand_aliasing={{1}: (2, {})} | custom-call | flops 4000000000 | bytes 16777216 | tf_op jit(solution)/shard_map/fill3/pallas_call | solution.py:416
  39.4 1.3 %collective-permute-done.4.dx_far = bf16[64,1024]{1,0:T(8,128)(2,1)S(1)} collective-permute-done((bf16[64,1024]{1,0:T(8,128)(2,1)S(1)}, bf16[64,1024]{1,0:T(8,128)(2,1)S(1)}, u32[]{:S(2)}, u32[]{:S(2)}) %collective-permute-start.4) | collective-permute-done | bytes 131104 | tf_op jit(solution)/shard_map/ppermute | solution.py:528
  40.8 1.6 %dx_all.1.dx = bf16[256,1024]{1,0:T(8,128)(2,1)S(1)} custom-call(bf16[64,1024]{1,0:T(8,128)(2,1)S(1)} %dx_rows.1.order.dx, bf16[64,1024]{1,0:T(8,128)(2,1)S(1)} %collective-permute-done.4.dx_far, f32[8,128]{1,0:T(8,128)S(1)} %get-tuple-element.70.order), custom_call_target="tpu_custom_call" | custom-call | flops 2000000000 | bytes 1048576 | tf_op jit(solution)/shard_map/dx_all/pallas_call | solution.py:446
  42.4 2.1 %put_rows.1 = (f32[12576,1024]{1,0:T(8,128)}, f32[8,128]{1,0:T(8,128)S(1)}) custom-call(s32[512]{0:T(512)S(1)} %get-tuple-element.66.puts, bf16[256,256]{1,0:T(8,128)(2,1)S(1)} %get-tuple-element.67.same, bf16[256,1024]{1,0:T(8,128)(2,1)S(1)} %dx_all.1.dx, f32[12576,1024]{1,0:T(8,128)} %get-tuple-element.71.table_in), custom_call_target="tpu_custom_call", output_to_operand_aliasing={{0}: (3, {})} | custom-call | flops 3000000000 | bytes 2097152 | tf_op jit(solution)/shard_map/put_rows/pallas_call | solution.py:495
  44.4 0.5 %collective-permute-done.3.y_in = f32[64,1024]{1,0:T(8,128)S(1)} collective-permute-done((f32[64,1024]{1,0:T(8,128)S(1)}, f32[64,1024]{1,0:T(8,128)S(1)}, u32[]{:S(2)}, u32[]{:S(2)}) %collective-permute-start.3) | collective-permute-done | bytes 262176 | tf_op jit(solution)/shard_map/ppermute | solution.py:528
  44.9 0.7 %finish.1 = bf16[64,1024]{1,0:T(8,128)(2,1)} custom-call(bf16[256,1024]{1,0:T(8,128)(2,1)S(1)} %get-tuple-element.47.x_f.x_own.x, f32[64,1024]{1,0:T(8,128)S(1)} %get-tuple-element.62.order.y, f32[64,1024]{1,0:T(8,128)S(1)} %collective-permute-done.3.y_in, f32[8,128]{1,0:T(8,128)S(1)} %get-tuple-element.72.order), custom_call_target="tpu_custom_call" | custom-call | flops 1000000000 | bytes 1048576 | tf_op jit(solution)/shard_map/finish/pallas_call | solution.py:513
Async XLA Ops:
  0.6 18.6 %copy-start = (bf16[1024]{0:T(1024)(128)(2,1)S(1)}, bf16[1024]{0:T(1024)(128)(2,1)}, u32[]{:S(2)}) copy-start(bf16[1024]{0:T(1024)(128)(2,1)} %gain.5) | copy-start | bytes 6148
  6.3 13.0 %collective-permute-start = (bf16[192,1024]{1,0:T(8,128)(2,1)S(1)}, bf16[192,1024]{1,0:T(8,128)(2,1)S(1)}, u32[]{:S(2)}, u32[]{:S(2)}) collective-permute-start(bf16[192,1024]{1,0:T(8,128)(2,1)S(1)} %get-tuple-element.41.order.send), channel_id=1, source_target_pairs={{0,2},{1,3},{2,0},{3,1},{4,6},{5,7},{6,4},{7,5}} | collective-permute-start | bytes 1179656 | tf_op jit(solution)/shard_map/ppermute | solution.py:528
  25.5 4.8 %collective-permute-start.1 = (f32[128,1024]{1,0:T(8,128)S(1)}, f32[128,1024]{1,0:T(8,128)S(1)}, u32[]{:S(2)}, u32[]{:S(2)}) collective-permute-start(f32[128,1024]{1,0:T(8,128)S(1)} %get-tuple-element.57), channel_id=1, source_target_pairs={{0,1},{1,0},{2,3},{3,2},{4,5},{5,4},{6,7},{7,6}} | collective-permute-start | bytes 1572872 | tf_op jit(solution)/shard_map/ppermute | solution.py:528
  25.6 8.6 %collective-permute-start.2 = (f32[64,1024]{1,0:T(8,128)S(1)}, f32[64,1024]{1,0:T(8,128)S(1)}, u32[]{:S(2)}, u32[]{:S(2)}) collective-permute-start(f32[64,1024]{1,0:T(8,128)S(1)} %get-tuple-element.63), channel_id=1, source_target_pairs={{0,2},{1,3},{2,0},{3,1},{4,6},{5,7},{6,4},{7,5}} | collective-permute-start | bytes 786440 | tf_op jit(solution)/shard_map/ppermute | solution.py:528
  26.6 7.6 %copy-start.1 = (bf16[64,1024]{1,0:T(8,128)(2,1)S(1)}, bf16[64,1024]{1,0:T(8,128)(2,1)}, u32[]{:S(2)}) copy-start(bf16[64,1024]{1,0:T(8,128)(2,1)} %d_own.1) | copy-start | bytes 393220
  34.4 6.4 %collective-permute-start.4 = (bf16[64,1024]{1,0:T(8,128)(2,1)S(1)}, bf16[64,1024]{1,0:T(8,128)(2,1)S(1)}, u32[]{:S(2)}, u32[]{:S(2)}) collective-permute-start(bf16[64,1024]{1,0:T(8,128)(2,1)S(1)} %dx_rows.1.order.dx), channel_id=1, source_target_pairs={{0,2},{1,3},{2,0},{3,1},{4,6},{5,7},{6,4},{7,5}} | collective-permute-start | bytes 393224 | tf_op jit(solution)/shard_map/ppermute | solution.py:528
  35.4 9.5 %collective-permute-start.3 = (f32[64,1024]{1,0:T(8,128)S(1)}, f32[64,1024]{1,0:T(8,128)S(1)}, u32[]{:S(2)}, u32[]{:S(2)}) collective-permute-start(f32[64,1024]{1,0:T(8,128)S(1)} %get-tuple-element.65), channel_id=1, source_target_pairs={{0,2},{1,3},{2,0},{3,1},{4,6},{5,7},{6,4},{7,5}} | collective-permute-start | bytes 786440 | tf_op jit(solution)/shard_map/ppermute | solution.py:528

commit v9 on v8

--- a/solution.py
+++ b/solution.py
@@ -19,7 +19,8 @@
 DMA = pltpu.SemaphoreType.DMA
 TILE = 256
 ZERO_ROWS = 96
-FILL_AT = (0, 4, 81, 93, 103, 112, 131)
+FILL_AT = (0, 4, 69, 82, 93, 102, 131)
+LATE_FILL = 8
 MIB = 1 << 20
 LOOKUP_VMEM = 48 * MIB
 PAIR_VMEM = 8 * MIB
@@ -39,6 +40,13 @@
 
 def fill_copy(zero, table_g, sem, i):
     return pltpu.make_async_copy(zero, table_g.at[pl.ds(pl.multiple_of(i * ZERO_ROWS, ZERO_ROWS), ZERO_ROWS)], sem)
+
+
+def fill_range(part):
+    late = (lax.axis_index("tp") >> 1) * LATE_FILL
+    if part == "late":
+        return FILL_AT[2] - late, FILL_AT[2]
+    return FILL_AT[part], FILL_AT[part + 1] - (late if part == 1 else 0)
 
 
 def fill_start(zero, table_g, sem, part):
@@ -46,7 +54,7 @@
         fill_copy(zero, table_g, sem, i).start()
         return carry
 
-    lax.fori_loop(FILL_AT[part], FILL_AT[part + 1], body, 0)
+    lax.fori_loop(*fill_range(part), body, 0)
 
 
 def fill_wait(zero, table_g, sem, part):
@@ -54,7 +62,7 @@
         fill_copy(zero, table_g, sem, i).wait()
         return carry
 
-    lax.fori_loop(FILL_AT[part], FILL_AT[part + 1], body, 0)
+    lax.fori_loop(*fill_range(part), body, 0)
 
 
 def swap_with_sibling():
@@ -128,13 +136,12 @@
     )(in_hbm(ids), in_hbm(ids.reshape(1, tokens)), in_hbm(table))
 
 
-def pair_kernel(part, d_out, w1, send, w1_v, part_r, sems, s_in):
+def pair_kernel(part, w1, send, w1_v, part_r, sems, s_in):
     me = lax.axis_index("tp")
-    rows = d_out.shape[0]
+    rows = part.shape[0] // 4
     blocks = (me, me ^ 2, me ^ 1, me ^ 3)
-    loads = [pltpu.make_async_copy(d_out, send.at[pl.ds(2 * rows, rows)], s_in.at[0]), pltpu.make_async_copy(w1, w1_v, s_in.at[1])]
-    for c in loads:
-        c.start()
+    load = pltpu.make_async_copy(w1, w1_v, s_in)
+    load.start()
     remote = swap_with_sibling()
     block = lambda k: pl.ds(pl.multiple_of(blocks[k] * rows, rows), rows)
     copies = [remote(part.at[block(2 + k)], part_r.at[pl.ds(k * rows, rows)], sems, k) for k in range(2)]
@@ -144,22 +151,21 @@
         copies[k].wait()
         at = pl.ds(k * rows, rows)
         send[at, :] = part[block(k), :] + part_r[at, :]
-    for c in loads:
-        c.wait()
-
-
-def pair(part, d_out, w1):
-    rows, width = d_out.shape
+    load.wait()
+
+
+def pair(part, w1):
+    rows, width = part.shape[0] // 4, part.shape[1]
     return pl.pallas_call(
         pair_kernel,
         name="pair",
-        out_shape=[sh((3 * rows, width), BF), sh(w1.shape, BF)],
-        in_specs=[VMEM_SPEC, HBM_SPEC, HBM_SPEC],
+        out_shape=[sh((2 * rows, width), BF), sh(w1.shape, BF)],
+        in_specs=[VMEM_SPEC, HBM_SPEC],
         out_specs=[VMEM_SPEC] * 2,
-        scratch_shapes=[VMEM((2 * rows, width), BF), DMA((2, 2)), DMA((2,))],
+        scratch_shapes=[VMEM((2 * rows, width), BF), DMA((2, 2)), DMA(())],
         compiler_params=pltpu.CompilerParams(collective_id=0, has_side_effects=True, vmem_limit_bytes=PAIR_VMEM),
         cost_estimate=pl.CostEstimate(flops=3_000_000_000, bytes_accessed=MIB, transcendentals=0),
-    )(part, in_hbm(d_out), in_hbm(w1))
+    )(part, in_hbm(w1))
 
 
 def fill1_kernel(rows_mine, zero, w2, order, table_in, puts, w2_v, table_g, mine_s, puts_s, s_zero, s_list, s_w):
@@ -219,8 +225,8 @@
         du[rows, cols] = (g * (cdf + u * (0.5 * (1.0 - t * t)) * (GELU_C * (1.0 + 3.0 * GELU_A * (u * u))))).astype(BF)
 
 
-def share_kernel(send, got, w1, w2, gain, x_f, d_full, n_a, h_a, du_a, x_r, d_r, sems):
-    rows = send.shape[0] // 3
+def share_kernel(send, got, d_own, d_far, w1, w2, gain, x_f, d_full, n_a, h_a, du_a, x_r, d_r, sems):
+    rows = d_own.shape[0]
     half = 2 * rows
     remote = swap_with_sibling()
     copies = []
@@ -229,10 +235,10 @@
         x_f[at, :] = send[at, :] + got[other, :]
         copies.append(remote(x_f.at[at], x_r.at[at], sems, k))
         copies[-1].start()
-    for k, src in enumerate((send, got)):
-        copies.append(remote(src.at[pl.ds(half, rows)], d_r.at[pl.ds(k * rows, rows)], sems, 2 + k))
+    for k, src in enumerate((d_own, d_far)):
+        copies.append(remote(src, d_r.at[pl.ds(k * rows, rows)], sems, 2 + k))
         copies[-1].start()
-        d_full[pl.ds(k * rows, rows), :] = src[pl.ds(half, rows), :]
+        d_full[pl.ds(k * rows, rows), :] = src[...]
     mlp_half(x_f, d_full, n_a, h_a, du_a, (0, half), w1, w2, gain)
     for k in range(2):
         copies[k].wait()
@@ -242,19 +248,19 @@
         d_full[pl.ds(half + k * rows, rows), :] = d_r[pl.ds(k * rows, rows), :]
 
 
-def share(send, got, w1, w2, gain):
-    rows, width = send.shape[0] // 3, send.shape[1]
+def share(send, got, d_own, d_far, w1, w2, gain):
+    rows, width = d_own.shape
     hid = w1.shape[1]
     return pl.pallas_call(
         share_kernel,
         name="share",
         out_shape=[sh((4 * rows, width), BF)] * 2 + [sh((2 * rows, width), BF)] + [sh((2 * rows, hid), BF)] * 2,
-        in_specs=[VMEM_SPEC] * 5,
+        in_specs=[VMEM_SPEC] * 7,
         out_specs=[VMEM_SPEC] * 5,
         scratch_shapes=[VMEM((2 * rows, width), BF), VMEM((2 * rows, width), BF), DMA((2, 4))],
         compiler_params=pltpu.CompilerParams(collective_id=1, has_side_effects=True, vmem_limit_bytes=16 * MIB),
         cost_estimate=pl.CostEstimate(flops=3_000_000_000, bytes_accessed=MIB, transcendentals=0),
-    )(send, got, w1, w2, gain)
+    )(send, got, d_own, d_far, w1, w2, gain)
 
 
 def mlp_kernel(x_f, d_full, n_a, h_a, du_a, w1, w2, gain, zero, table_in, n, h, du, dn_p, table_g, s_zero):
@@ -455,13 +461,15 @@
     )(dx, dx_far, order)
 
 
-def put_kernel(puts, same, dx, table_in, table_g, token, puts_s, total, s_in, s_row):
+def put_kernel(puts, same, dx, zero, table_in, table_g, token, puts_s, total, s_in, s_row, s_zero):
+    fill_start(zero, table_g, s_zero, "late")
     tokens = dx.shape[0]
     load = pltpu.make_async_copy(puts, puts_s, s_in)
     load.start()
     total[...] = mm(same[...], dx[...], 1, 0)
     token[...] = jnp.zeros_like(token)
     load.wait()
+    fill_wait(zero, table_g, s_zero, "late")
     count = puts_s[tokens]
 
     def put(i):
@@ -491,18 +499,18 @@
     lax.fori_loop(0, count & 7, put_wait(1), 0)
 
 
-def put_rows(puts, same, dx, table_g):
+def put_rows(puts, same, dx, zero, table_g):
     return pl.pallas_call(
         put_kernel,
         name="put_rows",
         out_shape=[sh(table_g.shape, F32), sh((8, 128), F32)],
-        in_specs=[ANY_SPEC, VMEM_SPEC, VMEM_SPEC, HBM_SPEC],
+        in_specs=[ANY_SPEC, VMEM_SPEC, VMEM_SPEC, VMEM_SPEC, HBM_SPEC],
         out_specs=[HBM_SPEC, VMEM_SPEC],
-        input_output_aliases={3: 0},
-        scratch_shapes=[pltpu.SMEM(puts.shape, I32), VMEM(dx.shape, F32), DMA(()), DMA(())],
+        input_output_aliases={4: 0},
+        scratch_shapes=[pltpu.SMEM(puts.shape, I32), VMEM(dx.shape, F32), DMA(()), DMA(()), DMA(())],
         compiler_params=pltpu.CompilerParams(vmem_limit_bytes=4 * MIB),
         cost_estimate=pl.CostEstimate(flops=3_000_000_000, bytes_accessed=2 * MIB, transcendentals=0),
-    )(puts, same, dx, table_g)
+    )(puts, same, dx, zero, table_g)
 
 
 def finish_kernel(x, y, y_in, order, out):
@@ -528,11 +536,12 @@
         return lax.ppermute(x, "tp", [(i, i ^ hop) for i in range(tp)])
 
     def shard_step(ids, table, gain, w1, w2, d_out):
+        d_far = permute(d_out, 2)
         part, rows_mine, same, zero, d_table = lookup(ids, table)
-        send, w1 = pair(part, d_out, w1)
+        send, w1 = pair(part, w1)
         got = permute(send, 2)
         puts, w2, d_table = fill1(rows_mine, zero, w2, send, d_table)
-        x_f, d_full, n_a, h_a, du_a = share(send, got, w1, w2, gain)
+        x_f, d_full, n_a, h_a, du_a = share(send, got, d_out, d_far, w1, w2, gain)
         n, h, du, dn_p, d_table = mlp(x_f, d_full, n_a, h_a, du_a, w1, w2, gain, zero, d_table)
         dn_own, dn_far, y_a, y_b = sums(dn_p, du, h, w1, w2)
         g2 = permute(dn_far, 2)
@@ -545,7 +554,7 @@
         y_in = permute(y_far, 2)
         token, d_table = fill3(zero, dx, d_table)
         dx_full = dx_all(dx, dx_far, token)
-        d_table, done = put_rows(puts, same, dx_full, d_table)
+        d_table, done = put_rows(puts, same, dx_full, zero, d_table)
         out = finish(x_f, y_own, y_in, done)
         return out, d_table, d_w1, d_w2
 

time: 45.8 us -> 44.5 us (0.972)
  waiting for transfers between devices: 2.66 us -> 1.4 us
  Pallas kernels: 36 us -> 35.5 us
    pallas_call x1, Pallas kernels: 10 us -> 8.58 us  [fill1(): pl.pallas_call(fill1_kernel, name='fill1', out_shape=[sh((2 * tokens,), I...]
    ppermute x5 -> x6, waiting for transfers between devices: 2.66 us -> 1.4 us  [permute(): return lax.ppermute(x, 'tp', [(i, i ^ hop) for i in range(tp)])]
    pallas_call x1, Pallas kernels: 3 us -> 4.18 us  [fill3(): pl.pallas_call(fill3_kernel, name='fill3', out_shape=[sh((8, 128), F32),...]
    ppermute x5 -> x6, starting transfers between devices: 6.2 us -> 6.64 us  [permute(): return lax.ppermute(x, 'tp', [(i, i ^ hop) for i in range(tp)])]
  transfers between devices with their start and end apart: 5 -> 6, of which waited for: 3 -> 3; matrix products, arithmetic and copies ran while one was open for 0% -> 0% of each run, Pallas kernels for 51% -> 64%
where the time goes in v9:
time: 44.5 us; the launch traced here: 44.3 us
  Pallas kernels  35.5 us (80%)
  starting transfers between devices  6.64 us (15%)
  waiting for transfers between devices  1.4 us (3%)
  between operations  0.78 us (2%)
    pallas_call x1, Pallas kernels, fill1(): pl.pallas_call(fill1_kernel, name='fill1', out_shape=[sh((2 * tokens,), I...  8.58 us
    ppermute x6, starting transfers between devices, permute(): return lax.ppermute(x, 'tp', [(i, i ^ hop) for i in range(tp)])  6.64 us
    pallas_call x1, Pallas kernels, fill3(): pl.pallas_call(fill3_kernel, name='fill3', out_shape=[sh((8, 128), F32),...  4.18 us
    pallas_call x1, Pallas kernels, grads1(): pl.pallas_call(grads1_kernel, name='grads1', out_shape=[sh((width, hid),...  3.71 us
    pallas_call x1, Pallas kernels, lookup(): pl.pallas_call(lookup_kernel, name='lookup', out_shape=[sh((tokens, width...  3.39 us
    pallas_call x1, Pallas kernels, grads2(): pl.pallas_call(grads2_kernel, name='grads2', out_shape=[sh((hid, width),...  3.15 us
    pallas_call x1, Pallas kernels, mlp(): pl.pallas_call(mlp_kernel, name='mlp', out_shape=[sh((tokens, width), BF)...  2.3 us
    pallas_call x1, Pallas kernels, put_rows(): pl.pallas_call(put_kernel, name='put_rows', out_shape=[sh(table_g.shape,...  2.08 us
  transfers between devices with their start and end apart: 6, of which 3 were waited for; matrix products, arithmetic and copies ran while one was open for 0% of the time, Pallas kernels for 64%

profile of v9, /device:TPU:0, one launch (start us, length us, event | category | flops | bytes accessed | tf_op | source)
XLA Modules:
  0.0 44.3 jit_solution(6910963943987483981)
XLA Ops:
  0.6 0.0 copy-start.1
  0.6 0.0 copy-start
  0.7 3.3 %collective-permute-start.1 = (bf16[64,1024]{1,0:T(8,128)(2,1)}, bf16[64,1024]{1,0:T(8,128)(2,1)S(1)}, u32[]{:S(2)}, u32[]{:S(2)}) collective-permute-start(bf16[64,1024]{1,0:T(8,128)(2,1)} %d_own.3), channel_id=1, source_target_pairs={{0,2},{1,3},{2,0},{3,1},{4,6},{5,7},{6,4},{7,5}} | collective-permute-start | bytes 393224 | tf_op jit(solution)/shard_map/ppermute | solution.py:536
  4.0 3.4 %lookup.1 = (bf16[256,1024]{1,0:T(8,128)(2,1)S(1)}, s32[1,256]{1,0:T(1,128)S(1)}, bf16[256,256]{1,0:T(8,128)(2,1)S(1)}, f32[96,1024]{1,0:T(8,128)S(1)}, f32[12576,1024]{1,0:T(8,128)}) custom-call(s32[256]{0:T(256)} %ids.1, s32[1,256]{1,0:T(1,128)} %bitcast.1, bf16[12576,1024]{1,0:T(8,128)(2,1)} %table.1), custom_call_target="tpu_custom_call" | custom-call | flops 5000000000 | bytes 10485760 | tf_op jit(solution)/shard_map/lookup/pallas_call | solution.py:127
  7.4 1.6 %pair.1 = (bf16[128,1024]{1,0:T(8,128)(2,1)S(1)}, bf16[1024,1024]{1,0:T(8,128)(2,1)S(1)}) custom-call(bf16[256,1024]{1,0:T(8,128)(2,1)S(1)} %get-tuple-element.40.part, bf16[1024,1024]{1,0:T(8,128)(2,1)} %w1.1), custom_call_target="tpu_custom_call" | custom-call | flops 3000000000 | bytes 1048576 | tf_op jit(solution)/shard_map/pair/pallas_call | solution.py:159
  9.0 0.2 collective-permute-start
  9.2 8.6 %fill1.1 = (s32[512]{0:T(512)S(1)}, bf16[1024,1024]{1,0:T(8,128)(2,1)S(1)}, f32[12576,1024]{1,0:T(8,128)}) custom-call(s32[1,256]{1,0:T(1,128)S(1)} %get-tuple-element.43.rows_mine, f32[96,1024]{1,0:T(8,128)S(1)} %get-tuple-element.44.zero, bf16[1024,1024]{1,0:T(8,128)(2,1)} %w2.1, ...), custom_call_target="tpu_custom_call", output_to_operand_aliasing={{2}: (4, {})} | custom-call | flops 8999999488 | bytes 20971520 | tf_op jit(solution)/shard_map/fill1/pallas_call | solution.py:195
  17.8 0.0 collective-permute-done.1.d_far
  17.8 0.0 collective-permute-done.got
  17.8 0.0 copy-done.1
  17.8 0.0 copy-done
  17.8 2.0 %share.1 = (bf16[256,1024]{1,0:T(8,128)(2,1)S(1)}, bf16[256,1024]{1,0:T(8,128)(2,1)S(1)}, bf16[128,1024]{1,0:T(8,128)(2,1)S(1)}, bf16[128,1024]{1,0:T(8,128)(2,1)S(1)}, bf16[128,1024]{1,0:T(8,128)(2,1)S(1)}) custom-call(bf16[128,1024]{1,0:T(8,128)(2,1)S(1)} %get-tuple-element.41.order.send, bf16[128,1024]{1,0:T(8,128)(2,1)S(1)} %collective-permute-done.got, ...), custom_call_target="tpu_custom_call" | custom-call | flops 3000000000 | bytes 1048576 | tf_op jit(solution)/shard_map/share/pallas_call | solution.py:254
  19.8 2.3 %mlp.1 = (bf16[256,1024]{1,0:T(8,128)(2,1)S(1)}, bf16[256,1024]{1,0:T(8,128)(2,1)S(1)}, bf16[256,1024]{1,0:T(8,128)(2,1)S(1)}, f32[128,1024]{1,0:T(8,128)S(1)}, f32[12576,1024]{1,0:T(8,128)}) custom-call(bf16[256,1024]{1,0:T(8,128)(2,1)S(1)} %get-tuple-element.47.x_f.x_own.x, ...), custom_call_target="tpu_custom_call", output_to_operand_aliasing={{4}: (9, {})} | custom-call | flops 6000000000 | bytes 4194304 | tf_op jit(solution)/shard_map/mlp/pallas_call | solution.py:282
  22.1 2.0 %sums.1 = (f32[64,1024]{1,0:T(8,128)S(1)}, f32[64,1024]{1,0:T(8,128)S(1)}, f32[128,1024]{1,0:T(8,128)S(1)}, f32[128,1024]{1,0:T(8,128)S(1)}) custom-call(f32[128,1024]{1,0:T(8,128)S(1)} %get-tuple-element.54.dn_p, bf16[256,1024]{1,0:T(8,128)(2,1)S(1)} %get-tuple-element.55.du, bf16[256,1024]{1,0:T(8,128)(2,1)S(1)} %get-tuple-element.53.h, ...), custom_call_target="tpu_custom_call" | custom-call | flops 4000000000 | bytes 4194304 | tf_op jit(solution)/shard_map/sums/pallas_call | solution.py:320
  24.1 0.2 collective-permute-start.2
  24.3 0.9 %collective-permute-start.3 = (f32[64,1024]{1,0:T(8,128)S(1)}, f32[64,1024]{1,0:T(8,128)S(1)}, u32[]{:S(2)}, u32[]{:S(2)}) collective-permute-start(f32[64,1024]{1,0:T(8,128)S(1)} %get-tuple-element.63), channel_id=1, source_target_pairs={{0,2},{1,3},{2,0},{3,1},{4,6},{5,7},{6,4},{7,5}} | collective-permute-start | bytes 786440 | tf_op jit(solution)/shard_map/ppermute | solution.py:536
  25.3 3.7 %grads1.1 = (f32[1024,1024]{1,0:T(8,128)}, f32[12576,1024]{1,0:T(8,128)}) custom-call(bf16[256,1024]{1,0:T(8,128)(2,1)S(1)} %get-tuple-element.58.n, bf16[256,1024]{1,0:T(8,128)(2,1)S(1)} %get-tuple-element.55.du, f32[96,1024]{1,0:T(8,128)S(1)} %get-tuple-element.44.zero, ...), custom_call_target="tpu_custom_call", output_to_operand_aliasing={{1}: (4, {})} | custom-call | flops 4000000000 | bytes 8388608 | tf_op jit(solution)/shard_map/grads1/pallas_call | solution.py:347
  29.0 0.0 collective-permute-done.2.y_sib
  29.0 3.1 %grads2.1 = (f32[1024,1024]{1,0:T(8,128)}, f32[64,1024]{1,0:T(8,128)S(1)}, f32[64,1024]{1,0:T(8,128)S(1)}, f32[12576,1024]{1,0:T(8,128)}) custom-call(bf16[256,1024]{1,0:T(8,128)(2,1)S(1)} %get-tuple-element.53.h, bf16[256,1024]{1,0:T(8,128)(2,1)S(1)} %get-tuple-element.48.d_full, ...), custom_call_target="tpu_custom_call", output_to_operand_aliasing={{3}: (5, {})} | custom-call | flops 4000000000 | bytes 8388608 | tf_op jit(solution)/shard_map/grads2/pallas_call | solution.py:379
  32.1 0.8 %collective-permute-done.3.g2 = f32[64,1024]{1,0:T(8,128)S(1)} collective-permute-done((f32[64,1024]{1,0:T(8,128)S(1)}, f32[64,1024]{1,0:T(8,128)S(1)}, u32[]{:S(2)}, u32[]{:S(2)}) %collective-permute-start.3) | collective-permute-done | bytes 262176 | tf_op jit(solution)/shard_map/ppermute | solution.py:536
  32.9 0.2 dx_rows.1.order.dx
  33.1 1.0 %collective-permute-start.5 = (bf16[64,1024]{1,0:T(8,128)(2,1)S(1)}, bf16[64,1024]{1,0:T(8,128)(2,1)S(1)}, u32[]{:S(2)}, u32[]{:S(2)}) collective-permute-start(bf16[64,1024]{1,0:T(8,128)(2,1)S(1)} %dx_rows.1.order.dx), channel_id=1, source_target_pairs={{0,2},{1,3},{2,0},{3,1},{4,6},{5,7},{6,4},{7,5}} | collective-permute-start | bytes 393224 | tf_op jit(solution)/shard_map/ppermute | solution.py:536
  34.0 1.1 %collective-permute-start.4 = (f32[64,1024]{1,0:T(8,128)S(1)}, f32[64,1024]{1,0:T(8,128)S(1)}, u32[]{:S(2)}, u32[]{:S(2)}) collective-permute-start(f32[64,1024]{1,0:T(8,128)S(1)} %get-tuple-element.65), channel_id=1, source_target_pairs={{0,2},{1,3},{2,0},{3,1},{4,6},{5,7},{6,4},{7,5}} | collective-permute-start | bytes 786440 | tf_op jit(solution)/shard_map/ppermute | solution.py:536
  35.1 4.2 %fill3.1 = (f32[8,128]{1,0:T(8,128)S(1)}, f32[12576,1024]{1,0:T(8,128)}) custom-call(f32[96,1024]{1,0:T(8,128)S(1)} %get-tuple-element.44.zero, bf16[64,1024]{1,0:T(8,128)(2,1)S(1)} %dx_rows.1.order.dx, f32[12576,1024]{1,0:T(8,128)} %get-tuple-element.69.table_in), custom_call_target="tpu_custom_call", output_to_operand_aliasing={{1}: (2, {})} | custom-call | flops 4000000000 | bytes 16777216 | tf_op jit(solution)/shard_map/fill3/pallas_call | solution.py:422
  39.3 0.2 collective-permute-done.5.dx_far
  39.5 1.6 %dx_all.1.dx = bf16[256,1024]{1,0:T(8,128)(2,1)S(1)} custom-call(bf16[64,1024]{1,0:T(8,128)(2,1)S(1)} %dx_rows.1.order.dx, bf16[64,1024]{1,0:T(8,128)(2,1)S(1)} %collective-permute-done.5.dx_far, f32[8,128]{1,0:T(8,128)S(1)} %get-tuple-element.70.order), custom_call_target="tpu_custom_call" | custom-call | flops 2000000000 | bytes 1048576 | tf_op jit(solution)/shard_map/dx_all/pallas_call | solution.py:452
  41.0 2.1 %put_rows.1 = (f32[12576,1024]{1,0:T(8,128)}, f32[8,128]{1,0:T(8,128)S(1)}) custom-call(s32[512]{0:T(512)S(1)} %get-tuple-element.66.puts, bf16[256,256]{1,0:T(8,128)(2,1)S(1)} %get-tuple-element.67.same, bf16[256,1024]{1,0:T(8,128)(2,1)S(1)} %dx_all.1.dx, f32[96,1024]{1,0:T(8,128)S(1)} %get-tuple-element.44.zero, ...), custom_call_target="tpu_custom_call", output_to_operand_aliasing={{0}: (4, {})} | custom-call | flops 3000000000 | bytes 2097152 | tf_op jit(solution)/shard_map/put_rows/pallas_call | solution.py:503
  43.1 0.5 %collective-permute-done.4.y_in = f32[64,1024]{1,0:T(8,128)S(1)} collective-permute-done((f32[64,1024]{1,0:T(8,128)S(1)}, f32[64,1024]{1,0:T(8,128)S(1)}, u32[]{:S(2)}, u32[]{:S(2)}) %collective-permute-start.4) | collective-permute-done | bytes 262176 | tf_op jit(solution)/shard_map/ppermute | solution.py:536
  43.6 0.7 %finish.1 = bf16[64,1024]{1,0:T(8,128)(2,1)} custom-call(bf16[256,1024]{1,0:T(8,128)(2,1)S(1)} %get-tuple-element.47.x_f.x_own.x, f32[64,1024]{1,0:T(8,128)S(1)} %get-tuple-element.62.order.y, f32[64,1024]{1,0:T(8,128)S(1)} %collective-permute-done.4.y_in, f32[8,128]{1,0:T(8,128)S(1)} %get-tuple-element.72.order), custom_call_target="tpu_custom_call" | custom-call | flops 1000000000 | bytes 1048576 | tf_op jit(solution)/shard_map/finish/pallas_call | solution.py:521
Async XLA Ops:
  0.6 17.2 %copy-start.1 = (bf16[64,1024]{1,0:T(8,128)(2,1)S(1)}, bf16[64,1024]{1,0:T(8,128)(2,1)}, u32[]{:S(2)}) copy-start(bf16[64,1024]{1,0:T(8,128)(2,1)} %d_own.3) | copy-start | bytes 393220
  0.6 17.2 %copy-start = (bf16[1024]{0:T(1024)(128)(2,1)S(1)}, bf16[1024]{0:T(1024)(128)(2,1)}, u32[]{:S(2)}) copy-start(bf16[1024]{0:T(1024)(128)(2,1)} %gain.5) | copy-start | bytes 6148
  0.7 17.1 %collective-permute-start.1 = (bf16[64,1024]{1,0:T(8,128)(2,1)}, bf16[64,1024]{1,0:T(8,128)(2,1)S(1)}, u32[]{:S(2)}, u32[]{:S(2)}) collective-permute-start(bf16[64,1024]{1,0:T(8,128)(2,1)} %d_own.3), channel_id=1, source_target_pairs={{0,2},{1,3},{2,0},{3,1},{4,6},{5,7},{6,4},{7,5}} | collective-permute-start | bytes 393224 | tf_op jit(solution)/shard_map/ppermute | solution.py:536
  9.0 8.8 %collective-permute-start = (bf16[128,1024]{1,0:T(8,128)(2,1)S(1)}, bf16[128,1024]{1,0:T(8,128)(2,1)S(1)}, u32[]{:S(2)}, u32[]{:S(2)}) collective-permute-start(bf16[128,1024]{1,0:T(8,128)(2,1)S(1)} %get-tuple-element.41.order.send), channel_id=1, source_target_pairs={{0,2},{1,3},{2,0},{3,1},{4,6},{5,7},{6,4},{7,5}} | collective-permute-start | bytes 786440 | tf_op jit(solution)/shard_map/ppermute | solution.py:536
  24.1 4.8 %collective-permute-start.2 = (f32[128,1024]{1,0:T(8,128)S(1)}, f32[128,1024]{1,0:T(8,128)S(1)}, u32[]{:S(2)}, u32[]{:S(2)}) collective-permute-start(f32[128,1024]{1,0:T(8,128)S(1)} %get-tuple-element.57), channel_id=1, source_target_pairs={{0,1},{1,0},{2,3},{3,2},{4,5},{5,4},{6,7},{7,6}} | collective-permute-start | bytes 1572872 | tf_op jit(solution)/shard_map/ppermute | solution.py:536
  24.3 8.6 %collective-permute-start.3 = (f32[64,1024]{1,0:T(8,128)S(1)}, f32[64,1024]{1,0:T(8,128)S(1)}, u32[]{:S(2)}, u32[]{:S(2)}) collective-permute-start(f32[64,1024]{1,0:T(8,128)S(1)} %get-tuple-element.63), channel_id=1, source_target_pairs={{0,2},{1,3},{2,0},{3,1},{4,6},{5,7},{6,4},{7,5}} | collective-permute-start | bytes 786440 | tf_op jit(solution)/shard_map/ppermute | solution.py:536
  33.1 6.4 %collective-permute-start.5 = (bf16[64,1024]{1,0:T(8,128)(2,1)S(1)}, bf16[64,1024]{1,0:T(8,128)(2,1)S(1)}, u32[]{:S(2)}, u32[]{:S(2)}) collective-permute-start(bf16[64,1024]{1,0:T(8,128)(2,1)S(1)} %dx_rows.1.order.dx), channel_id=1, source_target_pairs={{0,2},{1,3},{2,0},{3,1},{4,6},{5,7},{6,4},{7,5}} | collective-permute-start | bytes 393224 | tf_op jit(solution)/shard_map/ppermute | solution.py:536
  34.0 9.6 %collective-permute-start.4 = (f32[64,1024]{1,0:T(8,128)S(1)}, f32[64,1024]{1,0:T(8,128)S(1)}, u32[]{:S(2)}, u32[]{:S(2)}) collective-permute-start(f32[64,1024]{1,0:T(8,128)S(1)} %get-tuple-element.65), channel_id=1, source_target_pairs={{0,2},{1,3},{2,0},{3,1},{4,6},{5,7},{6,4},{7,5}} | collective-permute-start | bytes 786440 | tf_op jit(solution)/shard_map/ppermute | solution.py:536

commit v10 on v9

--- a/solution.py
+++ b/solution.py
@@ -20,7 +20,7 @@
 TILE = 256
 ZERO_ROWS = 96
 FILL_AT = (0, 4, 69, 82, 93, 102, 131)
-LATE_FILL = 8
+LATE_FILL = (5, 13)
 MIB = 1 << 20
 LOOKUP_VMEM = 48 * MIB
 PAIR_VMEM = 8 * MIB
@@ -43,7 +43,7 @@
 
 
 def fill_range(part):
-    late = (lax.axis_index("tp") >> 1) * LATE_FILL
+    late = LATE_FILL[0] + (lax.axis_index("tp") >> 1) * (LATE_FILL[1] - LATE_FILL[0])
     if part == "late":
         return FILL_AT[2] - late, FILL_AT[2]
     return FILL_AT[part], FILL_AT[part + 1] - (late if part == 1 else 0)
@@ -225,7 +225,7 @@
         du[rows, cols] = (g * (cdf + u * (0.5 * (1.0 - t * t)) * (GELU_C * (1.0 + 3.0 * GELU_A * (u * u))))).astype(BF)
 
 
-def share_kernel(send, got, d_own, d_far, w1, w2, gain, x_f, d_full, n_a, h_a, du_a, x_r, d_r, sems):
+def share_kernel(send, got, d_own, d_far, d_own_s, d_far_s, w1, w2, gain, x_f, d_full, n_a, h_a, du_a, x_r, sems):
     rows = d_own.shape[0]
     half = 2 * rows
     remote = swap_with_sibling()
@@ -235,35 +235,30 @@
         x_f[at, :] = send[at, :] + got[other, :]
         copies.append(remote(x_f.at[at], x_r.at[at], sems, k))
         copies[-1].start()
-    for k, src in enumerate((d_own, d_far)):
-        copies.append(remote(src, d_r.at[pl.ds(k * rows, rows)], sems, 2 + k))
-        copies[-1].start()
+    for k, src in enumerate((d_own, d_far, d_own_s, d_far_s)):
         d_full[pl.ds(k * rows, rows), :] = src[...]
     mlp_half(x_f, d_full, n_a, h_a, du_a, (0, half), w1, w2, gain)
     for k in range(2):
         copies[k].wait()
         x_f[pl.ds(half + k * rows, rows), :] = x_r[pl.ds(k * rows, rows), :]
-    for k in range(2):
-        copies[2 + k].wait()
-        d_full[pl.ds(half + k * rows, rows), :] = d_r[pl.ds(k * rows, rows), :]
-
-
-def share(send, got, d_own, d_far, w1, w2, gain):
-    rows, width = d_own.shape
+
+
+def share(send, got, ds, w1, w2, gain):
+    rows, width = ds[0].shape
     hid = w1.shape[1]
     return pl.pallas_call(
         share_kernel,
         name="share",
         out_shape=[sh((4 * rows, width), BF)] * 2 + [sh((2 * rows, width), BF)] + [sh((2 * rows, hid), BF)] * 2,
-        in_specs=[VMEM_SPEC] * 7,
+        in_specs=[VMEM_SPEC] * 9,
         out_specs=[VMEM_SPEC] * 5,
-        scratch_shapes=[VMEM((2 * rows, width), BF), VMEM((2 * rows, width), BF), DMA((2, 4))],
+        scratch_shapes=[VMEM((2 * rows, width), BF), DMA((2, 2))],
         compiler_params=pltpu.CompilerParams(collective_id=1, has_side_effects=True, vmem_limit_bytes=16 * MIB),
         cost_estimate=pl.CostEstimate(flops=3_000_000_000, bytes_accessed=MIB, transcendentals=0),
-    )(send, got, d_own, d_far, w1, w2, gain)
-
-
-def mlp_kernel(x_f, d_full, n_a, h_a, du_a, w1, w2, gain, zero, table_in, n, h, du, dn_p, table_g, s_zero):
+    )(send, got, *ds, w1, w2, gain)
+
+
+def mlp_kernel(x_f, d_full, n_a, h_a, du_a, w1, w2, gain, zero, table_in, n, h, du, dn_b0, dn_b1, table_g, s_zero):
     fill_start(zero, table_g, s_zero, 2)
     tokens, width = n.shape
     half = tokens // 2
@@ -272,7 +267,9 @@
     mlp_half(x_f, d_full, n, h, du, (half, half), w1, w2, gain)
     for j in range(width // TILE):
         cols = pl.ds(j * TILE, TILE)
-        dn_p[:, cols] = mm(du[pl.ds(half, half), :], w1[cols, :], 1, 1)
+        dn = mm(du[pl.ds(half, half), :], w1[cols, :], 1, 1)
+        dn_b0[:, cols] = dn[:half // 2]
+        dn_b1[:, cols] = dn[half // 2:]
     fill_wait(zero, table_g, s_zero, 2)
 
 
@@ -282,51 +279,49 @@
     return pl.pallas_call(
         mlp_kernel,
         name="mlp",
-        out_shape=[sh((tokens, width), BF), sh((tokens, hid), BF), sh((tokens, hid), BF), sh((tokens // 2, width), F32),
-                   sh(table_g.shape, F32)],
+        out_shape=[sh((tokens, width), BF), sh((tokens, hid), BF), sh((tokens, hid), BF), sh((tokens // 4, width), F32),
+                   sh((tokens // 4, width), F32), sh(table_g.shape, F32)],
         in_specs=[VMEM_SPEC] * 9 + [HBM_SPEC],
-        out_specs=[VMEM_SPEC] * 4 + [HBM_SPEC],
-        input_output_aliases={9: 4},
+        out_specs=[VMEM_SPEC] * 5 + [HBM_SPEC],
+        input_output_aliases={9: 5},
         scratch_shapes=[DMA(())],
         compiler_params=pltpu.CompilerParams(vmem_limit_bytes=16 * MIB),
         cost_estimate=pl.CostEstimate(flops=6_000_000_000, bytes_accessed=4 * MIB, transcendentals=0),
     )(x_f, d_full, n_a, h_a, du_a, w1, w2, gain, zero, table_g)
 
 
-def sums_kernel(dn_p, du, h, w1, w2, dn_own, dn_far, y_a, y_b, dn_r, dn_m, sems):
+def sums_kernel(dn_b1, du, h, w1, w2, dn_own, dn_far, y_a, y_b, dn_r, sems):
     rows, width = dn_own.shape
     half = 2 * rows
     remote = swap_with_sibling()
-    copies = [remote(dn_p.at[pl.ds(k * rows, rows)], dn_r.at[pl.ds(k * rows, rows)], sems, k) for k in (1, 0)]
-    for c in copies:
-        c.start()
+    copy = remote(dn_b1, dn_r, sems, 0)
+    copy.start()
     for j in range(width // TILE):
         cols = pl.ds(j * TILE, TILE)
-        dn_m[:, cols] = mm(du[pl.ds(0, half), :], w1[cols, :], 1, 1)
+        dn = mm(du[pl.ds(0, half), :], w1[cols, :], 1, 1)
+        dn_own[:, cols] = dn[:rows]
+        dn_far[:, cols] = dn[rows:]
     for j in range(width // TILE):
         cols = pl.ds(j * TILE, TILE)
         y = mm(h[...], w2[:, cols], 1, 0)
         y_a[:, cols] = y[:half]
         y_b[:, cols] = y[half:]
-    for c, out, k in zip(copies, (dn_far, dn_own), (1, 0)):
-        c.wait()
-        at = pl.ds(k * rows, rows)
-        out[...] = dn_m[at, :] + dn_r[at, :]
-
-
-def sums(dn_p, du, h, w1, w2):
-    half, width = dn_p.shape
-    rows = half // 2
+    copy.wait()
+    dn_far[...] += dn_r[...]
+
+
+def sums(dn_b1, du, h, w1, w2):
+    rows, width = dn_b1.shape
     return pl.pallas_call(
         sums_kernel,
         name="sums",
-        out_shape=[sh((rows, width), F32)] * 2 + [sh((half, width), F32)] * 2,
+        out_shape=[sh((rows, width), F32)] * 2 + [sh((2 * rows, width), F32)] * 2,
         in_specs=[VMEM_SPEC] * 5,
         out_specs=[VMEM_SPEC] * 4,
-        scratch_shapes=[VMEM((half, width), F32), VMEM((half, width), F32), DMA((2, 2))],
+        scratch_shapes=[VMEM((rows, width), F32), DMA((2, 1))],
         compiler_params=pltpu.CompilerParams(collective_id=2, has_side_effects=True, vmem_limit_bytes=16 * MIB),
         cost_estimate=pl.CostEstimate(flops=4_000_000_000, bytes_accessed=4 * MIB, transcendentals=0),
-    )(dn_p, du, h, w1, w2)
+    )(dn_b1, du, h, w1, w2)
 
 
 def grads1_kernel(n, du, zero, order, table_in, dw1, table_g, dw1_v, s_zero, s_w):
@@ -389,27 +384,27 @@
     )(h, d_full, y_a, y_sib, zero, table_g)
 
 
-def dx_kernel(dn_own, g2, x_own, d_own, gain, order, dx):
+def dx_kernel(dn_own, dn_sib, g2, x_own, d_own, gain, order, dx):
     gain_f = gain[...].astype(F32).reshape(1, dx.shape[1])
     for j in range(dx.shape[0] // 16):
         at = pl.ds(j * 16, 16)
-        a = (dn_own[at, :] + g2[at, :]) * gain_f
+        a = (dn_own[at, :] + dn_sib[at, :] + g2[at, :]) * gain_f
         x = x_own[at, :].astype(F32)
         r = lax.rsqrt(jnp.mean(x * x, axis=-1, keepdims=True) + EPS)
         proj = jnp.mean(a * x, axis=-1, keepdims=True)
         dx[at, :] = (d_own[at, :].astype(F32) + r * (a - x * r * r * proj)).astype(BF)
 
 
-def dx_rows(dn_own, g2, x_own, d_own, gain, order):
+def dx_rows(dn_own, dn_sib, g2, x_own, d_own, gain, order):
     return pl.pallas_call(
         dx_kernel,
         name="dx_rows",
         out_shape=sh(d_own.shape, BF),
-        in_specs=[VMEM_SPEC] * 5 + [ANY_SPEC],
+        in_specs=[VMEM_SPEC] * 6 + [ANY_SPEC],
         out_specs=VMEM_SPEC,
         compiler_params=pltpu.CompilerParams(vmem_limit_bytes=4 * MIB),
         cost_estimate=pl.CostEstimate(flops=1_000_000_000, bytes_accessed=MIB, transcendentals=0),
-    )(dn_own, g2, x_own, d_own, gain, order)
+    )(dn_own, dn_sib, g2, x_own, d_own, gain, order)
 
 
 def fill3_kernel(zero, order, table_in, token, table_g, s_zero):
@@ -432,33 +427,31 @@
     )(zero, order, table_g)
 
 
-def dx_all_kernel(dx, dx_far, order, dx_out, dx_r, sems):
+def dx_all_kernel(dx, dx_sib, dx_far, order, dx_out, dx_r, sems):
     me = lax.axis_index("tp")
     rows = dx.shape[0]
     remote = swap_with_sibling()
     block = lambda m: pl.ds(pl.multiple_of((me ^ m) * rows, rows), rows)
-    copies = [remote(src, dx_r.at[pl.ds(k * rows, rows)], sems, k) for k, src in enumerate((dx, dx_far))]
-    for c in copies:
-        c.start()
-    dx_out[block(0), :] = dx[...]
-    dx_out[block(2), :] = dx_far[...]
-    for k, c in enumerate(copies):
-        c.wait()
-        dx_out[block(1 + 2 * k), :] = dx_r[pl.ds(k * rows, rows), :]
-
-
-def dx_all(dx, dx_far, order):
+    copy = remote(dx_far, dx_r, sems, 0)
+    copy.start()
+    for m, src in enumerate((dx, dx_sib, dx_far)):
+        dx_out[block(m), :] = src[...]
+    copy.wait()
+    dx_out[block(3), :] = dx_r[...]
+
+
+def dx_all(dx, dx_sib, dx_far, order):
     rows, width = dx.shape
     return pl.pallas_call(
         dx_all_kernel,
         name="dx_all",
         out_shape=sh((4 * rows, width), BF),
-        in_specs=[VMEM_SPEC] * 2 + [ANY_SPEC],
+        in_specs=[VMEM_SPEC] * 3 + [ANY_SPEC],
         out_specs=VMEM_SPEC,
-        scratch_shapes=[VMEM((2 * rows, width), BF), DMA((2, 2))],
+        scratch_shapes=[VMEM((rows, width), BF), DMA((2, 1))],
         compiler_params=pltpu.CompilerParams(collective_id=3, has_side_effects=True, vmem_limit_bytes=4 * MIB),
         cost_estimate=pl.CostEstimate(flops=2_000_000_000, bytes_accessed=MIB, transcendentals=0),
-    )(dx, dx_far, order)
+    )(dx, dx_sib, dx_far, order)
 
 
 def put_kernel(puts, same, dx, zero, table_in, table_g, token, puts_s, total, s_in, s_row, s_zero):
@@ -540,20 +533,23 @@
         part, rows_mine, same, zero, d_table = lookup(ids, table)
         send, w1 = pair(part, w1)
         got = permute(send, 2)
+        ds = (d_out, d_far, permute(d_out, 1), permute(d_far, 1))
         puts, w2, d_table = fill1(rows_mine, zero, w2, send, d_table)
-        x_f, d_full, n_a, h_a, du_a = share(send, got, d_out, d_far, w1, w2, gain)
-        n, h, du, dn_p, d_table = mlp(x_f, d_full, n_a, h_a, du_a, w1, w2, gain, zero, d_table)
-        dn_own, dn_far, y_a, y_b = sums(dn_p, du, h, w1, w2)
+        x_f, d_full, n_a, h_a, du_a = share(send, got, ds, w1, w2, gain)
+        n, h, du, dn_b0, dn_b1, d_table = mlp(x_f, d_full, n_a, h_a, du_a, w1, w2, gain, zero, d_table)
+        dn_own, dn_far, y_a, y_b = sums(dn_b1, du, h, w1, w2)
         g2 = permute(dn_far, 2)
+        dn_sib = permute(dn_b0, 1)
         y_sib = permute(y_b, 1)
         d_w1, d_table = grads1(n, du, zero, dn_own, d_table)
         d_w2, y_own, y_far, d_table = grads2(h, d_full, y_a, y_sib, zero, d_table)
-        dx = dx_rows(dn_own, g2, x_f, d_out, gain, y_own)
+        dx = dx_rows(dn_own, dn_sib, g2, x_f, d_out, gain, y_own)
         dx_far = permute(dx, 2)
+        dx_sib = permute(dx, 1)
         dx, y_far = lax.optimization_barrier((dx, y_far))
         y_in = permute(y_far, 2)
         token, d_table = fill3(zero, dx, d_table)
-        dx_full = dx_all(dx, dx_far, token)
+        dx_full = dx_all(dx, dx_sib, dx_far, token)
         d_table, done = put_rows(puts, same, dx_full, zero, d_table)
         out = finish(x_f, y_own, y_in, done)
         return out, d_table, d_w1, d_w2

time: 44.5 us -> 44 us (0.989)
  Pallas kernels: 35.5 us -> 34.6 us
    pallas_call x1, Pallas kernels: 8.58 us -> 7.99 us  [fill1(): pl.pallas_call(fill1_kernel, name='fill1', out_shape=[sh((2 * tokens,), I...]
    pallas_call x1, Pallas kernels: 2.08 us -> 2.65 us  [put_rows(): pl.pallas_call(put_kernel, name='put_rows', out_shape=[sh(table_g.shape,...]
    ppermute x6 -> x10, starting transfers between devices: 6.64 us -> 6.95 us  [permute(): return lax.ppermute(x, 'tp', [(i, i ^ hop) for i in range(tp)])]
    ppermute x6 -> x10, waiting for transfers between devices: 1.4 us -> 1.44 us  [permute(): return lax.ppermute(x, 'tp', [(i, i ^ hop) for i in range(tp)])]
  transfers between devices with their start and end apart: 6 -> 10, of which waited for: 3 -> 4; matrix products, arithmetic and copies ran while one was open for 0% -> 0% of each run, Pallas kernels for 64% -> 64%
where the time goes in v10:
time: 44 us; the launch traced here: 43.8 us
  Pallas kernels  34.6 us (79%)
  starting transfers between devices  6.95 us (16%)
  waiting for transfers between devices  1.44 us (3%)
  between operations  0.77 us (2%)
    pallas_call x1, Pallas kernels, fill1(): pl.pallas_call(fill1_kernel, name='fill1', out_shape=[sh((2 * tokens,), I...  7.99 us
    ppermute x10, starting transfers between devices, permute(): return lax.ppermute(x, 'tp', [(i, i ^ hop) for i in range(tp)])  6.95 us
    pallas_call x1, Pallas kernels, fill3(): pl.pallas_call(fill3_kernel, name='fill3', out_shape=[sh((8, 128), F32),...  4.18 us
    pallas_call x1, Pallas kernels, grads1(): pl.pallas_call(grads1_kernel, name='grads1', out_shape=[sh((width, hid),...  3.7 us
    pallas_call x1, Pallas kernels, lookup(): pl.pallas_call(lookup_kernel, name='lookup', out_shape=[sh((tokens, width...  3.39 us
    pallas_call x1, Pallas kernels, grads2(): pl.pallas_call(grads2_kernel, name='grads2', out_shape=[sh((hid, width),...  3.15 us
    pallas_call x1, Pallas kernels, put_rows(): pl.pallas_call(put_kernel, name='put_rows', out_shape=[sh(table_g.shape,...  2.65 us
    pallas_call x1, Pallas kernels, mlp(): pl.pallas_call(mlp_kernel, name='mlp', out_shape=[sh((tokens, width), BF)...  2.3 us
  transfers between devices with their start and end apart: 10, of which 4 were waited for; matrix products, arithmetic and copies ran while one was open for 0% of the time, Pallas kernels for 64%

profile of v10, /device:TPU:0, one launch (start us, length us, event | category | flops | bytes accessed | tf_op | source)
XLA Modules:
  0.0 43.8 jit_solution(7689110552544040241)
XLA Ops:
  0.6 0.0 copy-start.1
  0.6 0.0 copy-start
  0.7 0.9 %collective-permute-start.2 = (bf16[64,1024]{1,0:T(8,128)(2,1)}, bf16[64,1024]{1,0:T(8,128)(2,1)S(1)}, u32[]{:S(2)}, u32[]{:S(2)}) collective-permute-start(bf16[64,1024]{1,0:T(8,128)(2,1)} %d_own.3), channel_id=1, source_target_pairs={{0,1},{1,0},{2,3},{3,2},{4,5},{5,4},{6,7},{7,6}} | collective-permute-start | bytes 393224 | tf_op jit(solution)/shard_map/ppermute | solution.py:529
  1.5 2.5 %collective-permute-start.1 = (bf16[64,1024]{1,0:T(8,128)(2,1)}, bf16[64,1024]{1,0:T(8,128)(2,1)S(1)}, u32[]{:S(2)}, u32[]{:S(2)}) collective-permute-start(bf16[64,1024]{1,0:T(8,128)(2,1)} %d_own.3), channel_id=1, source_target_pairs={{0,2},{1,3},{2,0},{3,1},{4,6},{5,7},{6,4},{7,5}} | collective-permute-start | bytes 393224 | tf_op jit(solution)/shard_map/ppermute | solution.py:529
  4.0 3.4 %lookup.1 = (bf16[256,1024]{1,0:T(8,128)(2,1)S(1)}, s32[1,256]{1,0:T(1,128)S(1)}, bf16[256,256]{1,0:T(8,128)(2,1)S(1)}, f32[96,1024]{1,0:T(8,128)S(1)}, f32[12576,1024]{1,0:T(8,128)}) custom-call(s32[256]{0:T(256)} %ids.1, s32[1,256]{1,0:T(1,128)} %bitcast.1, bf16[12576,1024]{1,0:T(8,128)(2,1)} %table.1), custom_call_target="tpu_custom_call" | custom-call | flops 5000000000 | bytes 10485760 | tf_op jit(solution)/shard_map/lookup/pallas_call | solution.py:127
  7.4 1.6 %pair.1 = (bf16[128,1024]{1,0:T(8,128)(2,1)S(1)}, bf16[1024,1024]{1,0:T(8,128)(2,1)S(1)}) custom-call(bf16[256,1024]{1,0:T(8,128)(2,1)S(1)} %get-tuple-element.41.part, bf16[1024,1024]{1,0:T(8,128)(2,1)} %w1.1), custom_call_target="tpu_custom_call" | custom-call | flops 3000000000 | bytes 1048576 | tf_op jit(solution)/shard_map/pair/pallas_call | solution.py:159
  9.1 0.1 collective-permute-start
  9.2 0.0 collective-permute-done.1.d_far
  9.2 0.2 collective-permute-start.3
  9.3 8.0 %fill1.1 = (s32[512]{0:T(512)S(1)}, bf16[1024,1024]{1,0:T(8,128)(2,1)S(1)}, f32[12576,1024]{1,0:T(8,128)}) custom-call(s32[1,256]{1,0:T(1,128)S(1)} %get-tuple-element.44.rows_mine, f32[96,1024]{1,0:T(8,128)S(1)} %get-tuple-element.45.zero, bf16[1024,1024]{1,0:T(8,128)(2,1)} %w2.1, ...), custom_call_target="tpu_custom_call", output_to_operand_aliasing={{2}: (4, {})} | custom-call | flops 8999999488 | bytes 20971520 | tf_op jit(solution)/shard_map/fill1/pallas_call | solution.py:195
  17.3 0.0 collective-permute-done.2.d_own_s
  17.3 0.0 collective-permute-done.3.d_far_s
  17.3 0.1 collective-permute-done.got
  17.5 0.0 copy-done.1
  17.5 0.0 copy-done
  17.5 1.6 %share.1 = (bf16[256,1024]{1,0:T(8,128)(2,1)S(1)}, bf16[256,1024]{1,0:T(8,128)(2,1)S(1)}, bf16[128,1024]{1,0:T(8,128)(2,1)S(1)}, bf16[128,1024]{1,0:T(8,128)(2,1)S(1)}, bf16[128,1024]{1,0:T(8,128)(2,1)S(1)}) custom-call(bf16[128,1024]{1,0:T(8,128)(2,1)S(1)} %get-tuple-element.42.order.send, bf16[128,1024]{1,0:T(8,128)(2,1)S(1)} %collective-permute-done.got, ...), custom_call_target="tpu_custom_call" | custom-call | flops 3000000000 | bytes 1048576 | tf_op jit(solution)/shard_map/share/pallas_call | solution.py:249
  19.1 2.3 %mlp.1 = (bf16[256,1024]{1,0:T(8,128)(2,1)S(1)}, bf16[256,1024]{1,0:T(8,128)(2,1)S(1)}, bf16[256,1024]{1,0:T(8,128)(2,1)S(1)}, f32[64,1024]{1,0:T(8,128)S(1)}, f...) custom-call(bf16[256,1024]{1,0:T(8,128)(2,1)S(1)} %get-tuple-element.48.x_f.x_own.x, ...), custom_call_target="tpu_custom_call", output_to_operand_aliasing={{5}: (9, {})} | custom-call | flops 6000000000 | bytes 4194304 | tf_op jit(solution)/shard_map/mlp/pallas_call | solution.py:279
  21.4 1.7 %sums.1 = (f32[64,1024]{1,0:T(8,128)S(1)}, f32[64,1024]{1,0:T(8,128)S(1)}, f32[128,1024]{1,0:T(8,128)S(1)}, f32[128,1024]{1,0:T(8,128)S(1)}) custom-call(f32[64,1024]{1,0:T(8,128)S(1)} %get-tuple-element.55.dn_b1, bf16[256,1024]{1,0:T(8,128)(2,1)S(1)} %get-tuple-element.56.du, bf16[256,1024]{1,0:T(8,128)(2,1)S(1)} %get-tuple-element.54.h, ...), custom_call_target="tpu_custom_call" | custom-call | flops 4000000000 | bytes 4194304 | tf_op jit(solution)/shard_map/sums/pallas_call | solution.py:315
  23.2 0.3 collective-permute-start.4
  23.4 1.0 %collective-permute-start.6 = (f32[64,1024]{1,0:T(8,128)S(1)}, f32[64,1024]{1,0:T(8,128)S(1)}, u32[]{:S(2)}, u32[]{:S(2)}) collective-permute-start(f32[64,1024]{1,0:T(8,128)S(1)} %get-tuple-element.65), channel_id=1, source_target_pairs={{0,2},{1,3},{2,0},{3,1},{4,6},{5,7},{6,4},{7,5}} | collective-permute-start | bytes 786440 | tf_op jit(solution)/shard_map/ppermute | solution.py:529
  24.5 0.0 collective-permute-start.5
  24.5 3.7 %grads1.1 = (f32[1024,1024]{1,0:T(8,128)}, f32[12576,1024]{1,0:T(8,128)}) custom-call(bf16[256,1024]{1,0:T(8,128)(2,1)S(1)} %get-tuple-element.59.n, bf16[256,1024]{1,0:T(8,128)(2,1)S(1)} %get-tuple-element.56.du, f32[96,1024]{1,0:T(8,128)S(1)} %get-tuple-element.45.zero, ...), custom_call_target="tpu_custom_call", output_to_operand_aliasing={{1}: (4, {})} | custom-call | flops 4000000000 | bytes 8388608 | tf_op jit(solution)/shard_map/grads1/pallas_call | solution.py:342
  28.2 0.0 collective-permute-done.4.y_sib
  28.2 3.1 %grads2.1 = (f32[1024,1024]{1,0:T(8,128)}, f32[64,1024]{1,0:T(8,128)S(1)}, f32[64,1024]{1,0:T(8,128)S(1)}, f32[12576,1024]{1,0:T(8,128)}) custom-call(bf16[256,1024]{1,0:T(8,128)(2,1)S(1)} %get-tuple-element.54.h, bf16[256,1024]{1,0:T(8,128)(2,1)S(1)} %get-tuple-element.49.d_full, ...), custom_call_target="tpu_custom_call", output_to_operand_aliasing={{3}: (5, {})} | custom-call | flops 4000000000 | bytes 8388608 | tf_op jit(solution)/shard_map/grads2/pallas_call | solution.py:374
  31.3 0.6 %collective-permute-done.6.g2 = f32[64,1024]{1,0:T(8,128)S(1)} collective-permute-done((f32[64,1024]{1,0:T(8,128)S(1)}, f32[64,1024]{1,0:T(8,128)S(1)}, u32[]{:S(2)}, u32[]{:S(2)}) %collective-permute-start.6) | collective-permute-done | bytes 262176 | tf_op jit(solution)/shard_map/ppermute | solution.py:529
  31.9 0.0 collective-permute-done.5.dn_sib
  31.9 0.2 dx_rows.1.order.dx
  32.1 1.0 %collective-permute-start.9 = (bf16[64,1024]{1,0:T(8,128)(2,1)S(1)}, bf16[64,1024]{1,0:T(8,128)(2,1)S(1)}, u32[]{:S(2)}, u32[]{:S(2)}) collective-permute-start(bf16[64,1024]{1,0:T(8,128)(2,1)S(1)} %dx_rows.1.order.dx), channel_id=1, source_target_pairs={{0,2},{1,3},{2,0},{3,1},{4,6},{5,7},{6,4},{7,5}} | collective-permute-start | bytes 393224 | tf_op jit(solution)/shard_map/ppermute | solution.py:529
  33.1 0.0 collective-permute-start.8
  33.1 1.1 %collective-permute-start.7 = (f32[64,1024]{1,0:T(8,128)S(1)}, f32[64,1024]{1,0:T(8,128)S(1)}, u32[]{:S(2)}, u32[]{:S(2)}) collective-permute-start(f32[64,1024]{1,0:T(8,128)S(1)} %get-tuple-element.67), channel_id=1, source_target_pairs={{0,2},{1,3},{2,0},{3,1},{4,6},{5,7},{6,4},{7,5}} | collective-permute-start | bytes 786440 | tf_op jit(solution)/shard_map/ppermute | solution.py:529
  34.1 4.2 %fill3.1 = (f32[8,128]{1,0:T(8,128)S(1)}, f32[12576,1024]{1,0:T(8,128)}) custom-call(f32[96,1024]{1,0:T(8,128)S(1)} %get-tuple-element.45.zero, bf16[64,1024]{1,0:T(8,128)(2,1)S(1)} %dx_rows.1.order.dx, f32[12576,1024]{1,0:T(8,128)} %get-tuple-element.71.table_in), custom_call_target="tpu_custom_call", output_to_operand_aliasing={{1}: (2, {})} | custom-call | flops 4000000000 | bytes 16777216 | tf_op jit(solution)/shard_map/fill3/pallas_call | solution.py:417
  38.3 0.2 collective-permute-done.9.dx_far
  38.5 0.0 collective-permute-done.8.dx_sib
  38.5 1.4 %dx_all.1.dx = bf16[256,1024]{1,0:T(8,128)(2,1)S(1)} custom-call(bf16[64,1024]{1,0:T(8,128)(2,1)S(1)} %dx_rows.1.order.dx, bf16[64,1024]{1,0:T(8,128)(2,1)S(1)} %collective-permute-done.8.dx_sib, bf16[64,1024]{1,0:T(8,128)(2,1)S(1)} %collective-permute-done.9.dx_far, f32[8,128]{1,0:T(8,128)S(1)} %get-tuple-element.72.order), custom_call_target="tpu_custom_call" | custom-call | flops 2000000000 | bytes 1048576 | tf_op jit(solution)/shard_map/dx_all/pallas_call | solution.py:445
  39.9 2.7 %put_rows.1 = (f32[12576,1024]{1,0:T(8,128)}, f32[8,128]{1,0:T(8,128)S(1)}) custom-call(s32[512]{0:T(512)S(1)} %get-tuple-element.68.puts, bf16[256,256]{1,0:T(8,128)(2,1)S(1)} %get-tuple-element.69.same, bf16[256,1024]{1,0:T(8,128)(2,1)S(1)} %dx_all.1.dx, f32[96,1024]{1,0:T(8,128)S(1)} %get-tuple-element.45.zero, ...), custom_call_target="tpu_custom_call", output_to_operand_aliasing={{0}: (4, {})} | custom-call | flops 3000000000 | bytes 2097152 | tf_op jit(solution)/shard_map/put_rows/pallas_call | solution.py:496
  42.5 0.5 %collective-permute-done.7.y_in = f32[64,1024]{1,0:T(8,128)S(1)} collective-permute-done((f32[64,1024]{1,0:T(8,128)S(1)}, f32[64,1024]{1,0:T(8,128)S(1)}, u32[]{:S(2)}, u32[]{:S(2)}) %collective-permute-start.7) | collective-permute-done | bytes 262176 | tf_op jit(solution)/shard_map/ppermute | solution.py:529
  43.1 0.7 %finish.1 = bf16[64,1024]{1,0:T(8,128)(2,1)} custom-call(bf16[256,1024]{1,0:T(8,128)(2,1)S(1)} %get-tuple-element.48.x_f.x_own.x, f32[64,1024]{1,0:T(8,128)S(1)} %get-tuple-element.63.order.y, f32[64,1024]{1,0:T(8,128)S(1)} %collective-permute-done.7.y_in, f32[8,128]{1,0:T(8,128)S(1)} %get-tuple-element.74.order), custom_call_target="tpu_custom_call" | custom-call | flops 1000000000 | bytes 1048576 | tf_op jit(solution)/shard_map/finish/pallas_call | solution.py:514
Async XLA Ops:
  0.6 16.8 %copy-start.1 = (bf16[64,1024]{1,0:T(8,128)(2,1)S(1)}, bf16[64,1024]{1,0:T(8,128)(2,1)}, u32[]{:S(2)}) copy-start(bf16[64,1024]{1,0:T(8,128)(2,1)} %d_own.3) | copy-start | bytes 393220
  0.6 16.8 %copy-start = (bf16[1024]{0:T(1024)(128)(2,1)S(1)}, bf16[1024]{0:T(1024)(128)(2,1)}, u32[]{:S(2)}) copy-start(bf16[1024]{0:T(1024)(128)(2,1)} %gain.5) | copy-start | bytes 6148
  0.7 16.7 %collective-permute-start.2 = (bf16[64,1024]{1,0:T(8,128)(2,1)}, bf16[64,1024]{1,0:T(8,128)(2,1)S(1)}, u32[]{:S(2)}, u32[]{:S(2)}) collective-permute-start(bf16[64,1024]{1,0:T(8,128)(2,1)} %d_own.3), channel_id=1, source_target_pairs={{0,1},{1,0},{2,3},{3,2},{4,5},{5,4},{6,7},{7,6}} | collective-permute-start | bytes 393224 | tf_op jit(solution)/shard_map/ppermute | solution.py:529
  1.5 7.6 %collective-permute-start.1 = (bf16[64,1024]{1,0:T(8,128)(2,1)}, bf16[64,1024]{1,0:T(8,128)(2,1)S(1)}, u32[]{:S(2)}, u32[]{:S(2)}) collective-permute-start(bf16[64,1024]{1,0:T(8,128)(2,1)} %d_own.3), channel_id=1, source_target_pairs={{0,2},{1,3},{2,0},{3,1},{4,6},{5,7},{6,4},{7,5}} | collective-permute-start | bytes 393224 | tf_op jit(solution)/shard_map/ppermute | solution.py:529
  9.1 8.4 %collective-permute-start = (bf16[128,1024]{1,0:T(8,128)(2,1)S(1)}, bf16[128,1024]{1,0:T(8,128)(2,1)S(1)}, u32[]{:S(2)}, u32[]{:S(2)}) collective-permute-start(bf16[128,1024]{1,0:T(8,128)(2,1)S(1)} %get-tuple-element.42.order.send), channel_id=1, source_target_pairs={{0,2},{1,3},{2,0},{3,1},{4,6},{5,7},{6,4},{7,5}} | collective-permute-start | bytes 786440 | tf_op jit(solution)/shard_map/ppermute | solution.py:529
  9.2 8.2 %collective-permute-start.3 = (bf16[64,1024]{1,0:T(8,128)(2,1)S(1)}, bf16[64,1024]{1,0:T(8,128)(2,1)S(1)}, u32[]{:S(2)}, u32[]{:S(2)}) collective-permute-start(bf16[64,1024]{1,0:T(8,128)(2,1)S(1)} %collective-permute-done.1.d_far), channel_id=1, source_target_pairs={{0,1},{1,0},{2,3},{3,2},{4,5},{5,4},{6,7},{7,6}} | collective-permute-start | bytes 393224 | tf_op jit(solution)/shard_map/ppermute | solution.py:529
  23.2 5.0 %collective-permute-start.4 = (f32[128,1024]{1,0:T(8,128)S(1)}, f32[128,1024]{1,0:T(8,128)S(1)}, u32[]{:S(2)}, u32[]{:S(2)}) collective-permute-start(f32[128,1024]{1,0:T(8,128)S(1)} %get-tuple-element.58), channel_id=1, source_target_pairs={{0,1},{1,0},{2,3},{3,2},{4,5},{5,4},{6,7},{7,6}} | collective-permute-start | bytes 1572872 | tf_op jit(solution)/shard_map/ppermute | solution.py:529
  23.4 8.5 %collective-permute-start.6 = (f32[64,1024]{1,0:T(8,128)S(1)}, f32[64,1024]{1,0:T(8,128)S(1)}, u32[]{:S(2)}, u32[]{:S(2)}) collective-permute-start(f32[64,1024]{1,0:T(8,128)S(1)} %get-tuple-element.65), channel_id=1, source_target_pairs={{0,2},{1,3},{2,0},{3,1},{4,6},{5,7},{6,4},{7,5}} | collective-permute-start | bytes 786440 | tf_op jit(solution)/shard_map/ppermute | solution.py:529
  24.5 7.5 %collective-permute-start.5 = (f32[64,1024]{1,0:T(8,128)S(1)}, f32[64,1024]{1,0:T(8,128)S(1)}, u32[]{:S(2)}, u32[]{:S(2)}) collective-permute-start(f32[64,1024]{1,0:T(8,128)S(1)} %get-tuple-element.64), channel_id=1, source_target_pairs={{0,1},{1,0},{2,3},{3,2},{4,5},{5,4},{6,7},{7,6}} | collective-permute-start | bytes 786440 | tf_op jit(solution)/shard_map/ppermute | solution.py:529
  32.1 6.4 %collective-permute-start.9 = (bf16[64,1024]{1,0:T(8,128)(2,1)S(1)}, bf16[64,1024]{1,0:T(8,128)(2,1)S(1)}, u32[]{:S(2)}, u32[]{:S(2)}) collective-permute-start(bf16[64,1024]{1,0:T(8,128)(2,1)S(1)} %dx_rows.1.order.dx), channel_id=1, source_target_pairs={{0,2},{1,3},{2,0},{3,1},{4,6},{5,7},{6,4},{7,5}} | collective-permute-start | bytes 393224 | tf_op jit(solution)/shard_map/ppermute | solution.py:529
  33.1 5.4 %collective-permute-start.8 = (bf16[64,1024]{1,0:T(8,128)(2,1)S(1)}, bf16[64,1024]{1,0:T(8,128)(2,1)S(1)}, u32[]{:S(2)}, u32[]{:S(2)}) collective-permute-start(bf16[64,1024]{1,0:T(8,128)(2,1)S(1)} %dx_rows.1.order.dx), channel_id=1, source_target_pairs={{0,1},{1,0},{2,3},{3,2},{4,5},{5,4},{6,7},{7,6}} | collective-permute-start | bytes 393224 | tf_op jit(solution)/shard_map/ppermute | solution.py:529
  33.1 10.0 %collective-permute-start.7 = (f32[64,1024]{1,0:T(8,128)S(1)}, f32[64,1024]{1,0:T(8,128)S(1)}, u32[]{:S(2)}, u32[]{:S(2)}) collective-permute-start(f32[64,1024]{1,0:T(8,128)S(1)} %get-tuple-element.67), channel_id=1, source_target_pairs={{0,2},{1,3},{2,0},{3,1},{4,6},{5,7},{6,4},{7,5}} | collective-permute-start | bytes 786440 | tf_op jit(solution)/shard_map/ppermute | solution.py:529

commit v11 on v10

--- a/solution.py
+++ b/solution.py
@@ -19,8 +19,8 @@
 DMA = pltpu.SemaphoreType.DMA
 TILE = 256
 ZERO_ROWS = 96
-FILL_AT = (0, 4, 69, 82, 93, 102, 131)
-LATE_FILL = (5, 13)
+FILL_COUNTS = ((22, 54, 13, 8, 8, 21, 5), (4, 50, 13, 9, 9, 23, 23))
+LATE = 6
 MIB = 1 << 20
 LOOKUP_VMEM = 48 * MIB
 PAIR_VMEM = 8 * MIB
@@ -43,10 +43,9 @@
 
 
 def fill_range(part):
-    late = LATE_FILL[0] + (lax.axis_index("tp") >> 1) * (LATE_FILL[1] - LATE_FILL[0])
-    if part == "late":
-        return FILL_AT[2] - late, FILL_AT[2]
-    return FILL_AT[part], FILL_AT[part + 1] - (late if part == 1 else 0)
+    chip = lax.axis_index("tp") >> 1
+    (lo0, hi0), (lo1, hi1) = ((sum(c[:part]), sum(c[:part + 1])) for c in FILL_COUNTS)
+    return lo0 + chip * (lo1 - lo0), hi0 + chip * (hi1 - hi0)
 
 
 def fill_start(zero, table_g, sem, part):
@@ -455,14 +454,14 @@
 
 
 def put_kernel(puts, same, dx, zero, table_in, table_g, token, puts_s, total, s_in, s_row, s_zero):
-    fill_start(zero, table_g, s_zero, "late")
+    fill_start(zero, table_g, s_zero, LATE)
     tokens = dx.shape[0]
     load = pltpu.make_async_copy(puts, puts_s, s_in)
     load.start()
     total[...] = mm(same[...], dx[...], 1, 0)
     token[...] = jnp.zeros_like(token)
     load.wait()
-    fill_wait(zero, table_g, s_zero, "late")
+    fill_wait(zero, table_g, s_zero, LATE)
     count = puts_s[tokens]
 
     def put(i):
@@ -529,8 +528,9 @@
         return lax.ppermute(x, "tp", [(i, i ^ hop) for i in range(tp)])
 
     def shard_step(ids, table, gain, w1, w2, d_out):
-        d_far = permute(d_out, 2)
         part, rows_mine, same, zero, d_table = lookup(ids, table)
+        part, d_send = lax.optimization_barrier((part, d_out))
+        d_far = permute(d_send, 2)
         send, w1 = pair(part, w1)
         got = permute(send, 2)
         ds = (d_out, d_far, permute(d_out, 1), permute(d_far, 1))

time: 44 us -> 46.9 us (1.066)
  waiting for transfers between devices: 1.44 us -> 4.94 us
  starting transfers between devices: 6.95 us -> 6.02 us
    ppermute x10, waiting for transfers between devices: 1.44 us -> 4.94 us  [permute(): return lax.ppermute(x, 'tp', [(i, i ^ hop) for i in range(tp)])]
    pallas_call x1, Pallas kernels: 3.39 us -> 5.2 us  [lookup(): pl.pallas_call(lookup_kernel, name='lookup', out_shape=[sh((tokens, width...]
    pallas_call x1, Pallas kernels: 4.18 us -> 3.23 us  [fill3(): pl.pallas_call(fill3_kernel, name='fill3', out_shape=[sh((8, 128), F32),...]
    ppermute x10, starting transfers between devices: 6.95 us -> 6.02 us  [permute(): return lax.ppermute(x, 'tp', [(i, i ^ hop) for i in range(tp)])]
    pallas_call x1, Pallas kernels: 7.99 us -> 7.29 us  [fill1(): pl.pallas_call(fill1_kernel, name='fill1', out_shape=[sh((2 * tokens,), I...]
  transfers between devices with their start and end apart: 10 -> 10, of which waited for: 4 -> 4; matrix products, arithmetic and copies ran while one was open for 0% -> 0% of each run, Pallas kernels for 64% -> 60%
where the time goes in v11:
time: 46.9 us; the launch traced here: 46.3 us
  Pallas kernels  34.5 us (74%)
  starting transfers between devices  6.02 us (13%)
  waiting for transfers between devices  4.94 us (11%)
  between operations  0.8 us (2%)
    pallas_call x1, Pallas kernels, fill1(): pl.pallas_call(fill1_kernel, name='fill1', out_shape=[sh((2 * tokens,), I...  7.29 us
    ppermute x10, starting transfers between devices, permute(): return lax.ppermute(x, 'tp', [(i, i ^ hop) for i in range(tp)])  6.02 us
    pallas_call x1, Pallas kernels, lookup(): pl.pallas_call(lookup_kernel, name='lookup', out_shape=[sh((tokens, width...  5.2 us
    ppermute x10, waiting for transfers between devices, permute(): return lax.ppermute(x, 'tp', [(i, i ^ hop) for i in range(tp)])  4.94 us
    pallas_call x1, Pallas kernels, grads1(): pl.pallas_call(grads1_kernel, name='grads1', out_shape=[sh((width, hid),...  3.34 us
    pallas_call x1, Pallas kernels, fill3(): pl.pallas_call(fill3_kernel, name='fill3', out_shape=[sh((8, 128), F32),...  3.23 us
    pallas_call x1, Pallas kernels, grads2(): pl.pallas_call(grads2_kernel, name='grads2', out_shape=[sh((hid, width),...  3.03 us
    pallas_call x1, Pallas kernels, put_rows(): pl.pallas_call(put_kernel, name='put_rows', out_shape=[sh(table_g.shape,...  2.65 us
  transfers between devices with their start and end apart: 10, of which 4 were waited for; matrix products, arithmetic and copies ran while one was open for 0% of the time, Pallas kernels for 60%

profile of v11, /device:TPU:0, one launch (start us, length us, event | category | flops | bytes accessed | tf_op | source)
XLA Modules:
  0.0 46.3 jit_solution(6649536080465769465)
XLA Ops:
  0.6 0.0 copy-start.1
  0.6 0.0 copy-start
  0.7 0.9 %collective-permute-start.2 = (bf16[64,1024]{1,0:T(8,128)(2,1)}, bf16[64,1024]{1,0:T(8,128)(2,1)S(1)}, u32[]{:S(2)}, u32[]{:S(2)}) collective-permute-start(bf16[64,1024]{1,0:T(8,128)(2,1)} %d_own.3), channel_id=1, source_target_pairs={{0,1},{1,0},{2,3},{3,2},{4,5},{5,4},{6,7},{7,6}} | collective-permute-start | bytes 393224 | tf_op jit(solution)/shard_map/ppermute | solution.py:528
  1.5 5.2 %lookup.1 = (bf16[256,1024]{1,0:T(8,128)(2,1)S(1)}, s32[1,256]{1,0:T(1,128)S(1)}, bf16[256,256]{1,0:T(8,128)(2,1)S(1)}, f32[96,1024]{1,0:T(8,128)S(1)}, f32[12576,1024]{1,0:T(8,128)}) custom-call(s32[256]{0:T(256)} %ids.1, s32[1,256]{1,0:T(1,128)} %bitcast.1, bf16[12576,1024]{1,0:T(8,128)(2,1)} %table.1), custom_call_target="tpu_custom_call" | custom-call | flops 5000000000 | bytes 10485760 | tf_op jit(solution)/shard_map/lookup/pallas_call | solution.py:126
  6.7 0.9 %collective-permute-start.1 = (bf16[64,1024]{1,0:T(8,128)(2,1)}, bf16[64,1024]{1,0:T(8,128)(2,1)S(1)}, u32[]{:S(2)}, u32[]{:S(2)}) collective-permute-start(bf16[64,1024]{1,0:T(8,128)(2,1)} %d_own.3), channel_id=1, source_target_pairs={{0,2},{1,3},{2,0},{3,1},{4,6},{5,7},{6,4},{7,5}} | collective-permute-start | bytes 393224 | tf_op jit(solution)/shard_map/ppermute | solution.py:528
  7.6 1.6 %pair.1 = (bf16[128,1024]{1,0:T(8,128)(2,1)S(1)}, bf16[1024,1024]{1,0:T(8,128)(2,1)S(1)}) custom-call(bf16[256,1024]{1,0:T(8,128)(2,1)S(1)} %get-tuple-element.44.part, bf16[1024,1024]{1,0:T(8,128)(2,1)} %w1.1), custom_call_target="tpu_custom_call" | custom-call | flops 3000000000 | bytes 1048576 | tf_op jit(solution)/shard_map/pair/pallas_call | solution.py:158
  9.2 1.2 %collective-permute-start = (bf16[128,1024]{1,0:T(8,128)(2,1)S(1)}, bf16[128,1024]{1,0:T(8,128)(2,1)S(1)}, u32[]{:S(2)}, u32[]{:S(2)}) collective-permute-start(bf16[128,1024]{1,0:T(8,128)(2,1)S(1)} %get-tuple-element.45.order.send), channel_id=1, source_target_pairs={{0,2},{1,3},{2,0},{3,1},{4,6},{5,7},{6,4},{7,5}} | collective-permute-start | bytes 786440 | tf_op jit(solution)/shard_map/ppermute | solution.py:528
  10.4 2.4 %collective-permute-done.1.d_far = bf16[64,1024]{1,0:T(8,128)(2,1)S(1)} collective-permute-done((bf16[64,1024]{1,0:T(8,128)(2,1)}, bf16[64,1024]{1,0:T(8,128)(2,1)S(1)}, u32[]{:S(2)}, u32[]{:S(2)}) %collective-permute-start.1) | collective-permute-done | bytes 131104 | tf_op jit(solution)/shard_map/ppermute | solution.py:528
  12.8 0.0 collective-permute-start.3
  12.8 7.3 %fill1.1 = (s32[512]{0:T(512)S(1)}, bf16[1024,1024]{1,0:T(8,128)(2,1)S(1)}, f32[12576,1024]{1,0:T(8,128)}) custom-call(s32[1,256]{1,0:T(1,128)S(1)} %get-tuple-element.48.rows_mine, f32[96,1024]{1,0:T(8,128)S(1)} %get-tuple-element.49.zero, bf16[1024,1024]{1,0:T(8,128)(2,1)} %w2.1, ...), custom_call_target="tpu_custom_call", output_to_operand_aliasing={{2}: (4, {})} | custom-call | flops 8999999488 | bytes 20971520 | tf_op jit(solution)/shard_map/fill1/pallas_call | solution.py:194
  20.1 0.0 collective-permute-done.2.d_own_s
  20.1 0.0 collective-permute-done.3.d_far_s
  20.1 0.0 collective-permute-done.got
  20.1 0.0 copy-done.1
  20.1 0.0 copy-done
  20.1 1.9 %share.1 = (bf16[256,1024]{1,0:T(8,128)(2,1)S(1)}, bf16[256,1024]{1,0:T(8,128)(2,1)S(1)}, bf16[128,1024]{1,0:T(8,128)(2,1)S(1)}, bf16[128,1024]{1,0:T(8,128)(2,1)S(1)}, bf16[128,1024]{1,0:T(8,128)(2,1)S(1)}) custom-call(bf16[128,1024]{1,0:T(8,128)(2,1)S(1)} %get-tuple-element.45.order.send, bf16[128,1024]{1,0:T(8,128)(2,1)S(1)} %collective-permute-done.got, ...), custom_call_target="tpu_custom_call" | custom-call | flops 3000000000 | bytes 1048576 | tf_op jit(solution)/shard_map/share/pallas_call | solution.py:248
  22.0 2.3 %mlp.1 = (bf16[256,1024]{1,0:T(8,128)(2,1)S(1)}, bf16[256,1024]{1,0:T(8,128)(2,1)S(1)}, bf16[256,1024]{1,0:T(8,128)(2,1)S(1)}, f32[64,1024]{1,0:T(8,128)S(1)}, f...) custom-call(bf16[256,1024]{1,0:T(8,128)(2,1)S(1)} %get-tuple-element.52.x_f.x_own.x, ...), custom_call_target="tpu_custom_call", output_to_operand_aliasing={{5}: (9, {})} | custom-call | flops 6000000000 | bytes 4194304 | tf_op jit(solution)/shard_map/mlp/pallas_call | solution.py:278
  24.4 1.7 %sums.1 = (f32[64,1024]{1,0:T(8,128)S(1)}, f32[64,1024]{1,0:T(8,128)S(1)}, f32[128,1024]{1,0:T(8,128)S(1)}, f32[128,1024]{1,0:T(8,128)S(1)}) custom-call(f32[64,1024]{1,0:T(8,128)S(1)} %get-tuple-element.59.dn_b1, bf16[256,1024]{1,0:T(8,128)(2,1)S(1)} %get-tuple-element.60.du, bf16[256,1024]{1,0:T(8,128)(2,1)S(1)} %get-tuple-element.58.h, ...), custom_call_target="tpu_custom_call" | custom-call | flops 4000000000 | bytes 4194304 | tf_op jit(solution)/shard_map/sums/pallas_call | solution.py:314
  26.0 0.3 collective-permute-start.4
  26.4 0.7 %collective-permute-start.6 = (f32[64,1024]{1,0:T(8,128)S(1)}, f32[64,1024]{1,0:T(8,128)S(1)}, u32[]{:S(2)}, u32[]{:S(2)}) collective-permute-start(f32[64,1024]{1,0:T(8,128)S(1)} %get-tuple-element.69), channel_id=1, source_target_pairs={{0,2},{1,3},{2,0},{3,1},{4,6},{5,7},{6,4},{7,5}} | collective-permute-start | bytes 786440 | tf_op jit(solution)/shard_map/ppermute | solution.py:528
  27.1 0.0 collective-permute-start.5
  27.1 3.3 %grads1.1 = (f32[1024,1024]{1,0:T(8,128)}, f32[12576,1024]{1,0:T(8,128)}) custom-call(bf16[256,1024]{1,0:T(8,128)(2,1)S(1)} %get-tuple-element.63.n, bf16[256,1024]{1,0:T(8,128)(2,1)S(1)} %get-tuple-element.60.du, f32[96,1024]{1,0:T(8,128)S(1)} %get-tuple-element.49.zero, ...), custom_call_target="tpu_custom_call", output_to_operand_aliasing={{1}: (4, {})} | custom-call | flops 4000000000 | bytes 8388608 | tf_op jit(solution)/shard_map/grads1/pallas_call | solution.py:341
  30.4 0.0 collective-permute-done.4.y_sib
  30.5 3.0 %grads2.1 = (f32[1024,1024]{1,0:T(8,128)}, f32[64,1024]{1,0:T(8,128)S(1)}, f32[64,1024]{1,0:T(8,128)S(1)}, f32[12576,1024]{1,0:T(8,128)}) custom-call(bf16[256,1024]{1,0:T(8,128)(2,1)S(1)} %get-tuple-element.58.h, bf16[256,1024]{1,0:T(8,128)(2,1)S(1)} %get-tuple-element.53.d_full, ...), custom_call_target="tpu_custom_call", output_to_operand_aliasing={{3}: (5, {})} | custom-call | flops 4000000000 | bytes 8388608 | tf_op jit(solution)/shard_map/grads2/pallas_call | solution.py:373
  33.5 1.3 %collective-permute-done.6.g2 = f32[64,1024]{1,0:T(8,128)S(1)} collective-permute-done((f32[64,1024]{1,0:T(8,128)S(1)}, f32[64,1024]{1,0:T(8,128)S(1)}, u32[]{:S(2)}, u32[]{:S(2)}) %collective-permute-start.6) | collective-permute-done | bytes 262176 | tf_op jit(solution)/shard_map/ppermute | solution.py:528
  34.8 0.0 collective-permute-done.5.dn_sib
  34.8 0.2 dx_rows.1.order.dx
  35.0 0.8 %collective-permute-start.9 = (bf16[64,1024]{1,0:T(8,128)(2,1)S(1)}, bf16[64,1024]{1,0:T(8,128)(2,1)S(1)}, u32[]{:S(2)}, u32[]{:S(2)}) collective-permute-start(bf16[64,1024]{1,0:T(8,128)(2,1)S(1)} %dx_rows.1.order.dx), channel_id=1, source_target_pairs={{0,2},{1,3},{2,0},{3,1},{4,6},{5,7},{6,4},{7,5}} | collective-permute-start | bytes 393224 | tf_op jit(solution)/shard_map/ppermute | solution.py:528
  35.7 0.0 collective-permute-start.8
  35.7 1.3 %collective-permute-start.7 = (f32[64,1024]{1,0:T(8,128)S(1)}, f32[64,1024]{1,0:T(8,128)S(1)}, u32[]{:S(2)}, u32[]{:S(2)}) collective-permute-start(f32[64,1024]{1,0:T(8,128)S(1)} %get-tuple-element.71), channel_id=1, source_target_pairs={{0,2},{1,3},{2,0},{3,1},{4,6},{5,7},{6,4},{7,5}} | collective-permute-start | bytes 786440 | tf_op jit(solution)/shard_map/ppermute | solution.py:528
  37.0 3.2 %fill3.1 = (f32[8,128]{1,0:T(8,128)S(1)}, f32[12576,1024]{1,0:T(8,128)}) custom-call(f32[96,1024]{1,0:T(8,128)S(1)} %get-tuple-element.49.zero, bf16[64,1024]{1,0:T(8,128)(2,1)S(1)} %dx_rows.1.order.dx, f32[12576,1024]{1,0:T(8,128)} %get-tuple-element.75.table_in), custom_call_target="tpu_custom_call", output_to_operand_aliasing={{1}: (2, {})} | custom-call | flops 4000000000 | bytes 16777216 | tf_op jit(solution)/shard_map/fill3/pallas_call | solution.py:416
  40.3 0.8 %collective-permute-done.9.dx_far = bf16[64,1024]{1,0:T(8,128)(2,1)S(1)} collective-permute-done((bf16[64,1024]{1,0:T(8,128)(2,1)S(1)}, bf16[64,1024]{1,0:T(8,128)(2,1)S(1)}, u32[]{:S(2)}, u32[]{:S(2)}) %collective-permute-start.9) | collective-permute-done | bytes 131104 | tf_op jit(solution)/shard_map/ppermute | solution.py:528
  41.1 0.0 collective-permute-done.8.dx_sib
  41.1 1.4 %dx_all.1.dx = bf16[256,1024]{1,0:T(8,128)(2,1)S(1)} custom-call(bf16[64,1024]{1,0:T(8,128)(2,1)S(1)} %dx_rows.1.order.dx, bf16[64,1024]{1,0:T(8,128)(2,1)S(1)} %collective-permute-done.8.dx_sib, bf16[64,1024]{1,0:T(8,128)(2,1)S(1)} %collective-permute-done.9.dx_far, f32[8,128]{1,0:T(8,128)S(1)} %get-tuple-element.76.order), custom_call_target="tpu_custom_call" | custom-call | flops 2000000000 | bytes 1048576 | tf_op jit(solution)/shard_map/dx_all/pallas_call | solution.py:444
  42.5 2.7 %put_rows.1 = (f32[12576,1024]{1,0:T(8,128)}, f32[8,128]{1,0:T(8,128)S(1)}) custom-call(s32[512]{0:T(512)S(1)} %get-tuple-element.72.puts, bf16[256,256]{1,0:T(8,128)(2,1)S(1)} %get-tuple-element.73.same, bf16[256,1024]{1,0:T(8,128)(2,1)S(1)} %dx_all.1.dx, f32[96,1024]{1,0:T(8,128)S(1)} %get-tuple-element.49.zero, ...), custom_call_target="tpu_custom_call", output_to_operand_aliasing={{0}: (4, {})} | custom-call | flops 3000000000 | bytes 2097152 | tf_op jit(solution)/shard_map/put_rows/pallas_call | solution.py:495
  45.1 0.4 collective-permute-done.7.y_in
  45.6 0.7 %finish.1 = bf16[64,1024]{1,0:T(8,128)(2,1)} custom-call(bf16[256,1024]{1,0:T(8,128)(2,1)S(1)} %get-tuple-element.52.x_f.x_own.x, f32[64,1024]{1,0:T(8,128)S(1)} %get-tuple-element.67.order.y, f32[64,1024]{1,0:T(8,128)S(1)} %collective-permute-done.7.y_in, f32[8,128]{1,0:T(8,128)S(1)} %get-tuple-element.78.order), custom_call_target="tpu_custom_call" | custom-call | flops 1000000000 | bytes 1048576 | tf_op jit(solution)/shard_map/finish/pallas_call | solution.py:513
Async XLA Ops:
  0.6 19.5 %copy-start.1 = (bf16[64,1024]{1,0:T(8,128)(2,1)S(1)}, bf16[64,1024]{1,0:T(8,128)(2,1)}, u32[]{:S(2)}) copy-start(bf16[64,1024]{1,0:T(8,128)(2,1)} %d_own.3) | copy-start | bytes 393220
  0.6 19.5 %copy-start = (bf16[1024]{0:T(1024)(128)(2,1)S(1)}, bf16[1024]{0:T(1024)(128)(2,1)}, u32[]{:S(2)}) copy-start(bf16[1024]{0:T(1024)(128)(2,1)} %gain.5) | copy-start | bytes 6148
  0.7 19.4 %collective-permute-start.2 = (bf16[64,1024]{1,0:T(8,128)(2,1)}, bf16[64,1024]{1,0:T(8,128)(2,1)S(1)}, u32[]{:S(2)}, u32[]{:S(2)}) collective-permute-start(bf16[64,1024]{1,0:T(8,128)(2,1)} %d_own.3), channel_id=1, source_target_pairs={{0,1},{1,0},{2,3},{3,2},{4,5},{5,4},{6,7},{7,6}} | collective-permute-start | bytes 393224 | tf_op jit(solution)/shard_map/ppermute | solution.py:528
  6.7 6.1 %collective-permute-start.1 = (bf16[64,1024]{1,0:T(8,128)(2,1)}, bf16[64,1024]{1,0:T(8,128)(2,1)S(1)}, u32[]{:S(2)}, u32[]{:S(2)}) collective-permute-start(bf16[64,1024]{1,0:T(8,128)(2,1)} %d_own.3), channel_id=1, source_target_pairs={{0,2},{1,3},{2,0},{3,1},{4,6},{5,7},{6,4},{7,5}} | collective-permute-start | bytes 393224 | tf_op jit(solution)/shard_map/ppermute | solution.py:528
  9.2 10.9 %collective-permute-start = (bf16[128,1024]{1,0:T(8,128)(2,1)S(1)}, bf16[128,1024]{1,0:T(8,128)(2,1)S(1)}, u32[]{:S(2)}, u32[]{:S(2)}) collective-permute-start(bf16[128,1024]{1,0:T(8,128)(2,1)S(1)} %get-tuple-element.45.order.send), channel_id=1, source_target_pairs={{0,2},{1,3},{2,0},{3,1},{4,6},{5,7},{6,4},{7,5}} | collective-permute-start | bytes 786440 | tf_op jit(solution)/shard_map/ppermute | solution.py:528
  12.8 7.3 %collective-permute-start.3 = (bf16[64,1024]{1,0:T(8,128)(2,1)S(1)}, bf16[64,1024]{1,0:T(8,128)(2,1)S(1)}, u32[]{:S(2)}, u32[]{:S(2)}) collective-permute-start(bf16[64,1024]{1,0:T(8,128)(2,1)S(1)} %collective-permute-done.1.d_far), channel_id=1, source_target_pairs={{0,1},{1,0},{2,3},{3,2},{4,5},{5,4},{6,7},{7,6}} | collective-permute-start | bytes 393224 | tf_op jit(solution)/shard_map/ppermute | solution.py:528
  26.0 4.4 %collective-permute-start.4 = (f32[128,1024]{1,0:T(8,128)S(1)}, f32[128,1024]{1,0:T(8,128)S(1)}, u32[]{:S(2)}, u32[]{:S(2)}) collective-permute-start(f32[128,1024]{1,0:T(8,128)S(1)} %get-tuple-element.62), channel_id=1, source_target_pairs={{0,1},{1,0},{2,3},{3,2},{4,5},{5,4},{6,7},{7,6}} | collective-permute-start | bytes 1572872 | tf_op jit(solution)/shard_map/ppermute | solution.py:528
  26.4 8.4 %collective-permute-start.6 = (f32[64,1024]{1,0:T(8,128)S(1)}, f32[64,1024]{1,0:T(8,128)S(1)}, u32[]{:S(2)}, u32[]{:S(2)}) collective-permute-start(f32[64,1024]{1,0:T(8,128)S(1)} %get-tuple-element.69), channel_id=1, source_target_pairs={{0,2},{1,3},{2,0},{3,1},{4,6},{5,7},{6,4},{7,5}} | collective-permute-start | bytes 786440 | tf_op jit(solution)/shard_map/ppermute | solution.py:528
  27.1 7.7 %collective-permute-start.5 = (f32[64,1024]{1,0:T(8,128)S(1)}, f32[64,1024]{1,0:T(8,128)S(1)}, u32[]{:S(2)}, u32[]{:S(2)}) collective-permute-start(f32[64,1024]{1,0:T(8,128)S(1)} %get-tuple-element.68), channel_id=1, source_target_pairs={{0,1},{1,0},{2,3},{3,2},{4,5},{5,4},{6,7},{7,6}} | collective-permute-start | bytes 786440 | tf_op jit(solution)/shard_map/ppermute | solution.py:528
  35.0 6.1 %collective-permute-start.9 = (bf16[64,1024]{1,0:T(8,128)(2,1)S(1)}, bf16[64,1024]{1,0:T(8,128)(2,1)S(1)}, u32[]{:S(2)}, u32[]{:S(2)}) collective-permute-start(bf16[64,1024]{1,0:T(8,128)(2,1)S(1)} %dx_rows.1.order.dx), channel_id=1, source_target_pairs={{0,2},{1,3},{2,0},{3,1},{4,6},{5,7},{6,4},{7,5}} | collective-permute-start | bytes 393224 | tf_op jit(solution)/shard_map/ppermute | solution.py:528
  35.7 5.4 %collective-permute-start.8 = (bf16[64,1024]{1,0:T(8,128)(2,1)S(1)}, bf16[64,1024]{1,0:T(8,128)(2,1)S(1)}, u32[]{:S(2)}, u32[]{:S(2)}) collective-permute-start(bf16[64,1024]{1,0:T(8,128)(2,1)S(1)} %dx_rows.1.order.dx), channel_id=1, source_target_pairs={{0,1},{1,0},{2,3},{3,2},{4,5},{5,4},{6,7},{7,6}} | collective-permute-start | bytes 393224 | tf_op jit(solution)/shard_map/ppermute | solution.py:528
  35.7 9.8 %collective-permute-start.7 = (f32[64,1024]{1,0:T(8,128)S(1)}, f32[64,1024]{1,0:T(8,128)S(1)}, u32[]{:S(2)}, u32[]{:S(2)}) collective-permute-start(f32[64,1024]{1,0:T(8,128)S(1)} %get-tuple-element.71), channel_id=1, source_target_pairs={{0,2},{1,3},{2,0},{3,1},{4,6},{5,7},{6,4},{7,5}} | collective-permute-start | bytes 786440 | tf_op jit(solution)/shard_map/ppermute | solution.py:528

commit v12 on v11

--- a/solution.py
+++ b/solution.py
@@ -224,7 +224,7 @@
         du[rows, cols] = (g * (cdf + u * (0.5 * (1.0 - t * t)) * (GELU_C * (1.0 + 3.0 * GELU_A * (u * u))))).astype(BF)
 
 
-def share_kernel(send, got, d_own, d_far, d_own_s, d_far_s, w1, w2, gain, x_f, d_full, n_a, h_a, du_a, x_r, sems):
+def share_kernel(send, got, d_own, d_far, w1, w2, gain, x_f, n_a, h_a, du_a, x_r, d_a, sems):
     rows = d_own.shape[0]
     half = 2 * rows
     remote = swap_with_sibling()
@@ -234,31 +234,35 @@
         x_f[at, :] = send[at, :] + got[other, :]
         copies.append(remote(x_f.at[at], x_r.at[at], sems, k))
         copies[-1].start()
-    for k, src in enumerate((d_own, d_far, d_own_s, d_far_s)):
-        d_full[pl.ds(k * rows, rows), :] = src[...]
-    mlp_half(x_f, d_full, n_a, h_a, du_a, (0, half), w1, w2, gain)
+    for k, src in enumerate((d_own, d_far)):
+        d_a[pl.ds(k * rows, rows), :] = src[...]
+    mlp_half(x_f, d_a, n_a, h_a, du_a, (0, half), w1, w2, gain)
     for k in range(2):
         copies[k].wait()
         x_f[pl.ds(half + k * rows, rows), :] = x_r[pl.ds(k * rows, rows), :]
 
 
-def share(send, got, ds, w1, w2, gain):
-    rows, width = ds[0].shape
+def share(send, got, d_own, d_far, w1, w2, gain):
+    rows, width = d_own.shape
     hid = w1.shape[1]
     return pl.pallas_call(
         share_kernel,
         name="share",
-        out_shape=[sh((4 * rows, width), BF)] * 2 + [sh((2 * rows, width), BF)] + [sh((2 * rows, hid), BF)] * 2,
-        in_specs=[VMEM_SPEC] * 9,
-        out_specs=[VMEM_SPEC] * 5,
-        scratch_shapes=[VMEM((2 * rows, width), BF), DMA((2, 2))],
+        out_shape=[sh((4 * rows, width), BF), sh((2 * rows, width), BF)] + [sh((2 * rows, hid), BF)] * 2,
+        in_specs=[VMEM_SPEC] * 7,
+        out_specs=[VMEM_SPEC] * 4,
+        scratch_shapes=[VMEM((2 * rows, width), BF), VMEM((2 * rows, width), BF), DMA((2, 2))],
         compiler_params=pltpu.CompilerParams(collective_id=1, has_side_effects=True, vmem_limit_bytes=16 * MIB),
         cost_estimate=pl.CostEstimate(flops=3_000_000_000, bytes_accessed=MIB, transcendentals=0),
-    )(send, got, *ds, w1, w2, gain)
-
-
-def mlp_kernel(x_f, d_full, n_a, h_a, du_a, w1, w2, gain, zero, table_in, n, h, du, dn_b0, dn_b1, table_g, s_zero):
+    )(send, got, d_own, d_far, w1, w2, gain)
+
+
+def mlp_kernel(x_f, d_own, d_far, d_own_s, d_far_s, n_a, h_a, du_a, w1, w2, gain, zero, table_in,
+               n, h, du, d_full, dn_b0, dn_b1, table_g, s_zero):
     fill_start(zero, table_g, s_zero, 2)
+    rows = d_own.shape[0]
+    for k, src in enumerate((d_own, d_far, d_own_s, d_far_s)):
+        d_full[pl.ds(k * rows, rows), :] = src[...]
     tokens, width = n.shape
     half = tokens // 2
     for out, src in ((n, n_a), (h, h_a), (du, du_a)):
@@ -272,21 +276,21 @@
     fill_wait(zero, table_g, s_zero, 2)
 
 
-def mlp(x_f, d_full, n_a, h_a, du_a, w1, w2, gain, zero, table_g):
+def mlp(x_f, ds, n_a, h_a, du_a, w1, w2, gain, zero, table_g):
     tokens, width = x_f.shape
     hid = w1.shape[1]
     return pl.pallas_call(
         mlp_kernel,
         name="mlp",
-        out_shape=[sh((tokens, width), BF), sh((tokens, hid), BF), sh((tokens, hid), BF), sh((tokens // 4, width), F32),
-                   sh((tokens // 4, width), F32), sh(table_g.shape, F32)],
-        in_specs=[VMEM_SPEC] * 9 + [HBM_SPEC],
-        out_specs=[VMEM_SPEC] * 5 + [HBM_SPEC],
-        input_output_aliases={9: 5},
+        out_shape=[sh((tokens, width), BF), sh((tokens, hid), BF), sh((tokens, hid), BF), sh((tokens, width), BF),
+                   sh((tokens // 4, width), F32), sh((tokens // 4, width), F32), sh(table_g.shape, F32)],
+        in_specs=[VMEM_SPEC] * 12 + [HBM_SPEC],
+        out_specs=[VMEM_SPEC] * 6 + [HBM_SPEC],
+        input_output_aliases={12: 6},
         scratch_shapes=[DMA(())],
         compiler_params=pltpu.CompilerParams(vmem_limit_bytes=16 * MIB),
         cost_estimate=pl.CostEstimate(flops=6_000_000_000, bytes_accessed=4 * MIB, transcendentals=0),
-    )(x_f, d_full, n_a, h_a, du_a, w1, w2, gain, zero, table_g)
+    )(x_f, *ds, n_a, h_a, du_a, w1, w2, gain, zero, table_g)
 
 
 def sums_kernel(dn_b1, du, h, w1, w2, dn_own, dn_far, y_a, y_b, dn_r, sems):
@@ -533,10 +537,12 @@
         d_far = permute(d_send, 2)
         send, w1 = pair(part, w1)
         got = permute(send, 2)
-        ds = (d_out, d_far, permute(d_out, 1), permute(d_far, 1))
+        d_own_s = permute(d_out, 1)
         puts, w2, d_table = fill1(rows_mine, zero, w2, send, d_table)
-        x_f, d_full, n_a, h_a, du_a = share(send, got, ds, w1, w2, gain)
-        n, h, du, dn_b0, dn_b1, d_table = mlp(x_f, d_full, n_a, h_a, du_a, w1, w2, gain, zero, d_table)
+        d_far_s = permute(d_far, 1)
+        x_f, n_a, h_a, du_a = share(send, got, d_out, d_far, w1, w2, gain)
+        ds = (d_out, d_far, d_own_s, d_far_s)
+        n, h, du, d_full, dn_b0, dn_b1, d_table = mlp(x_f, ds, n_a, h_a, du_a, w1, w2, gain, zero, d_table)
         dn_own, dn_far, y_a, y_b = sums(dn_b1, du, h, w1, w2)
         g2 = permute(dn_far, 2)
         dn_sib = permute(dn_b0, 1)

time: 46.9 us -> 44.6 us (0.951)
  waiting for transfers between devices: 4.94 us -> 2.45 us
    ppermute x10, waiting for transfers between devices: 4.94 us -> 2.45 us  [permute(): return lax.ppermute(x, 'tp', [(i, i ^ hop) for i in range(tp)])]
  transfers between devices with their start and end apart: 10 -> 10, of which waited for: 4 -> 4; matrix products, arithmetic and copies ran while one was open for 0% -> 0% of each run, Pallas kernels for 60% -> 67%
where the time goes in v12:
time: 44.6 us; the launch traced here: 44 us
  Pallas kernels  34.3 us (77%)
  starting transfers between devices  6.42 us (14%)
  waiting for transfers between devices  2.45 us (5%)
  between operations  0.79 us (2%)
    pallas_call x1, Pallas kernels, fill1(): pl.pallas_call(fill1_kernel, name='fill1', out_shape=[sh((2 * tokens,), I...  7.28 us
    ppermute x10, starting transfers between devices, permute(): return lax.ppermute(x, 'tp', [(i, i ^ hop) for i in range(tp)])  6.42 us
    pallas_call x1, Pallas kernels, lookup(): pl.pallas_call(lookup_kernel, name='lookup', out_shape=[sh((tokens, width...  5.2 us
    pallas_call x1, Pallas kernels, grads1(): pl.pallas_call(grads1_kernel, name='grads1', out_shape=[sh((width, hid),...  3.35 us
    pallas_call x1, Pallas kernels, fill3(): pl.pallas_call(fill3_kernel, name='fill3', out_shape=[sh((8, 128), F32),...  3.23 us
    pallas_call x1, Pallas kernels, grads2(): pl.pallas_call(grads2_kernel, name='grads2', out_shape=[sh((hid, width),...  3.03 us
    pallas_call x1, Pallas kernels, put_rows(): pl.pallas_call(put_kernel, name='put_rows', out_shape=[sh(table_g.shape,...  2.65 us
    ppermute x10, waiting for transfers between devices, permute(): return lax.ppermute(x, 'tp', [(i, i ^ hop) for i in range(tp)])  2.45 us
  transfers between devices with their start and end apart: 10, of which 4 were waited for; matrix products, arithmetic and copies ran while one was open for 0% of the time, Pallas kernels for 67%

profile of v12, /device:TPU:0, one launch (start us, length us, event | category | flops | bytes accessed | tf_op | source)
XLA Modules:
  0.0 44.0 jit_solution(15363409121594580146)
XLA Ops:
  0.6 0.0 copy-start
  0.6 0.0 copy-start.1
  0.7 0.9 %collective-permute-start.2 = (bf16[64,1024]{1,0:T(8,128)(2,1)}, bf16[64,1024]{1,0:T(8,128)(2,1)S(1)}, u32[]{:S(2)}, u32[]{:S(2)}) collective-permute-start(bf16[64,1024]{1,0:T(8,128)(2,1)} %d_own.5), channel_id=1, source_target_pairs={{0,1},{1,0},{2,3},{3,2},{4,5},{5,4},{6,7},{7,6}} | collective-permute-start | bytes 393224 | tf_op jit(solution)/shard_map/ppermute | solution.py:532
  1.5 5.2 %lookup.1 = (bf16[256,1024]{1,0:T(8,128)(2,1)S(1)}, s32[1,256]{1,0:T(1,128)S(1)}, bf16[256,256]{1,0:T(8,128)(2,1)S(1)}, f32[96,1024]{1,0:T(8,128)S(1)}, f32[12576,1024]{1,0:T(8,128)}) custom-call(s32[256]{0:T(256)} %ids.1, s32[1,256]{1,0:T(1,128)} %bitcast.1, bf16[12576,1024]{1,0:T(8,128)(2,1)} %table.1), custom_call_target="tpu_custom_call" | custom-call | flops 5000000000 | bytes 10485760 | tf_op jit(solution)/shard_map/lookup/pallas_call | solution.py:126
  6.7 0.9 %collective-permute-start.1 = (bf16[64,1024]{1,0:T(8,128)(2,1)}, bf16[64,1024]{1,0:T(8,128)(2,1)S(1)}, u32[]{:S(2)}, u32[]{:S(2)}) collective-permute-start(bf16[64,1024]{1,0:T(8,128)(2,1)} %d_own.5), channel_id=1, source_target_pairs={{0,2},{1,3},{2,0},{3,1},{4,6},{5,7},{6,4},{7,5}} | collective-permute-start | bytes 393224 | tf_op jit(solution)/shard_map/ppermute | solution.py:532
  7.6 1.6 %pair.1 = (bf16[128,1024]{1,0:T(8,128)(2,1)S(1)}, bf16[1024,1024]{1,0:T(8,128)(2,1)S(1)}) custom-call(bf16[256,1024]{1,0:T(8,128)(2,1)S(1)} %get-tuple-element.44.part, bf16[1024,1024]{1,0:T(8,128)(2,1)} %w1.1), custom_call_target="tpu_custom_call" | custom-call | flops 3000000000 | bytes 1048576 | tf_op jit(solution)/shard_map/pair/pallas_call | solution.py:158
  9.2 1.2 %collective-permute-start = (bf16[128,1024]{1,0:T(8,128)(2,1)S(1)}, bf16[128,1024]{1,0:T(8,128)(2,1)S(1)}, u32[]{:S(2)}, u32[]{:S(2)}) collective-permute-start(bf16[128,1024]{1,0:T(8,128)(2,1)S(1)} %get-tuple-element.45.order.send), channel_id=1, source_target_pairs={{0,2},{1,3},{2,0},{3,1},{4,6},{5,7},{6,4},{7,5}} | collective-permute-start | bytes 786440 | tf_op jit(solution)/shard_map/ppermute | solution.py:532
  10.4 7.3 %fill1.1 = (s32[512]{0:T(512)S(1)}, bf16[1024,1024]{1,0:T(8,128)(2,1)S(1)}, f32[12576,1024]{1,0:T(8,128)}) custom-call(s32[1,256]{1,0:T(1,128)S(1)} %get-tuple-element.48.rows_mine, f32[96,1024]{1,0:T(8,128)S(1)} %get-tuple-element.49.zero, bf16[1024,1024]{1,0:T(8,128)(2,1)} %w2.1, ...), custom_call_target="tpu_custom_call", output_to_operand_aliasing={{2}: (4, {})} | custom-call | flops 8999999488 | bytes 20971520 | tf_op jit(solution)/shard_map/fill1/pallas_call | solution.py:194
  17.7 0.0 collective-permute-done.1.d_far
  17.7 0.0 collective-permute-start.3
  17.8 0.2 collective-permute-done.got
  18.0 0.0 copy-done
  18.0 0.0 copy-done.1
  18.0 1.7 %share.1 = (bf16[256,1024]{1,0:T(8,128)(2,1)S(1)}, bf16[128,1024]{1,0:T(8,128)(2,1)S(1)}, bf16[128,1024]{1,0:T(8,128)(2,1)S(1)}, bf16[128,1024]{1,0:T(8,128)(2,1)S(1)}) custom-call(bf16[128,1024]{1,0:T(8,128)(2,1)S(1)} %get-tuple-element.45.order.send, bf16[128,1024]{1,0:T(8,128)(2,1)S(1)} %collective-permute-done.got, bf16[64,1024]{1,0:T(8,128)(2,1)S(1)} %copy-done, ...), custom_call_target="tpu_custom_call" | custom-call | flops 3000000000 | bytes 1048576 | tf_op jit(solution)/shard_map/share/pallas_call | solution.py:248
  19.7 0.0 collective-permute-done.2.d_own_s
  19.7 0.0 collective-permute-done.3.d_far_s
  19.7 2.3 %mlp.1 = (bf16[256,1024]{1,0:T(8,128)(2,1)S(1)}, bf16[256,1024]{1,0:T(8,128)(2,1)S(1)}, bf16[256,1024]{1,0:T(8,128)(2,1)S(1)}, bf16[256,1024]{1,0:T(8,128)(2,1)S...) custom-call(bf16[256,1024]{1,0:T(8,128)(2,1)S(1)} %get-tuple-element, ...), custom_call_target="tpu_custom_call", output_to_operand_aliasing={{6}: (12, {})} | custom-call | flops 6000000000 | bytes 4194304 | tf_op jit(solution)/shard_map/mlp/pallas_call | solution.py:282
  22.0 1.7 %sums.1 = (f32[64,1024]{1,0:T(8,128)S(1)}, f32[64,1024]{1,0:T(8,128)S(1)}, f32[128,1024]{1,0:T(8,128)S(1)}, f32[128,1024]{1,0:T(8,128)S(1)}) custom-call(f32[64,1024]{1,0:T(8,128)S(1)} %get-tuple-element.59.dn_b1, bf16[256,1024]{1,0:T(8,128)(2,1)S(1)} %get-tuple-element.60.du, bf16[256,1024]{1,0:T(8,128)(2,1)S(1)} %get-tuple-element.57.h, ...), custom_call_target="tpu_custom_call" | custom-call | flops 4000000000 | bytes 4194304 | tf_op jit(solution)/shard_map/sums/pallas_call | solution.py:318
  23.7 0.3 collective-permute-start.4
  24.0 1.1 %collective-permute-start.6 = (f32[64,1024]{1,0:T(8,128)S(1)}, f32[64,1024]{1,0:T(8,128)S(1)}, u32[]{:S(2)}, u32[]{:S(2)}) collective-permute-start(f32[64,1024]{1,0:T(8,128)S(1)} %get-tuple-element.69), channel_id=1, source_target_pairs={{0,2},{1,3},{2,0},{3,1},{4,6},{5,7},{6,4},{7,5}} | collective-permute-start | bytes 786440 | tf_op jit(solution)/shard_map/ppermute | solution.py:532
  25.1 0.0 collective-permute-start.5
  25.1 3.4 %grads1.1 = (f32[1024,1024]{1,0:T(8,128)}, f32[12576,1024]{1,0:T(8,128)}) custom-call(bf16[256,1024]{1,0:T(8,128)(2,1)S(1)} %get-tuple-element.63.n, bf16[256,1024]{1,0:T(8,128)(2,1)S(1)} %get-tuple-element.60.du, f32[96,1024]{1,0:T(8,128)S(1)} %get-tuple-element.49.zero, ...), custom_call_target="tpu_custom_call", output_to_operand_aliasing={{1}: (4, {})} | custom-call | flops 4000000000 | bytes 8388608 | tf_op jit(solution)/shard_map/grads1/pallas_call | solution.py:345
  28.5 0.0 collective-permute-done.4.y_sib
  28.5 3.0 %grads2.1 = (f32[1024,1024]{1,0:T(8,128)}, f32[64,1024]{1,0:T(8,128)S(1)}, f32[64,1024]{1,0:T(8,128)S(1)}, f32[12576,1024]{1,0:T(8,128)}) custom-call(bf16[256,1024]{1,0:T(8,128)(2,1)S(1)} %get-tuple-element.57.h, bf16[256,1024]{1,0:T(8,128)(2,1)S(1)} %get-tuple-element.58.d_full, ...), custom_call_target="tpu_custom_call", output_to_operand_aliasing={{3}: (5, {})} | custom-call | flops 4000000000 | bytes 8388608 | tf_op jit(solution)/shard_map/grads2/pallas_call | solution.py:377
  31.5 0.9 %collective-permute-done.6.g2 = f32[64,1024]{1,0:T(8,128)S(1)} collective-permute-done((f32[64,1024]{1,0:T(8,128)S(1)}, f32[64,1024]{1,0:T(8,128)S(1)}, u32[]{:S(2)}, u32[]{:S(2)}) %collective-permute-start.6) | collective-permute-done | bytes 262176 | tf_op jit(solution)/shard_map/ppermute | solution.py:532
  32.5 0.0 collective-permute-done.5.dn_sib
  32.5 0.2 dx_rows.1.order.dx
  32.6 1.2 %collective-permute-start.9 = (bf16[64,1024]{1,0:T(8,128)(2,1)S(1)}, bf16[64,1024]{1,0:T(8,128)(2,1)S(1)}, u32[]{:S(2)}, u32[]{:S(2)}) collective-permute-start(bf16[64,1024]{1,0:T(8,128)(2,1)S(1)} %dx_rows.1.order.dx), channel_id=1, source_target_pairs={{0,2},{1,3},{2,0},{3,1},{4,6},{5,7},{6,4},{7,5}} | collective-permute-start | bytes 393224 | tf_op jit(solution)/shard_map/ppermute | solution.py:532
  33.8 0.0 collective-permute-start.8
  33.8 0.9 %collective-permute-start.7 = (f32[64,1024]{1,0:T(8,128)S(1)}, f32[64,1024]{1,0:T(8,128)S(1)}, u32[]{:S(2)}, u32[]{:S(2)}) collective-permute-start(f32[64,1024]{1,0:T(8,128)S(1)} %get-tuple-element.71), channel_id=1, source_target_pairs={{0,2},{1,3},{2,0},{3,1},{4,6},{5,7},{6,4},{7,5}} | collective-permute-start | bytes 786440 | tf_op jit(solution)/shard_map/ppermute | solution.py:532
  34.7 3.2 %fill3.1 = (f32[8,128]{1,0:T(8,128)S(1)}, f32[12576,1024]{1,0:T(8,128)}) custom-call(f32[96,1024]{1,0:T(8,128)S(1)} %get-tuple-element.49.zero, bf16[64,1024]{1,0:T(8,128)(2,1)S(1)} %dx_rows.1.order.dx, f32[12576,1024]{1,0:T(8,128)} %get-tuple-element.75.table_in), custom_call_target="tpu_custom_call", output_to_operand_aliasing={{1}: (2, {})} | custom-call | flops 4000000000 | bytes 16777216 | tf_op jit(solution)/shard_map/fill3/pallas_call | solution.py:420
  37.9 0.5 %collective-permute-done.9.dx_far = bf16[64,1024]{1,0:T(8,128)(2,1)S(1)} collective-permute-done((bf16[64,1024]{1,0:T(8,128)(2,1)S(1)}, bf16[64,1024]{1,0:T(8,128)(2,1)S(1)}, u32[]{:S(2)}, u32[]{:S(2)}) %collective-permute-start.9) | collective-permute-done | bytes 131104 | tf_op jit(solution)/shard_map/ppermute | solution.py:532
  38.4 0.0 collective-permute-done.8.dx_sib
  38.4 1.4 %dx_all.1.dx = bf16[256,1024]{1,0:T(8,128)(2,1)S(1)} custom-call(bf16[64,1024]{1,0:T(8,128)(2,1)S(1)} %dx_rows.1.order.dx, bf16[64,1024]{1,0:T(8,128)(2,1)S(1)} %collective-permute-done.8.dx_sib, bf16[64,1024]{1,0:T(8,128)(2,1)S(1)} %collective-permute-done.9.dx_far, f32[8,128]{1,0:T(8,128)S(1)} %get-tuple-element.76.order), custom_call_target="tpu_custom_call" | custom-call | flops 2000000000 | bytes 1048576 | tf_op jit(solution)/shard_map/dx_all/pallas_call | solution.py:448
  39.8 2.7 %put_rows.1 = (f32[12576,1024]{1,0:T(8,128)}, f32[8,128]{1,0:T(8,128)S(1)}) custom-call(s32[512]{0:T(512)S(1)} %get-tuple-element.72.puts, bf16[256,256]{1,0:T(8,128)(2,1)S(1)} %get-tuple-element.73.same, bf16[256,1024]{1,0:T(8,128)(2,1)S(1)} %dx_all.1.dx, f32[96,1024]{1,0:T(8,128)S(1)} %get-tuple-element.49.zero, ...), custom_call_target="tpu_custom_call", output_to_operand_aliasing={{0}: (4, {})} | custom-call | flops 3000000000 | bytes 2097152 | tf_op jit(solution)/shard_map/put_rows/pallas_call | solution.py:499
  42.5 0.8 %collective-permute-done.7.y_in = f32[64,1024]{1,0:T(8,128)S(1)} collective-permute-done((f32[64,1024]{1,0:T(8,128)S(1)}, f32[64,1024]{1,0:T(8,128)S(1)}, u32[]{:S(2)}, u32[]{:S(2)}) %collective-permute-start.7) | collective-permute-done | bytes 262176 | tf_op jit(solution)/shard_map/ppermute | solution.py:532
  43.3 0.7 %finish.1 = bf16[64,1024]{1,0:T(8,128)(2,1)} custom-call(bf16[256,1024]{1,0:T(8,128)(2,1)S(1)} %get-tuple-element.52.x_f.x_own.x, f32[64,1024]{1,0:T(8,128)S(1)} %get-tuple-element.67.order.y, f32[64,1024]{1,0:T(8,128)S(1)} %collective-permute-done.7.y_in, f32[8,128]{1,0:T(8,128)S(1)} %get-tuple-element.78.order), custom_call_target="tpu_custom_call" | custom-call | flops 1000000000 | bytes 1048576 | tf_op jit(solution)/shard_map/finish/pallas_call | solution.py:517
Async XLA Ops:
  0.6 17.3 %copy-start = (bf16[64,1024]{1,0:T(8,128)(2,1)S(1)}, bf16[64,1024]{1,0:T(8,128)(2,1)}, u32[]{:S(2)}) copy-start(bf16[64,1024]{1,0:T(8,128)(2,1)} %d_own.5) | copy-start | bytes 393220
  0.6 17.3 %copy-start.1 = (bf16[1024]{0:T(1024)(128)(2,1)S(1)}, bf16[1024]{0:T(1024)(128)(2,1)}, u32[]{:S(2)}) copy-start(bf16[1024]{0:T(1024)(128)(2,1)} %gain.5) | copy-start | bytes 6148
  0.7 19.0 %collective-permute-start.2 = (bf16[64,1024]{1,0:T(8,128)(2,1)}, bf16[64,1024]{1,0:T(8,128)(2,1)S(1)}, u32[]{:S(2)}, u32[]{:S(2)}) collective-permute-start(bf16[64,1024]{1,0:T(8,128)(2,1)} %d_own.5), channel_id=1, source_target_pairs={{0,1},{1,0},{2,3},{3,2},{4,5},{5,4},{6,7},{7,6}} | collective-permute-start | bytes 393224 | tf_op jit(solution)/shard_map/ppermute | solution.py:532
  6.7 11.0 %collective-permute-start.1 = (bf16[64,1024]{1,0:T(8,128)(2,1)}, bf16[64,1024]{1,0:T(8,128)(2,1)S(1)}, u32[]{:S(2)}, u32[]{:S(2)}) collective-permute-start(bf16[64,1024]{1,0:T(8,128)(2,1)} %d_own.5), channel_id=1, source_target_pairs={{0,2},{1,3},{2,0},{3,1},{4,6},{5,7},{6,4},{7,5}} | collective-permute-start | bytes 393224 | tf_op jit(solution)/shard_map/ppermute | solution.py:532
  9.2 8.8 %collective-permute-start = (bf16[128,1024]{1,0:T(8,128)(2,1)S(1)}, bf16[128,1024]{1,0:T(8,128)(2,1)S(1)}, u32[]{:S(2)}, u32[]{:S(2)}) collective-permute-start(bf16[128,1024]{1,0:T(8,128)(2,1)S(1)} %get-tuple-element.45.order.send), channel_id=1, source_target_pairs={{0,2},{1,3},{2,0},{3,1},{4,6},{5,7},{6,4},{7,5}} | collective-permute-start | bytes 786440 | tf_op jit(solution)/shard_map/ppermute | solution.py:532
  17.7 1.9 %collective-permute-start.3 = (bf16[64,1024]{1,0:T(8,128)(2,1)S(1)}, bf16[64,1024]{1,0:T(8,128)(2,1)S(1)}, u32[]{:S(2)}, u32[]{:S(2)}) collective-permute-start(bf16[64,1024]{1,0:T(8,128)(2,1)S(1)} %collective-permute-done.1.d_far), channel_id=1, source_target_pairs={{0,1},{1,0},{2,3},{3,2},{4,5},{5,4},{6,7},{7,6}} | collective-permute-start | bytes 393224 | tf_op jit(solution)/shard_map/ppermute | solution.py:532
  23.7 4.8 %collective-permute-start.4 = (f32[128,1024]{1,0:T(8,128)S(1)}, f32[128,1024]{1,0:T(8,128)S(1)}, u32[]{:S(2)}, u32[]{:S(2)}) collective-permute-start(f32[128,1024]{1,0:T(8,128)S(1)} %get-tuple-element.62), channel_id=1, source_target_pairs={{0,1},{1,0},{2,3},{3,2},{4,5},{5,4},{6,7},{7,6}} | collective-permute-start | bytes 1572872 | tf_op jit(solution)/shard_map/ppermute | solution.py:532
  24.0 8.4 %collective-permute-start.6 = (f32[64,1024]{1,0:T(8,128)S(1)}, f32[64,1024]{1,0:T(8,128)S(1)}, u32[]{:S(2)}, u32[]{:S(2)}) collective-permute-start(f32[64,1024]{1,0:T(8,128)S(1)} %get-tuple-element.69), channel_id=1, source_target_pairs={{0,2},{1,3},{2,0},{3,1},{4,6},{5,7},{6,4},{7,5}} | collective-permute-start | bytes 786440 | tf_op jit(solution)/shard_map/ppermute | solution.py:532
  25.1 7.3 %collective-permute-start.5 = (f32[64,1024]{1,0:T(8,128)S(1)}, f32[64,1024]{1,0:T(8,128)S(1)}, u32[]{:S(2)}, u32[]{:S(2)}) collective-permute-start(f32[64,1024]{1,0:T(8,128)S(1)} %get-tuple-element.68), channel_id=1, source_target_pairs={{0,1},{1,0},{2,3},{3,2},{4,5},{5,4},{6,7},{7,6}} | collective-permute-start | bytes 786440 | tf_op jit(solution)/shard_map/ppermute | solution.py:532
  32.6 5.8 %collective-permute-start.9 = (bf16[64,1024]{1,0:T(8,128)(2,1)S(1)}, bf16[64,1024]{1,0:T(8,128)(2,1)S(1)}, u32[]{:S(2)}, u32[]{:S(2)}) collective-permute-start(bf16[64,1024]{1,0:T(8,128)(2,1)S(1)} %dx_rows.1.order.dx), channel_id=1, source_target_pairs={{0,2},{1,3},{2,0},{3,1},{4,6},{5,7},{6,4},{7,5}} | collective-permute-start | bytes 393224 | tf_op jit(solution)/shard_map/ppermute | solution.py:532
  33.8 4.6 %collective-permute-start.8 = (bf16[64,1024]{1,0:T(8,128)(2,1)S(1)}, bf16[64,1024]{1,0:T(8,128)(2,1)S(1)}, u32[]{:S(2)}, u32[]{:S(2)}) collective-permute-start(bf16[64,1024]{1,0:T(8,128)(2,1)S(1)} %dx_rows.1.order.dx), channel_id=1, source_target_pairs={{0,1},{1,0},{2,3},{3,2},{4,5},{5,4},{6,7},{7,6}} | collective-permute-start | bytes 393224 | tf_op jit(solution)/shard_map/ppermute | solution.py:532
  33.8 9.5 %collective-permute-start.7 = (f32[64,1024]{1,0:T(8,128)S(1)}, f32[64,1024]{1,0:T(8,128)S(1)}, u32[]{:S(2)}, u32[]{:S(2)}) collective-permute-start(f32[64,1024]{1,0:T(8,128)S(1)} %get-tuple-element.71), channel_id=1, source_target_pairs={{0,2},{1,3},{2,0},{3,1},{4,6},{5,7},{6,4},{7,5}} | collective-permute-start | bytes 786440 | tf_op jit(solution)/shard_map/ppermute | solution.py:532

commit v13 on v12

--- a/solution.py
+++ b/solution.py
@@ -19,7 +19,7 @@
 DMA = pltpu.SemaphoreType.DMA
 TILE = 256
 ZERO_ROWS = 96
-FILL_COUNTS = ((22, 54, 13, 8, 8, 21, 5), (4, 50, 13, 9, 9, 23, 23))
+FILL_COUNTS = ((24, 54, 13, 9, 9, 19, 3), (4, 51, 13, 10, 10, 23, 20), (4, 57, 13, 12, 11, 26, 8))
 LATE = 6
 MIB = 1 << 20
 LOOKUP_VMEM = 48 * MIB
@@ -43,9 +43,10 @@
 
 
 def fill_range(part):
-    chip = lax.axis_index("tp") >> 1
-    (lo0, hi0), (lo1, hi1) = ((sum(c[:part]), sum(c[:part + 1])) for c in FILL_COUNTS)
-    return lo0 + chip * (lo1 - lo0), hi0 + chip * (hi1 - hi0)
+    group, chip = lax.axis_index("dp"), lax.axis_index("tp") >> 1
+    (lo0, hi0), (lo1, hi1), (lo2, hi2) = ((sum(c[:part]), sum(c[:part + 1])) for c in FILL_COUNTS)
+    pick = lambda a, b, c: group * c + (1 - group) * (a + chip * (b - a))
+    return pick(lo0, lo1, lo2), pick(hi0, hi1, hi2)
 
 
 def fill_start(zero, table_g, sem, part):
@@ -224,7 +225,7 @@
         du[rows, cols] = (g * (cdf + u * (0.5 * (1.0 - t * t)) * (GELU_C * (1.0 + 3.0 * GELU_A * (u * u))))).astype(BF)
 
 
-def share_kernel(send, got, d_own, d_far, w1, w2, gain, x_f, n_a, h_a, du_a, x_r, d_a, sems):
+def share_kernel(send, got, d_own, d_far, w1, w2, gain, x_f, n_a, h_a, du_a, d_far_s, x_r, d_a, d_r, sems):
     rows = d_own.shape[0]
     half = 2 * rows
     remote = swap_with_sibling()
@@ -234,12 +235,16 @@
         x_f[at, :] = send[at, :] + got[other, :]
         copies.append(remote(x_f.at[at], x_r.at[at], sems, k))
         copies[-1].start()
+    copies.append(remote(d_far, d_r, sems, 2))
+    copies[-1].start()
     for k, src in enumerate((d_own, d_far)):
         d_a[pl.ds(k * rows, rows), :] = src[...]
     mlp_half(x_f, d_a, n_a, h_a, du_a, (0, half), w1, w2, gain)
     for k in range(2):
         copies[k].wait()
         x_f[pl.ds(half + k * rows, rows), :] = x_r[pl.ds(k * rows, rows), :]
+    copies[2].wait()
+    d_far_s[...] = d_r[...]
 
 
 def share(send, got, d_own, d_far, w1, w2, gain):
@@ -248,10 +253,10 @@
     return pl.pallas_call(
         share_kernel,
         name="share",
-        out_shape=[sh((4 * rows, width), BF), sh((2 * rows, width), BF)] + [sh((2 * rows, hid), BF)] * 2,
+        out_shape=[sh((4 * rows, width), BF), sh((2 * rows, width), BF)] + [sh((2 * rows, hid), BF)] * 2 + [sh((rows, width), BF)],
         in_specs=[VMEM_SPEC] * 7,
-        out_specs=[VMEM_SPEC] * 4,
-        scratch_shapes=[VMEM((2 * rows, width), BF), VMEM((2 * rows, width), BF), DMA((2, 2))],
+        out_specs=[VMEM_SPEC] * 5,
+        scratch_shapes=[VMEM((2 * rows, width), BF), VMEM((2 * rows, width), BF), VMEM((rows, width), BF), DMA((2, 3))],
         compiler_params=pltpu.CompilerParams(collective_id=1, has_side_effects=True, vmem_limit_bytes=16 * MIB),
         cost_estimate=pl.CostEstimate(flops=3_000_000_000, bytes_accessed=MIB, transcendentals=0),
     )(send, got, d_own, d_far, w1, w2, gain)
@@ -293,7 +298,7 @@
     )(x_f, *ds, n_a, h_a, du_a, w1, w2, gain, zero, table_g)
 
 
-def sums_kernel(dn_b1, du, h, w1, w2, dn_own, dn_far, y_a, y_b, dn_r, sems):
+def sums_kernel(dn_b0, dn_b1, du, h, w1, w2, dn_own, dn_far, y_a, y_b, dn_r, sems):
     rows, width = dn_own.shape
     half = 2 * rows
     remote = swap_with_sibling()
@@ -308,23 +313,24 @@
         cols = pl.ds(j * TILE, TILE)
         y = mm(h[...], w2[:, cols], 1, 0)
         y_a[:, cols] = y[:half]
-        y_b[:, cols] = y[half:]
+        y_b[pl.ds(0, half), cols] = y[half:]
+    y_b[pl.ds(half, rows), :] = dn_b0[...]
     copy.wait()
     dn_far[...] += dn_r[...]
 
 
-def sums(dn_b1, du, h, w1, w2):
+def sums(dn_b0, dn_b1, du, h, w1, w2):
     rows, width = dn_b1.shape
     return pl.pallas_call(
         sums_kernel,
         name="sums",
-        out_shape=[sh((rows, width), F32)] * 2 + [sh((2 * rows, width), F32)] * 2,
-        in_specs=[VMEM_SPEC] * 5,
+        out_shape=[sh((rows, width), F32)] * 2 + [sh((2 * rows, width), F32), sh((3 * rows, width), F32)],
+        in_specs=[VMEM_SPEC] * 6,
         out_specs=[VMEM_SPEC] * 4,
         scratch_shapes=[VMEM((rows, width), F32), DMA((2, 1))],
         compiler_params=pltpu.CompilerParams(collective_id=2, has_side_effects=True, vmem_limit_bytes=16 * MIB),
         cost_estimate=pl.CostEstimate(flops=4_000_000_000, bytes_accessed=4 * MIB, transcendentals=0),
-    )(dn_b1, du, h, w1, w2)
+    )(dn_b0, dn_b1, du, h, w1, w2)
 
 
 def grads1_kernel(n, du, zero, order, table_in, dw1, table_g, dw1_v, s_zero, s_w):
@@ -387,18 +393,19 @@
     )(h, d_full, y_a, y_sib, zero, table_g)
 
 
-def dx_kernel(dn_own, dn_sib, g2, x_own, d_own, gain, order, dx):
+def dx_kernel(dn_own, y_sib, g2, x_own, d_own, gain, order, dx):
     gain_f = gain[...].astype(F32).reshape(1, dx.shape[1])
     for j in range(dx.shape[0] // 16):
         at = pl.ds(j * 16, 16)
-        a = (dn_own[at, :] + dn_sib[at, :] + g2[at, :]) * gain_f
+        sib_at = pl.ds(2 * dx.shape[0] + j * 16, 16)
+        a = (dn_own[at, :] + y_sib[sib_at, :] + g2[at, :]) * gain_f
         x = x_own[at, :].astype(F32)
         r = lax.rsqrt(jnp.mean(x * x, axis=-1, keepdims=True) + EPS)
         proj = jnp.mean(a * x, axis=-1, keepdims=True)
         dx[at, :] = (d_own[at, :].astype(F32) + r * (a - x * r * r * proj)).astype(BF)
 
 
-def dx_rows(dn_own, dn_sib, g2, x_own, d_own, gain, order):
+def dx_rows(dn_own, y_sib, g2, x_own, d_own, gain, order):
     return pl.pallas_call(
         dx_kernel,
         name="dx_rows",
@@ -407,7 +414,7 @@
         out_specs=VMEM_SPEC,
         compiler_params=pltpu.CompilerParams(vmem_limit_bytes=4 * MIB),
         cost_estimate=pl.CostEstimate(flops=1_000_000_000, bytes_accessed=MIB, transcendentals=0),
-    )(dn_own, dn_sib, g2, x_own, d_own, gain, order)
+    )(dn_own, y_sib, g2, x_own, d_own, gain, order)
 
 
 def fill3_kernel(zero, order, table_in, token, table_g, s_zero):
@@ -539,17 +546,15 @@
         got = permute(send, 2)
         d_own_s = permute(d_out, 1)
         puts, w2, d_table = fill1(rows_mine, zero, w2, send, d_table)
-        d_far_s = permute(d_far, 1)
-        x_f, n_a, h_a, du_a = share(send, got, d_out, d_far, w1, w2, gain)
+        x_f, n_a, h_a, du_a, d_far_s = share(send, got, d_out, d_far, w1, w2, gain)
         ds = (d_out, d_far, d_own_s, d_far_s)
         n, h, du, d_full, dn_b0, dn_b1, d_table = mlp(x_f, ds, n_a, h_a, du_a, w1, w2, gain, zero, d_table)
-        dn_own, dn_far, y_a, y_b = sums(dn_b1, du, h, w1, w2)
+        dn_own, dn_far, y_a, y_b = sums(dn_b0, dn_b1, du, h, w1, w2)
         g2 = permute(dn_far, 2)
-        dn_sib = permute(dn_b0, 1)
         y_sib = permute(y_b, 1)
         d_w1, d_table = grads1(n, du, zero, dn_own, d_table)
         d_w2, y_own, y_far, d_table = grads2(h, d_full, y_a, y_sib, zero, d_table)
-        dx = dx_rows(dn_own, dn_sib, g2, x_f, d_out, gain, y_own)
+        dx = dx_rows(dn_own, y_sib, g2, x_f, d_out, gain, y_own)
         dx_far = permute(dx, 2)
         dx_sib = permute(dx, 1)
         dx, y_far = lax.optimization_barrier((dx, y_far))

time: 44.6 us -> 44.6 us (level)
    ppermute x10 -> x8, waiting for transfers between devices: 2.45 us -> 2.79 us  [permute(): return lax.ppermute(x, 'tp', [(i, i ^ hop) for i in range(tp)])]
    ppermute x10 -> x8, starting transfers between devices: 6.42 us -> 6.29 us  [permute(): return lax.ppermute(x, 'tp', [(i, i ^ hop) for i in range(tp)])]
  transfers between devices with their start and end apart: 10 -> 8, of which waited for: 4 -> 4; matrix products, arithmetic and copies ran while one was open for 0% -> 0% of each run, Pallas kernels for 67% -> 67%
where the time goes in v13:
time: 44.6 us; the launch traced here: 44.3 us
  Pallas kernels  34.4 us (77%)
  starting transfers between devices  6.29 us (14%)
  waiting for transfers between devices  2.79 us (6%)
  between operations  0.77 us (2%)
    pallas_call x1, Pallas kernels, fill1(): pl.pallas_call(fill1_kernel, name='fill1', out_shape=[sh((2 * tokens,), I...  7.28 us
    ppermute x8, starting transfers between devices, permute(): return lax.ppermute(x, 'tp', [(i, i ^ hop) for i in range(tp)])  6.29 us
    pallas_call x1, Pallas kernels, lookup(): pl.pallas_call(lookup_kernel, name='lookup', out_shape=[sh((tokens, width...  5.47 us
    pallas_call x1, Pallas kernels, grads1(): pl.pallas_call(grads1_kernel, name='grads1', out_shape=[sh((width, hid),...  3.46 us
    pallas_call x1, Pallas kernels, grads2(): pl.pallas_call(grads2_kernel, name='grads2', out_shape=[sh((hid, width),...  3.16 us
    pallas_call x1, Pallas kernels, fill3(): pl.pallas_call(fill3_kernel, name='fill3', out_shape=[sh((8, 128), F32),...  3 us
    ppermute x8, waiting for transfers between devices, permute(): return lax.ppermute(x, 'tp', [(i, i ^ hop) for i in range(tp)])  2.79 us
    pallas_call x1, Pallas kernels, put_rows(): pl.pallas_call(put_kernel, name='put_rows', out_shape=[sh(table_g.shape,...  2.4 us
  transfers between devices with their start and end apart: 8, of which 4 were waited for; matrix products, arithmetic and copies ran while one was open for 0% of the time, Pallas kernels for 67%

profile of v13, /device:TPU:0, one launch (start us, length us, event | category | flops | bytes accessed | tf_op | source)
XLA Modules:
  0.0 44.3 jit_solution(11000125417434165095)
XLA Ops:
  0.6 0.0 copy-start
  0.6 0.0 copy-start.1
  0.7 0.9 %collective-permute-start.2 = (bf16[64,1024]{1,0:T(8,128)(2,1)}, bf16[64,1024]{1,0:T(8,128)(2,1)S(1)}, u32[]{:S(2)}, u32[]{:S(2)}) collective-permute-start(bf16[64,1024]{1,0:T(8,128)(2,1)} %d_own.5), channel_id=1, source_target_pairs={{0,1},{1,0},{2,3},{3,2},{4,5},{5,4},{6,7},{7,6}} | collective-permute-start | bytes 393224 | tf_op jit(solution)/shard_map/ppermute | solution.py:539
  1.5 5.5 %lookup.1 = (bf16[256,1024]{1,0:T(8,128)(2,1)S(1)}, s32[1,256]{1,0:T(1,128)S(1)}, bf16[256,256]{1,0:T(8,128)(2,1)S(1)}, f32[96,1024]{1,0:T(8,128)S(1)}, f32[12576,1024]{1,0:T(8,128)}) custom-call(s32[256]{0:T(256)} %ids.1, s32[1,256]{1,0:T(1,128)} %bitcast.1, bf16[12576,1024]{1,0:T(8,128)(2,1)} %table.1), custom_call_target="tpu_custom_call" | custom-call | flops 5000000000 | bytes 10485760 | tf_op jit(solution)/shard_map/lookup/pallas_call | solution.py:127
  7.0 0.6 %collective-permute-start.1 = (bf16[64,1024]{1,0:T(8,128)(2,1)}, bf16[64,1024]{1,0:T(8,128)(2,1)S(1)}, u32[]{:S(2)}, u32[]{:S(2)}) collective-permute-start(bf16[64,1024]{1,0:T(8,128)(2,1)} %d_own.5), channel_id=1, source_target_pairs={{0,2},{1,3},{2,0},{3,1},{4,6},{5,7},{6,4},{7,5}} | collective-permute-start | bytes 393224 | tf_op jit(solution)/shard_map/ppermute | solution.py:539
  7.6 1.6 %pair.1 = (bf16[128,1024]{1,0:T(8,128)(2,1)S(1)}, bf16[1024,1024]{1,0:T(8,128)(2,1)S(1)}) custom-call(bf16[256,1024]{1,0:T(8,128)(2,1)S(1)} %get-tuple-element.45.part, bf16[1024,1024]{1,0:T(8,128)(2,1)} %w1.1), custom_call_target="tpu_custom_call" | custom-call | flops 3000000000 | bytes 1048576 | tf_op jit(solution)/shard_map/pair/pallas_call | solution.py:159
  9.2 1.5 %collective-permute-start = (bf16[128,1024]{1,0:T(8,128)(2,1)S(1)}, bf16[128,1024]{1,0:T(8,128)(2,1)S(1)}, u32[]{:S(2)}, u32[]{:S(2)}) collective-permute-start(bf16[128,1024]{1,0:T(8,128)(2,1)S(1)} %get-tuple-element.46.order.send), channel_id=1, source_target_pairs={{0,2},{1,3},{2,0},{3,1},{4,6},{5,7},{6,4},{7,5}} | collective-permute-start | bytes 786440 | tf_op jit(solution)/shard_map/ppermute | solution.py:539
  10.7 7.3 %fill1.1 = (s32[512]{0:T(512)S(1)}, bf16[1024,1024]{1,0:T(8,128)(2,1)S(1)}, f32[12576,1024]{1,0:T(8,128)}) custom-call(s32[1,256]{1,0:T(1,128)S(1)} %get-tuple-element.49.rows_mine, f32[96,1024]{1,0:T(8,128)S(1)} %get-tuple-element.50.zero, bf16[1024,1024]{1,0:T(8,128)(2,1)} %w2.1, ...), custom_call_target="tpu_custom_call", output_to_operand_aliasing={{2}: (4, {})} | custom-call | flops 8999999488 | bytes 20971520 | tf_op jit(solution)/shard_map/fill1/pallas_call | solution.py:195
  18.0 0.0 collective-permute-done.1.d_far
  18.0 0.2 collective-permute-done.got
  18.2 0.0 copy-done
  18.2 0.0 copy-done.1
  18.2 1.8 %share.1 = (bf16[256,1024]{1,0:T(8,128)(2,1)S(1)}, bf16[128,1024]{1,0:T(8,128)(2,1)S(1)}, bf16[128,1024]{1,0:T(8,128)(2,1)S(1)}, bf16[128,1024]{1,0:T(8,128)(2,1)S(1)}, bf16[64,1024]{1,0:T(8,128)(2,1)S(1)}) custom-call(bf16[128,1024]{1,0:T(8,128)(2,1)S(1)} %get-tuple-element.46.order.send, bf16[128,1024]{1,0:T(8,128)(2,1)S(1)} %collective-permute-done.got, ...), custom_call_target="tpu_custom_call" | custom-call | flops 3000000000 | bytes 1048576 | tf_op jit(solution)/shard_map/share/pallas_call | solution.py:253
  20.1 0.0 collective-permute-done.2.d_own_s
  20.1 2.3 %mlp.1 = (bf16[256,1024]{1,0:T(8,128)(2,1)S(1)}, bf16[256,1024]{1,0:T(8,128)(2,1)S(1)}, bf16[256,1024]{1,0:T(8,128)(2,1)S(1)}, bf16[256,1024]{1,0:T(8,128)(2,1)S...) custom-call(bf16[256,1024]{1,0:T(8,128)(2,1)S(1)} %get-tuple-element, ...), custom_call_target="tpu_custom_call", output_to_operand_aliasing={{6}: (12, {})} | custom-call | flops 6000000000 | bytes 4194304 | tf_op jit(solution)/shard_map/mlp/pallas_call | solution.py:287
  22.4 1.6 %sums.1 = (f32[64,1024]{1,0:T(8,128)S(1)}, f32[64,1024]{1,0:T(8,128)S(1)}, f32[128,1024]{1,0:T(8,128)S(1)}, f32[192,1024]{1,0:T(8,128)S(1)}) custom-call(f32[64,1024]{1,0:T(8,128)S(1)} %get-tuple-element.61.dn_b0, f32[64,1024]{1,0:T(8,128)S(1)} %get-tuple-element.62.dn_b1, bf16[256,1024]{1,0:T(8,128)(2,1)S(1)} %get-tuple-element.63.du, ...), custom_call_target="tpu_custom_call" | custom-call | flops 4000000000 | bytes 4194304 | tf_op jit(solution)/shard_map/sums/pallas_call | solution.py:324
  24.0 0.4 collective-permute-start.3
  24.4 0.9 %collective-permute-start.4 = (f32[64,1024]{1,0:T(8,128)S(1)}, f32[64,1024]{1,0:T(8,128)S(1)}, u32[]{:S(2)}, u32[]{:S(2)}) collective-permute-start(f32[64,1024]{1,0:T(8,128)S(1)} %get-tuple-element.71), channel_id=1, source_target_pairs={{0,2},{1,3},{2,0},{3,1},{4,6},{5,7},{6,4},{7,5}} | collective-permute-start | bytes 786440 | tf_op jit(solution)/shard_map/ppermute | solution.py:539
  25.3 3.5 %grads1.1 = (f32[1024,1024]{1,0:T(8,128)}, f32[12576,1024]{1,0:T(8,128)}) custom-call(bf16[256,1024]{1,0:T(8,128)(2,1)S(1)} %get-tuple-element.66.n, bf16[256,1024]{1,0:T(8,128)(2,1)S(1)} %get-tuple-element.63.du, f32[96,1024]{1,0:T(8,128)S(1)} %get-tuple-element.50.zero, ...), custom_call_target="tpu_custom_call", output_to_operand_aliasing={{1}: (4, {})} | custom-call | flops 4000000000 | bytes 8388608 | tf_op jit(solution)/shard_map/grads1/pallas_call | solution.py:351
  28.8 0.0 collective-permute-done.3.y_sib
  28.8 3.2 %grads2.1 = (f32[1024,1024]{1,0:T(8,128)}, f32[64,1024]{1,0:T(8,128)S(1)}, f32[64,1024]{1,0:T(8,128)S(1)}, f32[12576,1024]{1,0:T(8,128)}) custom-call(bf16[256,1024]{1,0:T(8,128)(2,1)S(1)} %get-tuple-element.59.h, bf16[256,1024]{1,0:T(8,128)(2,1)S(1)} %get-tuple-element.60.d_full, ...), custom_call_target="tpu_custom_call", output_to_operand_aliasing={{3}: (5, {})} | custom-call | flops 4000000000 | bytes 8388608 | tf_op jit(solution)/shard_map/grads2/pallas_call | solution.py:383
  32.0 0.8 %collective-permute-done.4.g2 = f32[64,1024]{1,0:T(8,128)S(1)} collective-permute-done((f32[64,1024]{1,0:T(8,128)S(1)}, f32[64,1024]{1,0:T(8,128)S(1)}, u32[]{:S(2)}, u32[]{:S(2)}) %collective-permute-start.4) | collective-permute-done | bytes 262176 | tf_op jit(solution)/shard_map/ppermute | solution.py:539
  32.8 0.2 dx_rows.1.order.dx
  32.9 0.9 %collective-permute-start.7 = (bf16[64,1024]{1,0:T(8,128)(2,1)S(1)}, bf16[64,1024]{1,0:T(8,128)(2,1)S(1)}, u32[]{:S(2)}, u32[]{:S(2)}) collective-permute-start(bf16[64,1024]{1,0:T(8,128)(2,1)S(1)} %dx_rows.1.order.dx), channel_id=1, source_target_pairs={{0,2},{1,3},{2,0},{3,1},{4,6},{5,7},{6,4},{7,5}} | collective-permute-start | bytes 393224 | tf_op jit(solution)/shard_map/ppermute | solution.py:539
  33.9 0.0 collective-permute-start.6
  33.9 1.1 %collective-permute-start.5 = (f32[64,1024]{1,0:T(8,128)S(1)}, f32[64,1024]{1,0:T(8,128)S(1)}, u32[]{:S(2)}, u32[]{:S(2)}) collective-permute-start(f32[64,1024]{1,0:T(8,128)S(1)} %get-tuple-element.73), channel_id=1, source_target_pairs={{0,2},{1,3},{2,0},{3,1},{4,6},{5,7},{6,4},{7,5}} | collective-permute-start | bytes 786440 | tf_op jit(solution)/shard_map/ppermute | solution.py:539
  35.0 3.0 %fill3.1 = (f32[8,128]{1,0:T(8,128)S(1)}, f32[12576,1024]{1,0:T(8,128)}) custom-call(f32[96,1024]{1,0:T(8,128)S(1)} %get-tuple-element.50.zero, bf16[64,1024]{1,0:T(8,128)(2,1)S(1)} %dx_rows.1.order.dx, f32[12576,1024]{1,0:T(8,128)} %get-tuple-element.77.table_in), custom_call_target="tpu_custom_call", output_to_operand_aliasing={{1}: (2, {})} | custom-call | flops 4000000000 | bytes 16777216 | tf_op jit(solution)/shard_map/fill3/pallas_call | solution.py:427
  38.0 0.9 %collective-permute-done.7.dx_far = bf16[64,1024]{1,0:T(8,128)(2,1)S(1)} collective-permute-done((bf16[64,1024]{1,0:T(8,128)(2,1)S(1)}, bf16[64,1024]{1,0:T(8,128)(2,1)S(1)}, u32[]{:S(2)}, u32[]{:S(2)}) %collective-permute-start.7) | collective-permute-done | bytes 131104 | tf_op jit(solution)/shard_map/ppermute | solution.py:539
  38.9 0.0 collective-permute-done.6.dx_sib
  38.9 1.4 %dx_all.1.dx = bf16[256,1024]{1,0:T(8,128)(2,1)S(1)} custom-call(bf16[64,1024]{1,0:T(8,128)(2,1)S(1)} %dx_rows.1.order.dx, bf16[64,1024]{1,0:T(8,128)(2,1)S(1)} %collective-permute-done.6.dx_sib, bf16[64,1024]{1,0:T(8,128)(2,1)S(1)} %collective-permute-done.7.dx_far, f32[8,128]{1,0:T(8,128)S(1)} %get-tuple-element.78.order), custom_call_target="tpu_custom_call" | custom-call | flops 2000000000 | bytes 1048576 | tf_op jit(solution)/shard_map/dx_all/pallas_call | solution.py:455
  40.3 2.4 %put_rows.1 = (f32[12576,1024]{1,0:T(8,128)}, f32[8,128]{1,0:T(8,128)S(1)}) custom-call(s32[512]{0:T(512)S(1)} %get-tuple-element.74.puts, bf16[256,256]{1,0:T(8,128)(2,1)S(1)} %get-tuple-element.75.same, bf16[256,1024]{1,0:T(8,128)(2,1)S(1)} %dx_all.1.dx, f32[96,1024]{1,0:T(8,128)S(1)} %get-tuple-element.50.zero, ...), custom_call_target="tpu_custom_call", output_to_operand_aliasing={{0}: (4, {})} | custom-call | flops 3000000000 | bytes 2097152 | tf_op jit(solution)/shard_map/put_rows/pallas_call | solution.py:506
  42.7 0.9 %collective-permute-done.5.y_in = f32[64,1024]{1,0:T(8,128)S(1)} collective-permute-done((f32[64,1024]{1,0:T(8,128)S(1)}, f32[64,1024]{1,0:T(8,128)S(1)}, u32[]{:S(2)}, u32[]{:S(2)}) %collective-permute-start.5) | collective-permute-done | bytes 262176 | tf_op jit(solution)/shard_map/ppermute | solution.py:539
  43.6 0.7 %finish.1 = bf16[64,1024]{1,0:T(8,128)(2,1)} custom-call(bf16[256,1024]{1,0:T(8,128)(2,1)S(1)} %get-tuple-element.53.x_f.x_own.x, f32[64,1024]{1,0:T(8,128)S(1)} %get-tuple-element.70.order.y, f32[64,1024]{1,0:T(8,128)S(1)} %collective-permute-done.5.y_in, f32[8,128]{1,0:T(8,128)S(1)} %get-tuple-element.80.order), custom_call_target="tpu_custom_call" | custom-call | flops 1000000000 | bytes 1048576 | tf_op jit(solution)/shard_map/finish/pallas_call | solution.py:524
Async XLA Ops:
  0.6 17.6 %copy-start = (bf16[64,1024]{1,0:T(8,128)(2,1)S(1)}, bf16[64,1024]{1,0:T(8,128)(2,1)}, u32[]{:S(2)}) copy-start(bf16[64,1024]{1,0:T(8,128)(2,1)} %d_own.5) | copy-start | bytes 393220
  0.6 17.6 %copy-start.1 = (bf16[1024]{0:T(1024)(128)(2,1)S(1)}, bf16[1024]{0:T(1024)(128)(2,1)}, u32[]{:S(2)}) copy-start(bf16[1024]{0:T(1024)(128)(2,1)} %gain.5) | copy-start | bytes 6148
  0.7 19.4 %collective-permute-start.2 = (bf16[64,1024]{1,0:T(8,128)(2,1)}, bf16[64,1024]{1,0:T(8,128)(2,1)S(1)}, u32[]{:S(2)}, u32[]{:S(2)}) collective-permute-start(bf16[64,1024]{1,0:T(8,128)(2,1)} %d_own.5), channel_id=1, source_target_pairs={{0,1},{1,0},{2,3},{3,2},{4,5},{5,4},{6,7},{7,6}} | collective-permute-start | bytes 393224 | tf_op jit(solution)/shard_map/ppermute | solution.py:539
  7.0 11.0 %collective-permute-start.1 = (bf16[64,1024]{1,0:T(8,128)(2,1)}, bf16[64,1024]{1,0:T(8,128)(2,1)S(1)}, u32[]{:S(2)}, u32[]{:S(2)}) collective-permute-start(bf16[64,1024]{1,0:T(8,128)(2,1)} %d_own.5), channel_id=1, source_target_pairs={{0,2},{1,3},{2,0},{3,1},{4,6},{5,7},{6,4},{7,5}} | collective-permute-start | bytes 393224 | tf_op jit(solution)/shard_map/ppermute | solution.py:539
  9.2 9.0 %collective-permute-start = (bf16[128,1024]{1,0:T(8,128)(2,1)S(1)}, bf16[128,1024]{1,0:T(8,128)(2,1)S(1)}, u32[]{:S(2)}, u32[]{:S(2)}) collective-permute-start(bf16[128,1024]{1,0:T(8,128)(2,1)S(1)} %get-tuple-element.46.order.send), channel_id=1, source_target_pairs={{0,2},{1,3},{2,0},{3,1},{4,6},{5,7},{6,4},{7,5}} | collective-permute-start | bytes 786440 | tf_op jit(solution)/shard_map/ppermute | solution.py:539
  24.0 4.8 %collective-permute-start.3 = (f32[192,1024]{1,0:T(8,128)S(1)}, f32[192,1024]{1,0:T(8,128)S(1)}, u32[]{:S(2)}, u32[]{:S(2)}) collective-permute-start(f32[192,1024]{1,0:T(8,128)S(1)} %get-tuple-element.65), channel_id=1, source_target_pairs={{0,1},{1,0},{2,3},{3,2},{4,5},{5,4},{6,7},{7,6}} | collective-permute-start | bytes 2359304 | tf_op jit(solution)/shard_map/ppermute | solution.py:539
  24.4 8.4 %collective-permute-start.4 = (f32[64,1024]{1,0:T(8,128)S(1)}, f32[64,1024]{1,0:T(8,128)S(1)}, u32[]{:S(2)}, u32[]{:S(2)}) collective-permute-start(f32[64,1024]{1,0:T(8,128)S(1)} %get-tuple-element.71), channel_id=1, source_target_pairs={{0,2},{1,3},{2,0},{3,1},{4,6},{5,7},{6,4},{7,5}} | collective-permute-start | bytes 786440 | tf_op jit(solution)/shard_map/ppermute | solution.py:539
  32.9 5.9 %collective-permute-start.7 = (bf16[64,1024]{1,0:T(8,128)(2,1)S(1)}, bf16[64,1024]{1,0:T(8,128)(2,1)S(1)}, u32[]{:S(2)}, u32[]{:S(2)}) collective-permute-start(bf16[64,1024]{1,0:T(8,128)(2,1)S(1)} %dx_rows.1.order.dx), channel_id=1, source_target_pairs={{0,2},{1,3},{2,0},{3,1},{4,6},{5,7},{6,4},{7,5}} | collective-permute-start | bytes 393224 | tf_op jit(solution)/shard_map/ppermute | solution.py:539
  33.9 5.0 %collective-permute-start.6 = (bf16[64,1024]{1,0:T(8,128)(2,1)S(1)}, bf16[64,1024]{1,0:T(8,128)(2,1)S(1)}, u32[]{:S(2)}, u32[]{:S(2)}) collective-permute-start(bf16[64,1024]{1,0:T(8,128)(2,1)S(1)} %dx_rows.1.order.dx), channel_id=1, source_target_pairs={{0,1},{1,0},{2,3},{3,2},{4,5},{5,4},{6,7},{7,6}} | collective-permute-start | bytes 393224 | tf_op jit(solution)/shard_map/ppermute | solution.py:539
  33.9 9.7 %collective-permute-start.5 = (f32[64,1024]{1,0:T(8,128)S(1)}, f32[64,1024]{1,0:T(8,128)S(1)}, u32[]{:S(2)}, u32[]{:S(2)}) collective-permute-start(f32[64,1024]{1,0:T(8,128)S(1)} %get-tuple-element.73), channel_id=1, source_target_pairs={{0,2},{1,3},{2,0},{3,1},{4,6},{5,7},{6,4},{7,5}} | collective-permute-start | bytes 786440 | tf_op jit(solution)/shard_map/ppermute | solution.py:539

commit v14 on v12

--- a/solution.py
+++ b/solution.py
@@ -19,7 +19,7 @@
 DMA = pltpu.SemaphoreType.DMA
 TILE = 256
 ZERO_ROWS = 96
-FILL_COUNTS = ((22, 54, 13, 8, 8, 21, 5), (4, 50, 13, 9, 9, 23, 23))
+FILL_COUNTS = ((22, 54, 2, 10, 10, 26, 7), (3, 50, 2, 9, 9, 31, 27), (4, 57, 13, 10, 9, 27, 11))
 LATE = 6
 MIB = 1 << 20
 LOOKUP_VMEM = 48 * MIB
@@ -43,9 +43,10 @@
 
 
 def fill_range(part):
-    chip = lax.axis_index("tp") >> 1
-    (lo0, hi0), (lo1, hi1) = ((sum(c[:part]), sum(c[:part + 1])) for c in FILL_COUNTS)
-    return lo0 + chip * (lo1 - lo0), hi0 + chip * (hi1 - hi0)
+    group, chip = lax.axis_index("dp"), lax.axis_index("tp") >> 1
+    (lo0, hi0), (lo1, hi1), (lo2, hi2) = ((sum(c[:part]), sum(c[:part + 1])) for c in FILL_COUNTS)
+    pick = lambda a, b, c: group * c + (1 - group) * (a + chip * (b - a))
+    return pick(lo0, lo1, lo2), pick(hi0, hi1, hi2)
 
 
 def fill_start(zero, table_g, sem, part):

time: 44.6 us -> 44.6 us (level)
  Pallas kernels: 34.3 us -> 35.4 us
  waiting for transfers between devices: 2.45 us -> 1.6 us
    ppermute x10, waiting for transfers between devices: 2.45 us -> 1.6 us  [permute(): return lax.ppermute(x, 'tp', [(i, i ^ hop) for i in range(tp)])]
    pallas_call x1, Pallas kernels: 3.23 us -> 3.82 us  [fill3(): pl.pallas_call(fill3_kernel, name='fill3', out_shape=[sh((8, 128), F32),...]
  transfers between devices with their start and end apart: 10 -> 10, of which waited for: 4 -> 4; matrix products, arithmetic and copies ran while one was open for 0% -> 0% of each run, Pallas kernels for 67% -> 70%
where the time goes in v14:
time: 44.6 us; the launch traced here: 44.2 us
  Pallas kernels  35.4 us (79%)
  starting transfers between devices  6.44 us (14%)
  waiting for transfers between devices  1.6 us (4%)
  between operations  0.79 us (2%)
    pallas_call x1, Pallas kernels, fill1(): pl.pallas_call(fill1_kernel, name='fill1', out_shape=[sh((2 * tokens,), I...  7.28 us
    ppermute x10, starting transfers between devices, permute(): return lax.ppermute(x, 'tp', [(i, i ^ hop) for i in range(tp)])  6.44 us
    pallas_call x1, Pallas kernels, lookup(): pl.pallas_call(lookup_kernel, name='lookup', out_shape=[sh((tokens, width...  5.19 us
    pallas_call x1, Pallas kernels, fill3(): pl.pallas_call(fill3_kernel, name='fill3', out_shape=[sh((8, 128), F32),...  3.82 us
    pallas_call x1, Pallas kernels, grads1(): pl.pallas_call(grads1_kernel, name='grads1', out_shape=[sh((width, hid),...  3.59 us
    pallas_call x1, Pallas kernels, grads2(): pl.pallas_call(grads2_kernel, name='grads2', out_shape=[sh((hid, width),...  3.29 us
    pallas_call x1, Pallas kernels, put_rows(): pl.pallas_call(put_kernel, name='put_rows', out_shape=[sh(table_g.shape,...  2.92 us
    pallas_call x1, Pallas kernels, mlp(): pl.pallas_call(mlp_kernel, name='mlp', out_shape=[sh((tokens, width), BF)...  2.06 us
  transfers between devices with their start and end apart: 10, of which 4 were waited for; matrix products, arithmetic and copies ran while one was open for 0% of the time, Pallas kernels for 70%

profile of v14, /device:TPU:0, one launch (start us, length us, event | category | flops | bytes accessed | tf_op | source)
XLA Modules:
  0.0 44.2 jit_solution(10997068935688269474)
XLA Ops:
  0.6 0.0 copy-start
  0.6 0.0 copy-start.1
  0.7 0.9 %collective-permute-start.2 = (bf16[64,1024]{1,0:T(8,128)(2,1)}, bf16[64,1024]{1,0:T(8,128)(2,1)S(1)}, u32[]{:S(2)}, u32[]{:S(2)}) collective-permute-start(bf16[64,1024]{1,0:T(8,128)(2,1)} %d_own.5), channel_id=1, source_target_pairs={{0,1},{1,0},{2,3},{3,2},{4,5},{5,4},{6,7},{7,6}} | collective-permute-start | bytes 393224 | tf_op jit(solution)/shard_map/ppermute | solution.py:533
  1.5 5.2 %lookup.1 = (bf16[256,1024]{1,0:T(8,128)(2,1)S(1)}, s32[1,256]{1,0:T(1,128)S(1)}, bf16[256,256]{1,0:T(8,128)(2,1)S(1)}, f32[96,1024]{1,0:T(8,128)S(1)}, f32[12576,1024]{1,0:T(8,128)}) custom-call(s32[256]{0:T(256)} %ids.1, s32[1,256]{1,0:T(1,128)} %bitcast.1, bf16[12576,1024]{1,0:T(8,128)(2,1)} %table.1), custom_call_target="tpu_custom_call" | custom-call | flops 5000000000 | bytes 10485760 | tf_op jit(solution)/shard_map/lookup/pallas_call | solution.py:127
  6.7 0.9 %collective-permute-start.1 = (bf16[64,1024]{1,0:T(8,128)(2,1)}, bf16[64,1024]{1,0:T(8,128)(2,1)S(1)}, u32[]{:S(2)}, u32[]{:S(2)}) collective-permute-start(bf16[64,1024]{1,0:T(8,128)(2,1)} %d_own.5), channel_id=1, source_target_pairs={{0,2},{1,3},{2,0},{3,1},{4,6},{5,7},{6,4},{7,5}} | collective-permute-start | bytes 393224 | tf_op jit(solution)/shard_map/ppermute | solution.py:533
  7.6 1.6 %pair.1 = (bf16[128,1024]{1,0:T(8,128)(2,1)S(1)}, bf16[1024,1024]{1,0:T(8,128)(2,1)S(1)}) custom-call(bf16[256,1024]{1,0:T(8,128)(2,1)S(1)} %get-tuple-element.44.part, bf16[1024,1024]{1,0:T(8,128)(2,1)} %w1.1), custom_call_target="tpu_custom_call" | custom-call | flops 3000000000 | bytes 1048576 | tf_op jit(solution)/shard_map/pair/pallas_call | solution.py:159
  9.2 1.2 %collective-permute-start = (bf16[128,1024]{1,0:T(8,128)(2,1)S(1)}, bf16[128,1024]{1,0:T(8,128)(2,1)S(1)}, u32[]{:S(2)}, u32[]{:S(2)}) collective-permute-start(bf16[128,1024]{1,0:T(8,128)(2,1)S(1)} %get-tuple-element.45.order.send), channel_id=1, source_target_pairs={{0,2},{1,3},{2,0},{3,1},{4,6},{5,7},{6,4},{7,5}} | collective-permute-start | bytes 786440 | tf_op jit(solution)/shard_map/ppermute | solution.py:533
  10.4 7.3 %fill1.1 = (s32[512]{0:T(512)S(1)}, bf16[1024,1024]{1,0:T(8,128)(2,1)S(1)}, f32[12576,1024]{1,0:T(8,128)}) custom-call(s32[1,256]{1,0:T(1,128)S(1)} %get-tuple-element.48.rows_mine, f32[96,1024]{1,0:T(8,128)S(1)} %get-tuple-element.49.zero, bf16[1024,1024]{1,0:T(8,128)(2,1)} %w2.1, ...), custom_call_target="tpu_custom_call", output_to_operand_aliasing={{2}: (4, {})} | custom-call | flops 8999999488 | bytes 20971520 | tf_op jit(solution)/shard_map/fill1/pallas_call | solution.py:195
  17.7 0.0 collective-permute-done.1.d_far
  17.7 0.0 collective-permute-start.3
  17.8 0.2 collective-permute-done.got
  18.0 0.0 copy-done
  18.0 0.0 copy-done.1
  18.0 1.7 %share.1 = (bf16[256,1024]{1,0:T(8,128)(2,1)S(1)}, bf16[128,1024]{1,0:T(8,128)(2,1)S(1)}, bf16[128,1024]{1,0:T(8,128)(2,1)S(1)}, bf16[128,1024]{1,0:T(8,128)(2,1)S(1)}) custom-call(bf16[128,1024]{1,0:T(8,128)(2,1)S(1)} %get-tuple-element.45.order.send, bf16[128,1024]{1,0:T(8,128)(2,1)S(1)} %collective-permute-done.got, bf16[64,1024]{1,0:T(8,128)(2,1)S(1)} %copy-done, ...), custom_call_target="tpu_custom_call" | custom-call | flops 3000000000 | bytes 1048576 | tf_op jit(solution)/shard_map/share/pallas_call | solution.py:249
  19.6 0.0 collective-permute-done.2.d_own_s
  19.7 0.0 collective-permute-done.3.d_far_s
  19.7 2.1 %mlp.1 = (bf16[256,1024]{1,0:T(8,128)(2,1)S(1)}, bf16[256,1024]{1,0:T(8,128)(2,1)S(1)}, bf16[256,1024]{1,0:T(8,128)(2,1)S(1)}, bf16[256,1024]{1,0:T(8,128)(2,1)S...) custom-call(bf16[256,1024]{1,0:T(8,128)(2,1)S(1)} %get-tuple-element, ...), custom_call_target="tpu_custom_call", output_to_operand_aliasing={{6}: (12, {})} | custom-call | flops 6000000000 | bytes 4194304 | tf_op jit(solution)/shard_map/mlp/pallas_call | solution.py:283
  21.7 1.7 %sums.1 = (f32[64,1024]{1,0:T(8,128)S(1)}, f32[64,1024]{1,0:T(8,128)S(1)}, f32[128,1024]{1,0:T(8,128)S(1)}, f32[128,1024]{1,0:T(8,128)S(1)}) custom-call(f32[64,1024]{1,0:T(8,128)S(1)} %get-tuple-element.59.dn_b1, bf16[256,1024]{1,0:T(8,128)(2,1)S(1)} %get-tuple-element.60.du, bf16[256,1024]{1,0:T(8,128)(2,1)S(1)} %get-tuple-element.57.h, ...), custom_call_target="tpu_custom_call" | custom-call | flops 4000000000 | bytes 4194304 | tf_op jit(solution)/shard_map/sums/pallas_call | solution.py:319
  23.4 0.3 collective-permute-start.4
  23.8 1.1 %collective-permute-start.6 = (f32[64,1024]{1,0:T(8,128)S(1)}, f32[64,1024]{1,0:T(8,128)S(1)}, u32[]{:S(2)}, u32[]{:S(2)}) collective-permute-start(f32[64,1024]{1,0:T(8,128)S(1)} %get-tuple-element.69), channel_id=1, source_target_pairs={{0,2},{1,3},{2,0},{3,1},{4,6},{5,7},{6,4},{7,5}} | collective-permute-start | bytes 786440 | tf_op jit(solution)/shard_map/ppermute | solution.py:533
  24.9 0.0 collective-permute-start.5
  24.9 3.6 %grads1.1 = (f32[1024,1024]{1,0:T(8,128)}, f32[12576,1024]{1,0:T(8,128)}) custom-call(bf16[256,1024]{1,0:T(8,128)(2,1)S(1)} %get-tuple-element.63.n, bf16[256,1024]{1,0:T(8,128)(2,1)S(1)} %get-tuple-element.60.du, f32[96,1024]{1,0:T(8,128)S(1)} %get-tuple-element.49.zero, ...), custom_call_target="tpu_custom_call", output_to_operand_aliasing={{1}: (4, {})} | custom-call | flops 4000000000 | bytes 8388608 | tf_op jit(solution)/shard_map/grads1/pallas_call | solution.py:346
  28.5 0.0 collective-permute-done.4.y_sib
  28.5 3.3 %grads2.1 = (f32[1024,1024]{1,0:T(8,128)}, f32[64,1024]{1,0:T(8,128)S(1)}, f32[64,1024]{1,0:T(8,128)S(1)}, f32[12576,1024]{1,0:T(8,128)}) custom-call(bf16[256,1024]{1,0:T(8,128)(2,1)S(1)} %get-tuple-element.57.h, bf16[256,1024]{1,0:T(8,128)(2,1)S(1)} %get-tuple-element.58.d_full, ...), custom_call_target="tpu_custom_call", output_to_operand_aliasing={{3}: (5, {})} | custom-call | flops 4000000000 | bytes 8388608 | tf_op jit(solution)/shard_map/grads2/pallas_call | solution.py:378
  31.8 0.4 collective-permute-done.6.g2
  32.2 0.0 collective-permute-done.5.dn_sib
  32.2 0.2 dx_rows.1.order.dx
  32.4 1.2 %collective-permute-start.9 = (bf16[64,1024]{1,0:T(8,128)(2,1)S(1)}, bf16[64,1024]{1,0:T(8,128)(2,1)S(1)}, u32[]{:S(2)}, u32[]{:S(2)}) collective-permute-start(bf16[64,1024]{1,0:T(8,128)(2,1)S(1)} %dx_rows.1.order.dx), channel_id=1, source_target_pairs={{0,2},{1,3},{2,0},{3,1},{4,6},{5,7},{6,4},{7,5}} | collective-permute-start | bytes 393224 | tf_op jit(solution)/shard_map/ppermute | solution.py:533
  33.6 0.0 collective-permute-start.8
  33.6 0.8 %collective-permute-start.7 = (f32[64,1024]{1,0:T(8,128)S(1)}, f32[64,1024]{1,0:T(8,128)S(1)}, u32[]{:S(2)}, u32[]{:S(2)}) collective-permute-start(f32[64,1024]{1,0:T(8,128)S(1)} %get-tuple-element.71), channel_id=1, source_target_pairs={{0,2},{1,3},{2,0},{3,1},{4,6},{5,7},{6,4},{7,5}} | collective-permute-start | bytes 786440 | tf_op jit(solution)/shard_map/ppermute | solution.py:533
  34.4 3.8 %fill3.1 = (f32[8,128]{1,0:T(8,128)S(1)}, f32[12576,1024]{1,0:T(8,128)}) custom-call(f32[96,1024]{1,0:T(8,128)S(1)} %get-tuple-element.49.zero, bf16[64,1024]{1,0:T(8,128)(2,1)S(1)} %dx_rows.1.order.dx, f32[12576,1024]{1,0:T(8,128)} %get-tuple-element.75.table_in), custom_call_target="tpu_custom_call", output_to_operand_aliasing={{1}: (2, {})} | custom-call | flops 4000000000 | bytes 16777216 | tf_op jit(solution)/shard_map/fill3/pallas_call | solution.py:421
  38.2 0.5 %collective-permute-done.9.dx_far = bf16[64,1024]{1,0:T(8,128)(2,1)S(1)} collective-permute-done((bf16[64,1024]{1,0:T(8,128)(2,1)S(1)}, bf16[64,1024]{1,0:T(8,128)(2,1)S(1)}, u32[]{:S(2)}, u32[]{:S(2)}) %collective-permute-start.9) | collective-permute-done | bytes 131104 | tf_op jit(solution)/shard_map/ppermute | solution.py:533
  38.7 0.0 collective-permute-done.8.dx_sib
  38.8 1.4 %dx_all.1.dx = bf16[256,1024]{1,0:T(8,128)(2,1)S(1)} custom-call(bf16[64,1024]{1,0:T(8,128)(2,1)S(1)} %dx_rows.1.order.dx, bf16[64,1024]{1,0:T(8,128)(2,1)S(1)} %collective-permute-done.8.dx_sib, bf16[64,1024]{1,0:T(8,128)(2,1)S(1)} %collective-permute-done.9.dx_far, f32[8,128]{1,0:T(8,128)S(1)} %get-tuple-element.76.order), custom_call_target="tpu_custom_call" | custom-call | flops 2000000000 | bytes 1048576 | tf_op jit(solution)/shard_map/dx_all/pallas_call | solution.py:449
  40.1 2.9 %put_rows.1 = (f32[12576,1024]{1,0:T(8,128)}, f32[8,128]{1,0:T(8,128)S(1)}) custom-call(s32[512]{0:T(512)S(1)} %get-tuple-element.72.puts, bf16[256,256]{1,0:T(8,128)(2,1)S(1)} %get-tuple-element.73.same, bf16[256,1024]{1,0:T(8,128)(2,1)S(1)} %dx_all.1.dx, f32[96,1024]{1,0:T(8,128)S(1)} %get-tuple-element.49.zero, ...), custom_call_target="tpu_custom_call", output_to_operand_aliasing={{0}: (4, {})} | custom-call | flops 3000000000 | bytes 2097152 | tf_op jit(solution)/shard_map/put_rows/pallas_call | solution.py:500
  43.1 0.5 %collective-permute-done.7.y_in = f32[64,1024]{1,0:T(8,128)S(1)} collective-permute-done((f32[64,1024]{1,0:T(8,128)S(1)}, f32[64,1024]{1,0:T(8,128)S(1)}, u32[]{:S(2)}, u32[]{:S(2)}) %collective-permute-start.7) | collective-permute-done | bytes 262176 | tf_op jit(solution)/shard_map/ppermute | solution.py:533
  43.5 0.7 %finish.1 = bf16[64,1024]{1,0:T(8,128)(2,1)} custom-call(bf16[256,1024]{1,0:T(8,128)(2,1)S(1)} %get-tuple-element.52.x_f.x_own.x, f32[64,1024]{1,0:T(8,128)S(1)} %get-tuple-element.67.order.y, f32[64,1024]{1,0:T(8,128)S(1)} %collective-permute-done.7.y_in, f32[8,128]{1,0:T(8,128)S(1)} %get-tuple-element.78.order), custom_call_target="tpu_custom_call" | custom-call | flops 1000000000 | bytes 1048576 | tf_op jit(solution)/shard_map/finish/pallas_call | solution.py:518
Async XLA Ops:
  0.6 17.3 %copy-start = (bf16[64,1024]{1,0:T(8,128)(2,1)S(1)}, bf16[64,1024]{1,0:T(8,128)(2,1)}, u32[]{:S(2)}) copy-start(bf16[64,1024]{1,0:T(8,128)(2,1)} %d_own.5) | copy-start | bytes 393220
  0.6 17.3 %copy-start.1 = (bf16[1024]{0:T(1024)(128)(2,1)S(1)}, bf16[1024]{0:T(1024)(128)(2,1)}, u32[]{:S(2)}) copy-start(bf16[1024]{0:T(1024)(128)(2,1)} %gain.5) | copy-start | bytes 6148
  0.7 19.0 %collective-permute-start.2 = (bf16[64,1024]{1,0:T(8,128)(2,1)}, bf16[64,1024]{1,0:T(8,128)(2,1)S(1)}, u32[]{:S(2)}, u32[]{:S(2)}) collective-permute-start(bf16[64,1024]{1,0:T(8,128)(2,1)} %d_own.5), channel_id=1, source_target_pairs={{0,1},{1,0},{2,3},{3,2},{4,5},{5,4},{6,7},{7,6}} | collective-permute-start | bytes 393224 | tf_op jit(solution)/shard_map/ppermute | solution.py:533
  6.7 11.0 %collective-permute-start.1 = (bf16[64,1024]{1,0:T(8,128)(2,1)}, bf16[64,1024]{1,0:T(8,128)(2,1)S(1)}, u32[]{:S(2)}, u32[]{:S(2)}) collective-permute-start(bf16[64,1024]{1,0:T(8,128)(2,1)} %d_own.5), channel_id=1, source_target_pairs={{0,2},{1,3},{2,0},{3,1},{4,6},{5,7},{6,4},{7,5}} | collective-permute-start | bytes 393224 | tf_op jit(solution)/shard_map/ppermute | solution.py:533
  9.2 8.8 %collective-permute-start = (bf16[128,1024]{1,0:T(8,128)(2,1)S(1)}, bf16[128,1024]{1,0:T(8,128)(2,1)S(1)}, u32[]{:S(2)}, u32[]{:S(2)}) collective-permute-start(bf16[128,1024]{1,0:T(8,128)(2,1)S(1)} %get-tuple-element.45.order.send), channel_id=1, source_target_pairs={{0,2},{1,3},{2,0},{3,1},{4,6},{5,7},{6,4},{7,5}} | collective-permute-start | bytes 786440 | tf_op jit(solution)/shard_map/ppermute | solution.py:533
  17.7 1.9 %collective-permute-start.3 = (bf16[64,1024]{1,0:T(8,128)(2,1)S(1)}, bf16[64,1024]{1,0:T(8,128)(2,1)S(1)}, u32[]{:S(2)}, u32[]{:S(2)}) collective-permute-start(bf16[64,1024]{1,0:T(8,128)(2,1)S(1)} %collective-permute-done.1.d_far), channel_id=1, source_target_pairs={{0,1},{1,0},{2,3},{3,2},{4,5},{5,4},{6,7},{7,6}} | collective-permute-start | bytes 393224 | tf_op jit(solution)/shard_map/ppermute | solution.py:533
  23.4 5.0 %collective-permute-start.4 = (f32[128,1024]{1,0:T(8,128)S(1)}, f32[128,1024]{1,0:T(8,128)S(1)}, u32[]{:S(2)}, u32[]{:S(2)}) collective-permute-start(f32[128,1024]{1,0:T(8,128)S(1)} %get-tuple-element.62), channel_id=1, source_target_pairs={{0,1},{1,0},{2,3},{3,2},{4,5},{5,4},{6,7},{7,6}} | collective-permute-start | bytes 1572872 | tf_op jit(solution)/shard_map/ppermute | solution.py:533
  23.8 8.4 %collective-permute-start.6 = (f32[64,1024]{1,0:T(8,128)S(1)}, f32[64,1024]{1,0:T(8,128)S(1)}, u32[]{:S(2)}, u32[]{:S(2)}) collective-permute-start(f32[64,1024]{1,0:T(8,128)S(1)} %get-tuple-element.69), channel_id=1, source_target_pairs={{0,2},{1,3},{2,0},{3,1},{4,6},{5,7},{6,4},{7,5}} | collective-permute-start | bytes 786440 | tf_op jit(solution)/shard_map/ppermute | solution.py:533
  24.9 7.3 %collective-permute-start.5 = (f32[64,1024]{1,0:T(8,128)S(1)}, f32[64,1024]{1,0:T(8,128)S(1)}, u32[]{:S(2)}, u32[]{:S(2)}) collective-permute-start(f32[64,1024]{1,0:T(8,128)S(1)} %get-tuple-element.68), channel_id=1, source_target_pairs={{0,1},{1,0},{2,3},{3,2},{4,5},{5,4},{6,7},{7,6}} | collective-permute-start | bytes 786440 | tf_op jit(solution)/shard_map/ppermute | solution.py:533
  32.4 6.4 %collective-permute-start.9 = (bf16[64,1024]{1,0:T(8,128)(2,1)S(1)}, bf16[64,1024]{1,0:T(8,128)(2,1)S(1)}, u32[]{:S(2)}, u32[]{:S(2)}) collective-permute-start(bf16[64,1024]{1,0:T(8,128)(2,1)S(1)} %dx_rows.1.order.dx), channel_id=1, source_target_pairs={{0,2},{1,3},{2,0},{3,1},{4,6},{5,7},{6,4},{7,5}} | collective-permute-start | bytes 393224 | tf_op jit(solution)/shard_map/ppermute | solution.py:533
  33.6 5.2 %collective-permute-start.8 = (bf16[64,1024]{1,0:T(8,128)(2,1)S(1)}, bf16[64,1024]{1,0:T(8,128)(2,1)S(1)}, u32[]{:S(2)}, u32[]{:S(2)}) collective-permute-start(bf16[64,1024]{1,0:T(8,128)(2,1)S(1)} %dx_rows.1.order.dx), channel_id=1, source_target_pairs={{0,1},{1,0},{2,3},{3,2},{4,5},{5,4},{6,7},{7,6}} | collective-permute-start | bytes 393224 | tf_op jit(solution)/shard_map/ppermute | solution.py:533
  33.6 10.0 %collective-permute-start.7 = (f32[64,1024]{1,0:T(8,128)S(1)}, f32[64,1024]{1,0:T(8,128)S(1)}, u32[]{:S(2)}, u32[]{:S(2)}) collective-permute-start(f32[64,1024]{1,0:T(8,128)S(1)} %get-tuple-element.71), channel_id=1, source_target_pairs={{0,2},{1,3},{2,0},{3,1},{4,6},{5,7},{6,4},{7,5}} | collective-permute-start | bytes 786440 | tf_op jit(solution)/shard_map/ppermute | solution.py:533
